TPU v7x, 128 devices: a whole 4x4x4 slice. The times are simulated.
128 devices in a mesh: fsdp: 16 (over z, y), model: 8 (over x, core).
Axes of the slice: x: 4, y: 4, z: 4, core: 2. Of those that a mesh axis runs over, the one named last changes fastest.
Arguments:
- x_in: bfloat16 [16, 512, 4096], P('fsdp', 'model')
- dy_in: bfloat16 [16, 512, 4096], P('fsdp', 'model')
- norm_gain: float32 [4096], replicated
- w_qkv: bfloat16 [4096, 6144], P('fsdp', 'model')
- w_out: bfloat16 [4096, 4096], P('model', 'fsdp')
- w_gate: bfloat16 [4096, 14336], P('fsdp', 'model')
- w_up: bfloat16 [4096, 14336], P('fsdp', 'model')
- w_down: bfloat16 [14336, 4096], P('model', 'fsdp')
- rope_cos: float32 [512, 64], replicated
- rope_sin: float32 [512, 64], replicated
Outputs:
- output 1: bfloat16 [16, 512, 4096], P('fsdp', 'model')
- output 2: bfloat16 [16, 512, 4096], P('fsdp', 'model')
- output 3: float32 [4096, 6144], P('fsdp', 'model')
- output 4: float32 [4096, 4096], P('model', 'fsdp')
- output 5: float32 [4096, 14336], P('fsdp', 'model')
- output 6: float32 [4096, 14336], P('fsdp', 'model')
- output 7: float32 [14336, 4096], P('model', 'fsdp')
All inputs are finite; a program needn't handle non-finite values.
Results may differ from a plain program's by a relative error of at most 0.00910965.
Values are sent between devices in bfloat16 or wider.
A program may use at most 1 GiB of HBM per device.

v0:
```python
import functools

import jax
import jax.numpy as jnp
from jax import lax
from jax.experimental import pallas as pl
from jax.experimental.pallas import tpu as pltpu
from jax.sharding import Mesh, PartitionSpec as P


NORM_EPS = 1e-5
NZ = 4
NY = 4
NX = 4
NC = 2
HEAD_GROUP = 4
F32 = jnp.float32
BF16 = jnp.bfloat16
VMEM_LIMIT = 60 * 1024 * 1024
TILE = 256


def norm_fwd(row_vals, norm_gain):
    return row_vals * lax.rsqrt(jnp.mean(row_vals * row_vals, axis=-1, keepdims=True) + NORM_EPS) * norm_gain


def rotate(wide, cos_tab, sin_tab):
    return wide * cos_tab + pltpu.roll(wide, wide.shape[-1] // 2, wide.ndim - 1) * sin_tab


def rotate_back(wide, cos_tab, sin_tab):
    return wide * cos_tab - pltpu.roll(wide, wide.shape[-1] // 2, wide.ndim - 1) * sin_tab


def cost(flops, bytes_accessed):
    return pl.CostEstimate(flops=int(flops) // 20, bytes_accessed=int(bytes_accessed), transcendentals=0)


def params(**extra):
    return pltpu.CompilerParams(vmem_limit_bytes=VMEM_LIMIT, **extra)


def head_probs(q_rot, k_rot, scale):
    scores = dot_nt(q_rot, k_rot) * scale
    row_ids = lax.broadcasted_iota(jnp.int32, scores.shape, 0)
    col_ids = lax.broadcasted_iota(jnp.int32, scores.shape, 1)
    scores = jnp.where(row_ids >= col_ids, scores, -1e30)
    weights = jnp.exp(scores - jnp.max(scores, axis=-1, keepdims=True))
    return weights / jnp.sum(weights, axis=-1, keepdims=True)


def half_rows(core, idx, chunk):
    return pl.ds(pl.multiple_of((NC * idx + core) * chunk, chunk), chunk)


def chunk_rows(idx, chunk):
    return slice(idx * chunk, (idx + 1) * chunk)


def attn_fwd_kernel(heads, head, pos_ref, own_ref, other_ref, own_third_ref, other_third_ref, cos_ref, sin_ref, seq_ref, o_ref, o_other_ref, o_buf):
    core, odd = pos_ref[1], pos_ref[2]
    chunk = own_ref.shape[0] // NX
    width = heads * head
    mine = pl.ds(pl.multiple_of(width + odd * head, head), head)
    theirs = pl.ds(pl.multiple_of(width + (1 - odd) * head, head), head)
    for side, part_ref, third_ref in ((core, own_ref, own_third_ref), (1 - core, other_ref, other_third_ref)):
        for idx in range(NX):
            rows = half_rows(side, idx, chunk)
            seq_ref[0, rows, pl.ds(0, width)] = part_ref[chunk_rows(idx, chunk), :width]
            seq_ref[0, rows, mine] = part_ref[chunk_rows(idx, chunk), width:]
            seq_ref[0, rows, theirs] = third_ref[chunk_rows(idx, chunk), :]
    cos_tab, sin_tab = cos_ref[...], sin_ref[...]
    k_rot = rotate(seq_ref[0, :, width : width + head].astype(F32), cos_tab, sin_tab).astype(BF16)
    values = seq_ref[0, :, width + head :]
    for idx in range(heads):
        lanes = slice(idx * head, (idx + 1) * head)
        q_rot = rotate(seq_ref[0, :, lanes].astype(F32), cos_tab, sin_tab).astype(BF16)
        probs = head_probs(q_rot, k_rot, head**-0.5)
        o_buf[:, lanes] = dot_nn(probs.astype(BF16), values).astype(BF16)
    for side, out_ref in ((core, o_ref), (1 - core, o_other_ref)):
        for idx in range(NX):
            out_ref[chunk_rows(idx, chunk), :] = o_buf[half_rows(side, idx, chunk), :]


def attn_bwd_kernel(heads, head, pos_ref, seq_ref, own_ref, other_ref, cos_ref, sin_ref, dq_ref, keep_ref, send_ref, do_buf):
    core, odd = pos_ref[1], pos_ref[2]
    chunk = own_ref.shape[0] // NX
    width = heads * head
    for side, part_ref in ((core, own_ref), (1 - core, other_ref)):
        for idx in range(NX):
            do_buf[half_rows(side, idx, chunk), :] = part_ref[chunk_rows(idx, chunk), :]
    cos_tab, sin_tab = cos_ref[...], sin_ref[...]
    k_rot = rotate(seq_ref[0, :, width : width + head].astype(F32), cos_tab, sin_tab).astype(BF16)
    values = seq_ref[0, :, width + head :]
    d_keys = jnp.zeros(k_rot.shape, F32)
    d_values = jnp.zeros(k_rot.shape, F32)
    for idx in range(heads):
        lanes = slice(idx * head, (idx + 1) * head)
        q_rot = rotate(seq_ref[0, :, lanes].astype(F32), cos_tab, sin_tab).astype(BF16)
        d_out = do_buf[:, lanes]
        probs = head_probs(q_rot, k_rot, head**-0.5)
        d_values += dot_tn(probs.astype(BF16), d_out)
        d_probs = dot_nt(d_out, values).astype(BF16).astype(F32)
        d_scores = probs * (d_probs - jnp.sum(d_probs * probs, axis=-1, keepdims=True))
        d_scores = (d_scores * head**-0.5).astype(BF16)
        d_q_rot = dot_nn(d_scores, k_rot).astype(BF16)
        dq_ref[0, :, lanes] = rotate_back(d_q_rot.astype(F32), cos_tab, sin_tab).astype(BF16)
        d_keys += dot_tn(d_scores, q_rot)

    @pl.when(odd == 0)
    def _():
        keep_ref[0] = d_keys
        send_ref[0] = d_values

    @pl.when(odd == 1)
    def _():
        keep_ref[0] = d_values
        send_ref[0] = d_keys


def attn_post_kernel(heads, head, pos_ref, dq_ref, keep_ref, got_ref, cos_ref, sin_ref, own_ref, other_ref, third_buf):
    core, odd = pos_ref[1], pos_ref[2]
    chunk = own_ref.shape[0] // NX
    width = heads * head
    total = (keep_ref[0] + got_ref[0]).astype(BF16)

    @pl.when(odd == 0)
    def _():
        third_buf[...] = rotate_back(total.astype(F32), cos_ref[...], sin_ref[...]).astype(BF16)

    @pl.when(odd == 1)
    def _():
        third_buf[...] = total

    for side, out_ref in ((core, own_ref), (1 - core, other_ref)):
        for idx in range(NX):
            rows = half_rows(side, idx, chunk)
            out_ref[chunk_rows(idx, chunk), :width] = dq_ref[0, rows, :]
            out_ref[chunk_rows(idx, chunk), width:] = third_buf[rows, :]


def per_sequence(kernel, pos, args, specs, out_specs, out_shape, scratch, flops):
    return pl.pallas_call(
        kernel,
        grid_spec=pltpu.PrefetchScalarGridSpec(num_scalar_prefetch=1, grid=(2,), in_specs=specs, out_specs=out_specs, scratch_shapes=scratch),
        out_shape=out_shape,
        compiler_params=params(),
        cost_estimate=cost(flops, 4e6),
    )(pos, *args)


def own_spec(rows, width):
    return pl.BlockSpec((rows, width), lambda i, pos: (2 * pos[1] + i, 0))


def pair_spec(rows, width):
    return pl.BlockSpec((rows, width), lambda i, pos: (i, 0))


def seq_spec(seq, width):
    return pl.BlockSpec((1, seq, width), lambda i, pos: (i, 0, 0))


def table_spec(table):
    return pl.BlockSpec(table.shape, lambda i, pos: (0, 0))


def attn_fwd(pos, qkv_tok, other, own_third, other_third, cos_tab, sin_tab):
    seq, head = cos_tab.shape
    width = qkv_tok.shape[1] - head
    rows = seq // 2
    half = jax.ShapeDtypeStruct((seq, width), BF16)
    return per_sequence(
        functools.partial(attn_fwd_kernel, width // head, head),
        pos,
        (qkv_tok, other, own_third, other_third, cos_tab, sin_tab),
        [own_spec(rows, width + head), pair_spec(rows, width + head), pair_spec(rows, head), pair_spec(rows, head), table_spec(cos_tab), table_spec(sin_tab)],
        [seq_spec(seq, width + 2 * head), pair_spec(rows, width), pair_spec(rows, width)],
        [jax.ShapeDtypeStruct((2, seq, width + 2 * head), BF16), half, half],
        [pltpu.VMEM((seq, width), BF16)],
        16e9,
    )


def attn_bwd(pos, qkv_seq, d_attn, other, cos_tab, sin_tab):
    seq, head = cos_tab.shape
    width = d_attn.shape[1]
    rows = seq // 2
    part = jax.ShapeDtypeStruct((2, seq, head), F32)
    return per_sequence(
        functools.partial(attn_bwd_kernel, width // head, head),
        pos,
        (qkv_seq, d_attn, other, cos_tab, sin_tab),
        [seq_spec(seq, width + 2 * head), own_spec(rows, width), pair_spec(rows, width), table_spec(cos_tab), table_spec(sin_tab)],
        [seq_spec(seq, width), seq_spec(seq, head), seq_spec(seq, head)],
        [jax.ShapeDtypeStruct((2, seq, width), BF16), part, part],
        [pltpu.VMEM((seq, width), BF16)],
        16e9,
    )


def attn_post(pos, d_queries, keep, got, cos_tab, sin_tab):
    seq, head = cos_tab.shape
    width = d_queries.shape[2]
    rows = seq // 2
    half = jax.ShapeDtypeStruct((seq, width + head), BF16)
    return per_sequence(
        functools.partial(attn_post_kernel, width // head, head),
        pos,
        (d_queries, keep, got, cos_tab, sin_tab),
        [seq_spec(seq, width), seq_spec(seq, head), seq_spec(seq, head), table_spec(cos_tab), table_spec(sin_tab)],
        [pair_spec(rows, width + head), pair_spec(rows, width + head)],
        [half, half],
        [pltpu.VMEM((seq, head), BF16)],
        2e9,
    )


def act_fwd_kernel(half, ab_ref, u_ref, ut_ref):
    gate_val = ab_ref[:, :half].astype(F32)
    up_val = ab_ref[:, half:].astype(F32)
    act_val = gate_val * jax.nn.sigmoid(gate_val) * up_val
    u_ref[...] = act_val.astype(BF16)
    ut_ref[...] = act_val.T.astype(BF16)


def act_fwd(gate_up):
    tokens, width = gate_up.shape
    half = width // 2
    rows = tokens // 4
    return pl.pallas_call(
        functools.partial(act_fwd_kernel, half),
        grid=(4,),
        in_specs=[pl.BlockSpec((rows, width), lambda i: (i, 0))],
        out_specs=[pl.BlockSpec((rows, half), lambda i: (i, 0)), pl.BlockSpec((half, rows), lambda i: (0, i))],
        out_shape=[jax.ShapeDtypeStruct((tokens, half), BF16), jax.ShapeDtypeStruct((half, tokens), BF16)],
        compiler_params=params(),
        cost_estimate=cost(4e9, 8e6),
        name="act_fwd",
    )(gate_up)


def act_bwd_kernel(half, ab_ref, du_ref, dab_ref, dabt_ref):
    gate_val = ab_ref[:, :half].astype(F32)
    up_val = ab_ref[:, half:].astype(F32)
    d_act = du_ref[...].astype(F32)
    sig = jax.nn.sigmoid(gate_val)
    d_silu = d_act * up_val
    d_gate = d_silu * sig + d_silu * gate_val * (sig * (1.0 - sig))
    d_up = d_act * (gate_val * sig)
    dab_ref[:, :half] = d_gate.astype(BF16)
    dab_ref[:, half:] = d_up.astype(BF16)
    dabt_ref[:half, :] = d_gate.T.astype(BF16)
    dabt_ref[half:, :] = d_up.T.astype(BF16)


def act_bwd(gate_up, d_mixed):
    tokens, width = gate_up.shape
    half = width // 2
    rows = tokens // 4
    return pl.pallas_call(
        functools.partial(act_bwd_kernel, half),
        grid=(4,),
        in_specs=[pl.BlockSpec((rows, width), lambda i: (i, 0)), pl.BlockSpec((rows, half), lambda i: (i, 0))],
        out_specs=[pl.BlockSpec((rows, width), lambda i: (i, 0)), pl.BlockSpec((width, rows), lambda i: (0, i))],
        out_shape=[jax.ShapeDtypeStruct((tokens, width), BF16), jax.ShapeDtypeStruct((width, tokens), BF16)],
        compiler_params=params(),
        cost_estimate=cost(8e9, 14e6),
        name="act_bwd",
    )(gate_up, d_mixed)


def piece_block(pos_ref, step, other):
    core = pos_ref[1]
    return lax.rem(pos_ref[0] + step, NZ) * NC + (1 - core if other else core)


def half_start(pos_ref, part, half):
    return pl.multiple_of((1 - pos_ref[2] if part else pos_ref[2]) * half, half)


def nn_kernel(keys, first, count_out, pos_ref, acts_ref, *refs):
    count = len(keys)
    halves = refs[: 2 * count]
    outs = refs[2 * count : 2 * count + count_out]
    acts_buf, w_buf, total, acts_sem, w_sem = refs[2 * count + count_out :]
    block = acts_buf.shape[1] // count
    half = block // 2
    copies = []
    for idx in range(count):
        cols = pl.ds(pl.multiple_of(piece_block(pos_ref, *keys[idx]) * block, block), block)
        copies.append([pltpu.make_async_copy(acts_ref.at[:, cols], acts_buf.at[:, pl.ds(idx * block, block)], acts_sem.at[idx])])
        for part in range(2):
            rows = pl.ds(idx * block + half_start(pos_ref, part, half), half)
            copies[-1].append(pltpu.make_async_copy(halves[2 * idx + part], w_buf.at[rows], w_sem.at[2 * idx + part]))
    for group in copies:
        for copy in group:
            copy.start()
    for lo, hi in ((0, first), (first, count)):
        for group in copies[lo:hi]:
            for copy in group:
                copy.wait()
        depth = pl.ds(lo * block, (hi - lo) * block)
        start = 0
        for out_ref in outs:
            width = out_ref.shape[1]

            def step(out_lo, size, start=start, out_ref=out_ref, depth=depth, hi=hi):
                cols = pl.ds(pl.multiple_of(start + out_lo, 128), size)
                part = dot_nn(acts_buf[:, depth], w_buf[depth, cols])
                if hi == count:
                    out_ref[:, pl.ds(pl.multiple_of(out_lo, 128), size)] = (total[:, cols] + part).astype(BF16)
                else:
                    total[:, cols] = part

            whole = width // TILE
            if whole:
                pl.loop(0, whole)(lambda n: step(n * TILE, TILE))
            if width % TILE:
                step(whole * TILE, width % TILE)
            start += width


def nn_pieces(pos, acts, parts, widths):
    keys = [(step, other) for step in (0, 1, 3, 2) for other in range(2)]
    halves = [parts[step][other][part] for step, other in keys for part in range(2)]
    tokens, depth = acts.shape
    width = sum(widths)
    count = len(keys)
    anywhere = pl.BlockSpec(memory_space=pl.ANY)
    return pl.pallas_call(
        functools.partial(nn_kernel, keys, 2, len(widths)),
        grid_spec=pltpu.PrefetchScalarGridSpec(
            num_scalar_prefetch=1,
            grid=(1,),
            in_specs=[anywhere] * (1 + 2 * count),
            out_specs=[pl.BlockSpec((tokens, size), lambda i, pos: (0, 0)) for size in widths],
            scratch_shapes=[
                pltpu.VMEM((tokens, depth), BF16),
                pltpu.VMEM((depth, width), BF16),
                pltpu.VMEM((tokens, width), F32),
                pltpu.SemaphoreType.DMA((count,)),
                pltpu.SemaphoreType.DMA((2 * count,)),
            ],
        ),
        out_shape=[jax.ShapeDtypeStruct((tokens, size), BF16) for size in widths],
        compiler_params=params(),
        cost_estimate=cost(2 * tokens * depth * width, 2 * depth * (tokens + width)),
    )(pos, acts, *halves)


def nt_kernel(keys, count_left, pos_ref, *refs):
    count = len(keys)
    lefts = refs[:count_left]
    halves = refs[count_left : count_left + 2 * count]
    out_ref, left_buf, w_buf, out_buf, left_sem, w_sem, out_sem = refs[count_left + 2 * count :]
    block = out_buf.shape[2]
    half = block // 2
    slots = w_buf.shape[0]
    left_copies = []
    start = 0
    for idx, left in enumerate(lefts):
        left_copies.append(pltpu.make_async_copy(left, left_buf.at[:, pl.ds(start, left.shape[1])], left_sem.at[idx]))
        left_copies[-1].start()
        start += left.shape[1]

    def copies(idx):
        for part in range(2):
            rows = pl.ds(half_start(pos_ref, part, half), half)
            yield pltpu.make_async_copy(halves[2 * idx + part], w_buf.at[idx % slots, rows], w_sem.at[idx % slots, part])

    def out_copy(idx):
        cols = pl.ds(pl.multiple_of(piece_block(pos_ref, *keys[idx]) * block, block), block)
        return pltpu.make_async_copy(out_buf.at[idx % 2], out_ref.at[:, cols], out_sem.at[idx % 2])

    for idx in range(slots - 1):
        for copy in copies(idx):
            copy.start()
    for idx in range(count):
        if idx + slots - 1 < count:
            for copy in copies(idx + slots - 1):
                copy.start()
        for copy in copies(idx):
            copy.wait()
        if idx == 0:
            for copy in left_copies:
                copy.wait()
        if idx >= 2:
            out_copy(idx - 2).wait()
        out_buf[idx % 2] = dot_nt(left_buf[...], w_buf[idx % slots])
        out_copy(idx).start()
    for idx in range(count - 2, count):
        out_copy(idx).wait()


def nt_pieces(pos, lefts, parts):
    keys = [(step, other) for step in range(NZ) for other in range(2)]
    halves = [parts[step][other][part] for step, other in keys for part in range(2)]
    tokens = lefts[0].shape[0]
    block = 2 * halves[0].shape[0]
    depth = block * len(keys)
    width = halves[0].shape[1]
    slots = 3
    anywhere = pl.BlockSpec(memory_space=pl.ANY)
    return pl.pallas_call(
        functools.partial(nt_kernel, keys, len(lefts)),
        grid_spec=pltpu.PrefetchScalarGridSpec(
            num_scalar_prefetch=1,
            grid=(1,),
            in_specs=[anywhere] * (len(lefts) + len(halves)),
            out_specs=anywhere,
            scratch_shapes=[
                pltpu.VMEM((tokens, width), BF16),
                pltpu.VMEM((slots, block, width), BF16),
                pltpu.VMEM((2, tokens, block), F32),
                pltpu.SemaphoreType.DMA((len(lefts),)),
                pltpu.SemaphoreType.DMA((slots, 2)),
                pltpu.SemaphoreType.DMA((2,)),
            ],
        ),
        out_shape=jax.ShapeDtypeStruct((tokens, depth), F32),
        compiler_params=params(),
        cost_estimate=cost(2 * tokens * depth * width, 2 * depth * width + 4 * tokens * depth),
    )(pos, *lefts, *halves)


def picked_cols(pos_ref, idx, block):
    return pl.ds(pl.multiple_of((NC * idx + 1 - pos_ref[1]) * block, block), block)


def dma_kernel(kernel, pos, args, out_shape, scratch):
    anywhere = pl.BlockSpec(memory_space=pl.ANY)
    return pl.pallas_call(
        kernel,
        grid_spec=pltpu.PrefetchScalarGridSpec(
            num_scalar_prefetch=1, grid=(1,), in_specs=[anywhere] * len(args), out_specs=[anywhere] * len(out_shape), scratch_shapes=scratch
        ),
        out_shape=out_shape,
        compiler_params=params(),
        cost_estimate=cost(3e9, 16e6),
    )(pos, *args)


def pick_cols(pos, acts):
    tokens, depth = acts.shape
    block = depth // (NC * NZ)

    def kernel(pos_ref, in_ref, out_ref, buf, in_sem, out_sem):
        reads = [pltpu.make_async_copy(in_ref.at[:, picked_cols(pos_ref, idx, block)], buf.at[idx], in_sem.at[idx]) for idx in range(NZ)]
        writes = [pltpu.make_async_copy(buf.at[idx], out_ref.at[:, pl.ds(idx * block, block)], out_sem.at[idx]) for idx in range(NZ)]
        for read in reads:
            read.start()
        for read, write in zip(reads, writes):
            read.wait()
            write.start()
        for write in writes:
            write.wait()

    sems = pltpu.SemaphoreType.DMA((NZ,))
    return dma_kernel(kernel, pos, [acts], [jax.ShapeDtypeStruct((tokens, depth // 2), BF16)], [pltpu.VMEM((NZ, tokens, block), BF16), sems, sems])[0]


def settle_y(pos, own, left, right, far):
    chunk, depth = own.shape
    half = chunk // 2
    sources = [(0, 0, own), (3, 0, left), (1, 0, right), (2, 0, far[0]), (2, half, far[1])]

    def kernel(pos_ref, *refs):
        ins, (out0, out1, buf, in_sem, out_sem) = refs[: len(sources)], refs[len(sources) :]
        reads = []
        for idx, (step, start, array) in enumerate(sources):
            row = pl.multiple_of(lax.rem(pos_ref[3] + step, NY) * chunk, chunk) + start
            reads.append(pltpu.make_async_copy(ins[idx], buf.at[pl.ds(row, array.shape[0])], in_sem.at[idx]))
            reads[-1].start()
        for read in reads:
            read.wait()
        writes = [pltpu.make_async_copy(buf.at[pl.ds(idx * 2 * chunk, 2 * chunk)], out, out_sem.at[idx]) for idx, out in enumerate((out0, out1))]
        for write in writes:
            write.start()
        for write in writes:
            write.wait()

    out = jax.ShapeDtypeStruct((2 * chunk, depth), BF16)
    scratch = [pltpu.VMEM((NY * chunk, depth), BF16), pltpu.SemaphoreType.DMA((len(sources),)), pltpu.SemaphoreType.DMA((2,))]
    return dma_kernel(kernel, pos, [array for _, _, array in sources], [out, out], scratch)


def settle_x(pos, parts):
    sources = [(step, half, parts[step][half]) for step in range(NX) for half in range(2)]
    chunk = sources[0][2].shape[0] // 2
    depth = sources[0][2].shape[1]
    block = depth // (NC * NZ)
    blocks = 2 * len(sources)

    def kernel(pos_ref, *refs):
        ins, (all_ref, out_ref, buf, in_sem, all_sem, out_sem) = refs[: len(sources)], refs[len(sources) :]
        reads = []
        rows = []
        for idx, (step, half, _) in enumerate(sources):
            x_pos = lax.rem(pos_ref[4] + step, NX)
            for part in range(2):
                rows.append(pl.ds(pl.multiple_of(((2 * half + part) * NX + x_pos) * chunk, chunk), chunk))
                reads.append(pltpu.make_async_copy(ins[idx].at[pl.ds(part * chunk, chunk)], buf.at[rows[-1]], in_sem.at[2 * idx + part]))
                reads[-1].start()
        writes = []
        for idx in range(blocks):
            reads[idx].wait()
            writes.append(pltpu.make_async_copy(buf.at[rows[idx]], all_ref.at[rows[idx]], all_sem.at[idx]))
            for col in range(NZ):
                cols = picked_cols(pos_ref, col, block)
                writes.append(pltpu.make_async_copy(buf.at[rows[idx], cols], out_ref.at[rows[idx], pl.ds(col * block, block)], out_sem.at[idx, col]))
            for write in writes[-1 - NZ :]:
                write.start()
        for write in writes:
            write.wait()

    tokens = blocks * chunk
    out_shape = [jax.ShapeDtypeStruct((tokens, depth), BF16), jax.ShapeDtypeStruct((tokens, depth // 2), BF16)]
    scratch = [pltpu.VMEM((tokens, depth), BF16), pltpu.SemaphoreType.DMA((blocks,)), pltpu.SemaphoreType.DMA((blocks,)), pltpu.SemaphoreType.DMA((blocks, NZ))]
    return dma_kernel(kernel, pos, [array for _, _, array in sources], out_shape, scratch)


def grad_kernel(heights, pos_ref, *refs):
    pairs = len(heights)
    ins = refs[: 6 * pairs]
    outs = refs[6 * pairs : 6 * pairs + 2 * NZ]
    buf, sem = refs[6 * pairs + 2 * NZ :]
    step = pl.program_id(0)
    slot = lax.rem(step, 2)

    def out_copy(idx, part):
        return pltpu.make_async_copy(buf.at[idx % 2, part], outs[2 * idx + part], sem.at[idx % 2, part])

    for idx in range(2, NZ):

        @pl.when(step == idx)
        def _(idx=idx):
            for part in range(2):
                out_copy(idx - 2, part).wait()

    start = 0
    for idx, height in enumerate(heights):
        own, recv, acts0, acts1, recv0, recv1 = ins[6 * idx : 6 * idx + 6]
        for part, acts, acts_recv in ((0, acts0, recv0), (1, acts1, recv1)):
            buf[slot, part, start : start + height, :] = dot_nn(own[...], acts[...]) + dot_nn(recv[...], acts_recv[...])
        start += height
    for idx in range(NZ):

        @pl.when(step == idx)
        def _(idx=idx):
            for part in range(2):
                out_copy(idx, part).start()

    @pl.when(step == NZ - 1)
    def _():
        for idx in (NZ - 2, NZ - 1):
            for part in range(2):
                out_copy(idx, part).wait()


def grad_pieces(pos, pairs):
    tokens, depth = pairs[0][2].shape
    cols = depth // (NZ * NY)
    in_specs = []
    args = []

    def z_of(n, pos):
        return lax.rem(pos[0] + jnp.where(n == 0, 2, jnp.where(n == 1, 1, jnp.where(n == 2, 3, 0))), NZ)

    def bit(pos, part):
        return 1 - pos[2] if part else pos[2]

    for own, recv, acts, acts_recv, height, block in pairs:
        in_specs += [pl.BlockSpec((height, tokens), lambda n, pos, block=block: (block, 0))] * 2
        in_specs += [pl.BlockSpec((tokens, cols), lambda n, pos, part=part: (0, z_of(n, pos) * NY + 2 * pos[1] + bit(pos, part))) for part in range(2)]
        in_specs += [pl.BlockSpec((tokens, cols), lambda n, pos, part=part: (0, z_of(n, pos) * 2 + bit(pos, part))) for part in range(2)]
        args += [own, recv, acts, acts, acts_recv, acts_recv]
    heights = [pair[4] for pair in pairs]
    rows = sum(heights)
    return pl.pallas_call(
        functools.partial(grad_kernel, heights),
        grid_spec=pltpu.PrefetchScalarGridSpec(
            num_scalar_prefetch=1,
            grid=(NZ,),
            in_specs=in_specs,
            out_specs=[pl.BlockSpec(memory_space=pl.ANY)] * (2 * NZ),
            scratch_shapes=[pltpu.VMEM((2, 2, rows, cols), F32), pltpu.SemaphoreType.DMA((2, 2))],
        ),
        out_shape=[jax.ShapeDtypeStruct((rows, cols), F32)] * (2 * NZ),
        compiler_params=params(),
        cost_estimate=cost(4 * rows * tokens * cols * 2 * NZ, 4 * tokens * cols * 2 * NZ),
        name="grad",
    )(pos, *args)


def place(pos, first, second, height, block, transpose):
    cols = first.shape[1]
    spec = pl.BlockSpec((height, cols), lambda n, pos: (block, 0))

    def kernel(pos_ref, first_ref, second_ref, out_ref):
        for idx, ref in enumerate((first_ref, second_ref)):

            @pl.when(pl.program_id(0) == idx)
            def _(ref=ref):
                out_ref[...] = ref[...].T if transpose else ref[...]

    def order(n, pos):
        return jnp.where(n == 0, pos[2], 1 - pos[2])

    return pl.pallas_call(
        kernel,
        grid_spec=pltpu.PrefetchScalarGridSpec(
            num_scalar_prefetch=1,
            grid=(2,),
            in_specs=[spec, spec],
            out_specs=pl.BlockSpec((cols, height), lambda n, pos: (0, order(n, pos))) if transpose else pl.BlockSpec((height, cols), lambda n, pos: (order(n, pos), 0)),
        ),
        out_shape=jax.ShapeDtypeStruct((cols, 2 * height) if transpose else (2 * height, cols), F32),
        compiler_params=params(),
        cost_estimate=cost(2e9, 16 * height * cols),
    )(pos, first, second)


def after(val, *earlier):
    return lax.optimization_barrier((val, *earlier))[0]


def ring(step, size):
    return [(src, (src + step) % size) for src in range(size)]


def hop_z(val, step):
    return lax.ppermute(val, "z", ring(step, NZ))


def hop_y(val, step):
    return lax.ppermute(val, "y", ring(step, NY))


def hop_x(val, step):
    return lax.ppermute(val, "x", ring(step, NX))


def swap_c(val):
    return lax.ppermute(val, "c", [(0, 1), (1, 0)])


def swap_y(val):
    return lax.ppermute(val, "y", [(src, src ^ 1) for src in range(NY)])


def turn(val, flip):
    def place_of(y_pos, c_pos):
        return y_pos * NC + c_pos

    pairs = [(place_of(2 * a + b, c), place_of(2 * c + (b ^ flip), a)) for a in range(2) for b in range(2) for c in range(NC)]
    return lax.ppermute(val, ("y", "c"), pairs)


def swap_yc(val):
    pairs = [(y_pos * NC + c_pos, (y_pos ^ 1) * NC + 1 - c_pos) for y_pos in range(NY) for c_pos in range(NC)]
    return lax.ppermute(val, ("y", "c"), pairs)


def dot_nn(left, right):
    return lax.dot_general(left, right, (((1,), (0,)), ((), ())), preferred_element_type=F32)


def dot_nt(left, right):
    return lax.dot_general(left, right, (((1,), (1,)), ((), ())), preferred_element_type=F32)


def dot_tn(left, right):
    return lax.dot_general(left, right, (((0,), (0,)), ((), ())), preferred_element_type=F32)


def solution(mesh):
    wide_mesh = Mesh(mesh.devices.reshape(NZ, NY, NX, NC), ("z", "y", "x", "c"))
    rows = ("z", "y")
    cols = ("x", "c")
    act_spec = P(rows, cols, None)
    col_spec = P(rows, cols)
    row_spec = P(cols, rows)

    def layer(x_in, dy_in, norm_gain, w_qkv, w_out, w_gate, w_up, w_down, rope_cos, rope_sin):
        z_pos = lax.axis_index("z")
        y_pos = lax.axis_index("y")
        c_pos = lax.axis_index("c")
        even_y = y_pos % 2 == 0
        first_c = c_pos == 0
        pos = jnp.stack([z_pos, c_pos, y_pos % 2, y_pos, lax.axis_index("x")]).astype(jnp.int32)
        head = 2 * rope_cos.shape[1]
        seq = rope_cos.shape[0]
        ff_blk = w_gate.shape[1] // 2
        o_blk = w_out.shape[0] // 2
        qkv_blk = o_blk + head

        def gather_rows(blocks):
            return [turn(jnp.where(even_y, blocks[flip], blocks[1 - flip]), flip) for flip in range(2)]

        def gather_weight(piece):
            left = [hop_z(half, 1) for half in piece]
            right = [hop_z(half, -1) for half in piece]
            far = [hop_z(left[0], 1), hop_z(right[1], -1)]
            parts = []
            for mine in (piece, right, far, left):
                parts.append((mine, [swap_c(half) for half in mine]))
            return parts

        def grad_start(pairs, *earlier):
            far0, far1, up0, up1, down0, down1, own0, own1 = grad_pieces(after(pos, *earlier), pairs)
            far = (hop_z(far0, 1), hop_z(far1, -1))
            direct = (hop_z(up1, 1), hop_z(down0, -1))
            return (up0, down1), far, direct, (own0, own1)

        def grad_pass(state, *earlier):
            (up0, down1), far, direct, own = state
            passed = (hop_z(up0 + after(far[0], *earlier), 1), hop_z(down1 + far[1], -1))
            return direct, passed, own

        def grad_back(state, *earlier):
            direct, passed, own = state
            first = own[0] + after(passed[0], *earlier) + direct[1]
            second = own[1] + direct[0] + passed[1]
            return turn(first, 0), turn(second, 1)

        def my_rows(val, mine):
            return lax.dynamic_slice_in_dim(val, (c_pos if mine else 1 - c_pos) * seq, seq, axis=0)

        def both_rows(own, other):
            got = swap_c(other)
            return jnp.concatenate([jnp.where(first_c, own, got), jnp.where(first_c, got, own)], axis=0)

        cos_tab = jnp.concatenate([rope_cos, rope_cos], axis=1)
        sin_tab = jnp.concatenate([-rope_sin, rope_sin], axis=1)

        def qkv_cols(bit):
            first = 2 * head * bit
            third = HEAD_GROUP * head + head * bit
            return [w_qkv[:, first : first + 2 * head], w_qkv[:, third : third + head]]

        def block(weight, bit):
            size = weight.shape[1] // 2
            return weight[:, bit * size : (bit + 1) * size]

        down_t = w_down.T
        out_t = w_out.T
        wf_piece = gather_rows([jnp.concatenate([block(w_gate, j), block(w_up, j), *qkv_cols(j)], axis=1) for j in range(2)])
        ws_piece = gather_rows([jnp.concatenate([block(down_t, j), block(out_t, j)], axis=1) for j in range(2)])

        x_rows = x_in[0].astype(F32)
        normed, norm_pull = jax.vjp(lambda row_vals: norm_fwd(row_vals, norm_gain), x_rows)
        h_all = lax.all_gather(after(normed.astype(BF16), *wf_piece), ("y", "x"), axis=0, tiled=True)
        dy_own = dy_in[0]
        dy_half = dy_own.shape[0] // 2
        dy_left = hop_y(dy_own, 1)
        dy_right = hop_y(dy_own, -1)
        dy_far = [hop_y(dy_left[:dy_half], 1), hop_y(dy_right[dy_half:], -1)]
        dy_piece = settle_y(pos, dy_own, dy_left, dy_right, dy_far)
        dx_left = [hop_x(half, 1) for half in dy_piece]
        dx_right = [hop_x(half, -1) for half in dy_piece]
        dx_far = [hop_x(dx_left[0], 1), hop_x(dx_right[1], -1)]
        wf_parts = gather_weight(wf_piece)
        ws_parts = gather_weight(ws_piece)

        gate_up, qkv_tok = nn_pieces(pos, h_all, wf_parts, (2 * ff_blk, qkv_blk))
        third = qkv_tok[:, o_blk:]
        qkv_other = swap_c(my_rows(qkv_tok, False))
        third_own = swap_y(my_rows(third, True))
        third_other = swap_yc(my_rows(third, False))
        act_val, act_t = act_fwd(after(gate_up, qkv_tok))
        act_recv = swap_c(act_t)
        dy_all, dy_picked = settle_x(after(pos, act_t), (dy_piece, dx_right, dx_far, dx_left))
        dy_recv = swap_c(dy_picked)
        qkv_seq, attn_own, attn_other = attn_fwd(after(pos, dy_picked), qkv_tok, qkv_other, third_own, third_other, cos_tab, sin_tab)
        attn_tok = both_rows(attn_own, attn_other)
        g_act = grad_start([(act_t, act_recv, dy_all, dy_recv, ff_blk, 0)], attn_own)
        h_picked = pick_cols(after(pos, g_act[3][0]), h_all)
        h_recv = swap_c(h_picked)
        y_part = nt_pieces(after(pos, h_picked), [act_val, attn_tok], ws_parts)
        mix_sum = lax.psum_scatter(y_part, ("y", "x"), scatter_dimension=0, tiled=True)
        y_out = (x_rows + mix_sum).astype(BF16)[None]

        d_act, d_attn = nn_pieces(after(pos, y_part), dy_all, ws_parts, (ff_blk, o_blk))
        d_attn_other = swap_c(my_rows(d_attn, False))
        g_act = grad_pass(g_act, d_attn)
        d_gate_up, d_gate_up_t = act_bwd(gate_up, d_act)
        d_gate_up_recv = swap_c(d_gate_up_t)
        d_queries, keep, send = attn_bwd(after(pos, d_gate_up_t), qkv_seq, d_attn, d_attn_other, cos_tab, sin_tab)
        got = swap_y(send)
        g_gate = grad_start([(d_gate_up_t, d_gate_up_recv, h_all, h_recv, ff_blk, 0)], d_queries)
        g_up = grad_start([(d_gate_up_t, d_gate_up_recv, h_all, h_recv, ff_blk, 1)], g_gate[3][0])
        d_own, d_other = attn_post(after(pos, g_up[3][0]), d_queries, keep, got, cos_tab, sin_tab)
        d_qkv = both_rows(d_own, d_other)
        g_gate = grad_pass(g_gate, d_own)
        dh_part = nt_pieces(pos, [d_gate_up, d_qkv], wf_parts)
        d_h = lax.psum_scatter(dh_part, ("y", "x"), scatter_dimension=0, tiled=True)
        d_h = d_h.astype(BF16)
        dx_out = (dy_in[0].astype(F32) + norm_pull(d_h.astype(F32))[0]).astype(BF16)[None]

        attn_t = attn_tok.T
        d_qkv_t = d_qkv.T
        attn_recv = swap_c(attn_t)
        d_qkv_recv = swap_c(d_qkv_t)
        g_up = grad_pass(g_up, dh_part)
        g_attn = grad_start([(attn_t, attn_recv, dy_all, dy_recv, o_blk, 0), (d_qkv_t, d_qkv_recv, h_all, h_recv, qkv_blk, 0)], dh_part)
        b_act = grad_back(g_act, g_attn[3][0])
        g_attn = grad_pass(g_attn, b_act[0])
        b_gate = grad_back(g_gate)
        b_up = grad_back(g_up)
        b_attn = grad_back(g_attn)
        dw_down = place(pos, *b_act, ff_blk, 0, False)
        dw_gate = place(pos, *b_gate, ff_blk, 0, True)
        dw_up = place(pos, *b_up, ff_blk, 0, True)
        dw_out = place(pos, *b_attn, o_blk, 0, False)
        dw_q = place(pos, *b_attn, 2 * head, 1, True)
        dw_kv = place(pos, *b_attn, head, 2 * o_blk // head, True)
        dw_qkv = jnp.concatenate([dw_q, dw_kv], axis=1)
        return y_out, dx_out, dw_qkv, dw_out, dw_gate, dw_up, dw_down


    return jax.shard_map(
        layer,
        mesh=wide_mesh,
        in_specs=(act_spec, act_spec, P(), col_spec, row_spec, col_spec, col_spec, row_spec, P(), P()),
        out_specs=(act_spec, act_spec, col_spec, row_spec, col_spec, col_spec, row_spec),
        check_vma=False,
    )
```

profile of v0, /device:TPU:1, one launch (start us, length us, event | category | flops | bytes accessed | tf_op | source)
XLA Modules:
  0.0 779.7 jit_solution(18040249660134601220)
XLA Ops:
  12.5 4.1 collective-permute-start.1
  20.0 21.3 %collective-permute-done.1.refs_1_.refs_3_ = bf16[256,2176]{1,0:T(8,128)(2,1)S(1)} collective-permute-done((bf16[256,2176]{1,0:T(8,128)(2,1)}, bf16[256,2176]{1,0:T(8,128)(2,1)S(1)}, u32[]{:S(2)}, u32[]{:S(2)}) %collective-permute-start.1) | collective-permute-done | bytes 1114144 | tf_op jit(solution)/shard_map/ppermute | solution.py:657
  44.3 8.4 %collective-permute-done.17.refs_2_ = bf16[64,4096]{1,0:T(8,128)(2,1)S(1)} collective-permute-done((bf16[64,4096]{1,0:T(8,128)(2,1)S(1)}, bf16[64,4096]{1,0:T(8,128)(2,1)S(1)}, u32[]{:S(2)}, u32[]{:S(2)}) %collective-permute-start.17) | collective-permute-done | bytes 524320 | tf_op jit(solution)/shard_map/ppermute | solution.py:637
  59.2 10.9 %collective-permute-done.19.refs_4_ = bf16[32,4096]{1,0:T(8,128)(2,1)S(1)} collective-permute-done((bf16[32,4096]{1,0:T(8,128)(2,1)}, bf16[32,4096]{1,0:T(8,128)(2,1)S(1)}, u32[]{:S(2)}, u32[]{:S(2)}) %collective-permute-start.19) | collective-permute-done | bytes 262176 | tf_op jit(solution)/shard_map/ppermute | solution.py:637
  71.5 3.6 shard_map.154
  83.5 31.5 %collective-permute-done.22.refs_6_ = bf16[128,4096]{1,0:T(8,128)(2,1)} collective-permute-done((bf16[128,4096]{1,0:T(8,128)(2,1)}, bf16[128,4096]{1,0:T(8,128)(2,1)}, u32[]{:S(2)}, u32[]{:S(2)}) %collective-permute-start.22) | collective-permute-done | bytes 1048608 | tf_op jit(solution)/shard_map/ppermute | solution.py:641
  117.6 12.4 %collective-permute-done.21.refs_3_ = bf16[128,4096]{1,0:T(8,128)(2,1)} collective-permute-done((bf16[128,4096]{1,0:T(8,128)(2,1)}, bf16[128,4096]{1,0:T(8,128)(2,1)}, u32[]{:S(2)}, u32[]{:S(2)}) %collective-permute-start.21) | collective-permute-done | bytes 1048608 | tf_op jit(solution)/shard_map/ppermute | solution.py:641
  133.1 4.6 collective-permute-done.8.refs_8_.refs_14_
  137.7 17.7 %collective-permute-done.4.refs_4_.refs_6_ = bf16[256,2176]{1,0:T(8,128)(2,1)S(1)} collective-permute-done((bf16[256,2176]{1,0:T(8,128)(2,1)S(1)}, bf16[256,2176]{1,0:T(8,128)(2,1)S(1)}, u32[]{:S(2)}, u32[]{:S(2)}) %collective-permute-start.4) | collective-permute-done | bytes 1114144 | tf_op jit(solution)/shard_map/ppermute | solution.py:633
  158.8 20.5 %collective-permute-done.13.refs_13_.refs_11_ = bf16[256,2176]{1,0:T(8,128)(2,1)S(1)} collective-permute-done((bf16[256,2176]{1,0:T(8,128)(2,1)S(1)}, bf16[256,2176]{1,0:T(8,128)(2,1)S(1)}, u32[]{:S(2)}, u32[]{:S(2)}) %collective-permute-start.13) | collective-permute-done | bytes 1114144 | tf_op jit(solution)/shard_map/ppermute | solution.py:633
  186.9 28.5 %shard_map.153 = (bf16[1024,1792]{1,0:T(8,128)(2,1)}, bf16[1024,384]{1,0:T(8,128)(2,1)}) custom-call(s32[5]{0:T(128)} %stack.23.pos_ref, bf16[1024,4096]{1,0:T(8,128)(2,1)} %all-gather.2.cloned.1.call-done.acts_ref.in_ref.refs_2_.refs_3_.refs_8_.refs_9_, bf16[256,2176]{1,0:T(8,128)(2,1)} %copy-done.6, bf16[256,2176]{1,0:T(8,128)(2,1)} %copy-done.5, ...), custom_call_target="tpu_custom_call" | custom-call | flops 912680576 | bytes 26214400 | tf_op jit(solution)/shard_map/pallas_call | solution.py:331
  215.4 4.8 act_fwd.1
  220.3 11.5 %collective-permute-done.23.refs_4_ = bf16[128,4096]{1,0:T(8,128)(2,1)} collective-permute-done((bf16[128,4096]{1,0:T(8,128)(2,1)}, bf16[128,4096]{1,0:T(8,128)(2,1)}, u32[]{:S(2)}, u32[]{:S(2)}) %collective-permute-start.23) | collective-permute-done | bytes 1048608 | tf_op jit(solution)/shard_map/ppermute | solution.py:641
  231.8 9.2 %shard_map.155 = (bf16[1024,4096]{1,0:T(8,128)(2,1)}, bf16[1024,2048]{1,0:T(8,128)(2,1)}) custom-call(s32[5]{0:T(128)} %stack.23.pos_ref, bf16[128,4096]{1,0:T(8,128)(2,1)} %get-tuple-element.81.refs_0_, bf16[128,4096]{1,0:T(8,128)(2,1)} %get-tuple-element.82.refs_1_, bf16[128,4096]{1,0:T(8,128)(2,1)} %collective-permute-done.20.refs_2_, ...), custom_call_target="tpu_custom_call" | custom-call | flops 150000000 | bytes 16000000 | tf_op jit(solution)/shard_map/pallas_call | solution.py:433
  248.9 10.1 %collective-permute-done.33.refs_3_.refs_1_ = bf16[256,1152]{1,0:T(8,128)(2,1)S(1)} collective-permute-done((bf16[256,1152]{1,0:T(8,128)(2,1)S(1)}, bf16[256,1152]{1,0:T(8,128)(2,1)S(1)}, u32[]{:S(2)}, u32[]{:S(2)}) %collective-permute-start.33) | collective-permute-done | bytes 589856 | tf_op jit(solution)/shard_map/ppermute | solution.py:657
  262.1 13.8 %collective-permute-done.45.refs_15_.refs_9_ = bf16[256,1152]{1,0:T(8,128)(2,1)S(1)} collective-permute-done((bf16[256,1152]{1,0:T(8,128)(2,1)S(1)}, bf16[256,1152]{1,0:T(8,128)(2,1)S(1)}, u32[]{:S(2)}, u32[]{:S(2)}) %collective-permute-start.45) | collective-permute-done | bytes 589856 | tf_op jit(solution)/shard_map/ppermute | solution.py:633
  278.1 7.8 collective-permute-done.40.refs_14_.refs_8_
  294.5 4.2 collective-permute-done.28.other_third_ref
  311.5 5.6 shard_map.156
  320.1 13.3 %grad.4 = (f32[896,256]{1,0:T(8,128)}, f32[896,256]{1,0:T(8,128)}, f32[896,256]{1,0:T(8,128)}, f32[896,256]{1,0:T(8,128)}, f32[896,256]{1,0:T(8,128)}, /*index=5...) custom-call(s32[5]{0:T(128)} %stack.23.pos_ref, bf16[896,1024]{1,0:T(8,128)(2,1)} %get-tuple-element.79.refs_0_, ...), custom_call_target="tpu_custom_call" | custom-call | flops 375809632 | bytes 8388608 | tf_op jit(solution)/shard_map/grad/pallas_call | solution.py:580
  333.4 4.2 shard_map.157
  343.0 17.1 %shard_map.158 = f32[1024,4096]{1,0:T(8,128)} custom-call(s32[5]{0:T(128)} %stack.23.pos_ref, bf16[1024,896]{1,0:T(8,128)(2,1)} %get-tuple-element.92.refs_0_, bf16[1024,256]{1,0:T(8,128)(2,1)} %copy.40.refs_1_, bf16[256,1152]{1,0:T(8,128)(2,1)} %copy-done.23, bf16[256,1152]{1,0:T(8,128)(2,1)} %copy-done.22, ...), custom_call_target="tpu_custom_call" | custom-call | flops 483183808 | bytes 26214400 | tf_op jit(solution)/shard_map/pallas_call | solution.py:405
  360.1 17.8 %shard_map.159 = (bf16[1024,896]{1,0:T(8,128)(2,1)}, bf16[1024,256]{1,0:T(8,128)(2,1)}) custom-call(s32[5]{0:T(128)} %stack.23.pos_ref, bf16[1024,4096]{1,0:T(8,128)(2,1)} %get-tuple-element.88.refs_2_.refs_3_.acts_ref, bf16[256,1152]{1,0:T(8,128)(2,1)} %copy-done.23, bf16[256,1152]{1,0:T(8,128)(2,1)} %copy-done.22, ...), custom_call_target="tpu_custom_call" | custom-call | flops 483183808 | bytes 17825792 | tf_op jit(solution)/shard_map/pallas_call | solution.py:331
  377.9 6.9 act_bwd.1
  386.4 5.5 collective-permute-done.48.other_ref
  392.6 8.1 %shard_map.160 = (bf16[2,512,256]{2,1,0:T(8,128)(2,1)}, f32[2,512,128]{2,1,0:T(8,128)}, f32[2,512,128]{2,1,0:T(8,128)}) custom-call(s32[5]{0:T(128)} %stack.23.pos_ref, bf16[2,512,512]{2,1,0:T(8,128)(2,1)} %get-tuple-element.99.seq_ref, bf16[1024,256]{1,0:T(8,128)(2,1)} %get-tuple-element.100.own_ref, bf16[512,256]{1,0:T(8,128)(2,1)} %copy-done.82, ...), custom_call_target="tpu_custom_call" | custom-call | flops 800000000 | bytes 4000000 | tf_op jit(solution)/shard_map/pallas_call | solution.py:143
  404.2 13.3 %grad.5 = (f32[896,256]{1,0:T(8,128)}, f32[896,256]{1,0:T(8,128)}, f32[896,256]{1,0:T(8,128)}, f32[896,256]{1,0:T(8,128)}, f32[896,256]{1,0:T(8,128)}, /*index=5...) custom-call(s32[5]{0:T(128)} %stack.23.pos_ref, bf16[1792,1024]{1,0:T(8,128)(2,1)} %get-tuple-element.97.refs_0_, ...), custom_call_target="tpu_custom_call" | custom-call | flops 375809632 | bytes 8388608 | tf_op jit(solution)/shard_map/grad/pallas_call | solution.py:580
  417.5 13.3 %grad.6 = (f32[896,256]{1,0:T(8,128)}, f32[896,256]{1,0:T(8,128)}, f32[896,256]{1,0:T(8,128)}, f32[896,256]{1,0:T(8,128)}, f32[896,256]{1,0:T(8,128)}, /*index=5...) custom-call(s32[5]{0:T(128)} %stack.23.pos_ref, bf16[1792,1024]{1,0:T(8,128)(2,1)} %get-tuple-element.97.refs_0_, ...), custom_call_target="tpu_custom_call" | custom-call | flops 375809632 | bytes 8388608 | tf_op jit(solution)/shard_map/grad/pallas_call | solution.py:580
  439.2 27.3 %shard_map.162 = f32[1024,4096]{1,0:T(8,128)} custom-call(s32[5]{0:T(128)} %stack.23.pos_ref, bf16[1024,1792]{1,0:T(8,128)(2,1)} %get-tuple-element.96.refs_0_, bf16[1024,384]{1,0:T(8,128)(2,1)} %copy.44.refs_1_, bf16[256,2176]{1,0:T(8,128)(2,1)} %copy-done.6, bf16[256,2176]{1,0:T(8,128)(2,1)} %copy-done.5, bf16[256,2176]{1,0:T(8,128)(2,1)} %copy-done.12, ...), custom_call_target="tpu_custom_call" | custom-call | flops 912680576 | bytes 34603008 | tf_op jit(solution)/shard_map/pallas_call | solution.py:405
  473.7 15.8 %collective-permute-done.84 = f32[896,256]{1,0:T(8,128)S(1)} collective-permute-done((f32[896,256]{1,0:T(8,128)}, f32[896,256]{1,0:T(8,128)S(1)}, u32[]{:S(2)}, u32[]{:S(2)}) %collective-permute-start.84) | collective-permute-done | bytes 917536 | tf_op jit(solution)/shard_map/ppermute | solution.py:633
  493.5 15.7 %collective-permute-done.58 = f32[896,256]{1,0:T(8,128)S(1)} collective-permute-done((f32[896,256]{1,0:T(8,128)}, f32[896,256]{1,0:T(8,128)S(1)}, u32[]{:S(2)}, u32[]{:S(2)}) %collective-permute-start.58) | collective-permute-done | bytes 917536 | tf_op jit(solution)/shard_map/ppermute | solution.py:633
  512.7 16.0 %collective-permute-done.85 = f32[896,256]{1,0:T(8,128)S(1)} collective-permute-done((f32[896,256]{1,0:T(8,128)S(1)}, f32[896,256]{1,0:T(8,128)S(1)}, u32[]{:S(2)}, u32[]{:S(2)}) %collective-permute-start.85) | collective-permute-done | bytes 917536 | tf_op jit(solution)/shard_map/ppermute | solution.py:633
  534.5 17.3 %collective-permute-done.75 = f32[896,256]{1,0:T(8,128)S(1)} collective-permute-done((f32[896,256]{1,0:T(8,128)S(1)}, f32[896,256]{1,0:T(8,128)S(1)}, u32[]{:S(2)}, u32[]{:S(2)}) %collective-permute-start.75) | collective-permute-done | bytes 917536 | tf_op jit(solution)/shard_map/ppermute | solution.py:633
  551.9 19.6 %collective-permute-done.67 = f32[896,256]{1,0:T(8,128)S(1)} collective-permute-done((f32[896,256]{1,0:T(8,128)S(1)}, f32[896,256]{1,0:T(8,128)S(1)}, u32[]{:S(2)}, u32[]{:S(2)}) %collective-permute-start.67) | collective-permute-done | bytes 917536 | tf_op jit(solution)/shard_map/ppermute | solution.py:633
  573.6 17.5 %collective-permute-done.79 = f32[896,256]{1,0:T(8,128)S(1)} collective-permute-done((f32[896,256]{1,0:T(8,128)S(1)}, f32[896,256]{1,0:T(8,128)S(1)}, u32[]{:S(2)}, u32[]{:S(2)}) %collective-permute-start.79) | collective-permute-done | bytes 917536 | tf_op jit(solution)/shard_map/ppermute | solution.py:633
  592.0 13.1 %grad.7 = (f32[640,256]{1,0:T(8,128)}, f32[640,256]{1,0:T(8,128)}, f32[640,256]{1,0:T(8,128)}, f32[640,256]{1,0:T(8,128)}, f32[640,256]{1,0:T(8,128)}, /*index=5...) custom-call(s32[5]{0:T(128)} %stack.23.pos_ref, bf16[256,1024]{1,0:T(8,128)(2,1)} %get-tuple-element.160.refs_0_, ...), custom_call_target="tpu_custom_call" | custom-call | flops 268435456 | bytes 8388608 | tf_op jit(solution)/shard_map/grad/pallas_call | solution.py:580
  610.9 10.9 %collective-permute-start.59 = (f32[896,256]{1,0:T(8,128)S(1)}, f32[896,256]{1,0:T(8,128)S(1)}, u32[]{:S(2)}, u32[]{:S(2)}) collective-permute-start(f32[896,256]{1,0:T(8,128)S(1)} %add_add_fusion.6), channel_id=1, source_target_pairs={{0,0},{1,16},{8,8},{9,24},{16,1},{17,17},{24,9},{25,25},{2,2},{3,1... | collective-permute-start | bytes 2752520 | tf_op jit(solution)/shard_map/ppermute | solution.py:657
  625.0 21.9 %collective-permute-done.55 = f32[640,256]{1,0:T(8,128)S(1)} collective-permute-done((f32[640,256]{1,0:T(8,128)}, f32[640,256]{1,0:T(8,128)S(1)}, u32[]{:S(2)}, u32[]{:S(2)}) %collective-permute-start.55) | collective-permute-done | bytes 655392 | tf_op jit(solution)/shard_map/ppermute | solution.py:633
  657.6 10.3 %collective-permute-done.71 = f32[896,256]{1,0:T(8,128)S(1)} collective-permute-done((f32[896,256]{1,0:T(8,128)S(1)}, f32[896,256]{1,0:T(8,128)S(1)}, u32[]{:S(2)}, u32[]{:S(2)}) %collective-permute-start.71) | collective-permute-done | bytes 917536 | tf_op jit(solution)/shard_map/ppermute | solution.py:633
  667.9 7.6 collective-permute-start.86
  675.6 6.3 collective-permute-done.63
  681.9 7.8 %collective-permute-start.78 = (f32[896,256]{1,0:T(8,128)S(1)}, f32[896,256]{1,0:T(8,128)S(1)}, u32[]{:S(2)}, u32[]{:S(2)}) collective-permute-start(f32[896,256]{1,0:T(8,128)S(1)} %add_add_fusion.3), channel_id=1, source_target_pairs={{0,0},{1,16},{8,8},{9,24},{16,1},{17,17},{24,9},{25,25},{2,2},{3,1... | collective-permute-start | bytes 2752520 | tf_op jit(solution)/shard_map/ppermute | solution.py:657
  693.0 7.6 collective-permute-done.65
  700.5 8.1 %collective-permute-start.82 = (f32[896,256]{1,0:T(8,128)S(1)}, f32[896,256]{1,0:T(8,128)}, u32[]{:S(2)}, u32[]{:S(2)}) collective-permute-start(f32[896,256]{1,0:T(8,128)S(1)} %add_add_fusion.2), channel_id=1, source_target_pairs={{0,8},{1,24},{8,0},{9,16},{16,9},{17,25},{24,1},{25,17},{2,10},{3,... | collective-permute-start | bytes 2752520 | tf_op jit(solution)/shard_map/ppermute | solution.py:657
  714.6 5.3 collective-permute-start.74
  730.5 3.7 shard_map.167
  735.7 14.2 %collective-permute-done.74.second_ref = f32[896,256]{1,0:T(8,128)} collective-permute-done((f32[896,256]{1,0:T(8,128)S(1)}, f32[896,256]{1,0:T(8,128)}, u32[]{:S(2)}, u32[]{:S(2)}) %collective-permute-start.74) | collective-permute-done | bytes 917536 | tf_op jit(solution)/shard_map/ppermute | solution.py:657
  750.0 3.7 shard_map.166
  (381 shorter events, 184.5 us)
Async XLA Ops:
  7.2 179.7 %all-gather.2.cloned.1.call-start = ((), (), s32[]{:S(2)}) async-start(), calls=%async_computation.2 | async-start | bytes 8912896 | tf_op jit(solution)/shard_map/all_gather | solution.py:753
  12.5 28.8 %collective-permute-start.1 = (bf16[256,2176]{1,0:T(8,128)(2,1)}, bf16[256,2176]{1,0:T(8,128)(2,1)S(1)}, u32[]{:S(2)}, u32[]{:S(2)}) collective-permute-start(bf16[256,2176]{1,0:T(8,128)(2,1)} %get-tuple-element.146), channel_id=1, source_target_pairs={{0,8},{1,24},{8,0},{9,16},{16,9},{17,25},{24,1},{25,17},{2,10},{3,... | collective-permute-start | bytes 3342344 | tf_op jit(solution)/shard_map/ppermute | solution.py:657
  42.3 726.4 %reduce-scatter.5.cloned.1.call-start = ((), (), s32[]{:S(2)}) async-start(), calls=%async_computation.4 | async-start | bytes 17825792 | tf_op jit(solution)/shard_map/reduce_scatter | solution.py:797
  75.1 39.9 %collective-permute-start.22 = (bf16[128,4096]{1,0:T(8,128)(2,1)}, bf16[128,4096]{1,0:T(8,128)(2,1)}, u32[]{:S(2)}, u32[]{:S(2)}) collective-permute-start(bf16[128,4096]{1,0:T(8,128)(2,1)} %get-tuple-element.81.refs_0_), channel_id=1, source_target_pairs={{0,2},{2,4},{4,6},{6,0},{1,3},{3,5},{5,7},{7,1},{8,10},{10,12},{12... | collective-permute-start | bytes 3145736 | tf_op jit(solution)/shard_map/ppermute | solution.py:641
  76.6 54.9 %collective-permute-start.9 = (bf16[256,2176]{1,0:T(8,128)(2,1)S(1)}, bf16[256,2176]{1,0:T(8,128)(2,1)S(1)}, u32[]{:S(2)}, u32[]{:S(2)}) collective-permute-start(bf16[256,2176]{1,0:T(8,128)(2,1)S(1)} %collective-permute-done.1.refs_1_.refs_3_), channel_id=1, source_target_pairs={{0,32},{32,64},{64,96},{96,0},{1,33},{33,65},{65,97},{97,1},{2,34}... | collective-permute-start | bytes 3342344 | tf_op jit(solution)/shard_map/ppermute | solution.py:633
  78.3 54.5 %collective-permute-start.5 = (bf16[256,2176]{1,0:T(8,128)(2,1)S(1)}, bf16[256,2176]{1,0:T(8,128)(2,1)S(1)}, u32[]{:S(2)}, u32[]{:S(2)}) collective-permute-start(bf16[256,2176]{1,0:T(8,128)(2,1)S(1)} %collective-permute-done.1.refs_1_.refs_3_), channel_id=1, source_target_pairs={{0,96},{32,0},{64,32},{96,64},{1,97},{33,1},{65,33},{97,65},{2,98}... | collective-permute-start | bytes 3342344 | tf_op jit(solution)/shard_map/ppermute | solution.py:633
  80.0 52.9 %collective-permute-start.3 = (bf16[256,2176]{1,0:T(8,128)(2,1)S(1)}, bf16[256,2176]{1,0:T(8,128)(2,1)S(1)}, u32[]{:S(2)}, u32[]{:S(2)}) collective-permute-start(bf16[256,2176]{1,0:T(8,128)(2,1)S(1)} %collective-permute-done.1.refs_1_.refs_3_), channel_id=1, source_target_pairs={{0,1},{1,0},{2,3},{3,2},{4,5},{5,4},{6,7},{7,6},{8,9},{9,8},{10,11... | collective-permute-start | bytes 3342344 | tf_op jit(solution)/shard_map/ppermute | solution.py:645
  82.0 48.0 %collective-permute-start.21 = (bf16[128,4096]{1,0:T(8,128)(2,1)}, bf16[128,4096]{1,0:T(8,128)(2,1)}, u32[]{:S(2)}, u32[]{:S(2)}) collective-permute-start(bf16[128,4096]{1,0:T(8,128)(2,1)} %get-tuple-element.82.refs_1_), channel_id=1, source_target_pairs={{0,6},{2,0},{4,2},{6,4},{1,7},{3,1},{5,3},{7,5},{8,14},{10,8},{12,... | collective-permute-start | bytes 3145736 | tf_op jit(solution)/shard_map/ppermute | solution.py:641
  131.5 26.6 %collective-permute-start.2 = (bf16[256,2176]{1,0:T(8,128)(2,1)S(1)}, bf16[256,2176]{1,0:T(8,128)(2,1)S(1)}, u32[]{:S(2)}, u32[]{:S(2)}) collective-permute-start(bf16[256,2176]{1,0:T(8,128)(2,1)S(1)} %collective-permute-done.refs_0_.refs_2_), channel_id=1, source_target_pairs={{0,1},{1,0},{2,3},{3,2},{4,5},{5,4},{6,7},{7,6},{8,9},{9,8},{10,11... | collective-permute-start | bytes 3342344 | tf_op jit(solution)/shard_map/ppermute | solution.py:645
  132.9 46.4 %collective-permute-start.13 = (bf16[256,2176]{1,0:T(8,128)(2,1)S(1)}, bf16[256,2176]{1,0:T(8,128)(2,1)S(1)}, u32[]{:S(2)}, u32[]{:S(2)}) collective-permute-start(bf16[256,2176]{1,0:T(8,128)(2,1)S(1)} %collective-permute-done.5.refs_5_.refs_7_), channel_id=1, source_target_pairs={{0,96},{32,0},{64,32},{96,64},{1,97},{33,1},{65,33},{97,65},{2,98}... | collective-permute-start | bytes 3342344 | tf_op jit(solution)/shard_map/ppermute | solution.py:633
  137.7 43.2 %collective-permute-start.12 = (bf16[256,2176]{1,0:T(8,128)(2,1)S(1)}, bf16[256,2176]{1,0:T(8,128)(2,1)S(1)}, u32[]{:S(2)}, u32[]{:S(2)}) collective-permute-start(bf16[256,2176]{1,0:T(8,128)(2,1)S(1)} %collective-permute-done.8.refs_8_.refs_14_), channel_id=1, source_target_pairs={{0,32},{32,64},{64,96},{96,0},{1,33},{33,65},{65,97},{97,1},{2,34}... | collective-permute-start | bytes 3342344 | tf_op jit(solution)/shard_map/ppermute | solution.py:633
  181.0 39.3 %collective-permute-start.20 = (bf16[128,4096]{1,0:T(8,128)(2,1)}, bf16[128,4096]{1,0:T(8,128)(2,1)}, u32[]{:S(2)}, u32[]{:S(2)}) collective-permute-start(bf16[128,4096]{1,0:T(8,128)(2,1)} %get-tuple-element.81.refs_0_), channel_id=1, source_target_pairs={{0,6},{2,0},{4,2},{6,4},{1,7},{3,1},{5,3},{7,5},{8,14},{10,8},{12,... | collective-permute-start | bytes 3145736 | tf_op jit(solution)/shard_map/ppermute | solution.py:641
  183.7 36.5 %collective-permute-start.25 = (bf16[128,4096]{1,0:T(8,128)(2,1)}, bf16[128,4096]{1,0:T(8,128)(2,1)}, u32[]{:S(2)}, u32[]{:S(2)}) collective-permute-start(bf16[128,4096]{1,0:T(8,128)(2,1)} %get-tuple-element.82.refs_1_), channel_id=1, source_target_pairs={{0,2},{2,4},{4,6},{6,0},{1,3},{3,5},{5,7},{7,1},{8,10},{10,12},{12... | collective-permute-start | bytes 3145736 | tf_op jit(solution)/shard_map/ppermute | solution.py:641
  183.8 48.0 %collective-permute-start.23 = (bf16[128,4096]{1,0:T(8,128)(2,1)}, bf16[128,4096]{1,0:T(8,128)(2,1)}, u32[]{:S(2)}, u32[]{:S(2)}) collective-permute-start(bf16[128,4096]{1,0:T(8,128)(2,1)} %collective-permute-done.22.refs_6_), channel_id=1, source_target_pairs={{0,2},{2,4},{4,6},{6,0},{1,3},{3,5},{5,7},{7,1},{8,10},{10,12},{12... | collective-permute-start | bytes 3145736 | tf_op jit(solution)/shard_map/ppermute | solution.py:641
  184.0 47.8 %collective-permute-start.24 = (bf16[128,4096]{1,0:T(8,128)(2,1)}, bf16[128,4096]{1,0:T(8,128)(2,1)}, u32[]{:S(2)}, u32[]{:S(2)}) collective-permute-start(bf16[128,4096]{1,0:T(8,128)(2,1)} %collective-permute-done.21.refs_3_), channel_id=1, source_target_pairs={{0,6},{2,0},{4,2},{6,4},{1,7},{3,1},{5,3},{7,5},{8,14},{10,8},{12,... | collective-permute-start | bytes 3145736 | tf_op jit(solution)/shard_map/ppermute | solution.py:641
  241.0 78.5 %collective-permute-start.30 = (bf16[1024,2048]{1,0:T(8,128)(2,1)}, bf16[1024,2048]{1,0:T(8,128)(2,1)}, u32[]{:S(2)}, u32[]{:S(2)}) collective-permute-start(bf16[1024,2048]{1,0:T(8,128)(2,1)} %get-tuple-element.83), channel_id=1, source_target_pairs={{0,1},{1,0},{2,3},{3,2},{4,5},{5,4},{6,7},{7,6},{8,9},{9,8},{10,11... | collective-permute-start | bytes 12582920 | tf_op jit(solution)/shard_map/ppermute | solution.py:645
  275.9 43.7 %collective-permute-start.29 = (bf16[896,1024]{1,0:T(8,128)(2,1)}, bf16[896,1024]{1,0:T(8,128)(2,1)}, u32[]{:S(2)}, u32[]{:S(2)}) collective-permute-start(bf16[896,1024]{1,0:T(8,128)(2,1)} %get-tuple-element.79.refs_0_), channel_id=1, source_target_pairs={{0,1},{1,0},{2,3},{3,2},{4,5},{5,4},{6,7},{7,6},{8,9},{9,8},{10,11... | collective-permute-start | bytes 5505032 | tf_op jit(solution)/shard_map/ppermute | solution.py:645
  338.4 63.9 %collective-permute-start.50 = (bf16[1024,2048]{1,0:T(8,128)(2,1)}, bf16[1024,2048]{1,0:T(8,128)(2,1)}, u32[]{:S(2)}, u32[]{:S(2)}) collective-permute-start(bf16[1024,2048]{1,0:T(8,128)(2,1)} %shard_map.157), channel_id=1, source_target_pairs={{0,1},{1,0},{2,3},{3,2},{4,5},{5,4},{6,7},{7,6},{8,9},{9,8},{10,11... | collective-permute-start | bytes 12582920 | tf_op jit(solution)/shard_map/ppermute | solution.py:645
  400.7 30.2 %collective-permute-start.51 = (f32[2,512,128]{2,1,0:T(8,128)}, f32[2,512,128]{2,1,0:T(8,128)}, u32[]{:S(2)}, u32[]{:S(2)}) collective-permute-start(f32[2,512,128]{2,1,0:T(8,128)} %get-tuple-element.108), channel_id=1, source_target_pairs={{0,8},{8,0},{16,24},{24,16},{1,9},{9,1},{17,25},{25,17},{2,10},{10... | collective-permute-start | bytes 1572872 | tf_op jit(solution)/shard_map/ppermute | solution.py:649
  466.5 303.8 %reduce-scatter.3.cloned.1.call-start = ((), (), s32[]{:S(2)}) async-start(), calls=%async_computation.3 | async-start | bytes 17825792 | tf_op jit(solution)/shard_map/reduce_scatter | solution.py:781
  470.0 39.2 %collective-permute-start.58 = (f32[896,256]{1,0:T(8,128)}, f32[896,256]{1,0:T(8,128)S(1)}, u32[]{:S(2)}, u32[]{:S(2)}) collective-permute-start(f32[896,256]{1,0:T(8,128)} %get-tuple-element.119), channel_id=1, source_target_pairs={{0,96},{32,0},{64,32},{96,64},{1,97},{33,1},{65,33},{97,65},{2,98}... | collective-permute-start | bytes 2752520 | tf_op jit(solution)/shard_map/ppermute | solution.py:633
  472.7 40.0 %collective-permute-start.83 = (f32[896,256]{1,0:T(8,128)}, f32[896,256]{1,0:T(8,128)S(1)}, u32[]{:S(2)}, u32[]{:S(2)}) collective-permute-start(f32[896,256]{1,0:T(8,128)} %get-tuple-element.143), channel_id=1, source_target_pairs={{0,32},{32,64},{64,96},{96,0},{1,33},{33,65},{65,97},{97,1},{2,34}... | collective-permute-start | bytes 2752520 | tf_op jit(solution)/shard_map/ppermute | solution.py:633
  489.7 39.1 %collective-permute-start.85 = (f32[896,256]{1,0:T(8,128)S(1)}, f32[896,256]{1,0:T(8,128)S(1)}, u32[]{:S(2)}, u32[]{:S(2)}) collective-permute-start(f32[896,256]{1,0:T(8,128)S(1)} %add.137), channel_id=1, source_target_pairs={{0,96},{32,0},{64,32},{96,64},{1,97},{33,1},{65,33},{97,65},{2,98}... | collective-permute-start | bytes 2752520 | tf_op jit(solution)/shard_map/ppermute | solution.py:633
  493.3 38.9 %collective-permute-start.57 = (f32[896,256]{1,0:T(8,128)S(1)}, f32[896,256]{1,0:T(8,128)S(1)}, u32[]{:S(2)}, u32[]{:S(2)}) collective-permute-start(f32[896,256]{1,0:T(8,128)S(1)} %add.115), channel_id=1, source_target_pairs={{0,32},{32,64},{64,96},{96,0},{1,33},{33,65},{65,97},{97,1},{2,34}... | collective-permute-start | bytes 2752520 | tf_op jit(solution)/shard_map/ppermute | solution.py:633
  493.4 58.3 %collective-permute-start.75 = (f32[896,256]{1,0:T(8,128)S(1)}, f32[896,256]{1,0:T(8,128)S(1)}, u32[]{:S(2)}, u32[]{:S(2)}) collective-permute-start(f32[896,256]{1,0:T(8,128)S(1)} %copy-done.79), channel_id=1, source_target_pairs={{0,32},{32,64},{64,96},{96,0},{1,33},{33,65},{65,97},{97,1},{2,34}... | collective-permute-start | bytes 2752520 | tf_op jit(solution)/shard_map/ppermute | solution.py:633
  509.2 42.6 %collective-permute-start.77 = (f32[896,256]{1,0:T(8,128)S(1)}, f32[896,256]{1,0:T(8,128)}, u32[]{:S(2)}, u32[]{:S(2)}) collective-permute-start(f32[896,256]{1,0:T(8,128)S(1)} %copy-done.78), channel_id=1, source_target_pairs={{0,96},{32,0},{64,32},{96,64},{1,97},{33,1},{65,33},{97,65},{2,98}... | collective-permute-start | bytes 2752520 | tf_op jit(solution)/shard_map/ppermute | solution.py:633
  512.6 58.9 %collective-permute-start.67 = (f32[896,256]{1,0:T(8,128)S(1)}, f32[896,256]{1,0:T(8,128)S(1)}, u32[]{:S(2)}, u32[]{:S(2)}) collective-permute-start(f32[896,256]{1,0:T(8,128)S(1)} %copy-done.77), channel_id=1, source_target_pairs={{0,32},{32,64},{64,96},{96,0},{1,33},{33,65},{65,97},{97,1},{2,34}... | collective-permute-start | bytes 2752520 | tf_op jit(solution)/shard_map/ppermute | solution.py:633
  529.8 61.3 %collective-permute-start.79 = (f32[896,256]{1,0:T(8,128)S(1)}, f32[896,256]{1,0:T(8,128)S(1)}, u32[]{:S(2)}, u32[]{:S(2)}) collective-permute-start(f32[896,256]{1,0:T(8,128)S(1)} %copy-done.76), channel_id=1, source_target_pairs={{0,32},{32,64},{64,96},{96,0},{1,33},{33,65},{65,97},{97,1},{2,34}... | collective-permute-start | bytes 2752520 | tf_op jit(solution)/shard_map/ppermute | solution.py:633
  532.2 58.9 %collective-permute-start.54 = (bf16[384,1024]{1,0:T(8,128)(2,1)S(1)}, bf16[384,1024]{1,0:T(8,128)(2,1)S(1)}, u32[]{:S(2)}, u32[]{:S(2)}) collective-permute-start(bf16[384,1024]{1,0:T(8,128)(2,1)S(1)} %get-tuple-element.156.refs_6_), channel_id=1, source_target_pairs={{0,1},{1,0},{2,3},{3,2},{4,5},{5,4},{6,7},{7,6},{8,9},{9,8},{10,11... | collective-permute-start | bytes 2359304 | tf_op jit(solution)/shard_map/ppermute | solution.py:645
  551.8 53.3 %collective-permute-start.80 = (f32[896,256]{1,0:T(8,128)}, f32[896,256]{1,0:T(8,128)}, u32[]{:S(2)}, u32[]{:S(2)}) collective-permute-start(f32[896,256]{1,0:T(8,128)} %get-tuple-element.141), channel_id=1, source_target_pairs={{0,96},{32,0},{64,32},{96,64},{1,97},{33,1},{65,33},{97,65},{2,98}... | collective-permute-start | bytes 2752520 | tf_op jit(solution)/shard_map/ppermute | solution.py:633
  551.8 53.9 %collective-permute-start.69 = (f32[896,256]{1,0:T(8,128)}, f32[896,256]{1,0:T(8,128)}, u32[]{:S(2)}, u32[]{:S(2)}) collective-permute-start(f32[896,256]{1,0:T(8,128)} %get-tuple-element.129), channel_id=1, source_target_pairs={{0,96},{32,0},{64,32},{96,64},{1,97},{33,1},{65,33},{97,65},{2,98}... | collective-permute-start | bytes 2752520 | tf_op jit(solution)/shard_map/ppermute | solution.py:633
  571.5 39.4 %collective-permute-start.72 = (f32[896,256]{1,0:T(8,128)}, f32[896,256]{1,0:T(8,128)}, u32[]{:S(2)}, u32[]{:S(2)}) collective-permute-start(f32[896,256]{1,0:T(8,128)} %get-tuple-element.133), channel_id=1, source_target_pairs={{0,96},{32,0},{64,32},{96,64},{1,97},{33,1},{65,33},{97,65},{2,98}... | collective-permute-start | bytes 2752520 | tf_op jit(solution)/shard_map/ppermute | solution.py:633
  591.1 58.4 %collective-permute-start.76 = (f32[896,256]{1,0:T(8,128)}, f32[896,256]{1,0:T(8,128)}, u32[]{:S(2)}, u32[]{:S(2)}) collective-permute-start(f32[896,256]{1,0:T(8,128)} %add.130), channel_id=1, source_target_pairs={{0,32},{32,64},{64,96},{96,0},{1,33},{33,65},{65,97},{97,1},{2,34}... | collective-permute-start | bytes 2752520 | tf_op jit(solution)/shard_map/ppermute | solution.py:633
  592.0 57.6 %collective-permute-start.68 = (f32[896,256]{1,0:T(8,128)}, f32[896,256]{1,0:T(8,128)}, u32[]{:S(2)}, u32[]{:S(2)}) collective-permute-start(f32[896,256]{1,0:T(8,128)} %add.124), channel_id=1, source_target_pairs={{0,32},{32,64},{64,96},{96,0},{1,33},{33,65},{65,97},{97,1},{2,34}... | collective-permute-start | bytes 2752520 | tf_op jit(solution)/shard_map/ppermute | solution.py:633
  605.1 41.7 %collective-permute-start.55 = (f32[640,256]{1,0:T(8,128)}, f32[640,256]{1,0:T(8,128)S(1)}, u32[]{:S(2)}, u32[]{:S(2)}) collective-permute-start(f32[640,256]{1,0:T(8,128)} %get-tuple-element.114), channel_id=1, source_target_pairs={{0,32},{32,64},{64,96},{96,0},{1,33},{33,65},{65,97},{97,1},{2,34}... | collective-permute-start | bytes 1966088 | tf_op jit(solution)/shard_map/ppermute | solution.py:633
  605.7 41.2 %collective-permute-start.64 = (f32[640,256]{1,0:T(8,128)}, f32[640,256]{1,0:T(8,128)S(1)}, u32[]{:S(2)}, u32[]{:S(2)}) collective-permute-start(f32[640,256]{1,0:T(8,128)} %get-tuple-element.125), channel_id=1, source_target_pairs={{0,96},{32,0},{64,32},{96,64},{1,97},{33,1},{65,33},{97,65},{2,98}... | collective-permute-start | bytes 1966088 | tf_op jit(solution)/shard_map/ppermute | solution.py:633
  610.9 43.5 %collective-permute-start.59 = (f32[896,256]{1,0:T(8,128)S(1)}, f32[896,256]{1,0:T(8,128)S(1)}, u32[]{:S(2)}, u32[]{:S(2)}) collective-permute-start(f32[896,256]{1,0:T(8,128)S(1)} %add_add_fusion.6), channel_id=1, source_target_pairs={{0,0},{1,16},{8,8},{9,24},{16,1},{17,17},{24,9},{25,25},{2,2},{3,1... | collective-permute-start | bytes 2752520 | tf_op jit(solution)/shard_map/ppermute | solution.py:657
  646.9 35.0 %collective-permute-start.81 = (f32[896,256]{1,0:T(8,128)S(1)}, f32[896,256]{1,0:T(8,128)S(1)}, u32[]{:S(2)}, u32[]{:S(2)}) collective-permute-start(f32[896,256]{1,0:T(8,128)S(1)} %add.134), channel_id=1, source_target_pairs={{0,96},{32,0},{64,32},{96,64},{1,97},{33,1},{65,33},{97,65},{2,98}... | collective-permute-start | bytes 2752520 | tf_op jit(solution)/shard_map/ppermute | solution.py:633
  649.5 40.2 %collective-permute-start.73 = (f32[896,256]{1,0:T(8,128)S(1)}, f32[896,256]{1,0:T(8,128)S(1)}, u32[]{:S(2)}, u32[]{:S(2)}) collective-permute-start(f32[896,256]{1,0:T(8,128)S(1)} %add.128), channel_id=1, source_target_pairs={{0,96},{32,0},{64,32},{96,64},{1,97},{33,1},{65,33},{97,65},{2,98}... | collective-permute-start | bytes 2752520 | tf_op jit(solution)/shard_map/ppermute | solution.py:633
  649.6 32.3 %collective-permute-start.63 = (f32[640,256]{1,0:T(8,128)S(1)}, f32[640,256]{1,0:T(8,128)S(1)}, u32[]{:S(2)}, u32[]{:S(2)}) collective-permute-start(f32[640,256]{1,0:T(8,128)S(1)} %copy-done.81), channel_id=1, source_target_pairs={{0,32},{32,64},{64,96},{96,0},{1,33},{33,65},{65,97},{97,1},{2,34}... | collective-permute-start | bytes 1966088 | tf_op jit(solution)/shard_map/ppermute | solution.py:633
  654.5 46.0 %collective-permute-start.65 = (f32[640,256]{1,0:T(8,128)S(1)}, f32[640,256]{1,0:T(8,128)S(1)}, u32[]{:S(2)}, u32[]{:S(2)}) collective-permute-start(f32[640,256]{1,0:T(8,128)S(1)} %add.122), channel_id=1, source_target_pairs={{0,96},{32,0},{64,32},{96,64},{1,97},{33,1},{65,33},{97,65},{2,98}... | collective-permute-start | bytes 1966088 | tf_op jit(solution)/shard_map/ppermute | solution.py:633
  667.9 52.9 %collective-permute-start.86 = (f32[896,256]{1,0:T(8,128)S(1)}, f32[896,256]{1,0:T(8,128)S(1)}, u32[]{:S(2)}, u32[]{:S(2)}) collective-permute-start(f32[896,256]{1,0:T(8,128)S(1)} %add_add_fusion.1), channel_id=1, source_target_pairs={{0,8},{1,24},{8,0},{9,16},{16,9},{17,25},{24,1},{25,17},{2,10},{3,... | collective-permute-start | bytes 2752520 | tf_op jit(solution)/shard_map/ppermute | solution.py:657
  681.9 32.7 %collective-permute-start.61 = (f32[640,256]{1,0:T(8,128)S(1)}, f32[640,256]{1,0:T(8,128)S(1)}, u32[]{:S(2)}, u32[]{:S(2)}) collective-permute-start(f32[640,256]{1,0:T(8,128)S(1)} %copy-done.80), channel_id=1, source_target_pairs={{0,96},{32,0},{64,32},{96,64},{1,97},{33,1},{65,33},{97,65},{2,98}... | collective-permute-start | bytes 1966088 | tf_op jit(solution)/shard_map/ppermute | solution.py:633
  681.9 39.0 %collective-permute-start.78 = (f32[896,256]{1,0:T(8,128)S(1)}, f32[896,256]{1,0:T(8,128)S(1)}, u32[]{:S(2)}, u32[]{:S(2)}) collective-permute-start(f32[896,256]{1,0:T(8,128)S(1)} %add_add_fusion.3), channel_id=1, source_target_pairs={{0,0},{1,16},{8,8},{9,24},{16,1},{17,17},{24,9},{25,25},{2,2},{3,1... | collective-permute-start | bytes 2752520 | tf_op jit(solution)/shard_map/ppermute | solution.py:657
  700.5 29.9 %collective-permute-start.82 = (f32[896,256]{1,0:T(8,128)S(1)}, f32[896,256]{1,0:T(8,128)}, u32[]{:S(2)}, u32[]{:S(2)}) collective-permute-start(f32[896,256]{1,0:T(8,128)S(1)} %add_add_fusion.2), channel_id=1, source_target_pairs={{0,8},{1,24},{8,0},{9,16},{16,9},{17,25},{24,1},{25,17},{2,10},{3,... | collective-permute-start | bytes 2752520 | tf_op jit(solution)/shard_map/ppermute | solution.py:657
  714.6 35.4 %collective-permute-start.74 = (f32[896,256]{1,0:T(8,128)S(1)}, f32[896,256]{1,0:T(8,128)}, u32[]{:S(2)}, u32[]{:S(2)}) collective-permute-start(f32[896,256]{1,0:T(8,128)S(1)} %add_add_fusion.4), channel_id=1, source_target_pairs={{0,8},{1,24},{8,0},{9,16},{16,9},{17,25},{24,1},{25,17},{2,10},{3,... | collective-permute-start | bytes 2752520 | tf_op jit(solution)/shard_map/ppermute | solution.py:657
  720.9 36.0 %collective-permute-start.66 = (f32[640,256]{1,0:T(8,128)}, f32[640,256]{1,0:T(8,128)S(1)}, u32[]{:S(2)}, u32[]{:S(2)}) collective-permute-start(f32[640,256]{1,0:T(8,128)} %add_add_fusion.7), channel_id=1, source_target_pairs={{0,8},{1,24},{8,0},{9,16},{16,9},{17,25},{24,1},{25,17},{2,10},{3,... | collective-permute-start | bytes 1966088 | tf_op jit(solution)/shard_map/ppermute | solution.py:657
  722.7 34.1 %collective-permute-start.62 = (f32[640,256]{1,0:T(8,128)}, f32[640,256]{1,0:T(8,128)S(1)}, u32[]{:S(2)}, u32[]{:S(2)}) collective-permute-start(f32[640,256]{1,0:T(8,128)} %add_add_fusion.8), channel_id=1, source_target_pairs={{0,0},{1,16},{8,8},{9,24},{16,1},{17,17},{24,9},{25,25},{2,2},{3,1... | collective-permute-start | bytes 1966088 | tf_op jit(solution)/shard_map/ppermute | solution.py:657
  (127 other events, 2368.1 us)
Sparse Core Ops, SparseCore 0:
  42.4 96.3 all-gather.1
  466.6 109.5 reduce-scatter.4
  579.7 132.8 reduce-scatter.2
where the time goes:
time: 789 us; the launch traced here: 780 us
  waiting for transfers between devices  357 us (45%)
  Pallas kernels  208 us (26%)
  starting transfers between devices  135 us (17%)
  local copies, waits for them, and re-layouts  35.7 us (5%)
  other arithmetic  28.6 us (4%)
  between operations  15.1 us (2%)
    ppermute x36, waiting for transfers between devices, hop_z(): return lax.ppermute(val, 'z', ring(step, NZ))  220 us
    ppermute x12, starting transfers between devices, turn(): return lax.ppermute(val, ('y', 'c'), pairs)  57.8 us
    ppermute x6, waiting for transfers between devices, hop_x(): return lax.ppermute(val, 'x', ring(step, NX))  55.4 us
    pallas_call x4, Pallas kernels, grad_pieces(): pl.pallas_call(functools.partial(grad_kernel, heights), grid_spec=pltpu.P...  53.1 us
    ppermute x12, waiting for transfers between devices, turn(): return lax.ppermute(val, ('y', 'c'), pairs)  52.1 us
    pallas_call x2, Pallas kernels, nn_pieces(): pl.pallas_call(functools.partial(nn_kernel, keys, 2, len(widths)), grid_s...  46.3 us
    pallas_call x2, Pallas kernels, nt_pieces(): pl.pallas_call(functools.partial(nt_kernel, keys, len(lefts)), grid_spec=...  44.4 us
    ppermute x36, starting transfers between devices, hop_z(): return lax.ppermute(val, 'z', ring(step, NZ))  39.4 us
  transfers between devices with their start and end apart: 90, of which 34 were waited for; matrix products, arithmetic and copies ran while one was open for 5% of the time, Pallas kernels for 22%

commit v1 on v0

--- a/solution.py
+++ b/solution.py
@@ -279,7 +279,7 @@
     return pl.multiple_of((1 - pos_ref[2] if part else pos_ref[2]) * half, half)
 
 
-def nn_kernel(keys, first, count_out, pos_ref, acts_ref, *refs):
+def nn_kernel(keys, first, count_out, which, pos_ref, acts_ref, *refs):
     count = len(keys)
     halves = refs[: 2 * count]
     outs = refs[2 * count : 2 * count + count_out]
@@ -289,7 +289,7 @@
     copies = []
     for idx in range(count):
         cols = pl.ds(pl.multiple_of(piece_block(pos_ref, *keys[idx]) * block, block), block)
-        copies.append([pltpu.make_async_copy(acts_ref.at[:, cols], acts_buf.at[:, pl.ds(idx * block, block)], acts_sem.at[idx])])
+        copies.append([pltpu.make_async_copy(acts_ref.at[which, :, cols], acts_buf.at[:, pl.ds(idx * block, block)], acts_sem.at[idx])])
         for part in range(2):
             rows = pl.ds(idx * block + half_start(pos_ref, part, half), half)
             copies[-1].append(pltpu.make_async_copy(halves[2 * idx + part], w_buf.at[rows], w_sem.at[2 * idx + part]))
@@ -321,15 +321,15 @@
             start += width
 
 
-def nn_pieces(pos, acts, parts, widths):
+def nn_pieces(pos, acts, which, parts, widths):
     keys = [(step, other) for step in (0, 1, 3, 2) for other in range(2)]
     halves = [parts[step][other][part] for step, other in keys for part in range(2)]
-    tokens, depth = acts.shape
+    _, tokens, depth = acts.shape
     width = sum(widths)
     count = len(keys)
     anywhere = pl.BlockSpec(memory_space=pl.ANY)
     return pl.pallas_call(
-        functools.partial(nn_kernel, keys, 2, len(widths)),
+        functools.partial(nn_kernel, keys, 2, len(widths), which),
         grid_spec=pltpu.PrefetchScalarGridSpec(
             num_scalar_prefetch=1,
             grid=(1,),
@@ -349,7 +349,8 @@
     )(pos, acts, *halves)
 
 
-def nt_kernel(keys, count_left, pos_ref, *refs):
+def nt_kernel(keys, sides, pos_ref, *refs):
+    count_left = len(sides)
     count = len(keys)
     lefts = refs[:count_left]
     halves = refs[count_left : count_left + 2 * count]
@@ -359,10 +360,12 @@
     slots = w_buf.shape[0]
     left_copies = []
     start = 0
-    for idx, left in enumerate(lefts):
-        left_copies.append(pltpu.make_async_copy(left, left_buf.at[:, pl.ds(start, left.shape[1])], left_sem.at[idx]))
+    for idx, (left, side) in enumerate(zip(lefts, sides)):
+        rows, width = left.shape
+        first = 0 if side is None else pl.multiple_of((1 - pos_ref[1] if side else pos_ref[1]) * rows, rows)
+        left_copies.append(pltpu.make_async_copy(left, left_buf.at[pl.ds(first, rows), pl.ds(start, width)], left_sem.at[idx]))
         left_copies[-1].start()
-        start += left.shape[1]
+        start += 0 if side == 0 else width
 
     def copies(idx):
         for part in range(2):
@@ -394,6 +397,7 @@
 
 
 def nt_pieces(pos, lefts, parts):
+    sides = (None, 0, 1)
     keys = [(step, other) for step in range(NZ) for other in range(2)]
     halves = [parts[step][other][part] for step, other in keys for part in range(2)]
     tokens = lefts[0].shape[0]
@@ -403,7 +407,7 @@
     slots = 3
     anywhere = pl.BlockSpec(memory_space=pl.ANY)
     return pl.pallas_call(
-        functools.partial(nt_kernel, keys, len(lefts)),
+        functools.partial(nt_kernel, keys, sides),
         grid_spec=pltpu.PrefetchScalarGridSpec(
             num_scalar_prefetch=1,
             grid=(1,),
@@ -442,82 +446,26 @@
 
 
 def pick_cols(pos, acts):
-    tokens, depth = acts.shape
+    count, tokens, depth = acts.shape
     block = depth // (NC * NZ)
+    places = [(which, idx) for which in range(count) for idx in range(NZ)]
 
     def kernel(pos_ref, in_ref, out_ref, buf, in_sem, out_sem):
-        reads = [pltpu.make_async_copy(in_ref.at[:, picked_cols(pos_ref, idx, block)], buf.at[idx], in_sem.at[idx]) for idx in range(NZ)]
-        writes = [pltpu.make_async_copy(buf.at[idx], out_ref.at[:, pl.ds(idx * block, block)], out_sem.at[idx]) for idx in range(NZ)]
-        for read in reads:
+        copies = []
+        for slot, (which, idx) in enumerate(places):
+            read = pltpu.make_async_copy(in_ref.at[which, :, picked_cols(pos_ref, idx, block)], buf.at[slot], in_sem.at[slot])
+            write = pltpu.make_async_copy(buf.at[slot], out_ref.at[which, :, pl.ds(idx * block, block)], out_sem.at[slot])
+            copies.append((read, write))
             read.start()
-        for read, write in zip(reads, writes):
+        for read, write in copies:
             read.wait()
             write.start()
-        for write in writes:
+        for _, write in copies:
             write.wait()
 
-    sems = pltpu.SemaphoreType.DMA((NZ,))
-    return dma_kernel(kernel, pos, [acts], [jax.ShapeDtypeStruct((tokens, depth // 2), BF16)], [pltpu.VMEM((NZ, tokens, block), BF16), sems, sems])[0]
-
-
-def settle_y(pos, own, left, right, far):
-    chunk, depth = own.shape
-    half = chunk // 2
-    sources = [(0, 0, own), (3, 0, left), (1, 0, right), (2, 0, far[0]), (2, half, far[1])]
-
-    def kernel(pos_ref, *refs):
-        ins, (out0, out1, buf, in_sem, out_sem) = refs[: len(sources)], refs[len(sources) :]
-        reads = []
-        for idx, (step, start, array) in enumerate(sources):
-            row = pl.multiple_of(lax.rem(pos_ref[3] + step, NY) * chunk, chunk) + start
-            reads.append(pltpu.make_async_copy(ins[idx], buf.at[pl.ds(row, array.shape[0])], in_sem.at[idx]))
-            reads[-1].start()
-        for read in reads:
-            read.wait()
-        writes = [pltpu.make_async_copy(buf.at[pl.ds(idx * 2 * chunk, 2 * chunk)], out, out_sem.at[idx]) for idx, out in enumerate((out0, out1))]
-        for write in writes:
-            write.start()
-        for write in writes:
-            write.wait()
-
-    out = jax.ShapeDtypeStruct((2 * chunk, depth), BF16)
-    scratch = [pltpu.VMEM((NY * chunk, depth), BF16), pltpu.SemaphoreType.DMA((len(sources),)), pltpu.SemaphoreType.DMA((2,))]
-    return dma_kernel(kernel, pos, [array for _, _, array in sources], [out, out], scratch)
-
-
-def settle_x(pos, parts):
-    sources = [(step, half, parts[step][half]) for step in range(NX) for half in range(2)]
-    chunk = sources[0][2].shape[0] // 2
-    depth = sources[0][2].shape[1]
-    block = depth // (NC * NZ)
-    blocks = 2 * len(sources)
-
-    def kernel(pos_ref, *refs):
-        ins, (all_ref, out_ref, buf, in_sem, all_sem, out_sem) = refs[: len(sources)], refs[len(sources) :]
-        reads = []
-        rows = []
-        for idx, (step, half, _) in enumerate(sources):
-            x_pos = lax.rem(pos_ref[4] + step, NX)
-            for part in range(2):
-                rows.append(pl.ds(pl.multiple_of(((2 * half + part) * NX + x_pos) * chunk, chunk), chunk))
-                reads.append(pltpu.make_async_copy(ins[idx].at[pl.ds(part * chunk, chunk)], buf.at[rows[-1]], in_sem.at[2 * idx + part]))
-                reads[-1].start()
-        writes = []
-        for idx in range(blocks):
-            reads[idx].wait()
-            writes.append(pltpu.make_async_copy(buf.at[rows[idx]], all_ref.at[rows[idx]], all_sem.at[idx]))
-            for col in range(NZ):
-                cols = picked_cols(pos_ref, col, block)
-                writes.append(pltpu.make_async_copy(buf.at[rows[idx], cols], out_ref.at[rows[idx], pl.ds(col * block, block)], out_sem.at[idx, col]))
-            for write in writes[-1 - NZ :]:
-                write.start()
-        for write in writes:
-            write.wait()
-
-    tokens = blocks * chunk
-    out_shape = [jax.ShapeDtypeStruct((tokens, depth), BF16), jax.ShapeDtypeStruct((tokens, depth // 2), BF16)]
-    scratch = [pltpu.VMEM((tokens, depth), BF16), pltpu.SemaphoreType.DMA((blocks,)), pltpu.SemaphoreType.DMA((blocks,)), pltpu.SemaphoreType.DMA((blocks, NZ))]
-    return dma_kernel(kernel, pos, [array for _, _, array in sources], out_shape, scratch)
+    sems = pltpu.SemaphoreType.DMA((len(places),))
+    out = jax.ShapeDtypeStruct((count, tokens, depth // 2), BF16)
+    return dma_kernel(kernel, pos, [acts], [out], [pltpu.VMEM((len(places), tokens, block), BF16), sems, sems])[0]
 
 
 def grad_kernel(heights, pos_ref, *refs):
@@ -559,7 +507,7 @@
 
 
 def grad_pieces(pos, pairs):
-    tokens, depth = pairs[0][2].shape
+    _, tokens, depth = pairs[0][2].shape
     cols = depth // (NZ * NY)
     in_specs = []
     args = []
@@ -570,10 +518,12 @@
     def bit(pos, part):
         return 1 - pos[2] if part else pos[2]
 
-    for own, recv, acts, acts_recv, height, block in pairs:
+    for own, recv, acts, acts_recv, height, block, which in pairs:
         in_specs += [pl.BlockSpec((height, tokens), lambda n, pos, block=block: (block, 0))] * 2
-        in_specs += [pl.BlockSpec((tokens, cols), lambda n, pos, part=part: (0, z_of(n, pos) * NY + 2 * pos[1] + bit(pos, part))) for part in range(2)]
-        in_specs += [pl.BlockSpec((tokens, cols), lambda n, pos, part=part: (0, z_of(n, pos) * 2 + bit(pos, part))) for part in range(2)]
+        for part in range(2):
+            in_specs.append(pl.BlockSpec((None, tokens, cols), lambda n, pos, part=part, which=which: (which, 0, z_of(n, pos) * NY + 2 * pos[1] + bit(pos, part))))
+        for part in range(2):
+            in_specs.append(pl.BlockSpec((None, tokens, cols), lambda n, pos, part=part, which=which: (which, 0, z_of(n, pos) * 2 + bit(pos, part))))
         args += [own, recv, acts, acts, acts_recv, acts_recv]
     heights = [pair[4] for pair in pairs]
     rows = sum(heights)
@@ -633,14 +583,6 @@
     return lax.ppermute(val, "z", ring(step, NZ))
 
 
-def hop_y(val, step):
-    return lax.ppermute(val, "y", ring(step, NY))
-
-
-def hop_x(val, step):
-    return lax.ppermute(val, "x", ring(step, NX))
-
-
 def swap_c(val):
     return lax.ppermute(val, "c", [(0, 1), (1, 0)])
 
@@ -688,7 +630,7 @@
         c_pos = lax.axis_index("c")
         even_y = y_pos % 2 == 0
         first_c = c_pos == 0
-        pos = jnp.stack([z_pos, c_pos, y_pos % 2, y_pos, lax.axis_index("x")]).astype(jnp.int32)
+        pos = jnp.stack([z_pos, c_pos, y_pos % 2]).astype(jnp.int32)
         head = 2 * rope_cos.shape[1]
         seq = rope_cos.shape[0]
         ff_blk = w_gate.shape[1] // 2
@@ -715,11 +657,12 @@
 
         def grad_pass(state, *earlier):
             (up0, down1), far, direct, own = state
-            passed = (hop_z(up0 + after(far[0], *earlier), 1), hop_z(down1 + far[1], -1))
-            return direct, passed, own
+            sums = (up0 + after(far[0], *earlier), down1 + far[1])
+            passed = (hop_z(sums[0], 1), hop_z(sums[1], -1))
+            return direct, passed, own, sums
 
         def grad_back(state, *earlier):
-            direct, passed, own = state
+            direct, passed, own = state[:3]
             first = own[0] + after(passed[0], *earlier) + direct[1]
             second = own[1] + direct[0] + passed[1]
             return turn(first, 0), turn(second, 1)
@@ -727,8 +670,7 @@
         def my_rows(val, mine):
             return lax.dynamic_slice_in_dim(val, (c_pos if mine else 1 - c_pos) * seq, seq, axis=0)
 
-        def both_rows(own, other):
-            got = swap_c(other)
+        def both_rows(own, got):
             return jnp.concatenate([jnp.where(first_c, own, got), jnp.where(first_c, got, own)], axis=0)
 
         cos_tab = jnp.concatenate([rope_cos, rope_cos], axis=1)
@@ -750,62 +692,52 @@
 
         x_rows = x_in[0].astype(F32)
         normed, norm_pull = jax.vjp(lambda row_vals: norm_fwd(row_vals, norm_gain), x_rows)
-        h_all = lax.all_gather(after(normed.astype(BF16), *wf_piece), ("y", "x"), axis=0, tiled=True)
-        dy_own = dy_in[0]
-        dy_half = dy_own.shape[0] // 2
-        dy_left = hop_y(dy_own, 1)
-        dy_right = hop_y(dy_own, -1)
-        dy_far = [hop_y(dy_left[:dy_half], 1), hop_y(dy_right[dy_half:], -1)]
-        dy_piece = settle_y(pos, dy_own, dy_left, dy_right, dy_far)
-        dx_left = [hop_x(half, 1) for half in dy_piece]
-        dx_right = [hop_x(half, -1) for half in dy_piece]
-        dx_far = [hop_x(dx_left[0], 1), hop_x(dx_right[1], -1)]
+        both = jnp.stack([normed.astype(BF16), dy_in[0]])
+        both_all = lax.all_gather(after(both, *wf_piece), ("y", "x"), axis=1, tiled=True)
         wf_parts = gather_weight(wf_piece)
         ws_parts = gather_weight(ws_piece)
 
-        gate_up, qkv_tok = nn_pieces(pos, h_all, wf_parts, (2 * ff_blk, qkv_blk))
+        gate_up, qkv_tok = nn_pieces(pos, both_all, 0, wf_parts, (2 * ff_blk, qkv_blk))
         third = qkv_tok[:, o_blk:]
         qkv_other = swap_c(my_rows(qkv_tok, False))
         third_own = swap_y(my_rows(third, True))
         third_other = swap_yc(my_rows(third, False))
         act_val, act_t = act_fwd(after(gate_up, qkv_tok))
         act_recv = swap_c(act_t)
-        dy_all, dy_picked = settle_x(after(pos, act_t), (dy_piece, dx_right, dx_far, dx_left))
-        dy_recv = swap_c(dy_picked)
-        qkv_seq, attn_own, attn_other = attn_fwd(after(pos, dy_picked), qkv_tok, qkv_other, third_own, third_other, cos_tab, sin_tab)
-        attn_tok = both_rows(attn_own, attn_other)
-        g_act = grad_start([(act_t, act_recv, dy_all, dy_recv, ff_blk, 0)], attn_own)
-        h_picked = pick_cols(after(pos, g_act[3][0]), h_all)
-        h_recv = swap_c(h_picked)
-        y_part = nt_pieces(after(pos, h_picked), [act_val, attn_tok], ws_parts)
+        qkv_seq, attn_own, attn_other = attn_fwd(after(pos, act_t), qkv_tok, qkv_other, third_own, third_other, cos_tab, sin_tab)
+        attn_got = swap_c(attn_other)
+        picked = pick_cols(after(pos, attn_own), both_all)
+        both_recv = swap_c(picked)
+        y_part = nt_pieces(after(pos, picked), [act_val, attn_own, attn_got], ws_parts)
         mix_sum = lax.psum_scatter(y_part, ("y", "x"), scatter_dimension=0, tiled=True)
         y_out = (x_rows + mix_sum).astype(BF16)[None]
 
-        d_act, d_attn = nn_pieces(after(pos, y_part), dy_all, ws_parts, (ff_blk, o_blk))
+        g_act = grad_start([(act_t, act_recv, both_all, both_recv, ff_blk, 0, 1)], y_part)
+        d_act, d_attn = nn_pieces(after(pos, g_act[3][0]), both_all, 1, ws_parts, (ff_blk, o_blk))
         d_attn_other = swap_c(my_rows(d_attn, False))
-        g_act = grad_pass(g_act, d_attn)
         d_gate_up, d_gate_up_t = act_bwd(gate_up, d_act)
         d_gate_up_recv = swap_c(d_gate_up_t)
         d_queries, keep, send = attn_bwd(after(pos, d_gate_up_t), qkv_seq, d_attn, d_attn_other, cos_tab, sin_tab)
         got = swap_y(send)
-        g_gate = grad_start([(d_gate_up_t, d_gate_up_recv, h_all, h_recv, ff_blk, 0)], d_queries)
-        g_up = grad_start([(d_gate_up_t, d_gate_up_recv, h_all, h_recv, ff_blk, 1)], g_gate[3][0])
-        d_own, d_other = attn_post(after(pos, g_up[3][0]), d_queries, keep, got, cos_tab, sin_tab)
-        d_qkv = both_rows(d_own, d_other)
-        g_gate = grad_pass(g_gate, d_own)
-        dh_part = nt_pieces(pos, [d_gate_up, d_qkv], wf_parts)
+        g_act = grad_pass(g_act, d_queries)
+        g_gate = grad_start([(d_gate_up_t, d_gate_up_recv, both_all, both_recv, ff_blk, 0, 0)], *g_act[3])
+        d_own, d_other = attn_post(after(pos, g_gate[3][0]), d_queries, keep, got, cos_tab, sin_tab)
+        d_got = swap_c(d_other)
+        dh_part = nt_pieces(pos, [d_gate_up, d_own, d_got], wf_parts)
         d_h = lax.psum_scatter(dh_part, ("y", "x"), scatter_dimension=0, tiled=True)
         d_h = d_h.astype(BF16)
         dx_out = (dy_in[0].astype(F32) + norm_pull(d_h.astype(F32))[0]).astype(BF16)[None]
-
-        attn_t = attn_tok.T
-        d_qkv_t = d_qkv.T
+        g_up = grad_start([(d_gate_up_t, d_gate_up_recv, both_all, both_recv, ff_blk, 1, 0)], dh_part)
+        g_gate = grad_pass(g_gate, g_up[3][0])
+
+        attn_t = both_rows(attn_own, attn_got).T
+        d_qkv_t = both_rows(d_own, d_got).T
         attn_recv = swap_c(attn_t)
         d_qkv_recv = swap_c(d_qkv_t)
-        g_up = grad_pass(g_up, dh_part)
-        g_attn = grad_start([(attn_t, attn_recv, dy_all, dy_recv, o_blk, 0), (d_qkv_t, d_qkv_recv, h_all, h_recv, qkv_blk, 0)], dh_part)
+        g_attn = grad_start([(attn_t, attn_recv, both_all, both_recv, o_blk, 0, 1), (d_qkv_t, d_qkv_recv, both_all, both_recv, qkv_blk, 0, 0)], *g_gate[3])
+        g_up = grad_pass(g_up, g_attn[3][0])
         b_act = grad_back(g_act, g_attn[3][0])
-        g_attn = grad_pass(g_attn, b_act[0])
+        g_attn = grad_pass(g_attn)
         b_gate = grad_back(g_gate)
         b_up = grad_back(g_up)
         b_attn = grad_back(g_attn)

time: 789 us -> 735 us (0.932)
  starting transfers between devices: 135 us -> 70.7 us
  waiting for transfers between devices: 357 us -> 388 us
  local copies, waits for them, and re-layouts: 35.7 us -> 24.6 us
  Pallas kernels: 208 us -> 200 us
    ppermute x10 -> x0, waiting for transfers between devices: 74.8 us -> none  [the longest x6 55.4 us: hop_x(): return lax.ppermute(val, 'x', ring(step, NX))]
    ppermute x12, waiting for transfers between devices: 52.1 us -> 95.5 us  [turn(): return lax.ppermute(val, ('y', 'c'), pairs)]
    ppermute x12, starting transfers between devices: 57.8 us -> 19.6 us  [turn(): return lax.ppermute(val, ('y', 'c'), pairs)]
    all_gather x1, waiting for transfers between devices: 0.02 us -> 34.1 us  [layer(): lax.all_gather(after(both, *wf_piece), ('y', 'x'), axis=1, tiled=True)]
    ppermute x36, waiting for transfers between devices: 220 us -> 250 us  [hop_z(): return lax.ppermute(val, 'z', ring(step, NZ))]
    ppermute x10 -> x0, starting transfers between devices: 15 us -> none  [the longest x6 8.76 us: hop_x(): return lax.ppermute(val, 'x', ring(step, NX))]
    pallas_call x3 -> x1, Pallas kernels: 17 us -> 7.48 us  [dma_kernel(): pl.pallas_call(kernel, grid_spec=pltpu.PrefetchScalarGridSpec(num_scalar_...]
    ppermute x26 -> x25, starting transfers between devices: 19.3 us -> 10.4 us  [swap_c(): return lax.ppermute(val, 'c', [(0, 1), (1, 0)])]
  transfers between devices with their start and end apart: 90 -> 79, of which waited for: 34 -> 37; matrix products, arithmetic and copies ran while one was open for 5% -> 5% of each run, Pallas kernels for 22% -> 12%
where the time goes in v1:
time: 735 us; the launch traced here: 729 us
  waiting for transfers between devices  388 us (53%)
  Pallas kernels  200 us (27%)
  starting transfers between devices  70.7 us (10%)
  other arithmetic  30.2 us (4%)
  local copies, waits for them, and re-layouts  24.6 us (3%)
  between operations  15.1 us (2%)
    ppermute x36, waiting for transfers between devices, hop_z(): return lax.ppermute(val, 'z', ring(step, NZ))  250 us
    ppermute x12, waiting for transfers between devices, turn(): return lax.ppermute(val, ('y', 'c'), pairs)  95.5 us
    pallas_call x4, Pallas kernels, grad_pieces(): pl.pallas_call(functools.partial(grad_kernel, heights), grid_spec=pltpu.P...  54.3 us
    pallas_call x2, Pallas kernels, nn_pieces(): pl.pallas_call(functools.partial(nn_kernel, keys, 2, len(widths), which),...  46.2 us
    pallas_call x2, Pallas kernels, nt_pieces(): pl.pallas_call(functools.partial(nt_kernel, keys, sides), grid_spec=pltpu...  44.4 us
    ppermute x36, starting transfers between devices, hop_z(): return lax.ppermute(val, 'z', ring(step, NZ))  38.9 us
    all_gather x1, waiting for transfers between devices, layer(): lax.all_gather(after(both, *wf_piece), ('y', 'x'), axis=1, tiled=True)  34.1 us
    ppermute x12, starting transfers between devices, turn(): return lax.ppermute(val, ('y', 'c'), pairs)  19.6 us
  transfers between devices with their start and end apart: 79, of which 37 were waited for; matrix products, arithmetic and copies ran while one was open for 5% of the time, Pallas kernels for 12%

profile of v1, /device:TPU:1, one launch (start us, length us, event | category | flops | bytes accessed | tf_op | source)
XLA Modules:
  0.0 728.5 jit_solution(2175077826459260159)
XLA Ops:
  12.1 4.1 collective-permute-start.1
  21.1 19.8 %collective-permute-done.1.refs_1_.refs_4_ = bf16[256,2176]{1,0:T(8,128)(2,1)S(1)} collective-permute-done((bf16[256,2176]{1,0:T(8,128)(2,1)}, bf16[256,2176]{1,0:T(8,128)(2,1)S(1)}, u32[]{:S(2)}, u32[]{:S(2)}) %collective-permute-start.1) | collective-permute-done | bytes 1114144 | tf_op jit(solution)/shard_map/ppermute | solution.py:599
  48.5 22.5 %collective-permute-done.9.refs_9_.refs_16_ = bf16[256,2176]{1,0:T(8,128)(2,1)S(1)} collective-permute-done((bf16[256,2176]{1,0:T(8,128)(2,1)S(1)}, bf16[256,2176]{1,0:T(8,128)(2,1)S(1)}, u32[]{:S(2)}, u32[]{:S(2)}) %collective-permute-start.9) | collective-permute-done | bytes 1114144 | tf_op jit(solution)/shard_map/ppermute | solution.py:583
  73.8 17.5 %collective-permute-done.8.refs_8_.refs_15_ = bf16[256,2176]{1,0:T(8,128)(2,1)} collective-permute-done((bf16[256,2176]{1,0:T(8,128)(2,1)S(1)}, bf16[256,2176]{1,0:T(8,128)(2,1)}, u32[]{:S(2)}, u32[]{:S(2)}) %collective-permute-start.8) | collective-permute-done | bytes 1114144 | tf_op jit(solution)/shard_map/ppermute | solution.py:583
  91.4 3.0 collective-permute-done.4.refs_4_.refs_7_
  95.4 19.7 %collective-permute-done.13.refs_13_.refs_12_ = bf16[256,2176]{1,0:T(8,128)(2,1)} collective-permute-done((bf16[256,2176]{1,0:T(8,128)(2,1)}, bf16[256,2176]{1,0:T(8,128)(2,1)}, u32[]{:S(2)}, u32[]{:S(2)}) %collective-permute-start.13) | collective-permute-done | bytes 1114144 | tf_op jit(solution)/shard_map/ppermute | solution.py:583
  120.4 34.1 %all-gather.2.cloned.1.call-done.acts_ref.in_ref.refs_2_.refs_3_.refs_8_.refs_9_ = bf16[2,1024,4096]{2,1,0:T(8,128)(2,1)} async-done(((bf16[2,64,4096]{2,1,0:T(8,128)(2,1)}), bf16[2,1024,4096]{2,1,0:T(8,128)(2,1)}) %all-gather.2.cloned.1.call-update) | async-done | bytes 16777232 | tf_op jit(solution)/shard_map/all_gather | solution.py:696
  154.5 28.5 %shard_map.153 = (bf16[1024,1792]{1,0:T(8,128)(2,1)}, bf16[1024,384]{1,0:T(8,128)(2,1)}) custom-call(s32[3]{0:T(128)} %pad_add_fusion.pos_ref, bf16[2,1024,4096]{2,1,0:T(8,128)(2,1)} %all-gather.2.cloned.1.call-done.acts_ref.in_ref.refs_2_.refs_3_.refs_8_.refs_9_, bf16[256,2176]{1,0:T(8,128)(2,1)} %copy-done.6, bf16[256,2176]{1,0:T(8,128)(2,1)} %copy-done.5, ...), custom_call_target="tpu_custom_call" | custom-call | flops 912680576 | bytes 26214400 | tf_op jit(solution)/shard_map/pallas_call | solution.py:331
  188.9 4.8 act_fwd.1
  194.9 5.6 shard_map.154
  200.5 7.5 %shard_map.155 = bf16[2,1024,2048]{2,1,0:T(8,128)(2,1)} custom-call(s32[3]{0:T(128)} %pad_add_fusion.pos_ref, bf16[2,1024,4096]{2,1,0:T(8,128)(2,1)} %all-gather.2.cloned.1.call-done.acts_ref.in_ref.refs_2_.refs_3_.refs_8_.refs_9_), custom_call_target="tpu_custom_call" | custom-call | flops 150000000 | bytes 16000000 | tf_op jit(solution)/shard_map/pallas_call | solution.py:437
  212.6 2.8 collective-permute-start.20
  215.5 10.3 %collective-permute-done.21.refs_4_.refs_1_ = bf16[256,1152]{1,0:T(8,128)(2,1)S(1)} collective-permute-done((bf16[256,1152]{1,0:T(8,128)(2,1)S(1)}, bf16[256,1152]{1,0:T(8,128)(2,1)S(1)}, u32[]{:S(2)}, u32[]{:S(2)}) %collective-permute-start.21) | collective-permute-done | bytes 589856 | tf_op jit(solution)/shard_map/ppermute | solution.py:599
  228.8 13.6 %collective-permute-done.33.refs_16_.refs_9_ = bf16[256,1152]{1,0:T(8,128)(2,1)S(1)} collective-permute-done((bf16[256,1152]{1,0:T(8,128)(2,1)S(1)}, bf16[256,1152]{1,0:T(8,128)(2,1)S(1)}, u32[]{:S(2)}, u32[]{:S(2)}) %collective-permute-start.33) | collective-permute-done | bytes 589856 | tf_op jit(solution)/shard_map/ppermute | solution.py:583
  244.6 7.9 %collective-permute-done.28.refs_15_.refs_8_ = bf16[256,1152]{1,0:T(8,128)(2,1)S(1)} collective-permute-done((bf16[256,1152]{1,0:T(8,128)(2,1)S(1)}, bf16[256,1152]{1,0:T(8,128)(2,1)S(1)}, u32[]{:S(2)}, u32[]{:S(2)}) %collective-permute-start.28) | collective-permute-done | bytes 589856 | tf_op jit(solution)/shard_map/ppermute | solution.py:583
  253.9 2.7 collective-permute-start.30
  257.2 11.3 %collective-permute-done.30.refs_12_.refs_13_ = bf16[256,1152]{1,0:T(8,128)(2,1)S(1)} collective-permute-done((bf16[256,1152]{1,0:T(8,128)(2,1)S(1)}, bf16[256,1152]{1,0:T(8,128)(2,1)S(1)}, u32[]{:S(2)}, u32[]{:S(2)}) %collective-permute-start.30) | collective-permute-done | bytes 589856 | tf_op jit(solution)/shard_map/ppermute | solution.py:583
  271.6 12.9 %collective-permute-done.29.refs_11_.refs_12_ = bf16[256,1152]{1,0:T(8,128)(2,1)} collective-permute-done((bf16[256,1152]{1,0:T(8,128)(2,1)S(1)}, bf16[256,1152]{1,0:T(8,128)(2,1)}, u32[]{:S(2)}, u32[]{:S(2)}) %collective-permute-start.29) | collective-permute-done | bytes 589856 | tf_op jit(solution)/shard_map/ppermute | solution.py:583
  288.4 17.1 %shard_map.156 = f32[1024,4096]{1,0:T(8,128)} custom-call(s32[3]{0:T(128)} %pad_add_fusion.pos_ref, bf16[1024,896]{1,0:T(8,128)(2,1)} %get-tuple-element.79.refs_0_, bf16[512,256]{1,0:T(8,128)(2,1)} %get-tuple-element.76.refs_1_, bf16[512,256]{1,0:T(8,128)(2,1)} %copy.38.refs_2_, bf16[256,1152]{1,0:T(8,128)(2,1)} %copy-done.14, ...), custom_call_target="tpu_custom_call" | custom-call | flops 483183808 | bytes 26214400 | tf_op jit(solution)/shard_map/pallas_call | solution.py:409
  305.6 13.8 %grad.4 = (f32[896,256]{1,0:T(8,128)}, f32[896,256]{1,0:T(8,128)}, f32[896,256]{1,0:T(8,128)}, f32[896,256]{1,0:T(8,128)}, f32[896,256]{1,0:T(8,128)}, /*index=5...) custom-call(s32[3]{0:T(128)} %pad_add_fusion.pos_ref, bf16[896,1024]{1,0:T(8,128)(2,1)} %get-tuple-element.73.refs_0_, ...), custom_call_target="tpu_custom_call" | custom-call | flops 375809632 | bytes 8388608 | tf_op jit(solution)/shard_map/grad/pallas_call | solution.py:530
  319.4 17.7 %shard_map.157 = (bf16[1024,896]{1,0:T(8,128)(2,1)}, bf16[1024,256]{1,0:T(8,128)(2,1)}) custom-call(s32[3]{0:T(128)} %pad_add_fusion.pos_ref, bf16[2,1024,4096]{2,1,0:T(8,128)(2,1)} %all-gather.2.cloned.1.call-done.acts_ref.in_ref.refs_2_.refs_3_.refs_8_.refs_9_, bf16[256,1152]{1,0:T(8,128)(2,1)} %copy-done.14, bf16[256,1152]{1,0:T(8,128)(2,1)} %copy-done.13, ...), custom_call_target="tpu_custom_call" | custom-call | flops 483183808 | bytes 17825792 | tf_op jit(solution)/shard_map/pallas_call | solution.py:331
  337.0 7.0 act_bwd.1
  351.8 8.1 %shard_map.158 = (bf16[2,512,256]{2,1,0:T(8,128)(2,1)}, f32[2,512,128]{2,1,0:T(8,128)}, f32[2,512,128]{2,1,0:T(8,128)}) custom-call(s32[3]{0:T(128)} %pad_add_fusion.pos_ref, bf16[2,512,512]{2,1,0:T(8,128)(2,1)} %get-tuple-element.90.seq_ref, bf16[1024,256]{1,0:T(8,128)(2,1)} %get-tuple-element.91.own_ref, bf16[512,256]{1,0:T(8,128)(2,1)} %copy-done.65, ...), custom_call_target="tpu_custom_call" | custom-call | flops 800000000 | bytes 4000000 | tf_op jit(solution)/shard_map/pallas_call | solution.py:143
  360.0 7.8 %collective-permute-done.38 = f32[896,256]{1,0:T(8,128)} collective-permute-done((f32[896,256]{1,0:T(8,128)}, f32[896,256]{1,0:T(8,128)}, u32[]{:S(2)}, u32[]{:S(2)}) %collective-permute-start.38) | collective-permute-done | bytes 917536 | tf_op jit(solution)/shard_map/ppermute | solution.py:583
  374.5 13.4 %grad.5 = (f32[896,256]{1,0:T(8,128)}, f32[896,256]{1,0:T(8,128)}, f32[896,256]{1,0:T(8,128)}, f32[896,256]{1,0:T(8,128)}, f32[896,256]{1,0:T(8,128)}, /*index=5...) custom-call(s32[3]{0:T(128)} %pad_add_fusion.pos_ref, bf16[1792,1024]{1,0:T(8,128)(2,1)} %get-tuple-element.88.refs_0_, ...), custom_call_target="tpu_custom_call" | custom-call | flops 375809632 | bytes 8388608 | tf_op jit(solution)/shard_map/grad/pallas_call | solution.py:530
  387.9 3.2 shard_map.159
  395.5 27.3 %shard_map.160 = f32[1024,4096]{1,0:T(8,128)} custom-call(s32[3]{0:T(128)} %pad_add_fusion.pos_ref, bf16[1024,1792]{1,0:T(8,128)(2,1)} %get-tuple-element.85.refs_0_, bf16[512,384]{1,0:T(8,128)(2,1)} %get-tuple-element.101.refs_1_, bf16[512,384]{1,0:T(8,128)(2,1)} %copy.40.refs_2_, bf16[256,2176]{1,0:T(8,128)(2,1)} %copy-done.6, ...), custom_call_target="tpu_custom_call" | custom-call | flops 912680576 | bytes 34603008 | tf_op jit(solution)/shard_map/pallas_call | solution.py:409
  431.7 15.2 %collective-permute-done.71 = f32[896,256]{1,0:T(8,128)S(1)} collective-permute-done((f32[896,256]{1,0:T(8,128)}, f32[896,256]{1,0:T(8,128)S(1)}, u32[]{:S(2)}, u32[]{:S(2)}) %collective-permute-start.71) | collective-permute-done | bytes 917536 | tf_op jit(solution)/shard_map/ppermute | solution.py:583
  448.2 13.7 %grad.6 = (f32[896,256]{1,0:T(8,128)}, f32[896,256]{1,0:T(8,128)}, f32[896,256]{1,0:T(8,128)}, f32[896,256]{1,0:T(8,128)}, f32[896,256]{1,0:T(8,128)}, /*index=5...) custom-call(s32[3]{0:T(128)} %pad_add_fusion.pos_ref, bf16[1792,1024]{1,0:T(8,128)(2,1)} %get-tuple-element.88.refs_0_, ...), custom_call_target="tpu_custom_call" | custom-call | flops 375809632 | bytes 8388608 | tf_op jit(solution)/shard_map/grad/pallas_call | solution.py:530
  462.4 6.8 collective-permute-done.44
  472.0 2.7 add.117
  477.0 13.4 %grad.7 = (f32[640,256]{1,0:T(8,128)}, f32[640,256]{1,0:T(8,128)}, f32[640,256]{1,0:T(8,128)}, f32[640,256]{1,0:T(8,128)}, f32[640,256]{1,0:T(8,128)}, /*index=5...) custom-call(s32[3]{0:T(128)} %pad_add_fusion.pos_ref, bf16[256,1024]{1,0:T(8,128)(2,1)} %copy-done.23, ...), custom_call_target="tpu_custom_call" | custom-call | flops 268435456 | bytes 8388608 | tf_op jit(solution)/shard_map/grad/pallas_call | solution.py:530
  491.6 16.8 %collective-permute-done.70 = f32[896,256]{1,0:T(8,128)S(1)} collective-permute-done((f32[896,256]{1,0:T(8,128)}, f32[896,256]{1,0:T(8,128)S(1)}, u32[]{:S(2)}, u32[]{:S(2)}) %collective-permute-start.70) | collective-permute-done | bytes 917536 | tf_op jit(solution)/shard_map/ppermute | solution.py:583
  513.0 12.6 %collective-permute-done.67 = f32[896,256]{1,0:T(8,128)} collective-permute-done((f32[896,256]{1,0:T(8,128)}, f32[896,256]{1,0:T(8,128)}, u32[]{:S(2)}, u32[]{:S(2)}) %collective-permute-start.67) | collective-permute-done | bytes 917536 | tf_op jit(solution)/shard_map/ppermute | solution.py:583
  531.7 10.5 %collective-permute-done.59 = f32[896,256]{1,0:T(8,128)S(1)} collective-permute-done((f32[896,256]{1,0:T(8,128)}, f32[896,256]{1,0:T(8,128)S(1)}, u32[]{:S(2)}, u32[]{:S(2)}) %collective-permute-start.59) | collective-permute-done | bytes 917536 | tf_op jit(solution)/shard_map/ppermute | solution.py:583
  542.1 19.8 %collective-permute-done.56 = f32[896,256]{1,0:T(8,128)S(1)} collective-permute-done((f32[896,256]{1,0:T(8,128)}, f32[896,256]{1,0:T(8,128)S(1)}, u32[]{:S(2)}, u32[]{:S(2)}) %collective-permute-start.56) | collective-permute-done | bytes 917536 | tf_op jit(solution)/shard_map/ppermute | solution.py:583
  564.8 16.8 %collective-permute-done.63 = f32[896,256]{1,0:T(8,128)S(1)} collective-permute-done((f32[896,256]{1,0:T(8,128)S(1)}, f32[896,256]{1,0:T(8,128)S(1)}, u32[]{:S(2)}, u32[]{:S(2)}) %collective-permute-start.63) | collective-permute-done | bytes 917536 | tf_op jit(solution)/shard_map/ppermute | solution.py:583
  585.1 16.1 %collective-permute-done.66 = f32[896,256]{1,0:T(8,128)S(1)} collective-permute-done((f32[896,256]{1,0:T(8,128)S(1)}, f32[896,256]{1,0:T(8,128)S(1)}, u32[]{:S(2)}, u32[]{:S(2)}) %collective-permute-start.66) | collective-permute-done | bytes 917536 | tf_op jit(solution)/shard_map/ppermute | solution.py:583
  603.4 9.2 %collective-permute-done.68 = f32[896,256]{1,0:T(8,128)S(1)} collective-permute-done((f32[896,256]{1,0:T(8,128)S(1)}, f32[896,256]{1,0:T(8,128)S(1)}, u32[]{:S(2)}, u32[]{:S(2)}) %collective-permute-start.68) | collective-permute-done | bytes 917536 | tf_op jit(solution)/shard_map/ppermute | solution.py:583
  619.5 3.8 collective-permute-done.75.second_ref
  623.2 6.0 collective-permute-done.52
  632.1 6.9 collective-permute-done.72.first_ref
  641.0 29.3 %collective-permute-done.58.first_ref = f32[896,256]{1,0:T(8,128)S(1)} collective-permute-done((f32[896,256]{1,0:T(8,128)S(1)}, f32[896,256]{1,0:T(8,128)S(1)}, u32[]{:S(2)}, u32[]{:S(2)}) %collective-permute-start.58) | collective-permute-done | bytes 917536 | tf_op jit(solution)/shard_map/ppermute | solution.py:599
  671.2 3.4 shard_map.166
  674.7 3.7 shard_map.164
  678.4 24.4 %collective-permute-done.51.first_ref = f32[640,256]{1,0:T(8,128)S(1)} collective-permute-done((f32[640,256]{1,0:T(8,128)}, f32[640,256]{1,0:T(8,128)S(1)}, u32[]{:S(2)}, u32[]{:S(2)}) %collective-permute-start.51) | collective-permute-done | bytes 655392 | tf_op jit(solution)/shard_map/ppermute | solution.py:599
  709.5 2.7 shard_map.161
  712.3 3.8 shard_map.165
  (322 shorter events, 131.7 us)
Async XLA Ops:
  7.2 147.3 %all-gather.2.cloned.1.call-start = ((), (), s32[]{:S(2)}) async-start(), calls=%async_computation.2 | async-start | bytes 17825792 | tf_op jit(solution)/shard_map/all_gather | solution.py:696
  12.1 28.8 %collective-permute-start.1 = (bf16[256,2176]{1,0:T(8,128)(2,1)}, bf16[256,2176]{1,0:T(8,128)(2,1)S(1)}, u32[]{:S(2)}, u32[]{:S(2)}) collective-permute-start(bf16[256,2176]{1,0:T(8,128)(2,1)} %get-tuple-element.134), channel_id=1, source_target_pairs={{0,8},{1,24},{8,0},{9,16},{16,9},{17,25},{24,1},{25,17},{2,10},{3,... | collective-permute-start | bytes 3342344 | tf_op jit(solution)/shard_map/ppermute | solution.py:599
  16.2 25.7 %collective-permute-start = (bf16[256,2176]{1,0:T(8,128)(2,1)S(1)}, bf16[256,2176]{1,0:T(8,128)(2,1)S(1)}, u32[]{:S(2)}, u32[]{:S(2)}) collective-permute-start(bf16[256,2176]{1,0:T(8,128)(2,1)S(1)} %get-tuple-element.135), channel_id=1, source_target_pairs={{0,0},{1,16},{8,8},{9,24},{16,1},{17,17},{24,9},{25,25},{2,2},{3,1... | collective-permute-start | bytes 3342344 | tf_op jit(solution)/shard_map/ppermute | solution.py:599
  41.9 675.1 %reduce-scatter.5.cloned.1.call-start = ((), (), s32[]{:S(2)}) async-start(), calls=%async_computation.4 | async-start | bytes 17825792 | tf_op jit(solution)/shard_map/reduce_scatter | solution.py:727
  42.0 29.1 %collective-permute-start.9 = (bf16[256,2176]{1,0:T(8,128)(2,1)S(1)}, bf16[256,2176]{1,0:T(8,128)(2,1)S(1)}, u32[]{:S(2)}, u32[]{:S(2)}) collective-permute-start(bf16[256,2176]{1,0:T(8,128)(2,1)S(1)} %collective-permute-done.1.refs_1_.refs_4_), channel_id=1, source_target_pairs={{0,32},{32,64},{64,96},{96,0},{1,33},{33,65},{65,97},{97,1},{2,34}... | collective-permute-start | bytes 3342344 | tf_op jit(solution)/shard_map/ppermute | solution.py:583
  43.7 27.4 %collective-permute-start.5 = (bf16[256,2176]{1,0:T(8,128)(2,1)S(1)}, bf16[256,2176]{1,0:T(8,128)(2,1)}, u32[]{:S(2)}, u32[]{:S(2)}) collective-permute-start(bf16[256,2176]{1,0:T(8,128)(2,1)S(1)} %collective-permute-done.1.refs_1_.refs_4_), channel_id=1, source_target_pairs={{0,96},{32,0},{64,32},{96,64},{1,97},{33,1},{65,33},{97,65},{2,98}... | collective-permute-start | bytes 3342344 | tf_op jit(solution)/shard_map/ppermute | solution.py:583
  45.9 25.7 %collective-permute-start.3 = (bf16[256,2176]{1,0:T(8,128)(2,1)S(1)}, bf16[256,2176]{1,0:T(8,128)(2,1)S(1)}, u32[]{:S(2)}, u32[]{:S(2)}) collective-permute-start(bf16[256,2176]{1,0:T(8,128)(2,1)S(1)} %collective-permute-done.1.refs_1_.refs_4_), channel_id=1, source_target_pairs={{0,1},{1,0},{2,3},{3,2},{4,5},{5,4},{6,7},{7,6},{8,9},{9,8},{10,11... | collective-permute-start | bytes 3342344 | tf_op jit(solution)/shard_map/ppermute | solution.py:587
  45.9 45.5 %collective-permute-start.8 = (bf16[256,2176]{1,0:T(8,128)(2,1)S(1)}, bf16[256,2176]{1,0:T(8,128)(2,1)}, u32[]{:S(2)}, u32[]{:S(2)}) collective-permute-start(bf16[256,2176]{1,0:T(8,128)(2,1)S(1)} %collective-permute-done.refs_0_.refs_3_), channel_id=1, source_target_pairs={{0,32},{32,64},{64,96},{96,0},{1,33},{33,65},{65,97},{97,1},{2,34}... | collective-permute-start | bytes 3342344 | tf_op jit(solution)/shard_map/ppermute | solution.py:583
  45.9 48.5 %collective-permute-start.4 = (bf16[256,2176]{1,0:T(8,128)(2,1)S(1)}, bf16[256,2176]{1,0:T(8,128)(2,1)}, u32[]{:S(2)}, u32[]{:S(2)}) collective-permute-start(bf16[256,2176]{1,0:T(8,128)(2,1)S(1)} %collective-permute-done.refs_0_.refs_3_), channel_id=1, source_target_pairs={{0,96},{32,0},{64,32},{96,64},{1,97},{33,1},{65,33},{97,65},{2,98}... | collective-permute-start | bytes 3342344 | tf_op jit(solution)/shard_map/ppermute | solution.py:583
  71.0 23.9 %collective-permute-start.11 = (bf16[256,2176]{1,0:T(8,128)(2,1)S(1)}, bf16[256,2176]{1,0:T(8,128)(2,1)S(1)}, u32[]{:S(2)}, u32[]{:S(2)}) collective-permute-start(bf16[256,2176]{1,0:T(8,128)(2,1)S(1)} %collective-permute-done.9.refs_9_.refs_16_), channel_id=1, source_target_pairs={{0,1},{1,0},{2,3},{3,2},{4,5},{5,4},{6,7},{7,6},{8,9},{9,8},{10,11... | collective-permute-start | bytes 3342344 | tf_op jit(solution)/shard_map/ppermute | solution.py:587
  71.5 43.6 %collective-permute-start.13 = (bf16[256,2176]{1,0:T(8,128)(2,1)}, bf16[256,2176]{1,0:T(8,128)(2,1)}, u32[]{:S(2)}, u32[]{:S(2)}) collective-permute-start(bf16[256,2176]{1,0:T(8,128)(2,1)} %collective-permute-done.5.refs_5_.refs_8_), channel_id=1, source_target_pairs={{0,96},{32,0},{64,32},{96,64},{1,97},{33,1},{65,33},{97,65},{2,98}... | collective-permute-start | bytes 3342344 | tf_op jit(solution)/shard_map/ppermute | solution.py:583
  91.4 25.4 %collective-permute-start.12 = (bf16[256,2176]{1,0:T(8,128)(2,1)}, bf16[256,2176]{1,0:T(8,128)(2,1)}, u32[]{:S(2)}, u32[]{:S(2)}) collective-permute-start(bf16[256,2176]{1,0:T(8,128)(2,1)} %collective-permute-done.8.refs_8_.refs_15_), channel_id=1, source_target_pairs={{0,32},{32,64},{64,96},{96,0},{1,33},{33,65},{65,97},{97,1},{2,34}... | collective-permute-start | bytes 3342344 | tf_op jit(solution)/shard_map/ppermute | solution.py:583
  208.0 97.6 %collective-permute-start.37 = (bf16[2,1024,2048]{2,1,0:T(8,128)(2,1)}, bf16[2,1024,2048]{2,1,0:T(8,128)(2,1)}, u32[]{:S(2)}, u32[]{:S(2)}) collective-permute-start(bf16[2,1024,2048]{2,1,0:T(8,128)(2,1)} %shard_map.155), channel_id=1, source_target_pairs={{0,1},{1,0},{2,3},{3,2},{4,5},{5,4},{6,7},{7,6},{8,9},{9,8},{10,11... | collective-permute-start | bytes 25165832 | tf_op jit(solution)/shard_map/ppermute | solution.py:587
  228.5 24.0 %collective-permute-start.28 = (bf16[256,1152]{1,0:T(8,128)(2,1)S(1)}, bf16[256,1152]{1,0:T(8,128)(2,1)S(1)}, u32[]{:S(2)}, u32[]{:S(2)}) collective-permute-start(bf16[256,1152]{1,0:T(8,128)(2,1)S(1)} %collective-permute-done.20.refs_3_.refs_0_), channel_id=1, source_target_pairs={{0,32},{32,64},{64,96},{96,0},{1,33},{33,65},{65,97},{97,1},{2,34}... | collective-permute-start | bytes 1769480 | tf_op jit(solution)/shard_map/ppermute | solution.py:583
  244.1 61.5 %collective-permute-start.36 = (bf16[896,1024]{1,0:T(8,128)(2,1)}, bf16[896,1024]{1,0:T(8,128)(2,1)}, u32[]{:S(2)}, u32[]{:S(2)}) collective-permute-start(bf16[896,1024]{1,0:T(8,128)(2,1)} %get-tuple-element.73.refs_0_), channel_id=1, source_target_pairs={{0,1},{1,0},{2,3},{3,2},{4,5},{5,4},{6,7},{7,6},{8,9},{9,8},{10,11... | collective-permute-start | bytes 5505032 | tf_op jit(solution)/shard_map/ppermute | solution.py:587
  344.0 28.6 %collective-permute-start.41 = (bf16[1792,1024]{1,0:T(8,128)(2,1)}, bf16[1792,1024]{1,0:T(8,128)(2,1)S(1)}, u32[]{:S(2)}, u32[]{:S(2)}) collective-permute-start(bf16[1792,1024]{1,0:T(8,128)(2,1)} %get-tuple-element.88.refs_0_), channel_id=1, source_target_pairs={{0,1},{1,0},{2,3},{3,2},{4,5},{5,4},{6,7},{7,6},{8,9},{9,8},{10,11... | collective-permute-start | bytes 11010056 | tf_op jit(solution)/shard_map/ppermute | solution.py:587
  344.4 25.9 %collective-permute-start.40 = (f32[896,256]{1,0:T(8,128)}, f32[896,256]{1,0:T(8,128)}, u32[]{:S(2)}, u32[]{:S(2)}) collective-permute-start(f32[896,256]{1,0:T(8,128)} %get-tuple-element.95), channel_id=1, source_target_pairs={{0,96},{32,0},{64,32},{96,64},{1,97},{33,1},{65,33},{97,65},{2,98}... | collective-permute-start | bytes 2752520 | tf_op jit(solution)/shard_map/ppermute | solution.py:583
  359.8 28.1 %collective-permute-start.42 = (f32[2,512,128]{2,1,0:T(8,128)}, f32[2,512,128]{2,1,0:T(8,128)}, u32[]{:S(2)}, u32[]{:S(2)}) collective-permute-start(f32[2,512,128]{2,1,0:T(8,128)} %get-tuple-element.100), channel_id=1, source_target_pairs={{0,8},{8,0},{16,24},{24,16},{1,9},{9,1},{17,25},{25,17},{2,10},{10... | collective-permute-start | bytes 1572872 | tf_op jit(solution)/shard_map/ppermute | solution.py:591
  422.9 296.1 %reduce-scatter.3.cloned.1.call-start = ((), (), s32[]{:S(2)}) async-start(), calls=%async_computation.3 | async-start | bytes 17825792 | tf_op jit(solution)/shard_map/reduce_scatter | solution.py:712
  426.2 35.7 %collective-permute-start.73 = (f32[896,256]{1,0:T(8,128)}, f32[896,256]{1,0:T(8,128)}, u32[]{:S(2)}, u32[]{:S(2)}) collective-permute-start(f32[896,256]{1,0:T(8,128)} %get-tuple-element.133), channel_id=1, source_target_pairs={{0,32},{32,64},{64,96},{96,0},{1,33},{33,65},{65,97},{97,1},{2,34}... | collective-permute-start | bytes 2752520 | tf_op jit(solution)/shard_map/ppermute | solution.py:583
  427.8 41.5 %collective-permute-start.44 = (f32[896,256]{1,0:T(8,128)}, f32[896,256]{1,0:T(8,128)}, u32[]{:S(2)}, u32[]{:S(2)}) collective-permute-start(f32[896,256]{1,0:T(8,128)} %get-tuple-element.104), channel_id=1, source_target_pairs={{0,32},{32,64},{64,96},{96,0},{1,33},{33,65},{65,97},{97,1},{2,34}... | collective-permute-start | bytes 2752520 | tf_op jit(solution)/shard_map/ppermute | solution.py:583
  427.8 41.5 %collective-permute-start.45 = (f32[896,256]{1,0:T(8,128)}, f32[896,256]{1,0:T(8,128)}, u32[]{:S(2)}, u32[]{:S(2)}) collective-permute-start(f32[896,256]{1,0:T(8,128)} %get-tuple-element.109), channel_id=1, source_target_pairs={{0,96},{32,0},{64,32},{96,64},{1,97},{33,1},{65,33},{97,65},{2,98}... | collective-permute-start | bytes 2752520 | tf_op jit(solution)/shard_map/ppermute | solution.py:583
  430.7 41.2 %collective-permute-start.47 = (bf16[384,1024]{1,0:T(8,128)(2,1)S(1)}, bf16[384,1024]{1,0:T(8,128)(2,1)S(1)}, u32[]{:S(2)}, u32[]{:S(2)}) collective-permute-start(bf16[384,1024]{1,0:T(8,128)(2,1)S(1)} %maximum_bitcast_fusion.refs_6_), channel_id=1, source_target_pairs={{0,1},{1,0},{2,3},{3,2},{4,5},{5,4},{6,7},{7,6},{8,9},{9,8},{10,11... | collective-permute-start | bytes 2359304 | tf_op jit(solution)/shard_map/ppermute | solution.py:587
  446.9 43.4 %collective-permute-start.74 = (f32[896,256]{1,0:T(8,128)}, f32[896,256]{1,0:T(8,128)}, u32[]{:S(2)}, u32[]{:S(2)}) collective-permute-start(f32[896,256]{1,0:T(8,128)} %add.115), channel_id=1, source_target_pairs={{0,96},{32,0},{64,32},{96,64},{1,97},{33,1},{65,33},{97,65},{2,98}... | collective-permute-start | bytes 2752520 | tf_op jit(solution)/shard_map/ppermute | solution.py:583
  461.9 29.6 %collective-permute-start.62 = (f32[896,256]{1,0:T(8,128)}, f32[896,256]{1,0:T(8,128)}, u32[]{:S(2)}, u32[]{:S(2)}) collective-permute-start(f32[896,256]{1,0:T(8,128)} %get-tuple-element.123), channel_id=1, source_target_pairs={{0,32},{32,64},{64,96},{96,0},{1,33},{33,65},{65,97},{97,1},{2,34}... | collective-permute-start | bytes 2752520 | tf_op jit(solution)/shard_map/ppermute | solution.py:583
  469.2 39.2 %collective-permute-start.70 = (f32[896,256]{1,0:T(8,128)}, f32[896,256]{1,0:T(8,128)S(1)}, u32[]{:S(2)}, u32[]{:S(2)}) collective-permute-start(f32[896,256]{1,0:T(8,128)} %add.114), channel_id=1, source_target_pairs={{0,32},{32,64},{64,96},{96,0},{1,33},{33,65},{65,97},{97,1},{2,34}... | collective-permute-start | bytes 2752520 | tf_op jit(solution)/shard_map/ppermute | solution.py:583
  469.4 41.1 %collective-permute-start.57 = (f32[896,256]{1,0:T(8,128)}, f32[896,256]{1,0:T(8,128)}, u32[]{:S(2)}, u32[]{:S(2)}) collective-permute-start(f32[896,256]{1,0:T(8,128)} %get-tuple-element.119), channel_id=1, source_target_pairs={{0,96},{32,0},{64,32},{96,64},{1,97},{33,1},{65,33},{97,65},{2,98}... | collective-permute-start | bytes 2752520 | tf_op jit(solution)/shard_map/ppermute | solution.py:583
  471.9 53.7 %collective-permute-start.67 = (f32[896,256]{1,0:T(8,128)}, f32[896,256]{1,0:T(8,128)}, u32[]{:S(2)}, u32[]{:S(2)}) collective-permute-start(f32[896,256]{1,0:T(8,128)} %get-tuple-element.129), channel_id=1, source_target_pairs={{0,96},{32,0},{64,32},{96,64},{1,97},{33,1},{65,33},{97,65},{2,98}... | collective-permute-start | bytes 2752520 | tf_op jit(solution)/shard_map/ppermute | solution.py:583
  490.4 35.2 %collective-permute-start.48 = (f32[640,256]{1,0:T(8,128)}, f32[640,256]{1,0:T(8,128)S(1)}, u32[]{:S(2)}, u32[]{:S(2)}) collective-permute-start(f32[640,256]{1,0:T(8,128)} %get-tuple-element.113), channel_id=1, source_target_pairs={{0,32},{32,64},{64,96},{96,0},{1,33},{33,65},{65,97},{97,1},{2,34}... | collective-permute-start | bytes 1966088 | tf_op jit(solution)/shard_map/ppermute | solution.py:583
  491.5 50.6 %collective-permute-start.59 = (f32[896,256]{1,0:T(8,128)}, f32[896,256]{1,0:T(8,128)S(1)}, u32[]{:S(2)}, u32[]{:S(2)}) collective-permute-start(f32[896,256]{1,0:T(8,128)} %get-tuple-element.121), channel_id=1, source_target_pairs={{0,32},{32,64},{64,96},{96,0},{1,33},{33,65},{65,97},{97,1},{2,34}... | collective-permute-start | bytes 2752520 | tf_op jit(solution)/shard_map/ppermute | solution.py:583
  508.4 53.5 %collective-permute-start.56 = (f32[896,256]{1,0:T(8,128)}, f32[896,256]{1,0:T(8,128)S(1)}, u32[]{:S(2)}, u32[]{:S(2)}) collective-permute-start(f32[896,256]{1,0:T(8,128)} %add.117), channel_id=1, source_target_pairs={{0,32},{32,64},{64,96},{96,0},{1,33},{33,65},{65,97},{97,1},{2,34}... | collective-permute-start | bytes 2752520 | tf_op jit(solution)/shard_map/ppermute | solution.py:583
  510.5 54.2 %collective-permute-start.60 = (f32[896,256]{1,0:T(8,128)S(1)}, f32[896,256]{1,0:T(8,128)S(1)}, u32[]{:S(2)}, u32[]{:S(2)}) collective-permute-start(f32[896,256]{1,0:T(8,128)S(1)} %copy-done.39), channel_id=1, source_target_pairs={{0,96},{32,0},{64,32},{96,64},{1,97},{33,1},{65,33},{97,65},{2,98}... | collective-permute-start | bytes 2752520 | tf_op jit(solution)/shard_map/ppermute | solution.py:583
  525.6 56.0 %collective-permute-start.63 = (f32[896,256]{1,0:T(8,128)S(1)}, f32[896,256]{1,0:T(8,128)S(1)}, u32[]{:S(2)}, u32[]{:S(2)}) collective-permute-start(f32[896,256]{1,0:T(8,128)S(1)} %add.129), channel_id=1, source_target_pairs={{0,32},{32,64},{64,96},{96,0},{1,33},{33,65},{65,97},{97,1},{2,34}... | collective-permute-start | bytes 2752520 | tf_op jit(solution)/shard_map/ppermute | solution.py:583
  525.6 36.5 %collective-permute-start.53 = (f32[640,256]{1,0:T(8,128)S(1)}, f32[640,256]{1,0:T(8,128)S(1)}, u32[]{:S(2)}, u32[]{:S(2)}) collective-permute-start(f32[640,256]{1,0:T(8,128)S(1)} %copy-done.63), channel_id=1, source_target_pairs={{0,96},{32,0},{64,32},{96,64},{1,97},{33,1},{65,33},{97,65},{2,98}... | collective-permute-start | bytes 1966088 | tf_op jit(solution)/shard_map/ppermute | solution.py:583
  542.1 42.6 %collective-permute-start.64 = (f32[896,256]{1,0:T(8,128)S(1)}, f32[896,256]{1,0:T(8,128)S(1)}, u32[]{:S(2)}, u32[]{:S(2)}) collective-permute-start(f32[896,256]{1,0:T(8,128)S(1)} %copy-done.60), channel_id=1, source_target_pairs={{0,96},{32,0},{64,32},{96,64},{1,97},{33,1},{65,33},{97,65},{2,98}... | collective-permute-start | bytes 2752520 | tf_op jit(solution)/shard_map/ppermute | solution.py:583
  561.9 39.3 %collective-permute-start.66 = (f32[896,256]{1,0:T(8,128)S(1)}, f32[896,256]{1,0:T(8,128)S(1)}, u32[]{:S(2)}, u32[]{:S(2)}) collective-permute-start(f32[896,256]{1,0:T(8,128)S(1)} %copy-done.59), channel_id=1, source_target_pairs={{0,32},{32,64},{64,96},{96,0},{1,33},{33,65},{65,97},{97,1},{2,34}... | collective-permute-start | bytes 2752520 | tf_op jit(solution)/shard_map/ppermute | solution.py:583
  562.1 39.3 %collective-permute-start.50 = (f32[640,256]{1,0:T(8,128)S(1)}, f32[640,256]{1,0:T(8,128)S(1)}, u32[]{:S(2)}, u32[]{:S(2)}) collective-permute-start(f32[640,256]{1,0:T(8,128)S(1)} %copy-done.62), channel_id=1, source_target_pairs={{0,96},{32,0},{64,32},{96,64},{1,97},{33,1},{65,33},{97,65},{2,98}... | collective-permute-start | bytes 1966088 | tf_op jit(solution)/shard_map/ppermute | solution.py:583
  564.7 48.0 %collective-permute-start.68 = (f32[896,256]{1,0:T(8,128)S(1)}, f32[896,256]{1,0:T(8,128)S(1)}, u32[]{:S(2)}, u32[]{:S(2)}) collective-permute-start(f32[896,256]{1,0:T(8,128)S(1)} %add.133), channel_id=1, source_target_pairs={{0,96},{32,0},{64,32},{96,64},{1,97},{33,1},{65,33},{97,65},{2,98}... | collective-permute-start | bytes 2752520 | tf_op jit(solution)/shard_map/ppermute | solution.py:583
  581.6 33.7 %collective-permute-start.49 = (f32[640,256]{1,0:T(8,128)S(1)}, f32[640,256]{1,0:T(8,128)S(1)}, u32[]{:S(2)}, u32[]{:S(2)}) collective-permute-start(f32[640,256]{1,0:T(8,128)S(1)} %add.119), channel_id=1, source_target_pairs={{0,32},{32,64},{64,96},{96,0},{1,33},{33,65},{65,97},{97,1},{2,34}... | collective-permute-start | bytes 1966088 | tf_op jit(solution)/shard_map/ppermute | solution.py:583
  584.8 38.5 %collective-permute-start.75 = (f32[896,256]{1,0:T(8,128)S(1)}, f32[896,256]{1,0:T(8,128)S(1)}, u32[]{:S(2)}, u32[]{:S(2)}) collective-permute-start(f32[896,256]{1,0:T(8,128)S(1)} %add_add_fusion.1), channel_id=1, source_target_pairs={{0,8},{1,24},{8,0},{9,16},{16,9},{17,25},{24,1},{25,17},{2,10},{3,... | collective-permute-start | bytes 2752520 | tf_op jit(solution)/shard_map/ppermute | solution.py:599
  601.2 28.0 %collective-permute-start.52 = (f32[640,256]{1,0:T(8,128)S(1)}, f32[640,256]{1,0:T(8,128)S(1)}, u32[]{:S(2)}, u32[]{:S(2)}) collective-permute-start(f32[640,256]{1,0:T(8,128)S(1)} %copy-done.61), channel_id=1, source_target_pairs={{0,32},{32,64},{64,96},{96,0},{1,33},{33,65},{65,97},{97,1},{2,34}... | collective-permute-start | bytes 1966088 | tf_op jit(solution)/shard_map/ppermute | solution.py:583
  601.4 37.7 %collective-permute-start.72 = (f32[896,256]{1,0:T(8,128)S(1)}, f32[896,256]{1,0:T(8,128)S(1)}, u32[]{:S(2)}, u32[]{:S(2)}) collective-permute-start(f32[896,256]{1,0:T(8,128)S(1)} %add_add_fusion.2), channel_id=1, source_target_pairs={{0,0},{1,16},{8,8},{9,24},{16,1},{17,17},{24,9},{25,25},{2,2},{3,1... | collective-permute-start | bytes 2752520 | tf_op jit(solution)/shard_map/ppermute | solution.py:599
  615.3 55.0 %collective-permute-start.58 = (f32[896,256]{1,0:T(8,128)S(1)}, f32[896,256]{1,0:T(8,128)S(1)}, u32[]{:S(2)}, u32[]{:S(2)}) collective-permute-start(f32[896,256]{1,0:T(8,128)S(1)} %add_add_fusion.6), channel_id=1, source_target_pairs={{0,0},{1,16},{8,8},{9,24},{16,1},{17,17},{24,9},{25,25},{2,2},{3,1... | collective-permute-start | bytes 2752520 | tf_op jit(solution)/shard_map/ppermute | solution.py:599
  623.2 51.5 %collective-permute-start.61 = (f32[896,256]{1,0:T(8,128)S(1)}, f32[896,256]{1,0:T(8,128)}, u32[]{:S(2)}, u32[]{:S(2)}) collective-permute-start(f32[896,256]{1,0:T(8,128)S(1)} %add_add_fusion.5), channel_id=1, source_target_pairs={{0,8},{1,24},{8,0},{9,16},{16,9},{17,25},{24,1},{25,17},{2,10},{3,... | collective-permute-start | bytes 2752520 | tf_op jit(solution)/shard_map/ppermute | solution.py:599
  629.2 83.0 %collective-permute-start.69 = (f32[896,256]{1,0:T(8,128)S(1)}, f32[896,256]{1,0:T(8,128)}, u32[]{:S(2)}, u32[]{:S(2)}) collective-permute-start(f32[896,256]{1,0:T(8,128)S(1)} %add_add_fusion.3), channel_id=1, source_target_pairs={{0,8},{1,24},{8,0},{9,16},{16,9},{17,25},{24,1},{25,17},{2,10},{3,... | collective-permute-start | bytes 2752520 | tf_op jit(solution)/shard_map/ppermute | solution.py:599
  629.2 83.0 %collective-permute-start.65 = (f32[896,256]{1,0:T(8,128)S(1)}, f32[896,256]{1,0:T(8,128)}, u32[]{:S(2)}, u32[]{:S(2)}) collective-permute-start(f32[896,256]{1,0:T(8,128)S(1)} %add_add_fusion.4), channel_id=1, source_target_pairs={{0,0},{1,16},{8,8},{9,24},{16,1},{17,17},{24,9},{25,25},{2,2},{3,1... | collective-permute-start | bytes 2752520 | tf_op jit(solution)/shard_map/ppermute | solution.py:599
  639.1 63.7 %collective-permute-start.51 = (f32[640,256]{1,0:T(8,128)}, f32[640,256]{1,0:T(8,128)S(1)}, u32[]{:S(2)}, u32[]{:S(2)}) collective-permute-start(f32[640,256]{1,0:T(8,128)} %add_add_fusion.8), channel_id=1, source_target_pairs={{0,0},{1,16},{8,8},{9,24},{16,1},{17,17},{24,9},{25,25},{2,2},{3,1... | collective-permute-start | bytes 1966088 | tf_op jit(solution)/shard_map/ppermute | solution.py:599
  671.2 31.5 %collective-permute-start.55 = (f32[640,256]{1,0:T(8,128)}, f32[640,256]{1,0:T(8,128)S(1)}, u32[]{:S(2)}, u32[]{:S(2)}) collective-permute-start(f32[640,256]{1,0:T(8,128)} %add_add_fusion.7), channel_id=1, source_target_pairs={{0,8},{1,24},{8,0},{9,16},{16,9},{17,25},{24,1},{25,17},{2,10},{3,... | collective-permute-start | bytes 1966088 | tf_op jit(solution)/shard_map/ppermute | solution.py:599
  (99 other events, 1614.2 us)
Sparse Core Ops, SparseCore 0:
  42.0 112.4 all-gather.1
  423.0 106.1 reduce-scatter.4
  532.6 149.6 reduce-scatter.2

commit v2 on v1

--- a/solution.py
+++ b/solution.py
@@ -17,7 +17,7 @@
 F32 = jnp.float32
 BF16 = jnp.bfloat16
 VMEM_LIMIT = 60 * 1024 * 1024
-TILE = 256
+TILE = 512
 
 
 def norm_fwd(row_vals, norm_gain):
@@ -279,7 +279,7 @@
     return pl.multiple_of((1 - pos_ref[2] if part else pos_ref[2]) * half, half)
 
 
-def nn_kernel(keys, first, count_out, which, pos_ref, acts_ref, *refs):
+def nn_kernel(keys, first, count_out, pos_ref, acts_ref, *refs):
     count = len(keys)
     halves = refs[: 2 * count]
     outs = refs[2 * count : 2 * count + count_out]
@@ -289,7 +289,7 @@
     copies = []
     for idx in range(count):
         cols = pl.ds(pl.multiple_of(piece_block(pos_ref, *keys[idx]) * block, block), block)
-        copies.append([pltpu.make_async_copy(acts_ref.at[which, :, cols], acts_buf.at[:, pl.ds(idx * block, block)], acts_sem.at[idx])])
+        copies.append([pltpu.make_async_copy(acts_ref.at[:, cols], acts_buf.at[:, pl.ds(idx * block, block)], acts_sem.at[idx])])
         for part in range(2):
             rows = pl.ds(idx * block + half_start(pos_ref, part, half), half)
             copies[-1].append(pltpu.make_async_copy(halves[2 * idx + part], w_buf.at[rows], w_sem.at[2 * idx + part]))
@@ -321,15 +321,15 @@
             start += width
 
 
-def nn_pieces(pos, acts, which, parts, widths):
+def nn_pieces(pos, acts, parts, widths):
     keys = [(step, other) for step in (0, 1, 3, 2) for other in range(2)]
     halves = [parts[step][other][part] for step, other in keys for part in range(2)]
-    _, tokens, depth = acts.shape
+    tokens, depth = acts.shape
     width = sum(widths)
     count = len(keys)
     anywhere = pl.BlockSpec(memory_space=pl.ANY)
     return pl.pallas_call(
-        functools.partial(nn_kernel, keys, 2, len(widths), which),
+        functools.partial(nn_kernel, keys, 2, len(widths)),
         grid_spec=pltpu.PrefetchScalarGridSpec(
             num_scalar_prefetch=1,
             grid=(1,),
@@ -446,26 +446,22 @@
 
 
 def pick_cols(pos, acts):
-    count, tokens, depth = acts.shape
+    tokens, depth = acts.shape
     block = depth // (NC * NZ)
-    places = [(which, idx) for which in range(count) for idx in range(NZ)]
 
     def kernel(pos_ref, in_ref, out_ref, buf, in_sem, out_sem):
-        copies = []
-        for slot, (which, idx) in enumerate(places):
-            read = pltpu.make_async_copy(in_ref.at[which, :, picked_cols(pos_ref, idx, block)], buf.at[slot], in_sem.at[slot])
-            write = pltpu.make_async_copy(buf.at[slot], out_ref.at[which, :, pl.ds(idx * block, block)], out_sem.at[slot])
-            copies.append((read, write))
+        reads = [pltpu.make_async_copy(in_ref.at[:, picked_cols(pos_ref, idx, block)], buf.at[idx], in_sem.at[idx]) for idx in range(NZ)]
+        writes = [pltpu.make_async_copy(buf.at[idx], out_ref.at[:, pl.ds(idx * block, block)], out_sem.at[idx]) for idx in range(NZ)]
+        for read in reads:
             read.start()
-        for read, write in copies:
+        for read, write in zip(reads, writes):
             read.wait()
             write.start()
-        for _, write in copies:
+        for write in writes:
             write.wait()
 
-    sems = pltpu.SemaphoreType.DMA((len(places),))
-    out = jax.ShapeDtypeStruct((count, tokens, depth // 2), BF16)
-    return dma_kernel(kernel, pos, [acts], [out], [pltpu.VMEM((len(places), tokens, block), BF16), sems, sems])[0]
+    sems = pltpu.SemaphoreType.DMA((NZ,))
+    return dma_kernel(kernel, pos, [acts], [jax.ShapeDtypeStruct((tokens, depth // 2), BF16)], [pltpu.VMEM((NZ, tokens, block), BF16), sems, sems])[0]
 
 
 def grad_kernel(heights, pos_ref, *refs):
@@ -507,7 +503,7 @@
 
 
 def grad_pieces(pos, pairs):
-    _, tokens, depth = pairs[0][2].shape
+    tokens, depth = pairs[0][2].shape
     cols = depth // (NZ * NY)
     in_specs = []
     args = []
@@ -518,12 +514,10 @@
     def bit(pos, part):
         return 1 - pos[2] if part else pos[2]
 
-    for own, recv, acts, acts_recv, height, block, which in pairs:
+    for own, recv, acts, acts_recv, height, block in pairs:
         in_specs += [pl.BlockSpec((height, tokens), lambda n, pos, block=block: (block, 0))] * 2
-        for part in range(2):
-            in_specs.append(pl.BlockSpec((None, tokens, cols), lambda n, pos, part=part, which=which: (which, 0, z_of(n, pos) * NY + 2 * pos[1] + bit(pos, part))))
-        for part in range(2):
-            in_specs.append(pl.BlockSpec((None, tokens, cols), lambda n, pos, part=part, which=which: (which, 0, z_of(n, pos) * 2 + bit(pos, part))))
+        in_specs += [pl.BlockSpec((tokens, cols), lambda n, pos, part=part: (0, z_of(n, pos) * NY + 2 * pos[1] + bit(pos, part))) for part in range(2)]
+        in_specs += [pl.BlockSpec((tokens, cols), lambda n, pos, part=part: (0, z_of(n, pos) * 2 + bit(pos, part))) for part in range(2)]
         args += [own, recv, acts, acts, acts_recv, acts_recv]
     heights = [pair[4] for pair in pairs]
     rows = sum(heights)
@@ -568,6 +562,31 @@
         out_shape=jax.ShapeDtypeStruct((cols, 2 * height) if transpose else (2 * height, cols), F32),
         compiler_params=params(),
         cost_estimate=cost(2e9, 16 * height * cols),
+    )(pos, first, second)
+
+
+def place_attn(pos, first, second, o_blk, head):
+    rows, cols = first.shape
+    qk = 2 * head
+
+    def kernel(pos_ref, first_ref, second_ref, out_ref, qkv_ref):
+        for idx, ref in enumerate((first_ref, second_ref)):
+            bit = 1 - pos_ref[2] if idx else pos_ref[2]
+            out_ref[pl.ds(pl.multiple_of(bit * o_blk, o_blk), o_blk), :] = ref[:o_blk, :]
+            qkv_ref[:, pl.ds(pl.multiple_of(bit * qk, qk), qk)] = ref[o_blk : o_blk + qk, :].T
+            qkv_ref[:, pl.ds(pl.multiple_of(2 * qk + bit * head, head), head)] = ref[o_blk + qk :, :].T
+
+    def whole(*shape):
+        return pl.BlockSpec(shape, lambda n, pos: (0, 0))
+
+    shapes = ((2 * o_blk, cols), (cols, 2 * (qk + head)))
+    return pl.pallas_call(
+        kernel,
+        grid_spec=pltpu.PrefetchScalarGridSpec(num_scalar_prefetch=1, grid=(1,), in_specs=[whole(rows, cols)] * 2, out_specs=[whole(*shape) for shape in shapes]),
+        out_shape=[jax.ShapeDtypeStruct(shape, F32) for shape in shapes],
+        compiler_params=params(),
+        cost_estimate=cost(2e9, 16 * rows * cols),
+        name="p_attn",
     )(pos, first, second)
 
 
@@ -641,8 +660,10 @@
             return [turn(jnp.where(even_y, blocks[flip], blocks[1 - flip]), flip) for flip in range(2)]
 
         def gather_weight(piece):
-            left = [hop_z(half, 1) for half in piece]
-            right = [hop_z(half, -1) for half in piece]
+            left, right = [], []
+            for part in (1, 0):
+                left.insert(0, hop_z(piece[part], 1))
+                right.insert(0, hop_z(piece[part], -1))
             far = [hop_z(left[0], 1), hop_z(right[1], -1)]
             parts = []
             for mine in (piece, right, far, left):
@@ -692,12 +713,12 @@
 
         x_rows = x_in[0].astype(F32)
         normed, norm_pull = jax.vjp(lambda row_vals: norm_fwd(row_vals, norm_gain), x_rows)
-        both = jnp.stack([normed.astype(BF16), dy_in[0]])
-        both_all = lax.all_gather(after(both, *wf_piece), ("y", "x"), axis=1, tiled=True)
+        h_all = lax.all_gather(after(normed.astype(BF16), wf_piece[0], wf_piece[1]), ("y", "x"), axis=0, tiled=True)
+        dy_all = lax.all_gather(after(dy_in[0], *wf_piece), ("y", "x"), axis=0, tiled=True)
         wf_parts = gather_weight(wf_piece)
         ws_parts = gather_weight(ws_piece)
 
-        gate_up, qkv_tok = nn_pieces(pos, both_all, 0, wf_parts, (2 * ff_blk, qkv_blk))
+        gate_up, qkv_tok = nn_pieces(pos, h_all, wf_parts, (2 * ff_blk, qkv_blk))
         third = qkv_tok[:, o_blk:]
         qkv_other = swap_c(my_rows(qkv_tok, False))
         third_own = swap_y(my_rows(third, True))
@@ -706,35 +727,37 @@
         act_recv = swap_c(act_t)
         qkv_seq, attn_own, attn_other = attn_fwd(after(pos, act_t), qkv_tok, qkv_other, third_own, third_other, cos_tab, sin_tab)
         attn_got = swap_c(attn_other)
-        picked = pick_cols(after(pos, attn_own), both_all)
-        both_recv = swap_c(picked)
-        y_part = nt_pieces(after(pos, picked), [act_val, attn_own, attn_got], ws_parts)
+        y_part = nt_pieces(after(pos, attn_own), [act_val, attn_own, attn_got], ws_parts)
         mix_sum = lax.psum_scatter(y_part, ("y", "x"), scatter_dimension=0, tiled=True)
         y_out = (x_rows + mix_sum).astype(BF16)[None]
 
-        g_act = grad_start([(act_t, act_recv, both_all, both_recv, ff_blk, 0, 1)], y_part)
-        d_act, d_attn = nn_pieces(after(pos, g_act[3][0]), both_all, 1, ws_parts, (ff_blk, o_blk))
+        dy_picked = pick_cols(after(pos, y_part), dy_all)
+        dy_recv = swap_c(dy_picked)
+        g_act = grad_start([(act_t, act_recv, dy_all, dy_recv, ff_blk, 0)], y_part)
+        h_picked = pick_cols(after(pos, g_act[3][0]), h_all)
+        h_recv = swap_c(h_picked)
+        d_act, d_attn = nn_pieces(after(pos, h_picked), dy_all, ws_parts, (ff_blk, o_blk))
         d_attn_other = swap_c(my_rows(d_attn, False))
         d_gate_up, d_gate_up_t = act_bwd(gate_up, d_act)
         d_gate_up_recv = swap_c(d_gate_up_t)
         d_queries, keep, send = attn_bwd(after(pos, d_gate_up_t), qkv_seq, d_attn, d_attn_other, cos_tab, sin_tab)
         got = swap_y(send)
         g_act = grad_pass(g_act, d_queries)
-        g_gate = grad_start([(d_gate_up_t, d_gate_up_recv, both_all, both_recv, ff_blk, 0, 0)], *g_act[3])
-        d_own, d_other = attn_post(after(pos, g_gate[3][0]), d_queries, keep, got, cos_tab, sin_tab)
+        g_gate = grad_start([(d_gate_up_t, d_gate_up_recv, h_all, h_recv, ff_blk, 0)], *g_act[3])
+        g_up = grad_start([(d_gate_up_t, d_gate_up_recv, h_all, h_recv, ff_blk, 1)], g_gate[3][0])
+        d_own, d_other = attn_post(after(pos, g_up[3][0]), d_queries, keep, got, cos_tab, sin_tab)
         d_got = swap_c(d_other)
         dh_part = nt_pieces(pos, [d_gate_up, d_own, d_got], wf_parts)
         d_h = lax.psum_scatter(dh_part, ("y", "x"), scatter_dimension=0, tiled=True)
         d_h = d_h.astype(BF16)
         dx_out = (dy_in[0].astype(F32) + norm_pull(d_h.astype(F32))[0]).astype(BF16)[None]
-        g_up = grad_start([(d_gate_up_t, d_gate_up_recv, both_all, both_recv, ff_blk, 1, 0)], dh_part)
-        g_gate = grad_pass(g_gate, g_up[3][0])
+        g_gate = grad_pass(g_gate, dh_part)
 
         attn_t = both_rows(attn_own, attn_got).T
         d_qkv_t = both_rows(d_own, d_got).T
         attn_recv = swap_c(attn_t)
         d_qkv_recv = swap_c(d_qkv_t)
-        g_attn = grad_start([(attn_t, attn_recv, both_all, both_recv, o_blk, 0, 1), (d_qkv_t, d_qkv_recv, both_all, both_recv, qkv_blk, 0, 0)], *g_gate[3])
+        g_attn = grad_start([(attn_t, attn_recv, dy_all, dy_recv, o_blk, 0), (d_qkv_t, d_qkv_recv, h_all, h_recv, qkv_blk, 0)], *g_gate[3])
         g_up = grad_pass(g_up, g_attn[3][0])
         b_act = grad_back(g_act, g_attn[3][0])
         g_attn = grad_pass(g_attn)
@@ -744,10 +767,7 @@
         dw_down = place(pos, *b_act, ff_blk, 0, False)
         dw_gate = place(pos, *b_gate, ff_blk, 0, True)
         dw_up = place(pos, *b_up, ff_blk, 0, True)
-        dw_out = place(pos, *b_attn, o_blk, 0, False)
-        dw_q = place(pos, *b_attn, 2 * head, 1, True)
-        dw_kv = place(pos, *b_attn, head, 2 * o_blk // head, True)
-        dw_qkv = jnp.concatenate([dw_q, dw_kv], axis=1)
+        dw_out, dw_qkv = place_attn(after(pos, dx_out, dw_up), *b_attn, o_blk, head)
         return y_out, dx_out, dw_qkv, dw_out, dw_gate, dw_up, dw_down
 
 

time: 735 us -> 670 us (0.912)
  waiting for transfers between devices: 388 us -> 300 us
  starting transfers between devices: 70.7 us -> 85.4 us
    ppermute x36, waiting for transfers between devices: 250 us -> 167 us  [hop_z(): return lax.ppermute(val, 'z', ring(step, NZ))]
    all_gather x1 -> x2, waiting for transfers between devices: 34.1 us -> 0.04 us  [the longest x1 0.02 us: layer(): lax.all_gather(after(normed.astype(BF16), wf_piece[0], wf_piece[1]), ('y'...]
    ppermute x12, starting transfers between devices: 19.6 us -> 28.3 us  [turn(): return lax.ppermute(val, ('y', 'c'), pairs)]
    ppermute x25 -> x26, waiting for transfers between devices: 7.03 us -> 15.4 us  [swap_c(): return lax.ppermute(val, 'c', [(0, 1), (1, 0)])]
    pallas_call x6 -> x3, Pallas kernels: 18.8 us -> 10.9 us  [place(): pl.pallas_call(kernel, grid_spec=pltpu.PrefetchScalarGridSpec(num_scalar_...]
    pallas_call x2 -> x3, Pallas kernels: 46.2 us -> 50 us  [the longest x2 46.8 us: nn_pieces(): pl.pallas_call(functools.partial(nn_kernel, keys, 2, len(widths)), grid_s...]
  transfers between devices with their start and end apart: 79 -> 81, of which waited for: 37 -> 34; matrix products, arithmetic and copies ran while one was open for 5% -> 7% of each run, Pallas kernels for 12% -> 21%
where the time goes in v2:
time: 670 us; the launch traced here: 661 us
  waiting for transfers between devices  300 us (45%)
  Pallas kernels  196 us (29%)
  starting transfers between devices  85.4 us (13%)
  other arithmetic  37.5 us (6%)
  local copies, waits for them, and re-layouts  26.2 us (4%)
  between operations  15.2 us (2%)
    ppermute x36, waiting for transfers between devices, hop_z(): return lax.ppermute(val, 'z', ring(step, NZ))  167 us
    ppermute x12, waiting for transfers between devices, turn(): return lax.ppermute(val, ('y', 'c'), pairs)  99.6 us
    pallas_call x4, Pallas kernels, grad_pieces(): pl.pallas_call(functools.partial(grad_kernel, heights), grid_spec=pltpu.P...  53.7 us
    pallas_call x2, Pallas kernels, nn_pieces(): pl.pallas_call(functools.partial(nn_kernel, keys, 2, len(widths)), grid_s...  46.8 us
    pallas_call x2, Pallas kernels, nt_pieces(): pl.pallas_call(functools.partial(nt_kernel, keys, sides), grid_spec=pltpu...  44.5 us
    ppermute x36, starting transfers between devices, hop_z(): return lax.ppermute(val, 'z', ring(step, NZ))  42.2 us
    ppermute x12, starting transfers between devices, turn(): return lax.ppermute(val, ('y', 'c'), pairs)  28.3 us
    pallas_call x3, Pallas kernels, per_sequence(): pl.pallas_call(kernel, grid_spec=pltpu.PrefetchScalarGridSpec(num_scalar_...  16.9 us
  transfers between devices with their start and end apart: 81, of which 34 were waited for; matrix products, arithmetic and copies ran while one was open for 7% of the time, Pallas kernels for 21%

profile of v2, /device:TPU:1, one launch (start us, length us, event | category | flops | bytes accessed | tf_op | source)
XLA Modules:
  0.0 660.6 jit_solution(8492002101143654692)
XLA Ops:
  12.1 4.1 collective-permute-start.1
  19.5 21.4 %collective-permute-done.1.refs_1_.refs_4_ = bf16[256,2176]{1,0:T(8,128)(2,1)S(1)} collective-permute-done((bf16[256,2176]{1,0:T(8,128)(2,1)}, bf16[256,2176]{1,0:T(8,128)(2,1)S(1)}, u32[]{:S(2)}, u32[]{:S(2)}) %collective-permute-start.1) | collective-permute-done | bytes 1114144 | tf_op jit(solution)/shard_map/ppermute | solution.py:618
  52.1 4.4 collective-permute-done.21.refs_4_.refs_1_
  59.1 15.5 %collective-permute-done.20.refs_3_.refs_0_ = bf16[256,1152]{1,0:T(8,128)(2,1)} collective-permute-done((bf16[256,1152]{1,0:T(8,128)(2,1)S(1)}, bf16[256,1152]{1,0:T(8,128)(2,1)}, u32[]{:S(2)}, u32[]{:S(2)}) %collective-permute-start.20) | collective-permute-done | bytes 589856 | tf_op jit(solution)/shard_map/ppermute | solution.py:618
  80.0 17.0 %collective-permute-done.8.refs_8_.refs_15_ = bf16[256,2176]{1,0:T(8,128)(2,1)S(1)} collective-permute-done((bf16[256,2176]{1,0:T(8,128)(2,1)S(1)}, bf16[256,2176]{1,0:T(8,128)(2,1)S(1)}, u32[]{:S(2)}, u32[]{:S(2)}) %collective-permute-start.8) | collective-permute-done | bytes 1114144 | tf_op jit(solution)/shard_map/ppermute | solution.py:602
  97.0 4.9 collective-permute-done.4.refs_4_.refs_7_
  102.6 17.8 %collective-permute-done.13.refs_13_.refs_12_ = bf16[256,2176]{1,0:T(8,128)(2,1)S(1)} collective-permute-done((bf16[256,2176]{1,0:T(8,128)(2,1)S(1)}, bf16[256,2176]{1,0:T(8,128)(2,1)S(1)}, u32[]{:S(2)}, u32[]{:S(2)}) %collective-permute-start.13) | collective-permute-done | bytes 1114144 | tf_op jit(solution)/shard_map/ppermute | solution.py:602
  127.2 27.6 %shard_map.153 = (bf16[1024,1792]{1,0:T(8,128)(2,1)}, bf16[1024,384]{1,0:T(8,128)(2,1)}) custom-call(s32[3]{0:T(128)} %pad_add_fusion.pos_ref, bf16[1024,4096]{1,0:T(8,128)(2,1)} %all-gather.3.cloned.1.call-done.acts_ref.in_ref.refs_2_.refs_3_.refs_8_.refs_9_, bf16[256,2176]{1,0:T(8,128)(2,1)} %copy-done.4, bf16[256,2176]{1,0:T(8,128)(2,1)} %copy-done.3, ...), custom_call_target="tpu_custom_call" | custom-call | flops 912680576 | bytes 26214400 | tf_op jit(solution)/shard_map/pallas_call | solution.py:331
  162.1 6.8 %collective-permute-done.18.other_third_ref = bf16[512,128]{1,0:T(8,128)(2,1)S(1)} collective-permute-done((bf16[512,128]{1,0:T(8,128)(2,1)S(1)}, bf16[512,128]{1,0:T(8,128)(2,1)S(1)}, u32[]{:S(2)}, u32[]{:S(2)}) %collective-permute-start.18) | collective-permute-done | bytes 131104 | tf_op jit(solution)/shard_map/ppermute | solution.py:623
  169.2 5.3 collective-permute-done.17.own_third_ref
  181.8 4.9 act_fwd.1
  186.7 5.6 shard_map.154
  200.8 17.1 %shard_map.155 = f32[1024,4096]{1,0:T(8,128)} custom-call(s32[3]{0:T(128)} %pad_add_fusion.pos_ref, bf16[1024,896]{1,0:T(8,128)(2,1)} %get-tuple-element.82.refs_0_, bf16[512,256]{1,0:T(8,128)(2,1)} %get-tuple-element.80.refs_1_, bf16[512,256]{1,0:T(8,128)(2,1)} %copy.38.refs_2_, bf16[256,1152]{1,0:T(8,128)(2,1)} %collective-permute-done.20.refs_3_.refs_0_, ...), custom_call_target="tpu_custom_call" | custom-call | flops 483183808 | bytes 26214400 | tf_op jit(solution)/shard_map/pallas_call | solution.py:409
  217.9 4.3 shard_map.156
  223.0 9.3 %collective-permute-done.36.refs_1_ = bf16[896,1024]{1,0:T(8,128)(2,1)S(1)} collective-permute-done((bf16[896,1024]{1,0:T(8,128)(2,1)S(1)}, bf16[896,1024]{1,0:T(8,128)(2,1)S(1)}, u32[]{:S(2)}, u32[]{:S(2)}) %collective-permute-start.36) | collective-permute-done | bytes 1835040 | tf_op jit(solution)/shard_map/ppermute | solution.py:606
  233.6 13.4 %grad.4 = (f32[896,256]{1,0:T(8,128)}, f32[896,256]{1,0:T(8,128)}, f32[896,256]{1,0:T(8,128)}, f32[896,256]{1,0:T(8,128)}, f32[896,256]{1,0:T(8,128)}, /*index=5...) custom-call(s32[3]{0:T(128)} %pad_add_fusion.pos_ref, bf16[896,1024]{1,0:T(8,128)(2,1)} %get-tuple-element.77.refs_0_, ...), custom_call_target="tpu_custom_call" | custom-call | flops 375809632 | bytes 8388608 | tf_op jit(solution)/shard_map/grad/pallas_call | solution.py:524
  246.9 4.1 shard_map.157
  251.5 19.2 %shard_map.158 = (bf16[1024,896]{1,0:T(8,128)(2,1)}, bf16[1024,256]{1,0:T(8,128)(2,1)}) custom-call(s32[3]{0:T(128)} %pad_add_fusion.pos_ref, bf16[1024,4096]{1,0:T(8,128)(2,1)} %all-gather.5.cloned.1.call-done.in_ref.refs_2_.refs_3_.acts_ref, bf16[256,1152]{1,0:T(8,128)(2,1)} %collective-permute-done.20.refs_3_.refs_0_, ...), custom_call_target="tpu_custom_call" | custom-call | flops 483183808 | bytes 17825792 | tf_op jit(solution)/shard_map/pallas_call | solution.py:331
  270.7 7.0 %act_bwd.1 = (bf16[1024,1792]{1,0:T(8,128)(2,1)}, bf16[1792,1024]{1,0:T(8,128)(2,1)}) custom-call(bf16[1024,1792]{1,0:T(8,128)(2,1)} %get-tuple-element.76.ab_ref, bf16[1024,896]{1,0:T(8,128)(2,1)} %get-tuple-element.89.du_ref), custom_call_target="tpu_custom_call" | custom-call | flops 400000000 | bytes 14000000 | tf_op jit(solution)/shard_map/act_bwd/pallas_call | solution.py:261
  285.8 8.1 %shard_map.159 = (bf16[2,512,256]{2,1,0:T(8,128)(2,1)}, f32[2,512,128]{2,1,0:T(8,128)}, f32[2,512,128]{2,1,0:T(8,128)}) custom-call(s32[3]{0:T(128)} %pad_add_fusion.pos_ref, bf16[2,512,512]{2,1,0:T(8,128)(2,1)} %get-tuple-element.95.seq_ref, bf16[1024,256]{1,0:T(8,128)(2,1)} %get-tuple-element.96.own_ref, bf16[512,256]{1,0:T(8,128)(2,1)} %copy-done.63, ...), custom_call_target="tpu_custom_call" | custom-call | flops 800000000 | bytes 4000000 | tf_op jit(solution)/shard_map/pallas_call | solution.py:143
  294.9 6.4 collective-permute-done.38
  307.9 13.4 %grad.5 = (f32[896,256]{1,0:T(8,128)}, f32[896,256]{1,0:T(8,128)}, f32[896,256]{1,0:T(8,128)}, f32[896,256]{1,0:T(8,128)}, f32[896,256]{1,0:T(8,128)}, /*index=5...) custom-call(s32[3]{0:T(128)} %pad_add_fusion.pos_ref, bf16[1792,1024]{1,0:T(8,128)(2,1)} %get-tuple-element.93.refs_0_, ...), custom_call_target="tpu_custom_call" | custom-call | flops 375809632 | bytes 8388608 | tf_op jit(solution)/shard_map/grad/pallas_call | solution.py:524
  321.2 13.4 %grad.6 = (f32[896,256]{1,0:T(8,128)}, f32[896,256]{1,0:T(8,128)}, f32[896,256]{1,0:T(8,128)}, f32[896,256]{1,0:T(8,128)}, f32[896,256]{1,0:T(8,128)}, /*index=5...) custom-call(s32[3]{0:T(128)} %pad_add_fusion.pos_ref, bf16[1792,1024]{1,0:T(8,128)(2,1)} %get-tuple-element.93.refs_0_, ...), custom_call_target="tpu_custom_call" | custom-call | flops 375809632 | bytes 8388608 | tf_op jit(solution)/shard_map/grad/pallas_call | solution.py:524
  334.6 3.2 shard_map.160
  342.7 27.3 %shard_map.161 = f32[1024,4096]{1,0:T(8,128)} custom-call(s32[3]{0:T(128)} %pad_add_fusion.pos_ref, bf16[1024,1792]{1,0:T(8,128)(2,1)} %get-tuple-element.90.refs_0_, bf16[512,384]{1,0:T(8,128)(2,1)} %get-tuple-element.108.refs_1_, bf16[512,384]{1,0:T(8,128)(2,1)} %copy.40.refs_2_, bf16[256,2176]{1,0:T(8,128)(2,1)} %copy-done.4, ...), custom_call_target="tpu_custom_call" | custom-call | flops 912680576 | bytes 34603008 | tf_op jit(solution)/shard_map/pallas_call | solution.py:409
  377.9 15.9 %collective-permute-done.74 = f32[896,256]{1,0:T(8,128)} collective-permute-done((f32[896,256]{1,0:T(8,128)}, f32[896,256]{1,0:T(8,128)}, u32[]{:S(2)}, u32[]{:S(2)}) %collective-permute-start.74) | collective-permute-done | bytes 917536 | tf_op jit(solution)/shard_map/ppermute | solution.py:602
  397.6 15.0 %collective-permute-done.72 = f32[896,256]{1,0:T(8,128)S(1)} collective-permute-done((f32[896,256]{1,0:T(8,128)}, f32[896,256]{1,0:T(8,128)S(1)}, u32[]{:S(2)}, u32[]{:S(2)}) %collective-permute-start.72) | collective-permute-done | bytes 917536 | tf_op jit(solution)/shard_map/ppermute | solution.py:602
  412.6 3.4 collective-permute-start.54
  417.4 13.5 %collective-permute-done.76.second_ref = f32[896,256]{1,0:T(8,128)} collective-permute-done((f32[896,256]{1,0:T(8,128)}, f32[896,256]{1,0:T(8,128)}, u32[]{:S(2)}, u32[]{:S(2)}) %collective-permute-start.76) | collective-permute-done | bytes 917536 | tf_op jit(solution)/shard_map/ppermute | solution.py:618
  433.1 19.7 %collective-permute-done.46 = f32[896,256]{1,0:T(8,128)} collective-permute-done((f32[896,256]{1,0:T(8,128)}, f32[896,256]{1,0:T(8,128)}, u32[]{:S(2)}, u32[]{:S(2)}) %collective-permute-start.46) | collective-permute-done | bytes 917536 | tf_op jit(solution)/shard_map/ppermute | solution.py:602
  463.7 13.6 %grad.7 = (f32[640,256]{1,0:T(8,128)}, f32[640,256]{1,0:T(8,128)}, f32[640,256]{1,0:T(8,128)}, f32[640,256]{1,0:T(8,128)}, f32[640,256]{1,0:T(8,128)}, /*index=5...) custom-call(s32[3]{0:T(128)} %pad_add_fusion.pos_ref, bf16[256,1024]{1,0:T(8,128)(2,1)} %copy-done.24, ...), custom_call_target="tpu_custom_call" | custom-call | flops 268435456 | bytes 8388608 | tf_op jit(solution)/shard_map/grad/pallas_call | solution.py:524
  481.7 10.3 %collective-permute-done.68 = f32[896,256]{1,0:T(8,128)S(1)} collective-permute-done((f32[896,256]{1,0:T(8,128)}, f32[896,256]{1,0:T(8,128)S(1)}, u32[]{:S(2)}, u32[]{:S(2)}) %collective-permute-start.68) | collective-permute-done | bytes 917536 | tf_op jit(solution)/shard_map/ppermute | solution.py:602
  492.0 19.8 %collective-permute-done.65 = f32[896,256]{1,0:T(8,128)} collective-permute-done((f32[896,256]{1,0:T(8,128)}, f32[896,256]{1,0:T(8,128)}, u32[]{:S(2)}, u32[]{:S(2)}) %collective-permute-start.65) | collective-permute-done | bytes 917536 | tf_op jit(solution)/shard_map/ppermute | solution.py:602
  514.7 11.1 %collective-permute-done.57 = f32[640,256]{1,0:T(8,128)S(1)} collective-permute-done((f32[640,256]{1,0:T(8,128)}, f32[640,256]{1,0:T(8,128)S(1)}, u32[]{:S(2)}, u32[]{:S(2)}) %collective-permute-start.57) | collective-permute-done | bytes 655392 | tf_op jit(solution)/shard_map/ppermute | solution.py:602
  531.6 13.8 %collective-permute-done.50 = f32[896,256]{1,0:T(8,128)S(1)} collective-permute-done((f32[896,256]{1,0:T(8,128)S(1)}, f32[896,256]{1,0:T(8,128)S(1)}, u32[]{:S(2)}, u32[]{:S(2)}) %collective-permute-start.50) | collective-permute-done | bytes 917536 | tf_op jit(solution)/shard_map/ppermute | solution.py:602
  551.5 9.4 %collective-permute-done.59 = f32[640,256]{1,0:T(8,128)S(1)} collective-permute-done((f32[640,256]{1,0:T(8,128)S(1)}, f32[640,256]{1,0:T(8,128)S(1)}, u32[]{:S(2)}, u32[]{:S(2)}) %collective-permute-start.59) | collective-permute-done | bytes 655392 | tf_op jit(solution)/shard_map/ppermute | solution.py:602
  561.0 4.2 collective-permute-start.67
  569.4 4.1 collective-permute-done.58
  576.3 3.5 shard_map.164
  582.3 5.1 collective-permute-start.60
  589.6 11.8 %collective-permute-done.67.first_ref = f32[896,256]{1,0:T(8,128)S(1)} collective-permute-done((f32[896,256]{1,0:T(8,128)S(1)}, f32[896,256]{1,0:T(8,128)S(1)}, u32[]{:S(2)}, u32[]{:S(2)}) %collective-permute-start.67) | collective-permute-done | bytes 917536 | tf_op jit(solution)/shard_map/ppermute | solution.py:618
  602.3 3.7 shard_map.163
  606.0 23.3 %collective-permute-done.56.second_ref = f32[896,256]{1,0:T(8,128)} collective-permute-done((f32[896,256]{1,0:T(8,128)S(1)}, f32[896,256]{1,0:T(8,128)}, u32[]{:S(2)}, u32[]{:S(2)}) %collective-permute-start.56) | collective-permute-done | bytes 917536 | tf_op jit(solution)/shard_map/ppermute | solution.py:618
  629.3 4.5 collective-permute-done.52.first_ref
  633.8 3.7 shard_map.162
  639.2 4.3 reduce-scatter.3.cloned.1.call-done
  646.1 4.3 collective-permute-done.60.first_ref
  650.4 3.2 p_attn.1
  (320 shorter events, 142.7 us)
Async XLA Ops:
  7.2 120.0 %all-gather.3.cloned.1.call-start = ((), (), s32[]{:S(2)}) async-start(), calls=%async_computation.2 | async-start | bytes 8912896 | tf_op jit(solution)/shard_map/all_gather | solution.py:716
  12.1 28.8 %collective-permute-start.1 = (bf16[256,2176]{1,0:T(8,128)(2,1)}, bf16[256,2176]{1,0:T(8,128)(2,1)S(1)}, u32[]{:S(2)}, u32[]{:S(2)}) collective-permute-start(bf16[256,2176]{1,0:T(8,128)(2,1)} %get-tuple-element.142), channel_id=1, source_target_pairs={{0,8},{1,24},{8,0},{9,16},{16,9},{17,25},{24,1},{25,17},{2,10},{3,... | collective-permute-start | bytes 3342344 | tf_op jit(solution)/shard_map/ppermute | solution.py:618
  41.9 176.0 %all-gather.5.cloned.1.call-start = ((), (), s32[]{:S(2)}) async-start(), calls=%async_computation.4 | async-start | bytes 8912896 | tf_op jit(solution)/shard_map/all_gather | solution.py:717
  42.7 594.9 %reduce-scatter.5.cloned.1.call-start = ((), (), s32[]{:S(2)}) async-start(), calls=%async_computation.5 | async-start | bytes 17825792 | tf_op jit(solution)/shard_map/reduce_scatter | solution.py:751
  48.3 29.2 %collective-permute-start.9 = (bf16[256,2176]{1,0:T(8,128)(2,1)S(1)}, bf16[256,2176]{1,0:T(8,128)(2,1)S(1)}, u32[]{:S(2)}, u32[]{:S(2)}) collective-permute-start(bf16[256,2176]{1,0:T(8,128)(2,1)S(1)} %collective-permute-done.1.refs_1_.refs_4_), channel_id=1, source_target_pairs={{0,32},{32,64},{64,96},{96,0},{1,33},{33,65},{65,97},{97,1},{2,34}... | collective-permute-start | bytes 3342344 | tf_op jit(solution)/shard_map/ppermute | solution.py:602
  50.0 27.6 %collective-permute-start.5 = (bf16[256,2176]{1,0:T(8,128)(2,1)S(1)}, bf16[256,2176]{1,0:T(8,128)(2,1)S(1)}, u32[]{:S(2)}, u32[]{:S(2)}) collective-permute-start(bf16[256,2176]{1,0:T(8,128)(2,1)S(1)} %collective-permute-done.1.refs_1_.refs_4_), channel_id=1, source_target_pairs={{0,96},{32,0},{64,32},{96,64},{1,97},{33,1},{65,33},{97,65},{2,98}... | collective-permute-start | bytes 3342344 | tf_op jit(solution)/shard_map/ppermute | solution.py:602
  52.1 44.9 %collective-permute-start.8 = (bf16[256,2176]{1,0:T(8,128)(2,1)S(1)}, bf16[256,2176]{1,0:T(8,128)(2,1)S(1)}, u32[]{:S(2)}, u32[]{:S(2)}) collective-permute-start(bf16[256,2176]{1,0:T(8,128)(2,1)S(1)} %collective-permute-done.refs_0_.refs_3_), channel_id=1, source_target_pairs={{0,32},{32,64},{64,96},{96,0},{1,33},{33,65},{65,97},{97,1},{2,34}... | collective-permute-start | bytes 3342344 | tf_op jit(solution)/shard_map/ppermute | solution.py:602
  74.6 27.3 %collective-permute-start.4 = (bf16[256,2176]{1,0:T(8,128)(2,1)S(1)}, bf16[256,2176]{1,0:T(8,128)(2,1)S(1)}, u32[]{:S(2)}, u32[]{:S(2)}) collective-permute-start(bf16[256,2176]{1,0:T(8,128)(2,1)S(1)} %collective-permute-done.refs_0_.refs_3_), channel_id=1, source_target_pairs={{0,96},{32,0},{64,32},{96,64},{1,97},{33,1},{65,33},{97,65},{2,98}... | collective-permute-start | bytes 3342344 | tf_op jit(solution)/shard_map/ppermute | solution.py:602
  78.1 42.2 %collective-permute-start.13 = (bf16[256,2176]{1,0:T(8,128)(2,1)S(1)}, bf16[256,2176]{1,0:T(8,128)(2,1)S(1)}, u32[]{:S(2)}, u32[]{:S(2)}) collective-permute-start(bf16[256,2176]{1,0:T(8,128)(2,1)S(1)} %collective-permute-done.5.refs_5_.refs_8_), channel_id=1, source_target_pairs={{0,96},{32,0},{64,32},{96,64},{1,97},{33,1},{65,33},{97,65},{2,98}... | collective-permute-start | bytes 3342344 | tf_op jit(solution)/shard_map/ppermute | solution.py:602
  121.1 34.9 %collective-permute-start.33 = (bf16[256,1152]{1,0:T(8,128)(2,1)}, bf16[256,1152]{1,0:T(8,128)(2,1)}, u32[]{:S(2)}, u32[]{:S(2)}) collective-permute-start(bf16[256,1152]{1,0:T(8,128)(2,1)} %collective-permute-done.21.refs_4_.refs_1_), channel_id=1, source_target_pairs={{0,32},{32,64},{64,96},{96,0},{1,33},{33,65},{65,97},{97,1},{2,34}... | collective-permute-start | bytes 1769480 | tf_op jit(solution)/shard_map/ppermute | solution.py:602
  122.6 37.3 %collective-permute-start.25 = (bf16[256,1152]{1,0:T(8,128)(2,1)}, bf16[256,1152]{1,0:T(8,128)(2,1)}, u32[]{:S(2)}, u32[]{:S(2)}) collective-permute-start(bf16[256,1152]{1,0:T(8,128)(2,1)} %collective-permute-done.21.refs_4_.refs_1_), channel_id=1, source_target_pairs={{0,96},{32,0},{64,32},{96,64},{1,97},{33,1},{65,33},{97,65},{2,98}... | collective-permute-start | bytes 1769480 | tf_op jit(solution)/shard_map/ppermute | solution.py:602
  125.1 36.2 %collective-permute-start.23 = (bf16[256,1152]{1,0:T(8,128)(2,1)}, bf16[256,1152]{1,0:T(8,128)(2,1)}, u32[]{:S(2)}, u32[]{:S(2)}) collective-permute-start(bf16[256,1152]{1,0:T(8,128)(2,1)} %collective-permute-done.21.refs_4_.refs_1_), channel_id=1, source_target_pairs={{0,1},{1,0},{2,3},{3,2},{4,5},{5,4},{6,7},{7,6},{8,9},{9,8},{10,11... | collective-permute-start | bytes 1769480 | tf_op jit(solution)/shard_map/ppermute | solution.py:606
  126.6 35.2 %collective-permute-start.28 = (bf16[256,1152]{1,0:T(8,128)(2,1)}, bf16[256,1152]{1,0:T(8,128)(2,1)}, u32[]{:S(2)}, u32[]{:S(2)}) collective-permute-start(bf16[256,1152]{1,0:T(8,128)(2,1)} %collective-permute-done.20.refs_3_.refs_0_), channel_id=1, source_target_pairs={{0,32},{32,64},{64,96},{96,0},{1,33},{33,65},{65,97},{97,1},{2,34}... | collective-permute-start | bytes 1769480 | tf_op jit(solution)/shard_map/ppermute | solution.py:602
  156.0 38.0 %collective-permute-start.24 = (bf16[256,1152]{1,0:T(8,128)(2,1)}, bf16[256,1152]{1,0:T(8,128)(2,1)S(1)}, u32[]{:S(2)}, u32[]{:S(2)}) collective-permute-start(bf16[256,1152]{1,0:T(8,128)(2,1)} %collective-permute-done.20.refs_3_.refs_0_), channel_id=1, source_target_pairs={{0,96},{32,0},{64,32},{96,64},{1,97},{33,1},{65,33},{97,65},{2,98}... | collective-permute-start | bytes 1769480 | tf_op jit(solution)/shard_map/ppermute | solution.py:602
  161.8 33.1 %collective-permute-start.22 = (bf16[256,1152]{1,0:T(8,128)(2,1)}, bf16[256,1152]{1,0:T(8,128)(2,1)S(1)}, u32[]{:S(2)}, u32[]{:S(2)}) collective-permute-start(bf16[256,1152]{1,0:T(8,128)(2,1)} %collective-permute-done.20.refs_3_.refs_0_), channel_id=1, source_target_pairs={{0,1},{1,0},{2,3},{3,2},{4,5},{5,4},{6,7},{7,6},{8,9},{9,8},{10,11... | collective-permute-start | bytes 1769480 | tf_op jit(solution)/shard_map/ppermute | solution.py:606
  169.0 26.1 %collective-permute-start.35 = (bf16[256,1152]{1,0:T(8,128)(2,1)}, bf16[256,1152]{1,0:T(8,128)(2,1)S(1)}, u32[]{:S(2)}, u32[]{:S(2)}) collective-permute-start(bf16[256,1152]{1,0:T(8,128)(2,1)} %collective-permute-done.33.refs_16_.refs_9_), channel_id=1, source_target_pairs={{0,1},{1,0},{2,3},{3,2},{4,5},{5,4},{6,7},{7,6},{8,9},{9,8},{10,11... | collective-permute-start | bytes 1769480 | tf_op jit(solution)/shard_map/ppermute | solution.py:606
  251.1 54.9 %collective-permute-start.42 = (bf16[1024,2048]{1,0:T(8,128)(2,1)}, bf16[1024,2048]{1,0:T(8,128)(2,1)}, u32[]{:S(2)}, u32[]{:S(2)}) collective-permute-start(bf16[1024,2048]{1,0:T(8,128)(2,1)} %shard_map.157), channel_id=1, source_target_pairs={{0,1},{1,0},{2,3},{3,2},{4,5},{5,4},{6,7},{7,6},{8,9},{9,8},{10,11... | collective-permute-start | bytes 12582920 | tf_op jit(solution)/shard_map/ppermute | solution.py:606
  277.7 28.3 %collective-permute-start.41 = (bf16[1792,1024]{1,0:T(8,128)(2,1)}, bf16[1792,1024]{1,0:T(8,128)(2,1)S(1)}, u32[]{:S(2)}, u32[]{:S(2)}) collective-permute-start(bf16[1792,1024]{1,0:T(8,128)(2,1)} %get-tuple-element.93.refs_0_), channel_id=1, source_target_pairs={{0,1},{1,0},{2,3},{3,2},{4,5},{5,4},{6,7},{7,6},{8,9},{9,8},{10,11... | collective-permute-start | bytes 11010056 | tf_op jit(solution)/shard_map/ppermute | solution.py:606
  293.9 40.7 %collective-permute-start.43 = (f32[2,512,128]{2,1,0:T(8,128)}, f32[2,512,128]{2,1,0:T(8,128)}, u32[]{:S(2)}, u32[]{:S(2)}) collective-permute-start(f32[2,512,128]{2,1,0:T(8,128)} %get-tuple-element.107), channel_id=1, source_target_pairs={{0,8},{8,0},{16,24},{24,16},{1,9},{9,1},{17,25},{25,17},{2,10},{10... | collective-permute-start | bytes 1572872 | tf_op jit(solution)/shard_map/ppermute | solution.py:610
  370.0 273.5 %reduce-scatter.3.cloned.1.call-start = ((), (), s32[]{:S(2)}) async-start(), calls=%async_computation.3 | async-start | bytes 17825792 | tf_op jit(solution)/shard_map/reduce_scatter | solution.py:731
  373.7 38.9 %collective-permute-start.72 = (f32[896,256]{1,0:T(8,128)}, f32[896,256]{1,0:T(8,128)S(1)}, u32[]{:S(2)}, u32[]{:S(2)}) collective-permute-start(f32[896,256]{1,0:T(8,128)} %get-tuple-element.139), channel_id=1, source_target_pairs={{0,96},{32,0},{64,32},{96,64},{1,97},{33,1},{65,33},{97,65},{2,98}... | collective-permute-start | bytes 2752520 | tf_op jit(solution)/shard_map/ppermute | solution.py:602
  373.8 42.2 %collective-permute-start.71 = (f32[896,256]{1,0:T(8,128)}, f32[896,256]{1,0:T(8,128)S(1)}, u32[]{:S(2)}, u32[]{:S(2)}) collective-permute-start(f32[896,256]{1,0:T(8,128)} %add.114), channel_id=1, source_target_pairs={{0,32},{32,64},{64,96},{96,0},{1,33},{33,65},{65,97},{97,1},{2,34}... | collective-permute-start | bytes 2752520 | tf_op jit(solution)/shard_map/ppermute | solution.py:602
  396.6 34.3 %collective-permute-start.76 = (f32[896,256]{1,0:T(8,128)}, f32[896,256]{1,0:T(8,128)}, u32[]{:S(2)}, u32[]{:S(2)}) collective-permute-start(f32[896,256]{1,0:T(8,128)} %add_add_fusion.1), channel_id=1, source_target_pairs={{0,8},{1,24},{8,0},{9,16},{16,9},{17,25},{24,1},{25,17},{2,10},{3,... | collective-permute-start | bytes 2752520 | tf_op jit(solution)/shard_map/ppermute | solution.py:618
  396.6 36.5 %collective-permute-start.45 = (f32[896,256]{1,0:T(8,128)}, f32[896,256]{1,0:T(8,128)}, u32[]{:S(2)}, u32[]{:S(2)}) collective-permute-start(f32[896,256]{1,0:T(8,128)} %get-tuple-element.111), channel_id=1, source_target_pairs={{0,32},{32,64},{64,96},{96,0},{1,33},{33,65},{65,97},{97,1},{2,34}... | collective-permute-start | bytes 2752520 | tf_op jit(solution)/shard_map/ppermute | solution.py:602
  396.6 56.1 %collective-permute-start.46 = (f32[896,256]{1,0:T(8,128)}, f32[896,256]{1,0:T(8,128)}, u32[]{:S(2)}, u32[]{:S(2)}) collective-permute-start(f32[896,256]{1,0:T(8,128)} %get-tuple-element.113), channel_id=1, source_target_pairs={{0,32},{32,64},{64,96},{96,0},{1,33},{33,65},{65,97},{97,1},{2,34}... | collective-permute-start | bytes 2752520 | tf_op jit(solution)/shard_map/ppermute | solution.py:602
  412.6 42.4 %collective-permute-start.54 = (f32[896,256]{1,0:T(8,128)}, f32[896,256]{1,0:T(8,128)}, u32[]{:S(2)}, u32[]{:S(2)}) collective-permute-start(f32[896,256]{1,0:T(8,128)} %get-tuple-element.124), channel_id=1, source_target_pairs={{0,96},{32,0},{64,32},{96,64},{1,97},{33,1},{65,33},{97,65},{2,98}... | collective-permute-start | bytes 2752520 | tf_op jit(solution)/shard_map/ppermute | solution.py:602
  417.0 39.5 %collective-permute-start.47 = (f32[896,256]{1,0:T(8,128)}, f32[896,256]{1,0:T(8,128)}, u32[]{:S(2)}, u32[]{:S(2)}) collective-permute-start(f32[896,256]{1,0:T(8,128)} %get-tuple-element.116), channel_id=1, source_target_pairs={{0,96},{32,0},{64,32},{96,64},{1,97},{33,1},{65,33},{97,65},{2,98}... | collective-permute-start | bytes 2752520 | tf_op jit(solution)/shard_map/ppermute | solution.py:602
  430.9 28.0 %collective-permute-start.49 = (bf16[384,1024]{1,0:T(8,128)(2,1)S(1)}, bf16[384,1024]{1,0:T(8,128)(2,1)S(1)}, u32[]{:S(2)}, u32[]{:S(2)}) collective-permute-start(bf16[384,1024]{1,0:T(8,128)(2,1)S(1)} %maximum_bitcast_fusion.refs_6_), channel_id=1, source_target_pairs={{0,1},{1,0},{2,3},{3,2},{4,5},{5,4},{6,7},{7,6},{8,9},{9,8},{10,11... | collective-permute-start | bytes 2359304 | tf_op jit(solution)/shard_map/ppermute | solution.py:606
  433.1 44.3 %collective-permute-start.53 = (f32[896,256]{1,0:T(8,128)}, f32[896,256]{1,0:T(8,128)S(1)}, u32[]{:S(2)}, u32[]{:S(2)}) collective-permute-start(f32[896,256]{1,0:T(8,128)} %get-tuple-element.122), channel_id=1, source_target_pairs={{0,32},{32,64},{64,96},{96,0},{1,33},{33,65},{65,97},{97,1},{2,34}... | collective-permute-start | bytes 2752520 | tf_op jit(solution)/shard_map/ppermute | solution.py:602
  455.0 36.9 %collective-permute-start.68 = (f32[896,256]{1,0:T(8,128)}, f32[896,256]{1,0:T(8,128)S(1)}, u32[]{:S(2)}, u32[]{:S(2)}) collective-permute-start(f32[896,256]{1,0:T(8,128)} %get-tuple-element.137), channel_id=1, source_target_pairs={{0,32},{32,64},{64,96},{96,0},{1,33},{33,65},{65,97},{97,1},{2,34}... | collective-permute-start | bytes 2752520 | tf_op jit(solution)/shard_map/ppermute | solution.py:602
  456.5 55.3 %collective-permute-start.65 = (f32[896,256]{1,0:T(8,128)}, f32[896,256]{1,0:T(8,128)}, u32[]{:S(2)}, u32[]{:S(2)}) collective-permute-start(f32[896,256]{1,0:T(8,128)} %add.117), channel_id=1, source_target_pairs={{0,32},{32,64},{64,96},{96,0},{1,33},{33,65},{65,97},{97,1},{2,34}... | collective-permute-start | bytes 2752520 | tf_op jit(solution)/shard_map/ppermute | solution.py:602
  458.8 53.1 %collective-permute-start.55 = (f32[896,256]{1,0:T(8,128)}, f32[896,256]{1,0:T(8,128)}, u32[]{:S(2)}, u32[]{:S(2)}) collective-permute-start(f32[896,256]{1,0:T(8,128)} %add.123), channel_id=1, source_target_pairs={{0,96},{32,0},{64,32},{96,64},{1,97},{33,1},{65,33},{97,65},{2,98}... | collective-permute-start | bytes 2752520 | tf_op jit(solution)/shard_map/ppermute | solution.py:602
  477.4 48.4 %collective-permute-start.57 = (f32[640,256]{1,0:T(8,128)}, f32[640,256]{1,0:T(8,128)S(1)}, u32[]{:S(2)}, u32[]{:S(2)}) collective-permute-start(f32[640,256]{1,0:T(8,128)} %get-tuple-element.127), channel_id=1, source_target_pairs={{0,32},{32,64},{64,96},{96,0},{1,33},{33,65},{65,97},{97,1},{2,34}... | collective-permute-start | bytes 1966088 | tf_op jit(solution)/shard_map/ppermute | solution.py:602
  477.5 48.3 %collective-permute-start.62 = (f32[640,256]{1,0:T(8,128)}, f32[640,256]{1,0:T(8,128)S(1)}, u32[]{:S(2)}, u32[]{:S(2)}) collective-permute-start(f32[640,256]{1,0:T(8,128)} %get-tuple-element.132), channel_id=1, source_target_pairs={{0,96},{32,0},{64,32},{96,64},{1,97},{33,1},{65,33},{97,65},{2,98}... | collective-permute-start | bytes 1966088 | tf_op jit(solution)/shard_map/ppermute | solution.py:602
  492.0 37.1 %collective-permute-start.69 = (f32[896,256]{1,0:T(8,128)S(1)}, f32[896,256]{1,0:T(8,128)S(1)}, u32[]{:S(2)}, u32[]{:S(2)}) collective-permute-start(f32[896,256]{1,0:T(8,128)S(1)} %copy-done.41), channel_id=1, source_target_pairs={{0,96},{32,0},{64,32},{96,64},{1,97},{33,1},{65,33},{97,65},{2,98}... | collective-permute-start | bytes 2752520 | tf_op jit(solution)/shard_map/ppermute | solution.py:602
  511.8 33.7 %collective-permute-start.50 = (f32[896,256]{1,0:T(8,128)S(1)}, f32[896,256]{1,0:T(8,128)S(1)}, u32[]{:S(2)}, u32[]{:S(2)}) collective-permute-start(f32[896,256]{1,0:T(8,128)S(1)} %add.119), channel_id=1, source_target_pairs={{0,32},{32,64},{64,96},{96,0},{1,33},{33,65},{65,97},{97,1},{2,34}... | collective-permute-start | bytes 2752520 | tf_op jit(solution)/shard_map/ppermute | solution.py:602
  512.0 36.6 %collective-permute-start.51 = (f32[896,256]{1,0:T(8,128)S(1)}, f32[896,256]{1,0:T(8,128)S(1)}, u32[]{:S(2)}, u32[]{:S(2)}) collective-permute-start(f32[896,256]{1,0:T(8,128)S(1)} %copy-done.60), channel_id=1, source_target_pairs={{0,96},{32,0},{64,32},{96,64},{1,97},{33,1},{65,33},{97,65},{2,98}... | collective-permute-start | bytes 2752520 | tf_op jit(solution)/shard_map/ppermute | solution.py:602
  525.8 35.2 %collective-permute-start.59 = (f32[640,256]{1,0:T(8,128)S(1)}, f32[640,256]{1,0:T(8,128)S(1)}, u32[]{:S(2)}, u32[]{:S(2)}) collective-permute-start(f32[640,256]{1,0:T(8,128)S(1)} %copy-done.62), channel_id=1, source_target_pairs={{0,96},{32,0},{64,32},{96,64},{1,97},{33,1},{65,33},{97,65},{2,98}... | collective-permute-start | bytes 1966088 | tf_op jit(solution)/shard_map/ppermute | solution.py:602
  525.8 39.3 %collective-permute-start.61 = (f32[640,256]{1,0:T(8,128)S(1)}, f32[640,256]{1,0:T(8,128)S(1)}, u32[]{:S(2)}, u32[]{:S(2)}) collective-permute-start(f32[640,256]{1,0:T(8,128)S(1)} %copy-done.61), channel_id=1, source_target_pairs={{0,32},{32,64},{64,96},{96,0},{1,33},{33,65},{65,97},{97,1},{2,34}... | collective-permute-start | bytes 1966088 | tf_op jit(solution)/shard_map/ppermute | solution.py:602
  529.1 38.4 %collective-permute-start.73 = (f32[896,256]{1,0:T(8,128)S(1)}, f32[896,256]{1,0:T(8,128)S(1)}, u32[]{:S(2)}, u32[]{:S(2)}) collective-permute-start(f32[896,256]{1,0:T(8,128)S(1)} %add_add_fusion.2), channel_id=1, source_target_pairs={{0,0},{1,16},{8,8},{9,24},{16,1},{17,17},{24,9},{25,25},{2,2},{3,1... | collective-permute-start | bytes 2752520 | tf_op jit(solution)/shard_map/ppermute | solution.py:618
  545.5 28.1 %collective-permute-start.58 = (f32[640,256]{1,0:T(8,128)S(1)}, f32[640,256]{1,0:T(8,128)S(1)}, u32[]{:S(2)}, u32[]{:S(2)}) collective-permute-start(f32[640,256]{1,0:T(8,128)S(1)} %add.125), channel_id=1, source_target_pairs={{0,32},{32,64},{64,96},{96,0},{1,33},{33,65},{65,97},{97,1},{2,34}... | collective-permute-start | bytes 1966088 | tf_op jit(solution)/shard_map/ppermute | solution.py:602
  548.6 33.8 %collective-permute-start.63 = (f32[640,256]{1,0:T(8,128)}, f32[640,256]{1,0:T(8,128)}, u32[]{:S(2)}, u32[]{:S(2)}) collective-permute-start(f32[640,256]{1,0:T(8,128)} %add.129), channel_id=1, source_target_pairs={{0,96},{32,0},{64,32},{96,64},{1,97},{33,1},{65,33},{97,65},{2,98}... | collective-permute-start | bytes 1966088 | tf_op jit(solution)/shard_map/ppermute | solution.py:602
  561.0 40.4 %collective-permute-start.67 = (f32[896,256]{1,0:T(8,128)S(1)}, f32[896,256]{1,0:T(8,128)S(1)}, u32[]{:S(2)}, u32[]{:S(2)}) collective-permute-start(f32[896,256]{1,0:T(8,128)S(1)} %add_add_fusion.4), channel_id=1, source_target_pairs={{0,0},{1,16},{8,8},{9,24},{16,1},{17,17},{24,9},{25,25},{2,2},{3,1... | collective-permute-start | bytes 2752520 | tf_op jit(solution)/shard_map/ppermute | solution.py:618
  565.2 36.2 %collective-permute-start.70 = (f32[896,256]{1,0:T(8,128)S(1)}, f32[896,256]{1,0:T(8,128)}, u32[]{:S(2)}, u32[]{:S(2)}) collective-permute-start(f32[896,256]{1,0:T(8,128)S(1)} %add_add_fusion.3), channel_id=1, source_target_pairs={{0,8},{1,24},{8,0},{9,16},{16,9},{17,25},{24,1},{25,17},{2,10},{3,... | collective-permute-start | bytes 2752520 | tf_op jit(solution)/shard_map/ppermute | solution.py:618
  567.5 61.8 %collective-permute-start.56 = (f32[896,256]{1,0:T(8,128)S(1)}, f32[896,256]{1,0:T(8,128)}, u32[]{:S(2)}, u32[]{:S(2)}) collective-permute-start(f32[896,256]{1,0:T(8,128)S(1)} %add_add_fusion.5), channel_id=1, source_target_pairs={{0,8},{1,24},{8,0},{9,16},{16,9},{17,25},{24,1},{25,17},{2,10},{3,... | collective-permute-start | bytes 2752520 | tf_op jit(solution)/shard_map/ppermute | solution.py:618
  574.4 59.4 %collective-permute-start.52 = (f32[896,256]{1,0:T(8,128)}, f32[896,256]{1,0:T(8,128)}, u32[]{:S(2)}, u32[]{:S(2)}) collective-permute-start(f32[896,256]{1,0:T(8,128)} %add_add_fusion.6), channel_id=1, source_target_pairs={{0,0},{1,16},{8,8},{9,24},{16,1},{17,17},{24,9},{25,25},{2,2},{3,1... | collective-permute-start | bytes 2752520 | tf_op jit(solution)/shard_map/ppermute | solution.py:618
  582.3 68.1 %collective-permute-start.60 = (f32[640,256]{1,0:T(8,128)}, f32[640,256]{1,0:T(8,128)}, u32[]{:S(2)}, u32[]{:S(2)}) collective-permute-start(f32[640,256]{1,0:T(8,128)} %add_add_fusion.8), channel_id=1, source_target_pairs={{0,0},{1,16},{8,8},{9,24},{16,1},{17,17},{24,9},{25,25},{2,2},{3,1... | collective-permute-start | bytes 1966088 | tf_op jit(solution)/shard_map/ppermute | solution.py:618
  601.4 49.0 %collective-permute-start.64 = (f32[640,256]{1,0:T(8,128)}, f32[640,256]{1,0:T(8,128)}, u32[]{:S(2)}, u32[]{:S(2)}) collective-permute-start(f32[640,256]{1,0:T(8,128)} %add_add_fusion.7), channel_id=1, source_target_pairs={{0,8},{1,24},{8,0},{9,16},{16,9},{17,25},{24,1},{25,17},{2,10},{3,... | collective-permute-start | bytes 1966088 | tf_op jit(solution)/shard_map/ppermute | solution.py:618
  (99 other events, 1495.8 us)
Sparse Core Ops, SparseCore 0:
  42.0 75.9 all-gather.2
  120.1 74.7 all-gather.4
  370.2 116.5 reduce-scatter.4
  490.0 153.4 reduce-scatter.2

commit v3 on v2

--- a/solution.py
+++ b/solution.py
@@ -17,7 +17,6 @@
 F32 = jnp.float32
 BF16 = jnp.bfloat16
 VMEM_LIMIT = 60 * 1024 * 1024
-TILE = 512
 
 
 def norm_fwd(row_vals, norm_gain):
@@ -279,7 +278,7 @@
     return pl.multiple_of((1 - pos_ref[2] if part else pos_ref[2]) * half, half)
 
 
-def nn_kernel(keys, first, count_out, pos_ref, acts_ref, *refs):
+def nn_kernel(keys, first, count_out, tile, pos_ref, acts_ref, *refs):
     count = len(keys)
     halves = refs[: 2 * count]
     outs = refs[2 * count : 2 * count + count_out]
@@ -313,15 +312,15 @@
                 else:
                     total[:, cols] = part
 
-            whole = width // TILE
+            whole = width // tile
             if whole:
-                pl.loop(0, whole)(lambda n: step(n * TILE, TILE))
-            if width % TILE:
-                step(whole * TILE, width % TILE)
+                pl.loop(0, whole)(lambda n: step(n * tile, tile))
+            if width % tile:
+                step(whole * tile, width % tile)
             start += width
 
 
-def nn_pieces(pos, acts, parts, widths):
+def nn_pieces(pos, acts, parts, widths, tile):
     keys = [(step, other) for step in (0, 1, 3, 2) for other in range(2)]
     halves = [parts[step][other][part] for step, other in keys for part in range(2)]
     tokens, depth = acts.shape
@@ -329,7 +328,7 @@
     count = len(keys)
     anywhere = pl.BlockSpec(memory_space=pl.ANY)
     return pl.pallas_call(
-        functools.partial(nn_kernel, keys, 2, len(widths)),
+        functools.partial(nn_kernel, keys, 2, len(widths), tile),
         grid_spec=pltpu.PrefetchScalarGridSpec(
             num_scalar_prefetch=1,
             grid=(1,),
@@ -718,7 +717,7 @@
         wf_parts = gather_weight(wf_piece)
         ws_parts = gather_weight(ws_piece)
 
-        gate_up, qkv_tok = nn_pieces(pos, h_all, wf_parts, (2 * ff_blk, qkv_blk))
+        gate_up, qkv_tok = nn_pieces(pos, h_all, wf_parts, (2 * ff_blk, qkv_blk), 512)
         third = qkv_tok[:, o_blk:]
         qkv_other = swap_c(my_rows(qkv_tok, False))
         third_own = swap_y(my_rows(third, True))
@@ -733,10 +732,10 @@
 
         dy_picked = pick_cols(after(pos, y_part), dy_all)
         dy_recv = swap_c(dy_picked)
-        g_act = grad_start([(act_t, act_recv, dy_all, dy_recv, ff_blk, 0)], y_part)
-        h_picked = pick_cols(after(pos, g_act[3][0]), h_all)
+        h_picked = pick_cols(after(pos, dy_picked), h_all)
         h_recv = swap_c(h_picked)
-        d_act, d_attn = nn_pieces(after(pos, h_picked), dy_all, ws_parts, (ff_blk, o_blk))
+        g_act = grad_start([(act_t, act_recv, dy_all, dy_recv, ff_blk, 0)], h_picked)
+        d_act, d_attn = nn_pieces(after(pos, g_act[3][0]), dy_all, ws_parts, (ff_blk, o_blk), 256)
         d_attn_other = swap_c(my_rows(d_attn, False))
         d_gate_up, d_gate_up_t = act_bwd(gate_up, d_act)
         d_gate_up_recv = swap_c(d_gate_up_t)
@@ -744,13 +743,13 @@
         got = swap_y(send)
         g_act = grad_pass(g_act, d_queries)
         g_gate = grad_start([(d_gate_up_t, d_gate_up_recv, h_all, h_recv, ff_blk, 0)], *g_act[3])
-        g_up = grad_start([(d_gate_up_t, d_gate_up_recv, h_all, h_recv, ff_blk, 1)], g_gate[3][0])
-        d_own, d_other = attn_post(after(pos, g_up[3][0]), d_queries, keep, got, cos_tab, sin_tab)
+        d_own, d_other = attn_post(after(pos, g_gate[3][0]), d_queries, keep, got, cos_tab, sin_tab)
         d_got = swap_c(d_other)
         dh_part = nt_pieces(pos, [d_gate_up, d_own, d_got], wf_parts)
         d_h = lax.psum_scatter(dh_part, ("y", "x"), scatter_dimension=0, tiled=True)
         d_h = d_h.astype(BF16)
         dx_out = (dy_in[0].astype(F32) + norm_pull(d_h.astype(F32))[0]).astype(BF16)[None]
+        g_up = grad_start([(d_gate_up_t, d_gate_up_recv, h_all, h_recv, ff_blk, 1)], dh_part)
         g_gate = grad_pass(g_gate, dh_part)
 
         attn_t = both_rows(attn_own, attn_got).T

time: 670 us -> 649 us (0.969)
  waiting for transfers between devices: 300 us -> 282 us
    ppermute x36, waiting for transfers between devices: 167 us -> 152 us  [hop_z(): return lax.ppermute(val, 'z', ring(step, NZ))]
  transfers between devices with their start and end apart: 81 -> 81, of which waited for: 34 -> 36; matrix products, arithmetic and copies ran while one was open for 7% -> 8% of each run, Pallas kernels for 21% -> 24%
where the time goes in v3:
time: 649 us; the launch traced here: 639 us
  waiting for transfers between devices  282 us (43%)
  Pallas kernels  194 us (30%)
  starting transfers between devices  85.1 us (13%)
  other arithmetic  38.1 us (6%)
  local copies, waits for them, and re-layouts  25.1 us (4%)
  between operations  15.2 us (2%)
    ppermute x36, waiting for transfers between devices, hop_z(): return lax.ppermute(val, 'z', ring(step, NZ))  152 us
    ppermute x12, waiting for transfers between devices, turn(): return lax.ppermute(val, ('y', 'c'), pairs)  99.7 us
    pallas_call x4, Pallas kernels, grad_pieces(): pl.pallas_call(functools.partial(grad_kernel, heights), grid_spec=pltpu.P...  53.6 us
    pallas_call x2, Pallas kernels, nn_pieces(): pl.pallas_call(functools.partial(nn_kernel, keys, 2, len(widths), tile),...  45.2 us
    pallas_call x2, Pallas kernels, nt_pieces(): pl.pallas_call(functools.partial(nt_kernel, keys, sides), grid_spec=pltpu...  44.4 us
    ppermute x36, starting transfers between devices, hop_z(): return lax.ppermute(val, 'z', ring(step, NZ))  42.7 us
    ppermute x12, starting transfers between devices, turn(): return lax.ppermute(val, ('y', 'c'), pairs)  27.9 us
    pallas_call x3, Pallas kernels, per_sequence(): pl.pallas_call(kernel, grid_spec=pltpu.PrefetchScalarGridSpec(num_scalar_...  16.9 us
  transfers between devices with their start and end apart: 81, of which 36 were waited for; matrix products, arithmetic and copies ran while one was open for 8% of the time, Pallas kernels for 24%

profile of v3, /device:TPU:1, one launch (start us, length us, event | category | flops | bytes accessed | tf_op | source)
XLA Modules:
  0.0 639.4 jit_solution(4204702039106472251)
XLA Ops:
  12.1 4.1 collective-permute-start.1
  19.5 21.4 %collective-permute-done.1.refs_1_.refs_4_ = bf16[256,2176]{1,0:T(8,128)(2,1)S(1)} collective-permute-done((bf16[256,2176]{1,0:T(8,128)(2,1)}, bf16[256,2176]{1,0:T(8,128)(2,1)S(1)}, u32[]{:S(2)}, u32[]{:S(2)}) %collective-permute-start.1) | collective-permute-done | bytes 1114144 | tf_op jit(solution)/shard_map/ppermute | solution.py:617
  52.1 4.4 collective-permute-done.21.refs_4_.refs_1_
  59.1 15.5 %collective-permute-done.20.refs_3_.refs_0_ = bf16[256,1152]{1,0:T(8,128)(2,1)} collective-permute-done((bf16[256,1152]{1,0:T(8,128)(2,1)S(1)}, bf16[256,1152]{1,0:T(8,128)(2,1)}, u32[]{:S(2)}, u32[]{:S(2)}) %collective-permute-start.20) | collective-permute-done | bytes 589856 | tf_op jit(solution)/shard_map/ppermute | solution.py:617
  80.0 17.0 %collective-permute-done.8.refs_8_.refs_15_ = bf16[256,2176]{1,0:T(8,128)(2,1)S(1)} collective-permute-done((bf16[256,2176]{1,0:T(8,128)(2,1)S(1)}, bf16[256,2176]{1,0:T(8,128)(2,1)S(1)}, u32[]{:S(2)}, u32[]{:S(2)}) %collective-permute-start.8) | collective-permute-done | bytes 1114144 | tf_op jit(solution)/shard_map/ppermute | solution.py:601
  97.0 4.9 collective-permute-done.4.refs_4_.refs_7_
  102.6 17.8 %collective-permute-done.13.refs_13_.refs_12_ = bf16[256,2176]{1,0:T(8,128)(2,1)S(1)} collective-permute-done((bf16[256,2176]{1,0:T(8,128)(2,1)S(1)}, bf16[256,2176]{1,0:T(8,128)(2,1)S(1)}, u32[]{:S(2)}, u32[]{:S(2)}) %collective-permute-start.13) | collective-permute-done | bytes 1114144 | tf_op jit(solution)/shard_map/ppermute | solution.py:601
  126.9 27.6 %shard_map.153 = (bf16[1024,1792]{1,0:T(8,128)(2,1)}, bf16[1024,384]{1,0:T(8,128)(2,1)}) custom-call(s32[3]{0:T(128)} %pad_add_fusion.pos_ref, bf16[1024,4096]{1,0:T(8,128)(2,1)} %all-gather.3.cloned.1.call-done.acts_ref.in_ref.refs_2_.refs_3_.refs_8_.refs_9_, bf16[256,2176]{1,0:T(8,128)(2,1)} %copy-done.4, bf16[256,2176]{1,0:T(8,128)(2,1)} %copy-done.3, ...), custom_call_target="tpu_custom_call" | custom-call | flops 912680576 | bytes 26214400 | tf_op jit(solution)/shard_map/pallas_call | solution.py:330
  162.0 6.9 %collective-permute-done.18.other_third_ref = bf16[512,128]{1,0:T(8,128)(2,1)S(1)} collective-permute-done((bf16[512,128]{1,0:T(8,128)(2,1)S(1)}, bf16[512,128]{1,0:T(8,128)(2,1)S(1)}, u32[]{:S(2)}, u32[]{:S(2)}) %collective-permute-start.18) | collective-permute-done | bytes 131104 | tf_op jit(solution)/shard_map/ppermute | solution.py:622
  169.0 5.3 collective-permute-done.17.own_third_ref
  181.6 4.9 act_fwd.1
  186.5 5.6 shard_map.154
  200.7 17.2 %shard_map.155 = f32[1024,4096]{1,0:T(8,128)} custom-call(s32[3]{0:T(128)} %pad_add_fusion.pos_ref, bf16[1024,896]{1,0:T(8,128)(2,1)} %get-tuple-element.83.refs_0_, bf16[512,256]{1,0:T(8,128)(2,1)} %get-tuple-element.81.refs_1_, bf16[512,256]{1,0:T(8,128)(2,1)} %copy.38.refs_2_, bf16[256,1152]{1,0:T(8,128)(2,1)} %collective-permute-done.20.refs_3_.refs_0_, ...), custom_call_target="tpu_custom_call" | custom-call | flops 483183808 | bytes 26214400 | tf_op jit(solution)/shard_map/pallas_call | solution.py:408
  217.9 4.3 shard_map.156
  222.7 4.1 shard_map.157
  227.7 4.6 collective-permute-done.36.refs_1_
  232.4 13.4 %grad.4 = (f32[896,256]{1,0:T(8,128)}, f32[896,256]{1,0:T(8,128)}, f32[896,256]{1,0:T(8,128)}, f32[896,256]{1,0:T(8,128)}, f32[896,256]{1,0:T(8,128)}, /*index=5...) custom-call(s32[3]{0:T(128)} %pad_add_fusion.pos_ref, bf16[896,1024]{1,0:T(8,128)(2,1)} %get-tuple-element.78.refs_0_, ...), custom_call_target="tpu_custom_call" | custom-call | flops 375809632 | bytes 8388608 | tf_op jit(solution)/shard_map/grad/pallas_call | solution.py:523
  245.8 17.7 %shard_map.158 = (bf16[1024,896]{1,0:T(8,128)(2,1)}, bf16[1024,256]{1,0:T(8,128)(2,1)}) custom-call(s32[3]{0:T(128)} %pad_add_fusion.pos_ref, bf16[1024,4096]{1,0:T(8,128)(2,1)} %all-gather.5.cloned.1.call-done.in_ref.refs_2_.refs_3_.acts_ref, bf16[256,1152]{1,0:T(8,128)(2,1)} %collective-permute-done.20.refs_3_.refs_0_, ...), custom_call_target="tpu_custom_call" | custom-call | flops 483183808 | bytes 17825792 | tf_op jit(solution)/shard_map/pallas_call | solution.py:330
  263.4 6.9 %act_bwd.1 = (bf16[1024,1792]{1,0:T(8,128)(2,1)}, bf16[1792,1024]{1,0:T(8,128)(2,1)}) custom-call(bf16[1024,1792]{1,0:T(8,128)(2,1)} %get-tuple-element.77.ab_ref, bf16[1024,896]{1,0:T(8,128)(2,1)} %get-tuple-element.91.du_ref), custom_call_target="tpu_custom_call" | custom-call | flops 400000000 | bytes 14000000 | tf_op jit(solution)/shard_map/act_bwd/pallas_call | solution.py:260
  278.0 8.1 %shard_map.159 = (bf16[2,512,256]{2,1,0:T(8,128)(2,1)}, f32[2,512,128]{2,1,0:T(8,128)}, f32[2,512,128]{2,1,0:T(8,128)}) custom-call(s32[3]{0:T(128)} %pad_add_fusion.pos_ref, bf16[2,512,512]{2,1,0:T(8,128)(2,1)} %get-tuple-element.97.seq_ref, bf16[1024,256]{1,0:T(8,128)(2,1)} %get-tuple-element.98.own_ref, bf16[512,256]{1,0:T(8,128)(2,1)} %copy-done.60, ...), custom_call_target="tpu_custom_call" | custom-call | flops 800000000 | bytes 4000000 | tf_op jit(solution)/shard_map/pallas_call | solution.py:142
  287.1 6.9 %collective-permute-done.38 = f32[896,256]{1,0:T(8,128)} collective-permute-done((f32[896,256]{1,0:T(8,128)}, f32[896,256]{1,0:T(8,128)}, u32[]{:S(2)}, u32[]{:S(2)}) %collective-permute-start.38) | collective-permute-done | bytes 917536 | tf_op jit(solution)/shard_map/ppermute | solution.py:601
  300.6 13.4 %grad.5 = (f32[896,256]{1,0:T(8,128)}, f32[896,256]{1,0:T(8,128)}, f32[896,256]{1,0:T(8,128)}, f32[896,256]{1,0:T(8,128)}, f32[896,256]{1,0:T(8,128)}, /*index=5...) custom-call(s32[3]{0:T(128)} %pad_add_fusion.pos_ref, bf16[1792,1024]{1,0:T(8,128)(2,1)} %get-tuple-element.95.refs_0_, ...), custom_call_target="tpu_custom_call" | custom-call | flops 375809632 | bytes 8388608 | tf_op jit(solution)/shard_map/grad/pallas_call | solution.py:523
  314.0 3.2 shard_map.160
  321.7 27.3 %shard_map.161 = f32[1024,4096]{1,0:T(8,128)} custom-call(s32[3]{0:T(128)} %pad_add_fusion.pos_ref, bf16[1024,1792]{1,0:T(8,128)(2,1)} %get-tuple-element.92.refs_0_, bf16[512,384]{1,0:T(8,128)(2,1)} %get-tuple-element.108.refs_1_, bf16[512,384]{1,0:T(8,128)(2,1)} %copy.40.refs_2_, bf16[256,2176]{1,0:T(8,128)(2,1)} %copy-done.4, ...), custom_call_target="tpu_custom_call" | custom-call | flops 912680576 | bytes 34603008 | tf_op jit(solution)/shard_map/pallas_call | solution.py:408
  356.9 15.8 %collective-permute-done.74 = f32[896,256]{1,0:T(8,128)} collective-permute-done((f32[896,256]{1,0:T(8,128)}, f32[896,256]{1,0:T(8,128)}, u32[]{:S(2)}, u32[]{:S(2)}) %collective-permute-start.74) | collective-permute-done | bytes 917536 | tf_op jit(solution)/shard_map/ppermute | solution.py:601
  378.2 13.3 %collective-permute-done.72 = f32[896,256]{1,0:T(8,128)S(1)} collective-permute-done((f32[896,256]{1,0:T(8,128)}, f32[896,256]{1,0:T(8,128)S(1)}, u32[]{:S(2)}, u32[]{:S(2)}) %collective-permute-start.72) | collective-permute-done | bytes 917536 | tf_op jit(solution)/shard_map/ppermute | solution.py:601
  391.5 3.4 collective-permute-start.66
  396.3 13.5 %collective-permute-done.76.second_ref = f32[896,256]{1,0:T(8,128)} collective-permute-done((f32[896,256]{1,0:T(8,128)}, f32[896,256]{1,0:T(8,128)}, u32[]{:S(2)}, u32[]{:S(2)}) %collective-permute-start.76) | collective-permute-done | bytes 917536 | tf_op jit(solution)/shard_map/ppermute | solution.py:617
  410.7 13.8 %grad.6 = (f32[896,256]{1,0:T(8,128)}, f32[896,256]{1,0:T(8,128)}, f32[896,256]{1,0:T(8,128)}, f32[896,256]{1,0:T(8,128)}, f32[896,256]{1,0:T(8,128)}, /*index=5...) custom-call(s32[3]{0:T(128)} %pad_add_fusion.pos_ref, bf16[1792,1024]{1,0:T(8,128)(2,1)} %get-tuple-element.95.refs_0_, ...), custom_call_target="tpu_custom_call" | custom-call | flops 375809632 | bytes 8388608 | tf_op jit(solution)/shard_map/grad/pallas_call | solution.py:523
  424.7 3.3 collective-permute-start.54
  436.6 13.0 %grad.7 = (f32[640,256]{1,0:T(8,128)}, f32[640,256]{1,0:T(8,128)}, f32[640,256]{1,0:T(8,128)}, f32[640,256]{1,0:T(8,128)}, f32[640,256]{1,0:T(8,128)}, /*index=5...) custom-call(s32[3]{0:T(128)} %pad_add_fusion.pos_ref, bf16[256,1024]{1,0:T(8,128)(2,1)} %copy-done.24, ...), custom_call_target="tpu_custom_call" | custom-call | flops 268435456 | bytes 8388608 | tf_op jit(solution)/shard_map/grad/pallas_call | solution.py:523
  457.2 13.7 %collective-permute-done.53 = f32[896,256]{1,0:T(8,128)S(1)} collective-permute-done((f32[896,256]{1,0:T(8,128)}, f32[896,256]{1,0:T(8,128)S(1)}, u32[]{:S(2)}, u32[]{:S(2)}) %collective-permute-start.53) | collective-permute-done | bytes 917536 | tf_op jit(solution)/shard_map/ppermute | solution.py:601
  470.9 19.8 %collective-permute-done.65 = f32[896,256]{1,0:T(8,128)} collective-permute-done((f32[896,256]{1,0:T(8,128)}, f32[896,256]{1,0:T(8,128)}, u32[]{:S(2)}, u32[]{:S(2)}) %collective-permute-start.65) | collective-permute-done | bytes 917536 | tf_op jit(solution)/shard_map/ppermute | solution.py:601
  490.9 13.8 %collective-permute-done.57 = f32[640,256]{1,0:T(8,128)S(1)} collective-permute-done((f32[640,256]{1,0:T(8,128)}, f32[640,256]{1,0:T(8,128)S(1)}, u32[]{:S(2)}, u32[]{:S(2)}) %collective-permute-start.57) | collective-permute-done | bytes 655392 | tf_op jit(solution)/shard_map/ppermute | solution.py:601
  510.8 13.6 %collective-permute-done.50 = f32[896,256]{1,0:T(8,128)S(1)} collective-permute-done((f32[896,256]{1,0:T(8,128)S(1)}, f32[896,256]{1,0:T(8,128)S(1)}, u32[]{:S(2)}, u32[]{:S(2)}) %collective-permute-start.50) | collective-permute-done | bytes 917536 | tf_op jit(solution)/shard_map/ppermute | solution.py:601
  531.4 7.4 %collective-permute-done.59 = f32[640,256]{1,0:T(8,128)S(1)} collective-permute-done((f32[640,256]{1,0:T(8,128)S(1)}, f32[640,256]{1,0:T(8,128)S(1)}, u32[]{:S(2)}, u32[]{:S(2)}) %collective-permute-start.59) | collective-permute-done | bytes 655392 | tf_op jit(solution)/shard_map/ppermute | solution.py:601
  538.8 4.9 collective-permute-start.67
  548.8 3.7 collective-permute-done.58
  554.4 3.5 shard_map.164
  560.4 5.1 collective-permute-start.60
  567.6 12.7 %collective-permute-done.67.first_ref = f32[896,256]{1,0:T(8,128)S(1)} collective-permute-done((f32[896,256]{1,0:T(8,128)S(1)}, f32[896,256]{1,0:T(8,128)S(1)}, u32[]{:S(2)}, u32[]{:S(2)}) %collective-permute-start.67) | collective-permute-done | bytes 917536 | tf_op jit(solution)/shard_map/ppermute | solution.py:617
  581.2 3.7 shard_map.163
  584.9 22.6 %collective-permute-done.56.second_ref = f32[896,256]{1,0:T(8,128)} collective-permute-done((f32[896,256]{1,0:T(8,128)}, f32[896,256]{1,0:T(8,128)}, u32[]{:S(2)}, u32[]{:S(2)}) %collective-permute-start.56) | collective-permute-done | bytes 917536 | tf_op jit(solution)/shard_map/ppermute | solution.py:617
  607.5 4.5 collective-permute-done.52.first_ref
  612.0 3.7 shard_map.162
  617.3 5.9 reduce-scatter.3.cloned.1.call-done
  625.8 3.3 collective-permute-done.60.first_ref
  629.2 3.2 p_attn.1
  (314 shorter events, 140.6 us)
Async XLA Ops:
  7.2 119.7 %all-gather.3.cloned.1.call-start = ((), (), s32[]{:S(2)}) async-start(), calls=%async_computation.2 | async-start | bytes 8912896 | tf_op jit(solution)/shard_map/all_gather | solution.py:715
  12.1 28.8 %collective-permute-start.1 = (bf16[256,2176]{1,0:T(8,128)(2,1)}, bf16[256,2176]{1,0:T(8,128)(2,1)S(1)}, u32[]{:S(2)}, u32[]{:S(2)}) collective-permute-start(bf16[256,2176]{1,0:T(8,128)(2,1)} %get-tuple-element.144), channel_id=1, source_target_pairs={{0,8},{1,24},{8,0},{9,16},{16,9},{17,25},{24,1},{25,17},{2,10},{3,... | collective-permute-start | bytes 3342344 | tf_op jit(solution)/shard_map/ppermute | solution.py:617
  41.9 176.0 %all-gather.5.cloned.1.call-start = ((), (), s32[]{:S(2)}) async-start(), calls=%async_computation.4 | async-start | bytes 8912896 | tf_op jit(solution)/shard_map/all_gather | solution.py:716
  42.7 573.0 %reduce-scatter.5.cloned.1.call-start = ((), (), s32[]{:S(2)}) async-start(), calls=%async_computation.5 | async-start | bytes 17825792 | tf_op jit(solution)/shard_map/reduce_scatter | solution.py:749
  48.3 29.2 %collective-permute-start.9 = (bf16[256,2176]{1,0:T(8,128)(2,1)S(1)}, bf16[256,2176]{1,0:T(8,128)(2,1)S(1)}, u32[]{:S(2)}, u32[]{:S(2)}) collective-permute-start(bf16[256,2176]{1,0:T(8,128)(2,1)S(1)} %collective-permute-done.1.refs_1_.refs_4_), channel_id=1, source_target_pairs={{0,32},{32,64},{64,96},{96,0},{1,33},{33,65},{65,97},{97,1},{2,34}... | collective-permute-start | bytes 3342344 | tf_op jit(solution)/shard_map/ppermute | solution.py:601
  50.0 27.6 %collective-permute-start.5 = (bf16[256,2176]{1,0:T(8,128)(2,1)S(1)}, bf16[256,2176]{1,0:T(8,128)(2,1)S(1)}, u32[]{:S(2)}, u32[]{:S(2)}) collective-permute-start(bf16[256,2176]{1,0:T(8,128)(2,1)S(1)} %collective-permute-done.1.refs_1_.refs_4_), channel_id=1, source_target_pairs={{0,96},{32,0},{64,32},{96,64},{1,97},{33,1},{65,33},{97,65},{2,98}... | collective-permute-start | bytes 3342344 | tf_op jit(solution)/shard_map/ppermute | solution.py:601
  52.1 26.0 %collective-permute-start.3 = (bf16[256,2176]{1,0:T(8,128)(2,1)S(1)}, bf16[256,2176]{1,0:T(8,128)(2,1)S(1)}, u32[]{:S(2)}, u32[]{:S(2)}) collective-permute-start(bf16[256,2176]{1,0:T(8,128)(2,1)S(1)} %collective-permute-done.1.refs_1_.refs_4_), channel_id=1, source_target_pairs={{0,1},{1,0},{2,3},{3,2},{4,5},{5,4},{6,7},{7,6},{8,9},{9,8},{10,11... | collective-permute-start | bytes 3342344 | tf_op jit(solution)/shard_map/ppermute | solution.py:605
  52.1 44.9 %collective-permute-start.8 = (bf16[256,2176]{1,0:T(8,128)(2,1)S(1)}, bf16[256,2176]{1,0:T(8,128)(2,1)S(1)}, u32[]{:S(2)}, u32[]{:S(2)}) collective-permute-start(bf16[256,2176]{1,0:T(8,128)(2,1)S(1)} %collective-permute-done.refs_0_.refs_3_), channel_id=1, source_target_pairs={{0,32},{32,64},{64,96},{96,0},{1,33},{33,65},{65,97},{97,1},{2,34}... | collective-permute-start | bytes 3342344 | tf_op jit(solution)/shard_map/ppermute | solution.py:601
  74.6 27.3 %collective-permute-start.4 = (bf16[256,2176]{1,0:T(8,128)(2,1)S(1)}, bf16[256,2176]{1,0:T(8,128)(2,1)S(1)}, u32[]{:S(2)}, u32[]{:S(2)}) collective-permute-start(bf16[256,2176]{1,0:T(8,128)(2,1)S(1)} %collective-permute-done.refs_0_.refs_3_), channel_id=1, source_target_pairs={{0,96},{32,0},{64,32},{96,64},{1,97},{33,1},{65,33},{97,65},{2,98}... | collective-permute-start | bytes 3342344 | tf_op jit(solution)/shard_map/ppermute | solution.py:601
  78.1 42.2 %collective-permute-start.13 = (bf16[256,2176]{1,0:T(8,128)(2,1)S(1)}, bf16[256,2176]{1,0:T(8,128)(2,1)S(1)}, u32[]{:S(2)}, u32[]{:S(2)}) collective-permute-start(bf16[256,2176]{1,0:T(8,128)(2,1)S(1)} %collective-permute-done.5.refs_5_.refs_8_), channel_id=1, source_target_pairs={{0,96},{32,0},{64,32},{96,64},{1,97},{33,1},{65,33},{97,65},{2,98}... | collective-permute-start | bytes 3342344 | tf_op jit(solution)/shard_map/ppermute | solution.py:601
  121.1 34.8 %collective-permute-start.33 = (bf16[256,1152]{1,0:T(8,128)(2,1)}, bf16[256,1152]{1,0:T(8,128)(2,1)}, u32[]{:S(2)}, u32[]{:S(2)}) collective-permute-start(bf16[256,1152]{1,0:T(8,128)(2,1)} %collective-permute-done.21.refs_4_.refs_1_), channel_id=1, source_target_pairs={{0,32},{32,64},{64,96},{96,0},{1,33},{33,65},{65,97},{97,1},{2,34}... | collective-permute-start | bytes 1769480 | tf_op jit(solution)/shard_map/ppermute | solution.py:601
  122.6 37.1 %collective-permute-start.25 = (bf16[256,1152]{1,0:T(8,128)(2,1)}, bf16[256,1152]{1,0:T(8,128)(2,1)}, u32[]{:S(2)}, u32[]{:S(2)}) collective-permute-start(bf16[256,1152]{1,0:T(8,128)(2,1)} %collective-permute-done.21.refs_4_.refs_1_), channel_id=1, source_target_pairs={{0,96},{32,0},{64,32},{96,64},{1,97},{33,1},{65,33},{97,65},{2,98}... | collective-permute-start | bytes 1769480 | tf_op jit(solution)/shard_map/ppermute | solution.py:601
  125.1 35.8 %collective-permute-start.23 = (bf16[256,1152]{1,0:T(8,128)(2,1)}, bf16[256,1152]{1,0:T(8,128)(2,1)}, u32[]{:S(2)}, u32[]{:S(2)}) collective-permute-start(bf16[256,1152]{1,0:T(8,128)(2,1)} %collective-permute-done.21.refs_4_.refs_1_), channel_id=1, source_target_pairs={{0,1},{1,0},{2,3},{3,2},{4,5},{5,4},{6,7},{7,6},{8,9},{9,8},{10,11... | collective-permute-start | bytes 1769480 | tf_op jit(solution)/shard_map/ppermute | solution.py:605
  126.7 35.0 %collective-permute-start.28 = (bf16[256,1152]{1,0:T(8,128)(2,1)}, bf16[256,1152]{1,0:T(8,128)(2,1)}, u32[]{:S(2)}, u32[]{:S(2)}) collective-permute-start(bf16[256,1152]{1,0:T(8,128)(2,1)} %collective-permute-done.20.refs_3_.refs_0_), channel_id=1, source_target_pairs={{0,32},{32,64},{64,96},{96,0},{1,33},{33,65},{65,97},{97,1},{2,34}... | collective-permute-start | bytes 1769480 | tf_op jit(solution)/shard_map/ppermute | solution.py:601
  155.9 38.0 %collective-permute-start.24 = (bf16[256,1152]{1,0:T(8,128)(2,1)}, bf16[256,1152]{1,0:T(8,128)(2,1)S(1)}, u32[]{:S(2)}, u32[]{:S(2)}) collective-permute-start(bf16[256,1152]{1,0:T(8,128)(2,1)} %collective-permute-done.20.refs_3_.refs_0_), channel_id=1, source_target_pairs={{0,96},{32,0},{64,32},{96,64},{1,97},{33,1},{65,33},{97,65},{2,98}... | collective-permute-start | bytes 1769480 | tf_op jit(solution)/shard_map/ppermute | solution.py:601
  161.7 33.2 %collective-permute-start.22 = (bf16[256,1152]{1,0:T(8,128)(2,1)}, bf16[256,1152]{1,0:T(8,128)(2,1)S(1)}, u32[]{:S(2)}, u32[]{:S(2)}) collective-permute-start(bf16[256,1152]{1,0:T(8,128)(2,1)} %collective-permute-done.20.refs_3_.refs_0_), channel_id=1, source_target_pairs={{0,1},{1,0},{2,3},{3,2},{4,5},{5,4},{6,7},{7,6},{8,9},{9,8},{10,11... | collective-permute-start | bytes 1769480 | tf_op jit(solution)/shard_map/ppermute | solution.py:605
  168.8 26.2 %collective-permute-start.35 = (bf16[256,1152]{1,0:T(8,128)(2,1)}, bf16[256,1152]{1,0:T(8,128)(2,1)S(1)}, u32[]{:S(2)}, u32[]{:S(2)}) collective-permute-start(bf16[256,1152]{1,0:T(8,128)(2,1)} %collective-permute-done.33.refs_16_.refs_9_), channel_id=1, source_target_pairs={{0,1},{1,0},{2,3},{3,2},{4,5},{5,4},{6,7},{7,6},{8,9},{9,8},{10,11... | collective-permute-start | bytes 1769480 | tf_op jit(solution)/shard_map/ppermute | solution.py:605
  226.8 71.9 %collective-permute-start.42 = (bf16[1024,2048]{1,0:T(8,128)(2,1)}, bf16[1024,2048]{1,0:T(8,128)(2,1)}, u32[]{:S(2)}, u32[]{:S(2)}) collective-permute-start(bf16[1024,2048]{1,0:T(8,128)(2,1)} %shard_map.157), channel_id=1, source_target_pairs={{0,1},{1,0},{2,3},{3,2},{4,5},{5,4},{6,7},{7,6},{8,9},{9,8},{10,11... | collective-permute-start | bytes 12582920 | tf_op jit(solution)/shard_map/ppermute | solution.py:605
  270.3 28.4 %collective-permute-start.41 = (bf16[1792,1024]{1,0:T(8,128)(2,1)}, bf16[1792,1024]{1,0:T(8,128)(2,1)S(1)}, u32[]{:S(2)}, u32[]{:S(2)}) collective-permute-start(bf16[1792,1024]{1,0:T(8,128)(2,1)} %get-tuple-element.95.refs_0_), channel_id=1, source_target_pairs={{0,1},{1,0},{2,3},{3,2},{4,5},{5,4},{6,7},{7,6},{8,9},{9,8},{10,11... | collective-permute-start | bytes 11010056 | tf_op jit(solution)/shard_map/ppermute | solution.py:605
  286.1 27.9 %collective-permute-start.43 = (f32[2,512,128]{2,1,0:T(8,128)}, f32[2,512,128]{2,1,0:T(8,128)}, u32[]{:S(2)}, u32[]{:S(2)}) collective-permute-start(f32[2,512,128]{2,1,0:T(8,128)} %get-tuple-element.107), channel_id=1, source_target_pairs={{0,8},{8,0},{16,24},{24,16},{1,9},{9,1},{17,25},{25,17},{2,10},{10... | collective-permute-start | bytes 1572872 | tf_op jit(solution)/shard_map/ppermute | solution.py:609
  349.0 274.2 %reduce-scatter.3.cloned.1.call-start = ((), (), s32[]{:S(2)}) async-start(), calls=%async_computation.3 | async-start | bytes 17825792 | tf_op jit(solution)/shard_map/reduce_scatter | solution.py:730
  352.7 38.9 %collective-permute-start.72 = (f32[896,256]{1,0:T(8,128)}, f32[896,256]{1,0:T(8,128)S(1)}, u32[]{:S(2)}, u32[]{:S(2)}) collective-permute-start(f32[896,256]{1,0:T(8,128)} %get-tuple-element.141), channel_id=1, source_target_pairs={{0,96},{32,0},{64,32},{96,64},{1,97},{33,1},{65,33},{97,65},{2,98}... | collective-permute-start | bytes 2752520 | tf_op jit(solution)/shard_map/ppermute | solution.py:601
  352.8 42.2 %collective-permute-start.71 = (f32[896,256]{1,0:T(8,128)}, f32[896,256]{1,0:T(8,128)S(1)}, u32[]{:S(2)}, u32[]{:S(2)}) collective-permute-start(f32[896,256]{1,0:T(8,128)} %add.114), channel_id=1, source_target_pairs={{0,32},{32,64},{64,96},{96,0},{1,33},{33,65},{65,97},{97,1},{2,34}... | collective-permute-start | bytes 2752520 | tf_op jit(solution)/shard_map/ppermute | solution.py:601
  375.5 34.3 %collective-permute-start.76 = (f32[896,256]{1,0:T(8,128)}, f32[896,256]{1,0:T(8,128)}, u32[]{:S(2)}, u32[]{:S(2)}) collective-permute-start(f32[896,256]{1,0:T(8,128)} %add_add_fusion.1), channel_id=1, source_target_pairs={{0,8},{1,24},{8,0},{9,16},{16,9},{17,25},{24,1},{25,17},{2,10},{3,... | collective-permute-start | bytes 2752520 | tf_op jit(solution)/shard_map/ppermute | solution.py:617
  375.5 49.1 %collective-permute-start.46 = (f32[896,256]{1,0:T(8,128)}, f32[896,256]{1,0:T(8,128)}, u32[]{:S(2)}, u32[]{:S(2)}) collective-permute-start(f32[896,256]{1,0:T(8,128)} %get-tuple-element.115), channel_id=1, source_target_pairs={{0,32},{32,64},{64,96},{96,0},{1,33},{33,65},{65,97},{97,1},{2,34}... | collective-permute-start | bytes 2752520 | tf_op jit(solution)/shard_map/ppermute | solution.py:601
  375.5 49.1 %collective-permute-start.47 = (f32[896,256]{1,0:T(8,128)}, f32[896,256]{1,0:T(8,128)}, u32[]{:S(2)}, u32[]{:S(2)}) collective-permute-start(f32[896,256]{1,0:T(8,128)} %get-tuple-element.118), channel_id=1, source_target_pairs={{0,96},{32,0},{64,32},{96,64},{1,97},{33,1},{65,33},{97,65},{2,98}... | collective-permute-start | bytes 2752520 | tf_op jit(solution)/shard_map/ppermute | solution.py:601
  391.5 39.3 %collective-permute-start.66 = (f32[896,256]{1,0:T(8,128)}, f32[896,256]{1,0:T(8,128)}, u32[]{:S(2)}, u32[]{:S(2)}) collective-permute-start(f32[896,256]{1,0:T(8,128)} %get-tuple-element.137), channel_id=1, source_target_pairs={{0,96},{32,0},{64,32},{96,64},{1,97},{33,1},{65,33},{97,65},{2,98}... | collective-permute-start | bytes 2752520 | tf_op jit(solution)/shard_map/ppermute | solution.py:601
  395.9 35.8 %collective-permute-start.68 = (f32[896,256]{1,0:T(8,128)}, f32[896,256]{1,0:T(8,128)}, u32[]{:S(2)}, u32[]{:S(2)}) collective-permute-start(f32[896,256]{1,0:T(8,128)} %get-tuple-element.139), channel_id=1, source_target_pairs={{0,32},{32,64},{64,96},{96,0},{1,33},{33,65},{65,97},{97,1},{2,34}... | collective-permute-start | bytes 2752520 | tf_op jit(solution)/shard_map/ppermute | solution.py:601
  424.6 26.8 %collective-permute-start.45 = (f32[896,256]{1,0:T(8,128)}, f32[896,256]{1,0:T(8,128)}, u32[]{:S(2)}, u32[]{:S(2)}) collective-permute-start(f32[896,256]{1,0:T(8,128)} %get-tuple-element.113), channel_id=1, source_target_pairs={{0,32},{32,64},{64,96},{96,0},{1,33},{33,65},{65,97},{97,1},{2,34}... | collective-permute-start | bytes 2752520 | tf_op jit(solution)/shard_map/ppermute | solution.py:601
  424.7 26.7 %collective-permute-start.54 = (f32[896,256]{1,0:T(8,128)}, f32[896,256]{1,0:T(8,128)}, u32[]{:S(2)}, u32[]{:S(2)}) collective-permute-start(f32[896,256]{1,0:T(8,128)} %get-tuple-element.126), channel_id=1, source_target_pairs={{0,96},{32,0},{64,32},{96,64},{1,97},{33,1},{65,33},{97,65},{2,98}... | collective-permute-start | bytes 2752520 | tf_op jit(solution)/shard_map/ppermute | solution.py:601
  430.9 40.0 %collective-permute-start.53 = (f32[896,256]{1,0:T(8,128)}, f32[896,256]{1,0:T(8,128)S(1)}, u32[]{:S(2)}, u32[]{:S(2)}) collective-permute-start(f32[896,256]{1,0:T(8,128)} %get-tuple-element.124), channel_id=1, source_target_pairs={{0,32},{32,64},{64,96},{96,0},{1,33},{33,65},{65,97},{97,1},{2,34}... | collective-permute-start | bytes 2752520 | tf_op jit(solution)/shard_map/ppermute | solution.py:601
  431.7 59.0 %collective-permute-start.65 = (f32[896,256]{1,0:T(8,128)}, f32[896,256]{1,0:T(8,128)}, u32[]{:S(2)}, u32[]{:S(2)}) collective-permute-start(f32[896,256]{1,0:T(8,128)} %add.117), channel_id=1, source_target_pairs={{0,32},{32,64},{64,96},{96,0},{1,33},{33,65},{65,97},{97,1},{2,34}... | collective-permute-start | bytes 2752520 | tf_op jit(solution)/shard_map/ppermute | solution.py:601
  435.0 69.8 %collective-permute-start.69 = (f32[896,256]{1,0:T(8,128)}, f32[896,256]{1,0:T(8,128)}, u32[]{:S(2)}, u32[]{:S(2)}) collective-permute-start(f32[896,256]{1,0:T(8,128)} %add.118), channel_id=1, source_target_pairs={{0,96},{32,0},{64,32},{96,64},{1,97},{33,1},{65,33},{97,65},{2,98}... | collective-permute-start | bytes 2752520 | tf_op jit(solution)/shard_map/ppermute | solution.py:601
  451.4 53.4 %collective-permute-start.57 = (f32[640,256]{1,0:T(8,128)}, f32[640,256]{1,0:T(8,128)S(1)}, u32[]{:S(2)}, u32[]{:S(2)}) collective-permute-start(f32[640,256]{1,0:T(8,128)} %get-tuple-element.129), channel_id=1, source_target_pairs={{0,32},{32,64},{64,96},{96,0},{1,33},{33,65},{65,97},{97,1},{2,34}... | collective-permute-start | bytes 1966088 | tf_op jit(solution)/shard_map/ppermute | solution.py:601
  451.4 53.3 %collective-permute-start.62 = (f32[640,256]{1,0:T(8,128)}, f32[640,256]{1,0:T(8,128)S(1)}, u32[]{:S(2)}, u32[]{:S(2)}) collective-permute-start(f32[640,256]{1,0:T(8,128)} %get-tuple-element.134), channel_id=1, source_target_pairs={{0,96},{32,0},{64,32},{96,64},{1,97},{33,1},{65,33},{97,65},{2,98}... | collective-permute-start | bytes 1966088 | tf_op jit(solution)/shard_map/ppermute | solution.py:601
  470.9 37.5 %collective-permute-start.55 = (f32[896,256]{1,0:T(8,128)S(1)}, f32[896,256]{1,0:T(8,128)S(1)}, u32[]{:S(2)}, u32[]{:S(2)}) collective-permute-start(f32[896,256]{1,0:T(8,128)S(1)} %add.123), channel_id=1, source_target_pairs={{0,96},{32,0},{64,32},{96,64},{1,97},{33,1},{65,33},{97,65},{2,98}... | collective-permute-start | bytes 2752520 | tf_op jit(solution)/shard_map/ppermute | solution.py:601
  490.7 33.7 %collective-permute-start.50 = (f32[896,256]{1,0:T(8,128)S(1)}, f32[896,256]{1,0:T(8,128)S(1)}, u32[]{:S(2)}, u32[]{:S(2)}) collective-permute-start(f32[896,256]{1,0:T(8,128)S(1)} %add.119), channel_id=1, source_target_pairs={{0,32},{32,64},{64,96},{96,0},{1,33},{33,65},{65,97},{97,1},{2,34}... | collective-permute-start | bytes 2752520 | tf_op jit(solution)/shard_map/ppermute | solution.py:601
  504.7 34.1 %collective-permute-start.59 = (f32[640,256]{1,0:T(8,128)S(1)}, f32[640,256]{1,0:T(8,128)S(1)}, u32[]{:S(2)}, u32[]{:S(2)}) collective-permute-start(f32[640,256]{1,0:T(8,128)S(1)} %copy-done.59), channel_id=1, source_target_pairs={{0,96},{32,0},{64,32},{96,64},{1,97},{33,1},{65,33},{97,65},{2,98}... | collective-permute-start | bytes 1966088 | tf_op jit(solution)/shard_map/ppermute | solution.py:601
  504.9 38.8 %collective-permute-start.61 = (f32[640,256]{1,0:T(8,128)S(1)}, f32[640,256]{1,0:T(8,128)S(1)}, u32[]{:S(2)}, u32[]{:S(2)}) collective-permute-start(f32[640,256]{1,0:T(8,128)S(1)} %copy-done.58), channel_id=1, source_target_pairs={{0,32},{32,64},{64,96},{96,0},{1,33},{33,65},{65,97},{97,1},{2,34}... | collective-permute-start | bytes 1966088 | tf_op jit(solution)/shard_map/ppermute | solution.py:601
  508.4 37.6 %collective-permute-start.73 = (f32[896,256]{1,0:T(8,128)S(1)}, f32[896,256]{1,0:T(8,128)S(1)}, u32[]{:S(2)}, u32[]{:S(2)}) collective-permute-start(f32[896,256]{1,0:T(8,128)S(1)} %add_add_fusion.2), channel_id=1, source_target_pairs={{0,0},{1,16},{8,8},{9,24},{16,1},{17,17},{24,9},{25,25},{2,2},{3,1... | collective-permute-start | bytes 2752520 | tf_op jit(solution)/shard_map/ppermute | solution.py:617
  524.4 28.1 %collective-permute-start.58 = (f32[640,256]{1,0:T(8,128)S(1)}, f32[640,256]{1,0:T(8,128)}, u32[]{:S(2)}, u32[]{:S(2)}) collective-permute-start(f32[640,256]{1,0:T(8,128)S(1)} %add.125), channel_id=1, source_target_pairs={{0,32},{32,64},{64,96},{96,0},{1,33},{33,65},{65,97},{97,1},{2,34}... | collective-permute-start | bytes 1966088 | tf_op jit(solution)/shard_map/ppermute | solution.py:601
  528.7 31.7 %collective-permute-start.63 = (f32[640,256]{1,0:T(8,128)}, f32[640,256]{1,0:T(8,128)}, u32[]{:S(2)}, u32[]{:S(2)}) collective-permute-start(f32[640,256]{1,0:T(8,128)} %add.129), channel_id=1, source_target_pairs={{0,96},{32,0},{64,32},{96,64},{1,97},{33,1},{65,33},{97,65},{2,98}... | collective-permute-start | bytes 1966088 | tf_op jit(solution)/shard_map/ppermute | solution.py:601
  538.8 41.5 %collective-permute-start.67 = (f32[896,256]{1,0:T(8,128)S(1)}, f32[896,256]{1,0:T(8,128)S(1)}, u32[]{:S(2)}, u32[]{:S(2)}) collective-permute-start(f32[896,256]{1,0:T(8,128)S(1)} %add_add_fusion.4), channel_id=1, source_target_pairs={{0,0},{1,16},{8,8},{9,24},{16,1},{17,17},{24,9},{25,25},{2,2},{3,1... | collective-permute-start | bytes 2752520 | tf_op jit(solution)/shard_map/ppermute | solution.py:617
  543.7 36.6 %collective-permute-start.70 = (f32[896,256]{1,0:T(8,128)S(1)}, f32[896,256]{1,0:T(8,128)}, u32[]{:S(2)}, u32[]{:S(2)}) collective-permute-start(f32[896,256]{1,0:T(8,128)S(1)} %add_add_fusion.3), channel_id=1, source_target_pairs={{0,8},{1,24},{8,0},{9,16},{16,9},{17,25},{24,1},{25,17},{2,10},{3,... | collective-permute-start | bytes 2752520 | tf_op jit(solution)/shard_map/ppermute | solution.py:617
  547.0 60.5 %collective-permute-start.56 = (f32[896,256]{1,0:T(8,128)}, f32[896,256]{1,0:T(8,128)}, u32[]{:S(2)}, u32[]{:S(2)}) collective-permute-start(f32[896,256]{1,0:T(8,128)} %add_add_fusion.5), channel_id=1, source_target_pairs={{0,8},{1,24},{8,0},{9,16},{16,9},{17,25},{24,1},{25,17},{2,10},{3,... | collective-permute-start | bytes 2752520 | tf_op jit(solution)/shard_map/ppermute | solution.py:617
  552.5 59.5 %collective-permute-start.52 = (f32[896,256]{1,0:T(8,128)}, f32[896,256]{1,0:T(8,128)}, u32[]{:S(2)}, u32[]{:S(2)}) collective-permute-start(f32[896,256]{1,0:T(8,128)} %add_add_fusion.6), channel_id=1, source_target_pairs={{0,0},{1,16},{8,8},{9,24},{16,1},{17,17},{24,9},{25,25},{2,2},{3,1... | collective-permute-start | bytes 2752520 | tf_op jit(solution)/shard_map/ppermute | solution.py:617
  560.4 68.8 %collective-permute-start.60 = (f32[640,256]{1,0:T(8,128)}, f32[640,256]{1,0:T(8,128)}, u32[]{:S(2)}, u32[]{:S(2)}) collective-permute-start(f32[640,256]{1,0:T(8,128)} %add_add_fusion.8), channel_id=1, source_target_pairs={{0,0},{1,16},{8,8},{9,24},{16,1},{17,17},{24,9},{25,25},{2,2},{3,1... | collective-permute-start | bytes 1966088 | tf_op jit(solution)/shard_map/ppermute | solution.py:617
  580.3 48.9 %collective-permute-start.64 = (f32[640,256]{1,0:T(8,128)}, f32[640,256]{1,0:T(8,128)}, u32[]{:S(2)}, u32[]{:S(2)}) collective-permute-start(f32[640,256]{1,0:T(8,128)} %add_add_fusion.7), channel_id=1, source_target_pairs={{0,8},{1,24},{8,0},{9,16},{16,9},{17,25},{24,1},{25,17},{2,10},{3,... | collective-permute-start | bytes 1966088 | tf_op jit(solution)/shard_map/ppermute | solution.py:617
  (96 other events, 1454.1 us)
Sparse Core Ops, SparseCore 0:
  42.0 75.9 all-gather.2
  120.1 74.7 all-gather.4
  349.1 116.3 reduce-scatter.4
  468.7 154.4 reduce-scatter.2

commit v4 on v3

--- a/solution.py
+++ b/solution.py
@@ -16,7 +16,7 @@
 HEAD_GROUP = 4
 F32 = jnp.float32
 BF16 = jnp.bfloat16
-VMEM_LIMIT = 60 * 1024 * 1024
+VMEM_LIMIT = 67043328
 
 
 def norm_fwd(row_vals, norm_gain):
@@ -366,31 +366,44 @@
         left_copies[-1].start()
         start += 0 if side == 0 else width
 
-    def copies(idx):
+    def copies(idx, slot):
         for part in range(2):
             rows = pl.ds(half_start(pos_ref, part, half), half)
-            yield pltpu.make_async_copy(halves[2 * idx + part], w_buf.at[idx % slots, rows], w_sem.at[idx % slots, part])
+            yield pltpu.make_async_copy(halves[2 * idx + part], w_buf.at[slot, rows], w_sem.at[slot, part])
 
     def out_copy(idx):
-        cols = pl.ds(pl.multiple_of(piece_block(pos_ref, *keys[idx]) * block, block), block)
-        return pltpu.make_async_copy(out_buf.at[idx % 2], out_ref.at[:, cols], out_sem.at[idx % 2])
+        core = pos_ref[1]
+        other = lax.rem(idx, 2)
+        block_id = lax.rem(pos_ref[0] + idx // 2, NZ) * NC + core + other - 2 * core * other
+        slot = lax.rem(idx, 2)
+        return pltpu.make_async_copy(out_buf.at[slot], out_ref.at[:, pl.ds(pl.multiple_of(block_id * block, block), block)], out_sem.at[slot])
 
     for idx in range(slots - 1):
-        for copy in copies(idx):
+        for copy in copies(idx, idx):
             copy.start()
-    for idx in range(count):
-        if idx + slots - 1 < count:
-            for copy in copies(idx + slots - 1):
-                copy.start()
-        for copy in copies(idx):
+    for copy in left_copies:
+        copy.wait()
+
+    @pl.loop(0, count)
+    def _(step):
+        slot = lax.rem(step, slots)
+        for idx in range(slots - 1, count):
+
+            @pl.when(step + slots - 1 == idx)
+            def _(idx=idx):
+                for copy in copies(idx, idx % slots):
+                    copy.start()
+
+        for copy in copies(0, slot):
             copy.wait()
-        if idx == 0:
-            for copy in left_copies:
-                copy.wait()
-        if idx >= 2:
-            out_copy(idx - 2).wait()
-        out_buf[idx % 2] = dot_nt(left_buf[...], w_buf[idx % slots])
-        out_copy(idx).start()
+
+        @pl.when(step >= 2)
+        def _():
+            out_copy(step - 2).wait()
+
+        out_buf[lax.rem(step, 2)] = dot_nt(left_buf[...], w_buf[slot])
+        out_copy(step).start()
+
     for idx in range(count - 2, count):
         out_copy(idx).wait()
 
@@ -465,14 +478,16 @@
 
 def grad_kernel(heights, pos_ref, *refs):
     pairs = len(heights)
-    ins = refs[: 6 * pairs]
-    outs = refs[6 * pairs : 6 * pairs + 2 * NZ]
-    buf, sem = refs[6 * pairs + 2 * NZ :]
+    ins = refs[: 4 * pairs]
+    outs = refs[4 * pairs : 4 * pairs + 2 * NZ]
+    buf, sem = refs[4 * pairs + 2 * NZ :]
+    half = buf.shape[2] // 2
     step = pl.program_id(0)
     slot = lax.rem(step, 2)
 
     def out_copy(idx, part):
-        return pltpu.make_async_copy(buf.at[idx % 2, part], outs[2 * idx + part], sem.at[idx % 2, part])
+        cols = pl.ds(half_start(pos_ref, part, half), half)
+        return pltpu.make_async_copy(buf.at[idx % 2, :, cols], outs[2 * idx + part], sem.at[idx % 2, part])
 
     for idx in range(2, NZ):
 
@@ -483,9 +498,8 @@
 
     start = 0
     for idx, height in enumerate(heights):
-        own, recv, acts0, acts1, recv0, recv1 = ins[6 * idx : 6 * idx + 6]
-        for part, acts, acts_recv in ((0, acts0, recv0), (1, acts1, recv1)):
-            buf[slot, part, start : start + height, :] = dot_nn(own[...], acts[...]) + dot_nn(recv[...], acts_recv[...])
+        own, recv, acts, acts_recv = ins[4 * idx : 4 * idx + 4]
+        buf[slot, start : start + height, :] = dot_nn(own[...], acts[...]) + dot_nn(recv[...], acts_recv[...])
         start += height
     for idx in range(NZ):
 
@@ -503,21 +517,18 @@
 
 def grad_pieces(pos, pairs):
     tokens, depth = pairs[0][2].shape
-    cols = depth // (NZ * NY)
+    cols = depth // (NZ * NC)
     in_specs = []
     args = []
 
     def z_of(n, pos):
         return lax.rem(pos[0] + jnp.where(n == 0, 2, jnp.where(n == 1, 1, jnp.where(n == 2, 3, 0))), NZ)
 
-    def bit(pos, part):
-        return 1 - pos[2] if part else pos[2]
-
     for own, recv, acts, acts_recv, height, block in pairs:
         in_specs += [pl.BlockSpec((height, tokens), lambda n, pos, block=block: (block, 0))] * 2
-        in_specs += [pl.BlockSpec((tokens, cols), lambda n, pos, part=part: (0, z_of(n, pos) * NY + 2 * pos[1] + bit(pos, part))) for part in range(2)]
-        in_specs += [pl.BlockSpec((tokens, cols), lambda n, pos, part=part: (0, z_of(n, pos) * 2 + bit(pos, part))) for part in range(2)]
-        args += [own, recv, acts, acts, acts_recv, acts_recv]
+        in_specs.append(pl.BlockSpec((tokens, cols), lambda n, pos: (0, z_of(n, pos) * NC + pos[1])))
+        in_specs.append(pl.BlockSpec((tokens, cols), lambda n, pos: (0, z_of(n, pos))))
+        args += [own, recv, acts, acts_recv]
     heights = [pair[4] for pair in pairs]
     rows = sum(heights)
     return pl.pallas_call(
@@ -527,11 +538,11 @@
             grid=(NZ,),
             in_specs=in_specs,
             out_specs=[pl.BlockSpec(memory_space=pl.ANY)] * (2 * NZ),
-            scratch_shapes=[pltpu.VMEM((2, 2, rows, cols), F32), pltpu.SemaphoreType.DMA((2, 2))],
+            scratch_shapes=[pltpu.VMEM((2, rows, cols), F32), pltpu.SemaphoreType.DMA((2, 2))],
         ),
-        out_shape=[jax.ShapeDtypeStruct((rows, cols), F32)] * (2 * NZ),
-        compiler_params=params(),
-        cost_estimate=cost(4 * rows * tokens * cols * 2 * NZ, 4 * tokens * cols * 2 * NZ),
+        out_shape=[jax.ShapeDtypeStruct((rows, cols // 2), F32)] * (2 * NZ),
+        compiler_params=params(),
+        cost_estimate=cost(4 * rows * tokens * cols * NZ, 4 * tokens * cols * NZ),
         name="grad",
     )(pos, *args)
 
@@ -710,7 +721,7 @@
         wf_piece = gather_rows([jnp.concatenate([block(w_gate, j), block(w_up, j), *qkv_cols(j)], axis=1) for j in range(2)])
         ws_piece = gather_rows([jnp.concatenate([block(down_t, j), block(out_t, j)], axis=1) for j in range(2)])
 
-        x_rows = x_in[0].astype(F32)
+        x_rows = after(x_in[0], cos_tab, sin_tab).astype(F32)
         normed, norm_pull = jax.vjp(lambda row_vals: norm_fwd(row_vals, norm_gain), x_rows)
         h_all = lax.all_gather(after(normed.astype(BF16), wf_piece[0], wf_piece[1]), ("y", "x"), axis=0, tiled=True)
         dy_all = lax.all_gather(after(dy_in[0], *wf_piece), ("y", "x"), axis=0, tiled=True)
@@ -743,6 +754,7 @@
         got = swap_y(send)
         g_act = grad_pass(g_act, d_queries)
         g_gate = grad_start([(d_gate_up_t, d_gate_up_recv, h_all, h_recv, ff_blk, 0)], *g_act[3])
+        b_act = grad_back(g_act, g_gate[3][0])
         d_own, d_other = attn_post(after(pos, g_gate[3][0]), d_queries, keep, got, cos_tab, sin_tab)
         d_got = swap_c(d_other)
         dh_part = nt_pieces(pos, [d_gate_up, d_own, d_got], wf_parts)
@@ -758,7 +770,6 @@
         d_qkv_recv = swap_c(d_qkv_t)
         g_attn = grad_start([(attn_t, attn_recv, dy_all, dy_recv, o_blk, 0), (d_qkv_t, d_qkv_recv, h_all, h_recv, qkv_blk, 0)], *g_gate[3])
         g_up = grad_pass(g_up, g_attn[3][0])
-        b_act = grad_back(g_act, g_attn[3][0])
         g_attn = grad_pass(g_attn)
         b_gate = grad_back(g_gate)
         b_up = grad_back(g_up)

time: 649 us -> 644 us (level)
  waiting for transfers between devices: 282 us -> 273 us
    ppermute x26, starting transfers between devices: 11.4 us -> 21 us  [swap_c(): return lax.ppermute(val, 'c', [(0, 1), (1, 0)])]
    ppermute x36, waiting for transfers between devices: 152 us -> 143 us  [hop_z(): return lax.ppermute(val, 'z', ring(step, NZ))]
  transfers between devices with their start and end apart: 81 -> 81, of which waited for: 36 -> 31; matrix products, arithmetic and copies ran while one was open for 8% -> 7% of each run, Pallas kernels for 24% -> 24%
where the time goes in v4:
time: 644 us; the launch traced here: 634 us
  waiting for transfers between devices  273 us (42%)
  Pallas kernels  192 us (30%)
  starting transfers between devices  90.2 us (14%)
  other arithmetic  39.4 us (6%)
  local copies, waits for them, and re-layouts  24 us (4%)
  between operations  15.2 us (2%)
    ppermute x36, waiting for transfers between devices, hop_z(): return lax.ppermute(val, 'z', ring(step, NZ))  143 us
    ppermute x12, waiting for transfers between devices, turn(): return lax.ppermute(val, ('y', 'c'), pairs)  105 us
    pallas_call x4, Pallas kernels, grad_pieces(): pl.pallas_call(functools.partial(grad_kernel, heights), grid_spec=pltpu.P...  52.7 us
    pallas_call x2, Pallas kernels, nn_pieces(): pl.pallas_call(functools.partial(nn_kernel, keys, 2, len(widths), tile),...  45.1 us
    pallas_call x2, Pallas kernels, nt_pieces(): pl.pallas_call(functools.partial(nt_kernel, keys, sides), grid_spec=pltpu...  43.7 us
    ppermute x36, starting transfers between devices, hop_z(): return lax.ppermute(val, 'z', ring(step, NZ))  39.4 us
    ppermute x12, starting transfers between devices, turn(): return lax.ppermute(val, ('y', 'c'), pairs)  27 us
    ppermute x26, starting transfers between devices, swap_c(): return lax.ppermute(val, 'c', [(0, 1), (1, 0)])  21 us
  transfers between devices with their start and end apart: 81, of which 31 were waited for; matrix products, arithmetic and copies ran while one was open for 7% of the time, Pallas kernels for 24%

profile of v4, /device:TPU:1, one launch (start us, length us, event | category | flops | bytes accessed | tf_op | source)
XLA Modules:
  0.0 634.2 jit_solution(9586227205333172212)
XLA Ops:
  12.5 4.1 collective-permute-start.1
  22.4 18.9 %collective-permute-done.1.refs_1_.refs_4_ = bf16[256,2176]{1,0:T(8,128)(2,1)S(1)} collective-permute-done((bf16[256,2176]{1,0:T(8,128)(2,1)}, bf16[256,2176]{1,0:T(8,128)(2,1)S(1)}, u32[]{:S(2)}, u32[]{:S(2)}) %collective-permute-start.1) | collective-permute-done | bytes 1114144 | tf_op jit(solution)/shard_map/ppermute | solution.py:628
  51.5 4.4 collective-permute-done.21.refs_4_.refs_1_
  58.5 15.9 %collective-permute-done.20.refs_3_.refs_0_ = bf16[256,1152]{1,0:T(8,128)(2,1)} collective-permute-done((bf16[256,1152]{1,0:T(8,128)(2,1)S(1)}, bf16[256,1152]{1,0:T(8,128)(2,1)}, u32[]{:S(2)}, u32[]{:S(2)}) %collective-permute-start.20) | collective-permute-done | bytes 589856 | tf_op jit(solution)/shard_map/ppermute | solution.py:628
  74.3 3.3 collective-permute-start.4
  79.4 16.7 %collective-permute-done.8.refs_8_.refs_15_ = bf16[256,2176]{1,0:T(8,128)(2,1)S(1)} collective-permute-done((bf16[256,2176]{1,0:T(8,128)(2,1)S(1)}, bf16[256,2176]{1,0:T(8,128)(2,1)S(1)}, u32[]{:S(2)}, u32[]{:S(2)}) %collective-permute-start.8) | collective-permute-done | bytes 1114144 | tf_op jit(solution)/shard_map/ppermute | solution.py:612
  96.4 5.6 collective-permute-done.4.refs_4_.refs_7_
  102.7 16.8 %collective-permute-done.13.refs_13_.refs_12_ = bf16[256,2176]{1,0:T(8,128)(2,1)S(1)} collective-permute-done((bf16[256,2176]{1,0:T(8,128)(2,1)S(1)}, bf16[256,2176]{1,0:T(8,128)(2,1)S(1)}, u32[]{:S(2)}, u32[]{:S(2)}) %collective-permute-start.13) | collective-permute-done | bytes 1114144 | tf_op jit(solution)/shard_map/ppermute | solution.py:612
  127.3 27.4 %shard_map.153 = (bf16[1024,1792]{1,0:T(8,128)(2,1)}, bf16[1024,384]{1,0:T(8,128)(2,1)}) custom-call(s32[3]{0:T(128)} %pad_add_fusion.pos_ref, bf16[1024,4096]{1,0:T(8,128)(2,1)} %all-gather.3.cloned.1.call-done.acts_ref.in_ref.refs_2_.refs_6_, bf16[256,2176]{1,0:T(8,128)(2,1)} %copy-done.3, bf16[256,2176]{1,0:T(8,128)(2,1)} %copy-done.2, ...), custom_call_target="tpu_custom_call" | custom-call | flops 912680576 | bytes 26214400 | tf_op jit(solution)/shard_map/pallas_call | solution.py:330
  161.3 6.8 %collective-permute-done.18.other_third_ref = bf16[512,128]{1,0:T(8,128)(2,1)S(1)} collective-permute-done((bf16[512,128]{1,0:T(8,128)(2,1)S(1)}, bf16[512,128]{1,0:T(8,128)(2,1)S(1)}, u32[]{:S(2)}, u32[]{:S(2)}) %collective-permute-start.18) | collective-permute-done | bytes 131104 | tf_op jit(solution)/shard_map/ppermute | solution.py:633
  168.4 5.3 collective-permute-done.17.own_third_ref
  175.9 4.8 act_fwd.1
  180.7 5.6 shard_map.154
  194.8 16.9 %shard_map.155 = f32[1024,4096]{1,0:T(8,128)} custom-call(s32[3]{0:T(128)} %pad_add_fusion.pos_ref, bf16[1024,896]{1,0:T(8,128)(2,1)} %get-tuple-element.85.refs_0_, bf16[512,256]{1,0:T(8,128)(2,1)} %get-tuple-element.83.refs_1_, bf16[512,256]{1,0:T(8,128)(2,1)} %copy.38.refs_2_, bf16[256,1152]{1,0:T(8,128)(2,1)} %collective-permute-done.20.refs_3_.refs_0_, ...), custom_call_target="tpu_custom_call" | custom-call | flops 483183808 | bytes 26214400 | tf_op jit(solution)/shard_map/pallas_call | solution.py:421
  211.8 4.1 shard_map.156
  216.5 4.1 shard_map.157
  220.6 9.0 %collective-permute-start.42 = (bf16[1024,2048]{1,0:T(8,128)(2,1)}, bf16[1024,2048]{1,0:T(8,128)(2,1)}, u32[]{:S(2)}, u32[]{:S(2)}) collective-permute-start(bf16[1024,2048]{1,0:T(8,128)(2,1)} %shard_map.157), channel_id=1, source_target_pairs={{0,1},{1,0},{2,3},{3,2},{4,5},{5,4},{6,7},{7,6},{8,9},{9,8},{10,11... | collective-permute-start | bytes 12582920 | tf_op jit(solution)/shard_map/ppermute | solution.py:616
  229.7 13.2 %grad.4 = (f32[896,256]{1,0:T(8,128)}, f32[896,256]{1,0:T(8,128)}, f32[896,256]{1,0:T(8,128)}, f32[896,256]{1,0:T(8,128)}, f32[896,256]{1,0:T(8,128)}, /*index=5...) custom-call(s32[3]{0:T(128)} %pad_add_fusion.pos_ref, bf16[896,1024]{1,0:T(8,128)(2,1)} %get-tuple-element.80.refs_0_, ...), custom_call_target="tpu_custom_call" | custom-call | flops 375809632 | bytes 8388608 | tf_op jit(solution)/shard_map/grad/pallas_call | solution.py:534
  242.9 17.6 %shard_map.158 = (bf16[1024,896]{1,0:T(8,128)(2,1)}, bf16[1024,256]{1,0:T(8,128)(2,1)}) custom-call(s32[3]{0:T(128)} %pad_add_fusion.pos_ref, bf16[1024,4096]{1,0:T(8,128)(2,1)} %all-gather.5.cloned.1.call-done.in_ref.refs_2_.acts_ref, bf16[256,1152]{1,0:T(8,128)(2,1)} %collective-permute-done.20.refs_3_.refs_0_, ...), custom_call_target="tpu_custom_call" | custom-call | flops 483183808 | bytes 17825792 | tf_op jit(solution)/shard_map/pallas_call | solution.py:330
  260.5 6.9 %act_bwd.1 = (bf16[1024,1792]{1,0:T(8,128)(2,1)}, bf16[1792,1024]{1,0:T(8,128)(2,1)}) custom-call(bf16[1024,1792]{1,0:T(8,128)(2,1)} %get-tuple-element.79.ab_ref, bf16[1024,896]{1,0:T(8,128)(2,1)} %get-tuple-element.93.du_ref), custom_call_target="tpu_custom_call" | custom-call | flops 400000000 | bytes 14000000 | tf_op jit(solution)/shard_map/act_bwd/pallas_call | solution.py:260
  275.1 8.1 %shard_map.159 = (bf16[2,512,256]{2,1,0:T(8,128)(2,1)}, f32[2,512,128]{2,1,0:T(8,128)}, f32[2,512,128]{2,1,0:T(8,128)}) custom-call(s32[3]{0:T(128)} %pad_add_fusion.pos_ref, bf16[2,512,512]{2,1,0:T(8,128)(2,1)} %get-tuple-element.99.seq_ref, bf16[1024,256]{1,0:T(8,128)(2,1)} %get-tuple-element.100.own_ref, bf16[512,256]{1,0:T(8,128)(2,1)} %copy-done.59, ...), custom_call_target="tpu_custom_call" | custom-call | flops 800000000 | bytes 4000000 | tf_op jit(solution)/shard_map/pallas_call | solution.py:142
  284.0 6.7 %collective-permute-done.38 = f32[896,256]{1,0:T(8,128)} collective-permute-done((f32[896,256]{1,0:T(8,128)}, f32[896,256]{1,0:T(8,128)}, u32[]{:S(2)}, u32[]{:S(2)}) %collective-permute-start.38) | collective-permute-done | bytes 917536 | tf_op jit(solution)/shard_map/ppermute | solution.py:612
  295.5 13.1 %grad.5 = (f32[896,256]{1,0:T(8,128)}, f32[896,256]{1,0:T(8,128)}, f32[896,256]{1,0:T(8,128)}, f32[896,256]{1,0:T(8,128)}, f32[896,256]{1,0:T(8,128)}, /*index=5...) custom-call(s32[3]{0:T(128)} %pad_add_fusion.pos_ref, bf16[1792,1024]{1,0:T(8,128)(2,1)} %get-tuple-element.97.refs_0_, ...), custom_call_target="tpu_custom_call" | custom-call | flops 375809632 | bytes 8388608 | tf_op jit(solution)/shard_map/grad/pallas_call | solution.py:534
  308.6 3.2 shard_map.160
  317.2 26.8 %shard_map.161 = f32[1024,4096]{1,0:T(8,128)} custom-call(s32[3]{0:T(128)} %pad_add_fusion.pos_ref, bf16[1024,1792]{1,0:T(8,128)(2,1)} %get-tuple-element.94.refs_0_, bf16[512,384]{1,0:T(8,128)(2,1)} %get-tuple-element.110.refs_1_, bf16[512,384]{1,0:T(8,128)(2,1)} %copy.40.refs_2_, bf16[256,2176]{1,0:T(8,128)(2,1)} %copy-done.3, ...), custom_call_target="tpu_custom_call" | custom-call | flops 912680576 | bytes 34603008 | tf_op jit(solution)/shard_map/pallas_call | solution.py:421
  350.8 17.1 %collective-permute-done.74 = f32[896,256]{1,0:T(8,128)S(1)} collective-permute-done((f32[896,256]{1,0:T(8,128)}, f32[896,256]{1,0:T(8,128)S(1)}, u32[]{:S(2)}, u32[]{:S(2)}) %collective-permute-start.74) | collective-permute-done | bytes 917536 | tf_op jit(solution)/shard_map/ppermute | solution.py:612
  373.5 13.0 %collective-permute-done.72 = f32[896,256]{1,0:T(8,128)S(1)} collective-permute-done((f32[896,256]{1,0:T(8,128)}, f32[896,256]{1,0:T(8,128)S(1)}, u32[]{:S(2)}, u32[]{:S(2)}) %collective-permute-start.72) | collective-permute-done | bytes 917536 | tf_op jit(solution)/shard_map/ppermute | solution.py:612
  386.5 3.4 collective-permute-start.66
  392.1 12.7 %collective-permute-done.76.second_ref = f32[896,256]{1,0:T(8,128)S(1)} collective-permute-done((f32[896,256]{1,0:T(8,128)S(1)}, f32[896,256]{1,0:T(8,128)S(1)}, u32[]{:S(2)}, u32[]{:S(2)}) %collective-permute-start.76) | collective-permute-done | bytes 917536 | tf_op jit(solution)/shard_map/ppermute | solution.py:628
  406.3 13.4 %grad.6 = (f32[896,256]{1,0:T(8,128)}, f32[896,256]{1,0:T(8,128)}, f32[896,256]{1,0:T(8,128)}, f32[896,256]{1,0:T(8,128)}, f32[896,256]{1,0:T(8,128)}, /*index=5...) custom-call(s32[3]{0:T(128)} %pad_add_fusion.pos_ref, bf16[1792,1024]{1,0:T(8,128)(2,1)} %get-tuple-element.97.refs_0_, ...), custom_call_target="tpu_custom_call" | custom-call | flops 375809632 | bytes 8388608 | tf_op jit(solution)/shard_map/grad/pallas_call | solution.py:534
  422.5 3.3 collective-permute-done.66
  434.3 13.0 %grad.7 = (f32[640,256]{1,0:T(8,128)}, f32[640,256]{1,0:T(8,128)}, f32[640,256]{1,0:T(8,128)}, f32[640,256]{1,0:T(8,128)}, f32[640,256]{1,0:T(8,128)}, /*index=5...) custom-call(s32[3]{0:T(128)} %pad_add_fusion.pos_ref, bf16[256,1024]{1,0:T(8,128)(2,1)} %copy-done.17, ...), custom_call_target="tpu_custom_call" | custom-call | flops 268435456 | bytes 8388608 | tf_op jit(solution)/shard_map/grad/pallas_call | solution.py:534
  451.6 14.5 %collective-permute-done.53 = f32[896,256]{1,0:T(8,128)} collective-permute-done((f32[896,256]{1,0:T(8,128)}, f32[896,256]{1,0:T(8,128)}, u32[]{:S(2)}, u32[]{:S(2)}) %collective-permute-start.53) | collective-permute-done | bytes 917536 | tf_op jit(solution)/shard_map/ppermute | solution.py:612
  467.5 18.3 %collective-permute-done.65 = f32[896,256]{1,0:T(8,128)} collective-permute-done((f32[896,256]{1,0:T(8,128)}, f32[896,256]{1,0:T(8,128)}, u32[]{:S(2)}, u32[]{:S(2)}) %collective-permute-start.65) | collective-permute-done | bytes 917536 | tf_op jit(solution)/shard_map/ppermute | solution.py:612
  486.0 13.8 %collective-permute-done.57 = f32[640,256]{1,0:T(8,128)S(1)} collective-permute-done((f32[640,256]{1,0:T(8,128)}, f32[640,256]{1,0:T(8,128)S(1)}, u32[]{:S(2)}, u32[]{:S(2)}) %collective-permute-start.57) | collective-permute-done | bytes 655392 | tf_op jit(solution)/shard_map/ppermute | solution.py:612
  507.4 12.1 %collective-permute-done.50 = f32[896,256]{1,0:T(8,128)S(1)} collective-permute-done((f32[896,256]{1,0:T(8,128)S(1)}, f32[896,256]{1,0:T(8,128)S(1)}, u32[]{:S(2)}, u32[]{:S(2)}) %collective-permute-start.50) | collective-permute-done | bytes 917536 | tf_op jit(solution)/shard_map/ppermute | solution.py:612
  526.0 9.9 %collective-permute-done.73.first_ref = f32[896,256]{1,0:T(8,128)S(1)} collective-permute-done((f32[896,256]{1,0:T(8,128)S(1)}, f32[896,256]{1,0:T(8,128)S(1)}, u32[]{:S(2)}, u32[]{:S(2)}) %collective-permute-start.73) | collective-permute-done | bytes 917536 | tf_op jit(solution)/shard_map/ppermute | solution.py:628
  537.8 4.1 collective-permute-start.70
  543.9 3.7 collective-permute-done.58
  549.5 3.5 shard_map.164
  555.5 5.2 collective-permute-start.60
  562.9 12.4 %collective-permute-done.67.first_ref = f32[896,256]{1,0:T(8,128)} collective-permute-done((f32[896,256]{1,0:T(8,128)}, f32[896,256]{1,0:T(8,128)}, u32[]{:S(2)}, u32[]{:S(2)}) %collective-permute-start.67) | collective-permute-done | bytes 917536 | tf_op jit(solution)/shard_map/ppermute | solution.py:628
  575.3 3.7 shard_map.163
  579.0 21.9 %collective-permute-done.56.second_ref = f32[896,256]{1,0:T(8,128)} collective-permute-done((f32[896,256]{1,0:T(8,128)}, f32[896,256]{1,0:T(8,128)}, u32[]{:S(2)}, u32[]{:S(2)}) %collective-permute-start.56) | collective-permute-done | bytes 917536 | tf_op jit(solution)/shard_map/ppermute | solution.py:628
  600.9 5.4 collective-permute-done.52.first_ref
  606.3 3.7 shard_map.162
  611.8 6.9 %reduce-scatter.3.cloned.1.call-done = f32[64,4096]{1,0:T(8,128)} async-done(((f32[1024,4096]{1,0:T(8,128)}), f32[64,4096]{1,0:T(8,128)}) %reduce-scatter.3.cloned.1.call-update) | async-done | bytes 1048592 | tf_op jit(solution)/shard_map/reduce_scatter | solution.py:741
  624.0 3.2 p_attn.1
  (312 shorter events, 135.3 us)
Async XLA Ops:
  7.2 120.1 %all-gather.3.cloned.1.call-start = ((), (), s32[]{:S(2)}) async-start(), calls=%async_computation.2 | async-start | bytes 8912896 | tf_op jit(solution)/shard_map/all_gather | solution.py:726
  12.5 28.8 %collective-permute-start.1 = (bf16[256,2176]{1,0:T(8,128)(2,1)}, bf16[256,2176]{1,0:T(8,128)(2,1)S(1)}, u32[]{:S(2)}, u32[]{:S(2)}) collective-permute-start(bf16[256,2176]{1,0:T(8,128)(2,1)} %get-tuple-element.146), channel_id=1, source_target_pairs={{0,8},{1,24},{8,0},{9,16},{16,9},{17,25},{24,1},{25,17},{2,10},{3,... | collective-permute-start | bytes 3342344 | tf_op jit(solution)/shard_map/ppermute | solution.py:628
  16.6 25.7 %collective-permute-start = (bf16[256,2176]{1,0:T(8,128)(2,1)}, bf16[256,2176]{1,0:T(8,128)(2,1)S(1)}, u32[]{:S(2)}, u32[]{:S(2)}) collective-permute-start(bf16[256,2176]{1,0:T(8,128)(2,1)} %get-tuple-element.147), channel_id=1, source_target_pairs={{0,0},{1,16},{8,8},{9,24},{16,1},{17,17},{24,9},{25,25},{2,2},{3,1... | collective-permute-start | bytes 3342344 | tf_op jit(solution)/shard_map/ppermute | solution.py:628
  42.3 169.5 %all-gather.5.cloned.1.call-start = ((), (), s32[]{:S(2)}) async-start(), calls=%async_computation.4 | async-start | bytes 8912896 | tf_op jit(solution)/shard_map/all_gather | solution.py:727
  43.0 567.0 %reduce-scatter.5.cloned.1.call-start = ((), (), s32[]{:S(2)}) async-start(), calls=%async_computation.5 | async-start | bytes 17825792 | tf_op jit(solution)/shard_map/reduce_scatter | solution.py:761
  47.7 29.9 %collective-permute-start.9 = (bf16[256,2176]{1,0:T(8,128)(2,1)S(1)}, bf16[256,2176]{1,0:T(8,128)(2,1)S(1)}, u32[]{:S(2)}, u32[]{:S(2)}) collective-permute-start(bf16[256,2176]{1,0:T(8,128)(2,1)S(1)} %collective-permute-done.1.refs_1_.refs_4_), channel_id=1, source_target_pairs={{0,32},{32,64},{64,96},{96,0},{1,33},{33,65},{65,97},{97,1},{2,34}... | collective-permute-start | bytes 3342344 | tf_op jit(solution)/shard_map/ppermute | solution.py:612
  49.4 28.3 %collective-permute-start.5 = (bf16[256,2176]{1,0:T(8,128)(2,1)S(1)}, bf16[256,2176]{1,0:T(8,128)(2,1)S(1)}, u32[]{:S(2)}, u32[]{:S(2)}) collective-permute-start(bf16[256,2176]{1,0:T(8,128)(2,1)S(1)} %collective-permute-done.1.refs_1_.refs_4_), channel_id=1, source_target_pairs={{0,96},{32,0},{64,32},{96,64},{1,97},{33,1},{65,33},{97,65},{2,98}... | collective-permute-start | bytes 3342344 | tf_op jit(solution)/shard_map/ppermute | solution.py:612
  51.5 26.7 %collective-permute-start.3 = (bf16[256,2176]{1,0:T(8,128)(2,1)S(1)}, bf16[256,2176]{1,0:T(8,128)(2,1)S(1)}, u32[]{:S(2)}, u32[]{:S(2)}) collective-permute-start(bf16[256,2176]{1,0:T(8,128)(2,1)S(1)} %collective-permute-done.1.refs_1_.refs_4_), channel_id=1, source_target_pairs={{0,1},{1,0},{2,3},{3,2},{4,5},{5,4},{6,7},{7,6},{8,9},{9,8},{10,11... | collective-permute-start | bytes 3342344 | tf_op jit(solution)/shard_map/ppermute | solution.py:616
  51.5 44.5 %collective-permute-start.8 = (bf16[256,2176]{1,0:T(8,128)(2,1)S(1)}, bf16[256,2176]{1,0:T(8,128)(2,1)S(1)}, u32[]{:S(2)}, u32[]{:S(2)}) collective-permute-start(bf16[256,2176]{1,0:T(8,128)(2,1)S(1)} %collective-permute-done.refs_0_.refs_3_), channel_id=1, source_target_pairs={{0,32},{32,64},{64,96},{96,0},{1,33},{33,65},{65,97},{97,1},{2,34}... | collective-permute-start | bytes 3342344 | tf_op jit(solution)/shard_map/ppermute | solution.py:612
  74.3 27.7 %collective-permute-start.4 = (bf16[256,2176]{1,0:T(8,128)(2,1)S(1)}, bf16[256,2176]{1,0:T(8,128)(2,1)S(1)}, u32[]{:S(2)}, u32[]{:S(2)}) collective-permute-start(bf16[256,2176]{1,0:T(8,128)(2,1)S(1)} %collective-permute-done.refs_0_.refs_3_), channel_id=1, source_target_pairs={{0,96},{32,0},{64,32},{96,64},{1,97},{33,1},{65,33},{97,65},{2,98}... | collective-permute-start | bytes 3342344 | tf_op jit(solution)/shard_map/ppermute | solution.py:612
  78.2 41.3 %collective-permute-start.13 = (bf16[256,2176]{1,0:T(8,128)(2,1)S(1)}, bf16[256,2176]{1,0:T(8,128)(2,1)S(1)}, u32[]{:S(2)}, u32[]{:S(2)}) collective-permute-start(bf16[256,2176]{1,0:T(8,128)(2,1)S(1)} %collective-permute-done.5.refs_5_.refs_8_), channel_id=1, source_target_pairs={{0,96},{32,0},{64,32},{96,64},{1,97},{33,1},{65,33},{97,65},{2,98}... | collective-permute-start | bytes 3342344 | tf_op jit(solution)/shard_map/ppermute | solution.py:612
  120.0 36.4 %collective-permute-start.33 = (bf16[256,1152]{1,0:T(8,128)(2,1)}, bf16[256,1152]{1,0:T(8,128)(2,1)}, u32[]{:S(2)}, u32[]{:S(2)}) collective-permute-start(bf16[256,1152]{1,0:T(8,128)(2,1)} %collective-permute-done.21.refs_4_.refs_1_), channel_id=1, source_target_pairs={{0,32},{32,64},{64,96},{96,0},{1,33},{33,65},{65,97},{97,1},{2,34}... | collective-permute-start | bytes 1769480 | tf_op jit(solution)/shard_map/ppermute | solution.py:612
  121.7 37.4 %collective-permute-start.25 = (bf16[256,1152]{1,0:T(8,128)(2,1)}, bf16[256,1152]{1,0:T(8,128)(2,1)}, u32[]{:S(2)}, u32[]{:S(2)}) collective-permute-start(bf16[256,1152]{1,0:T(8,128)(2,1)} %collective-permute-done.21.refs_4_.refs_1_), channel_id=1, source_target_pairs={{0,96},{32,0},{64,32},{96,64},{1,97},{33,1},{65,33},{97,65},{2,98}... | collective-permute-start | bytes 1769480 | tf_op jit(solution)/shard_map/ppermute | solution.py:612
  124.2 36.1 %collective-permute-start.23 = (bf16[256,1152]{1,0:T(8,128)(2,1)}, bf16[256,1152]{1,0:T(8,128)(2,1)}, u32[]{:S(2)}, u32[]{:S(2)}) collective-permute-start(bf16[256,1152]{1,0:T(8,128)(2,1)} %collective-permute-done.21.refs_4_.refs_1_), channel_id=1, source_target_pairs={{0,1},{1,0},{2,3},{3,2},{4,5},{5,4},{6,7},{7,6},{8,9},{9,8},{10,11... | collective-permute-start | bytes 1769480 | tf_op jit(solution)/shard_map/ppermute | solution.py:616
  126.5 34.5 %collective-permute-start.28 = (bf16[256,1152]{1,0:T(8,128)(2,1)}, bf16[256,1152]{1,0:T(8,128)(2,1)}, u32[]{:S(2)}, u32[]{:S(2)}) collective-permute-start(bf16[256,1152]{1,0:T(8,128)(2,1)} %collective-permute-done.20.refs_3_.refs_0_), channel_id=1, source_target_pairs={{0,32},{32,64},{64,96},{96,0},{1,33},{33,65},{65,97},{97,1},{2,34}... | collective-permute-start | bytes 1769480 | tf_op jit(solution)/shard_map/ppermute | solution.py:612
  156.4 31.0 %collective-permute-start.24 = (bf16[256,1152]{1,0:T(8,128)(2,1)}, bf16[256,1152]{1,0:T(8,128)(2,1)}, u32[]{:S(2)}, u32[]{:S(2)}) collective-permute-start(bf16[256,1152]{1,0:T(8,128)(2,1)} %collective-permute-done.20.refs_3_.refs_0_), channel_id=1, source_target_pairs={{0,96},{32,0},{64,32},{96,64},{1,97},{33,1},{65,33},{97,65},{2,98}... | collective-permute-start | bytes 1769480 | tf_op jit(solution)/shard_map/ppermute | solution.py:612
  161.0 27.4 %collective-permute-start.22 = (bf16[256,1152]{1,0:T(8,128)(2,1)}, bf16[256,1152]{1,0:T(8,128)(2,1)}, u32[]{:S(2)}, u32[]{:S(2)}) collective-permute-start(bf16[256,1152]{1,0:T(8,128)(2,1)} %collective-permute-done.20.refs_3_.refs_0_), channel_id=1, source_target_pairs={{0,1},{1,0},{2,3},{3,2},{4,5},{5,4},{6,7},{7,6},{8,9},{9,8},{10,11... | collective-permute-start | bytes 1769480 | tf_op jit(solution)/shard_map/ppermute | solution.py:616
  220.6 74.8 %collective-permute-start.42 = (bf16[1024,2048]{1,0:T(8,128)(2,1)}, bf16[1024,2048]{1,0:T(8,128)(2,1)}, u32[]{:S(2)}, u32[]{:S(2)}) collective-permute-start(bf16[1024,2048]{1,0:T(8,128)(2,1)} %shard_map.157), channel_id=1, source_target_pairs={{0,1},{1,0},{2,3},{3,2},{4,5},{5,4},{6,7},{7,6},{8,9},{9,8},{10,11... | collective-permute-start | bytes 12582920 | tf_op jit(solution)/shard_map/ppermute | solution.py:616
  267.4 28.0 %collective-permute-start.41 = (bf16[1792,1024]{1,0:T(8,128)(2,1)}, bf16[1792,1024]{1,0:T(8,128)(2,1)}, u32[]{:S(2)}, u32[]{:S(2)}) collective-permute-start(bf16[1792,1024]{1,0:T(8,128)(2,1)} %get-tuple-element.97.refs_0_), channel_id=1, source_target_pairs={{0,1},{1,0},{2,3},{3,2},{4,5},{5,4},{6,7},{7,6},{8,9},{9,8},{10,11... | collective-permute-start | bytes 11010056 | tf_op jit(solution)/shard_map/ppermute | solution.py:616
  344.1 274.6 %reduce-scatter.3.cloned.1.call-start = ((), (), s32[]{:S(2)}) async-start(), calls=%async_computation.3 | async-start | bytes 17825792 | tf_op jit(solution)/shard_map/reduce_scatter | solution.py:741
  347.6 38.9 %collective-permute-start.72 = (f32[896,256]{1,0:T(8,128)}, f32[896,256]{1,0:T(8,128)S(1)}, u32[]{:S(2)}, u32[]{:S(2)}) collective-permute-start(f32[896,256]{1,0:T(8,128)} %get-tuple-element.143), channel_id=1, source_target_pairs={{0,96},{32,0},{64,32},{96,64},{1,97},{33,1},{65,33},{97,65},{2,98}... | collective-permute-start | bytes 2752520 | tf_op jit(solution)/shard_map/ppermute | solution.py:612
  347.6 42.2 %collective-permute-start.71 = (f32[896,256]{1,0:T(8,128)}, f32[896,256]{1,0:T(8,128)S(1)}, u32[]{:S(2)}, u32[]{:S(2)}) collective-permute-start(f32[896,256]{1,0:T(8,128)} %add.114), channel_id=1, source_target_pairs={{0,32},{32,64},{64,96},{96,0},{1,33},{33,65},{65,97},{97,1},{2,34}... | collective-permute-start | bytes 2752520 | tf_op jit(solution)/shard_map/ppermute | solution.py:612
  370.6 34.2 %collective-permute-start.76 = (f32[896,256]{1,0:T(8,128)S(1)}, f32[896,256]{1,0:T(8,128)S(1)}, u32[]{:S(2)}, u32[]{:S(2)}) collective-permute-start(f32[896,256]{1,0:T(8,128)S(1)} %add_add_fusion.1), channel_id=1, source_target_pairs={{0,8},{1,24},{8,0},{9,16},{16,9},{17,25},{24,1},{25,17},{2,10},{3,... | collective-permute-start | bytes 2752520 | tf_op jit(solution)/shard_map/ppermute | solution.py:628
  370.7 49.0 %collective-permute-start.46 = (f32[896,256]{1,0:T(8,128)}, f32[896,256]{1,0:T(8,128)}, u32[]{:S(2)}, u32[]{:S(2)}) collective-permute-start(f32[896,256]{1,0:T(8,128)} %get-tuple-element.117), channel_id=1, source_target_pairs={{0,32},{32,64},{64,96},{96,0},{1,33},{33,65},{65,97},{97,1},{2,34}... | collective-permute-start | bytes 2752520 | tf_op jit(solution)/shard_map/ppermute | solution.py:612
  370.8 49.0 %collective-permute-start.47 = (f32[896,256]{1,0:T(8,128)}, f32[896,256]{1,0:T(8,128)}, u32[]{:S(2)}, u32[]{:S(2)}) collective-permute-start(f32[896,256]{1,0:T(8,128)} %get-tuple-element.120), channel_id=1, source_target_pairs={{0,96},{32,0},{64,32},{96,64},{1,97},{33,1},{65,33},{97,65},{2,98}... | collective-permute-start | bytes 2752520 | tf_op jit(solution)/shard_map/ppermute | solution.py:612
  386.5 39.3 %collective-permute-start.66 = (f32[896,256]{1,0:T(8,128)}, f32[896,256]{1,0:T(8,128)}, u32[]{:S(2)}, u32[]{:S(2)}) collective-permute-start(f32[896,256]{1,0:T(8,128)} %get-tuple-element.139), channel_id=1, source_target_pairs={{0,96},{32,0},{64,32},{96,64},{1,97},{33,1},{65,33},{97,65},{2,98}... | collective-permute-start | bytes 2752520 | tf_op jit(solution)/shard_map/ppermute | solution.py:612
  390.8 37.5 %collective-permute-start.68 = (f32[896,256]{1,0:T(8,128)}, f32[896,256]{1,0:T(8,128)}, u32[]{:S(2)}, u32[]{:S(2)}) collective-permute-start(f32[896,256]{1,0:T(8,128)} %get-tuple-element.141), channel_id=1, source_target_pairs={{0,32},{32,64},{64,96},{96,0},{1,33},{33,65},{65,97},{97,1},{2,34}... | collective-permute-start | bytes 2752520 | tf_op jit(solution)/shard_map/ppermute | solution.py:612
  405.8 26.7 %collective-permute-start.49 = (bf16[384,1024]{1,0:T(8,128)(2,1)}, bf16[384,1024]{1,0:T(8,128)(2,1)}, u32[]{:S(2)}, u32[]{:S(2)}) collective-permute-start(bf16[384,1024]{1,0:T(8,128)(2,1)} %maximum_bitcast_fusion.refs_4_), channel_id=1, source_target_pairs={{0,1},{1,0},{2,3},{3,2},{4,5},{5,4},{6,7},{7,6},{8,9},{9,8},{10,11... | collective-permute-start | bytes 2359304 | tf_op jit(solution)/shard_map/ppermute | solution.py:616
  419.7 27.5 %collective-permute-start.45 = (f32[896,256]{1,0:T(8,128)}, f32[896,256]{1,0:T(8,128)}, u32[]{:S(2)}, u32[]{:S(2)}) collective-permute-start(f32[896,256]{1,0:T(8,128)} %get-tuple-element.115), channel_id=1, source_target_pairs={{0,32},{32,64},{64,96},{96,0},{1,33},{33,65},{65,97},{97,1},{2,34}... | collective-permute-start | bytes 2752520 | tf_op jit(solution)/shard_map/ppermute | solution.py:612
  419.8 28.4 %collective-permute-start.54 = (f32[896,256]{1,0:T(8,128)}, f32[896,256]{1,0:T(8,128)}, u32[]{:S(2)}, u32[]{:S(2)}) collective-permute-start(f32[896,256]{1,0:T(8,128)} %get-tuple-element.128), channel_id=1, source_target_pairs={{0,96},{32,0},{64,32},{96,64},{1,97},{33,1},{65,33},{97,65},{2,98}... | collective-permute-start | bytes 2752520 | tf_op jit(solution)/shard_map/ppermute | solution.py:612
  425.8 40.3 %collective-permute-start.53 = (f32[896,256]{1,0:T(8,128)}, f32[896,256]{1,0:T(8,128)}, u32[]{:S(2)}, u32[]{:S(2)}) collective-permute-start(f32[896,256]{1,0:T(8,128)} %get-tuple-element.126), channel_id=1, source_target_pairs={{0,32},{32,64},{64,96},{96,0},{1,33},{33,65},{65,97},{97,1},{2,34}... | collective-permute-start | bytes 2752520 | tf_op jit(solution)/shard_map/ppermute | solution.py:612
  428.3 57.5 %collective-permute-start.65 = (f32[896,256]{1,0:T(8,128)}, f32[896,256]{1,0:T(8,128)}, u32[]{:S(2)}, u32[]{:S(2)}) collective-permute-start(f32[896,256]{1,0:T(8,128)} %add.117), channel_id=1, source_target_pairs={{0,32},{32,64},{64,96},{96,0},{1,33},{33,65},{65,97},{97,1},{2,34}... | collective-permute-start | bytes 2752520 | tf_op jit(solution)/shard_map/ppermute | solution.py:612
  432.5 69.6 %collective-permute-start.69 = (f32[896,256]{1,0:T(8,128)}, f32[896,256]{1,0:T(8,128)}, u32[]{:S(2)}, u32[]{:S(2)}) collective-permute-start(f32[896,256]{1,0:T(8,128)} %add.118), channel_id=1, source_target_pairs={{0,96},{32,0},{64,32},{96,64},{1,97},{33,1},{65,33},{97,65},{2,98}... | collective-permute-start | bytes 2752520 | tf_op jit(solution)/shard_map/ppermute | solution.py:612
  447.2 52.6 %collective-permute-start.57 = (f32[640,256]{1,0:T(8,128)}, f32[640,256]{1,0:T(8,128)S(1)}, u32[]{:S(2)}, u32[]{:S(2)}) collective-permute-start(f32[640,256]{1,0:T(8,128)} %get-tuple-element.131), channel_id=1, source_target_pairs={{0,32},{32,64},{64,96},{96,0},{1,33},{33,65},{65,97},{97,1},{2,34}... | collective-permute-start | bytes 1966088 | tf_op jit(solution)/shard_map/ppermute | solution.py:612
  448.2 53.7 %collective-permute-start.62 = (f32[640,256]{1,0:T(8,128)}, f32[640,256]{1,0:T(8,128)S(1)}, u32[]{:S(2)}, u32[]{:S(2)}) collective-permute-start(f32[640,256]{1,0:T(8,128)} %get-tuple-element.136), channel_id=1, source_target_pairs={{0,96},{32,0},{64,32},{96,64},{1,97},{33,1},{65,33},{97,65},{2,98}... | collective-permute-start | bytes 1966088 | tf_op jit(solution)/shard_map/ppermute | solution.py:612
  466.1 38.8 %collective-permute-start.55 = (f32[896,256]{1,0:T(8,128)S(1)}, f32[896,256]{1,0:T(8,128)S(1)}, u32[]{:S(2)}, u32[]{:S(2)}) collective-permute-start(f32[896,256]{1,0:T(8,128)S(1)} %add.123), channel_id=1, source_target_pairs={{0,96},{32,0},{64,32},{96,64},{1,97},{33,1},{65,33},{97,65},{2,98}... | collective-permute-start | bytes 2752520 | tf_op jit(solution)/shard_map/ppermute | solution.py:612
  485.8 33.7 %collective-permute-start.50 = (f32[896,256]{1,0:T(8,128)S(1)}, f32[896,256]{1,0:T(8,128)S(1)}, u32[]{:S(2)}, u32[]{:S(2)}) collective-permute-start(f32[896,256]{1,0:T(8,128)S(1)} %add.119), channel_id=1, source_target_pairs={{0,32},{32,64},{64,96},{96,0},{1,33},{33,65},{65,97},{97,1},{2,34}... | collective-permute-start | bytes 2752520 | tf_op jit(solution)/shard_map/ppermute | solution.py:612
  499.8 36.0 %collective-permute-start.73 = (f32[896,256]{1,0:T(8,128)S(1)}, f32[896,256]{1,0:T(8,128)S(1)}, u32[]{:S(2)}, u32[]{:S(2)}) collective-permute-start(f32[896,256]{1,0:T(8,128)S(1)} %add_add_fusion.2), channel_id=1, source_target_pairs={{0,0},{1,16},{8,8},{9,24},{16,1},{17,17},{24,9},{25,25},{2,2},{3,1... | collective-permute-start | bytes 2752520 | tf_op jit(solution)/shard_map/ppermute | solution.py:628
  502.0 33.9 %collective-permute-start.51 = (f32[896,256]{1,0:T(8,128)S(1)}, f32[896,256]{1,0:T(8,128)S(1)}, u32[]{:S(2)}, u32[]{:S(2)}) collective-permute-start(f32[896,256]{1,0:T(8,128)S(1)} %copy-done.55), channel_id=1, source_target_pairs={{0,96},{32,0},{64,32},{96,64},{1,97},{33,1},{65,33},{97,65},{2,98}... | collective-permute-start | bytes 2752520 | tf_op jit(solution)/shard_map/ppermute | solution.py:612
  502.1 35.7 %collective-permute-start.59 = (f32[640,256]{1,0:T(8,128)S(1)}, f32[640,256]{1,0:T(8,128)S(1)}, u32[]{:S(2)}, u32[]{:S(2)}) collective-permute-start(f32[640,256]{1,0:T(8,128)S(1)} %copy-done.57), channel_id=1, source_target_pairs={{0,96},{32,0},{64,32},{96,64},{1,97},{33,1},{65,33},{97,65},{2,98}... | collective-permute-start | bytes 1966088 | tf_op jit(solution)/shard_map/ppermute | solution.py:612
  506.0 37.1 %collective-permute-start.61 = (f32[640,256]{1,0:T(8,128)S(1)}, f32[640,256]{1,0:T(8,128)S(1)}, u32[]{:S(2)}, u32[]{:S(2)}) collective-permute-start(f32[640,256]{1,0:T(8,128)S(1)} %copy-done.56), channel_id=1, source_target_pairs={{0,32},{32,64},{64,96},{96,0},{1,33},{33,65},{65,97},{97,1},{2,34}... | collective-permute-start | bytes 1966088 | tf_op jit(solution)/shard_map/ppermute | solution.py:612
  519.5 28.1 %collective-permute-start.58 = (f32[640,256]{1,0:T(8,128)S(1)}, f32[640,256]{1,0:T(8,128)}, u32[]{:S(2)}, u32[]{:S(2)}) collective-permute-start(f32[640,256]{1,0:T(8,128)S(1)} %add.125), channel_id=1, source_target_pairs={{0,32},{32,64},{64,96},{96,0},{1,33},{33,65},{65,97},{97,1},{2,34}... | collective-permute-start | bytes 1966088 | tf_op jit(solution)/shard_map/ppermute | solution.py:612
  535.9 39.4 %collective-permute-start.67 = (f32[896,256]{1,0:T(8,128)}, f32[896,256]{1,0:T(8,128)}, u32[]{:S(2)}, u32[]{:S(2)}) collective-permute-start(f32[896,256]{1,0:T(8,128)} %add_add_fusion.4), channel_id=1, source_target_pairs={{0,0},{1,16},{8,8},{9,24},{16,1},{17,17},{24,9},{25,25},{2,2},{3,1... | collective-permute-start | bytes 2752520 | tf_op jit(solution)/shard_map/ppermute | solution.py:628
  537.8 37.4 %collective-permute-start.70 = (f32[896,256]{1,0:T(8,128)}, f32[896,256]{1,0:T(8,128)}, u32[]{:S(2)}, u32[]{:S(2)}) collective-permute-start(f32[896,256]{1,0:T(8,128)} %add_add_fusion.3), channel_id=1, source_target_pairs={{0,8},{1,24},{8,0},{9,16},{16,9},{17,25},{24,1},{25,17},{2,10},{3,... | collective-permute-start | bytes 2752520 | tf_op jit(solution)/shard_map/ppermute | solution.py:628
  543.9 57.0 %collective-permute-start.56 = (f32[896,256]{1,0:T(8,128)}, f32[896,256]{1,0:T(8,128)}, u32[]{:S(2)}, u32[]{:S(2)}) collective-permute-start(f32[896,256]{1,0:T(8,128)} %add_add_fusion.5), channel_id=1, source_target_pairs={{0,8},{1,24},{8,0},{9,16},{16,9},{17,25},{24,1},{25,17},{2,10},{3,... | collective-permute-start | bytes 2752520 | tf_op jit(solution)/shard_map/ppermute | solution.py:628
  547.6 58.7 %collective-permute-start.52 = (f32[896,256]{1,0:T(8,128)}, f32[896,256]{1,0:T(8,128)}, u32[]{:S(2)}, u32[]{:S(2)}) collective-permute-start(f32[896,256]{1,0:T(8,128)} %add_add_fusion.6), channel_id=1, source_target_pairs={{0,0},{1,16},{8,8},{9,24},{16,1},{17,17},{24,9},{25,25},{2,2},{3,1... | collective-permute-start | bytes 2752520 | tf_op jit(solution)/shard_map/ppermute | solution.py:628
  555.5 68.5 %collective-permute-start.60 = (f32[640,256]{1,0:T(8,128)}, f32[640,256]{1,0:T(8,128)}, u32[]{:S(2)}, u32[]{:S(2)}) collective-permute-start(f32[640,256]{1,0:T(8,128)} %add_add_fusion.8), channel_id=1, source_target_pairs={{0,0},{1,16},{8,8},{9,24},{16,1},{17,17},{24,9},{25,25},{2,2},{3,1... | collective-permute-start | bytes 1966088 | tf_op jit(solution)/shard_map/ppermute | solution.py:628
  575.3 48.7 %collective-permute-start.64 = (f32[640,256]{1,0:T(8,128)}, f32[640,256]{1,0:T(8,128)}, u32[]{:S(2)}, u32[]{:S(2)}) collective-permute-start(f32[640,256]{1,0:T(8,128)} %add_add_fusion.7), channel_id=1, source_target_pairs={{0,8},{1,24},{8,0},{9,16},{16,9},{17,25},{24,1},{25,17},{2,10},{3,... | collective-permute-start | bytes 1966088 | tf_op jit(solution)/shard_map/ppermute | solution.py:628
  (95 other events, 1295.4 us)
Sparse Core Ops, SparseCore 0:
  42.4 76.8 all-gather.2
  121.5 74.7 all-gather.4
  344.2 116.0 reduce-scatter.4
  463.6 155.0 reduce-scatter.2

commit v5 on v4

--- a/solution.py
+++ b/solution.py
@@ -348,7 +348,7 @@
     )(pos, acts, *halves)
 
 
-def nt_kernel(keys, sides, pos_ref, *refs):
+def nt_kernel(keys, sides, first_row, pos_ref, *refs):
     count_left = len(sides)
     count = len(keys)
     lefts = refs[:count_left]
@@ -360,9 +360,10 @@
     left_copies = []
     start = 0
     for idx, (left, side) in enumerate(zip(lefts, sides)):
-        rows, width = left.shape
-        first = 0 if side is None else pl.multiple_of((1 - pos_ref[1] if side else pos_ref[1]) * rows, rows)
-        left_copies.append(pltpu.make_async_copy(left, left_buf.at[pl.ds(first, rows), pl.ds(start, width)], left_sem.at[idx]))
+        chunks, _, width = left.shape
+        first = 0 if side is None else (1 - pos_ref[1] if side else pos_ref[1]) * chunks
+        source = left.at[:, pl.ds(first_row, left_buf.shape[1]), :]
+        left_copies.append(pltpu.make_async_copy(source, left_buf.at[pl.ds(first, chunks), :, pl.ds(start, width)], left_sem.at[idx]))
         left_copies[-1].start()
         start += 0 if side == 0 else width
 
@@ -401,32 +402,34 @@
         def _():
             out_copy(step - 2).wait()
 
-        out_buf[lax.rem(step, 2)] = dot_nt(left_buf[...], w_buf[slot])
+        out_buf[lax.rem(step, 2)] = dot_nt(left_buf[...].reshape(out_buf.shape[1], left_buf.shape[2]), w_buf[slot])
         out_copy(step).start()
 
     for idx in range(count - 2, count):
         out_copy(idx).wait()
 
 
-def nt_pieces(pos, lefts, parts):
+def nt_pieces(pos, lefts, parts, chunk, first_row, rows):
     sides = (None, 0, 1)
     keys = [(step, other) for step in range(NZ) for other in range(2)]
     halves = [parts[step][other][part] for step, other in keys for part in range(2)]
-    tokens = lefts[0].shape[0]
+    lefts = [left.reshape(-1, chunk, left.shape[1]) for left in lefts]
+    chunks = lefts[0].shape[0]
+    tokens = chunks * rows
     block = 2 * halves[0].shape[0]
     depth = block * len(keys)
     width = halves[0].shape[1]
     slots = 3
     anywhere = pl.BlockSpec(memory_space=pl.ANY)
     return pl.pallas_call(
-        functools.partial(nt_kernel, keys, sides),
+        functools.partial(nt_kernel, keys, sides, first_row),
         grid_spec=pltpu.PrefetchScalarGridSpec(
             num_scalar_prefetch=1,
             grid=(1,),
             in_specs=[anywhere] * (len(lefts) + len(halves)),
             out_specs=anywhere,
             scratch_shapes=[
-                pltpu.VMEM((tokens, width), BF16),
+                pltpu.VMEM((chunks, rows, width), BF16),
                 pltpu.VMEM((slots, block, width), BF16),
                 pltpu.VMEM((2, tokens, block), F32),
                 pltpu.SemaphoreType.DMA((len(lefts),)),
@@ -660,6 +663,7 @@
         even_y = y_pos % 2 == 0
         first_c = c_pos == 0
         pos = jnp.stack([z_pos, c_pos, y_pos % 2]).astype(jnp.int32)
+        chunk = x_in.shape[1]
         head = 2 * rope_cos.shape[1]
         seq = rope_cos.shape[0]
         ff_blk = w_gate.shape[1] // 2
@@ -735,17 +739,17 @@
         third_other = swap_yc(my_rows(third, False))
         act_val, act_t = act_fwd(after(gate_up, qkv_tok))
         act_recv = swap_c(act_t)
-        qkv_seq, attn_own, attn_other = attn_fwd(after(pos, act_t), qkv_tok, qkv_other, third_own, third_other, cos_tab, sin_tab)
+        h_picked = pick_cols(after(pos, act_t), h_all)
+        h_recv = swap_c(h_picked)
+        qkv_seq, attn_own, attn_other = attn_fwd(after(pos, h_picked), qkv_tok, qkv_other, third_own, third_other, cos_tab, sin_tab)
         attn_got = swap_c(attn_other)
-        y_part = nt_pieces(after(pos, attn_own), [act_val, attn_own, attn_got], ws_parts)
+        y_part = nt_pieces(after(pos, attn_own), [act_val, attn_own, attn_got], ws_parts, chunk, 0, chunk)
         mix_sum = lax.psum_scatter(y_part, ("y", "x"), scatter_dimension=0, tiled=True)
         y_out = (x_rows + mix_sum).astype(BF16)[None]
 
         dy_picked = pick_cols(after(pos, y_part), dy_all)
         dy_recv = swap_c(dy_picked)
-        h_picked = pick_cols(after(pos, dy_picked), h_all)
-        h_recv = swap_c(h_picked)
-        g_act = grad_start([(act_t, act_recv, dy_all, dy_recv, ff_blk, 0)], h_picked)
+        g_act = grad_start([(act_t, act_recv, dy_all, dy_recv, ff_blk, 0)], dy_picked)
         d_act, d_attn = nn_pieces(after(pos, g_act[3][0]), dy_all, ws_parts, (ff_blk, o_blk), 256)
         d_attn_other = swap_c(my_rows(d_attn, False))
         d_gate_up, d_gate_up_t = act_bwd(gate_up, d_act)
@@ -754,21 +758,24 @@
         got = swap_y(send)
         g_act = grad_pass(g_act, d_queries)
         g_gate = grad_start([(d_gate_up_t, d_gate_up_recv, h_all, h_recv, ff_blk, 0)], *g_act[3])
-        b_act = grad_back(g_act, g_gate[3][0])
         d_own, d_other = attn_post(after(pos, g_gate[3][0]), d_queries, keep, got, cos_tab, sin_tab)
         d_got = swap_c(d_other)
-        dh_part = nt_pieces(pos, [d_gate_up, d_own, d_got], wf_parts)
-        d_h = lax.psum_scatter(dh_part, ("y", "x"), scatter_dimension=0, tiled=True)
-        d_h = d_h.astype(BF16)
+        half = chunk // 2
+        dh_low = nt_pieces(pos, [d_gate_up, d_own, d_got], wf_parts, chunk, 0, half)
+        d_h_low = lax.psum_scatter(dh_low, ("y", "x"), scatter_dimension=0, tiled=True)
+        g_gate = grad_pass(g_gate, dh_low)
+        g_up = grad_start([(d_gate_up_t, d_gate_up_recv, h_all, h_recv, ff_blk, 1)], *g_gate[3])
+        dh_high = nt_pieces(after(pos, g_up[3][0]), [d_gate_up, d_own, d_got], wf_parts, chunk, half, half)
+        d_h_high = lax.psum_scatter(dh_high, ("y", "x"), scatter_dimension=0, tiled=True)
+        b_act = grad_back(g_act, dh_high)
+        d_h = jnp.concatenate([d_h_low, d_h_high], axis=0).astype(BF16)
         dx_out = (dy_in[0].astype(F32) + norm_pull(d_h.astype(F32))[0]).astype(BF16)[None]
-        g_up = grad_start([(d_gate_up_t, d_gate_up_recv, h_all, h_recv, ff_blk, 1)], dh_part)
-        g_gate = grad_pass(g_gate, dh_part)
 
         attn_t = both_rows(attn_own, attn_got).T
         d_qkv_t = both_rows(d_own, d_got).T
         attn_recv = swap_c(attn_t)
         d_qkv_recv = swap_c(d_qkv_t)
-        g_attn = grad_start([(attn_t, attn_recv, dy_all, dy_recv, o_blk, 0), (d_qkv_t, d_qkv_recv, h_all, h_recv, qkv_blk, 0)], *g_gate[3])
+        g_attn = grad_start([(attn_t, attn_recv, dy_all, dy_recv, o_blk, 0), (d_qkv_t, d_qkv_recv, h_all, h_recv, qkv_blk, 0)], dh_high)
         g_up = grad_pass(g_up, g_attn[3][0])
         g_attn = grad_pass(g_attn)
         b_gate = grad_back(g_gate)

time: 644 us -> 690 us (1.071)
  waiting for transfers between devices: 273 us -> 298 us
  starting transfers between devices: 90.2 us -> 112 us
    ppermute x36, waiting for transfers between devices: 143 us -> 166 us  [hop_z(): return lax.ppermute(val, 'z', ring(step, NZ))]
    ppermute x12, waiting for transfers between devices: 105 us -> 89.6 us  [turn(): return lax.ppermute(val, ('y', 'c'), pairs)]
    reduce_scatter x1, waiting for transfers between devices: 6.92 us -> 20.4 us  [layer(): lax.psum_scatter(y_part, ('y', 'x'), scatter_dimension=0, tiled=True)]
    ppermute x12, starting transfers between devices: 27 us -> 40.2 us  [turn(): return lax.ppermute(val, ('y', 'c'), pairs)]
    pallas_call x2 -> x3, Pallas kernels: 43.7 us -> 48 us  [nt_pieces(): pl.pallas_call(functools.partial(nt_kernel, keys, sides, first_row), grid...]
  transfers between devices with their start and end apart: 81 -> 82, of which waited for: 31 -> 35; matrix products, arithmetic and copies ran while one was open for 7% -> 6% of each run, Pallas kernels for 24% -> 25%
where the time goes in v5:
time: 690 us; the launch traced here: 681 us
  waiting for transfers between devices  298 us (43%)
  Pallas kernels  197 us (29%)
  starting transfers between devices  112 us (16%)
  other arithmetic  36.9 us (5%)
  local copies, waits for them, and re-layouts  22.5 us (3%)
  between operations  15.2 us (2%)
    ppermute x36, waiting for transfers between devices, hop_z(): return lax.ppermute(val, 'z', ring(step, NZ))  166 us
    ppermute x12, waiting for transfers between devices, turn(): return lax.ppermute(val, ('y', 'c'), pairs)  89.6 us
    pallas_call x4, Pallas kernels, grad_pieces(): pl.pallas_call(functools.partial(grad_kernel, heights), grid_spec=pltpu.P...  52.7 us
    pallas_call x3, Pallas kernels, nt_pieces(): pl.pallas_call(functools.partial(nt_kernel, keys, sides, first_row), grid...  48 us
    ppermute x36, starting transfers between devices, hop_z(): return lax.ppermute(val, 'z', ring(step, NZ))  46.1 us
    pallas_call x2, Pallas kernels, nn_pieces(): pl.pallas_call(functools.partial(nn_kernel, keys, 2, len(widths), tile),...  44.7 us
    ppermute x12, starting transfers between devices, turn(): return lax.ppermute(val, ('y', 'c'), pairs)  40.2 us
    ppermute x26, starting transfers between devices, swap_c(): return lax.ppermute(val, 'c', [(0, 1), (1, 0)])  22.3 us
  transfers between devices with their start and end apart: 82, of which 35 were waited for; matrix products, arithmetic and copies ran while one was open for 6% of the time, Pallas kernels for 25%

profile of v5, /device:TPU:1, one launch (start us, length us, event | category | flops | bytes accessed | tf_op | source)
XLA Modules:
  0.0 680.5 jit_solution(15084299393427334783)
XLA Ops:
  12.5 4.1 collective-permute-start.1
  22.4 18.9 %collective-permute-done.1.refs_1_.refs_4_ = bf16[256,2176]{1,0:T(8,128)(2,1)S(1)} collective-permute-done((bf16[256,2176]{1,0:T(8,128)(2,1)}, bf16[256,2176]{1,0:T(8,128)(2,1)S(1)}, u32[]{:S(2)}, u32[]{:S(2)}) %collective-permute-start.1) | collective-permute-done | bytes 1114144 | tf_op jit(solution)/shard_map/ppermute | solution.py:631
  51.5 4.4 collective-permute-done.21.refs_4_.refs_1_
  58.5 15.9 %collective-permute-done.20.refs_3_.refs_0_ = bf16[256,1152]{1,0:T(8,128)(2,1)} collective-permute-done((bf16[256,1152]{1,0:T(8,128)(2,1)S(1)}, bf16[256,1152]{1,0:T(8,128)(2,1)}, u32[]{:S(2)}, u32[]{:S(2)}) %collective-permute-start.20) | collective-permute-done | bytes 589856 | tf_op jit(solution)/shard_map/ppermute | solution.py:631
  79.4 16.7 %collective-permute-done.8.refs_8_.refs_15_ = bf16[256,2176]{1,0:T(8,128)(2,1)S(1)} collective-permute-done((bf16[256,2176]{1,0:T(8,128)(2,1)S(1)}, bf16[256,2176]{1,0:T(8,128)(2,1)S(1)}, u32[]{:S(2)}, u32[]{:S(2)}) %collective-permute-start.8) | collective-permute-done | bytes 1114144 | tf_op jit(solution)/shard_map/ppermute | solution.py:615
  96.4 5.6 collective-permute-done.4.refs_4_.refs_7_
  102.7 16.8 %collective-permute-done.13.refs_13_.refs_12_ = bf16[256,2176]{1,0:T(8,128)(2,1)S(1)} collective-permute-done((bf16[256,2176]{1,0:T(8,128)(2,1)S(1)}, bf16[256,2176]{1,0:T(8,128)(2,1)S(1)}, u32[]{:S(2)}, u32[]{:S(2)}) %collective-permute-start.13) | collective-permute-done | bytes 1114144 | tf_op jit(solution)/shard_map/ppermute | solution.py:615
  125.7 27.1 %shard_map.153 = (bf16[1024,1792]{1,0:T(8,128)(2,1)}, bf16[1024,384]{1,0:T(8,128)(2,1)}) custom-call(s32[3]{0:T(128)} %pad_add_fusion.pos_ref, bf16[1024,4096]{1,0:T(8,128)(2,1)} %all-gather.3.cloned.1.call-done.acts_ref.in_ref.refs_2_.refs_6_, bf16[256,2176]{1,0:T(8,128)(2,1)} %copy-done.1, bf16[256,2176]{1,0:T(8,128)(2,1)} %copy-done, ...), custom_call_target="tpu_custom_call" | custom-call | flops 912680576 | bytes 26214400 | tf_op jit(solution)/shard_map/pallas_call | solution.py:330
  159.9 6.8 %collective-permute-done.18.other_third_ref = bf16[512,128]{1,0:T(8,128)(2,1)S(1)} collective-permute-done((bf16[512,128]{1,0:T(8,128)(2,1)S(1)}, bf16[512,128]{1,0:T(8,128)(2,1)S(1)}, u32[]{:S(2)}, u32[]{:S(2)}) %collective-permute-start.18) | collective-permute-done | bytes 131104 | tf_op jit(solution)/shard_map/ppermute | solution.py:636
  167.0 5.3 collective-permute-done.17.own_third_ref
  174.5 4.9 act_fwd.1
  179.4 4.3 shard_map.154
  183.7 5.6 shard_map.155
  197.3 16.9 %shard_map.156 = f32[1024,4096]{1,0:T(8,128)} custom-call(s32[3]{0:T(128)} %pad_add_fusion.pos_ref, bf16[16,64,896]{2,1,0:T(8,128)(2,1)} %bitcast.34, bf16[8,64,256]{2,1,0:T(8,128)(2,1)} %bitcast.35, bf16[8,64,256]{2,1,0:T(8,128)(2,1)} %bitcast.36, bf16[256,1152]{1,0:T(8,128)(2,1)} %collective-permute-done.20.refs_3_.refs_0_, ...), custom_call_target="tpu_custom_call" | custom-call | flops 483183808 | bytes 26214400 | tf_op jit(solution)/shard_map/pallas_call | solution.py:424
  214.2 4.1 shard_map.157
  218.9 8.5 %collective-permute-start.42 = (bf16[1024,2048]{1,0:T(8,128)(2,1)}, bf16[1024,2048]{1,0:T(8,128)(2,1)}, u32[]{:S(2)}, u32[]{:S(2)}) collective-permute-start(bf16[1024,2048]{1,0:T(8,128)(2,1)} %shard_map.154), channel_id=1, source_target_pairs={{0,1},{1,0},{2,3},{3,2},{4,5},{5,4},{6,7},{7,6},{8,9},{9,8},{10,11... | collective-permute-start | bytes 12582920 | tf_op jit(solution)/shard_map/ppermute | solution.py:619
  228.6 13.2 %grad.4 = (f32[896,256]{1,0:T(8,128)}, f32[896,256]{1,0:T(8,128)}, f32[896,256]{1,0:T(8,128)}, f32[896,256]{1,0:T(8,128)}, f32[896,256]{1,0:T(8,128)}, /*index=5...) custom-call(s32[3]{0:T(128)} %pad_add_fusion.pos_ref, bf16[896,1024]{1,0:T(8,128)(2,1)} %get-tuple-element.81.refs_0_, ...), custom_call_target="tpu_custom_call" | custom-call | flops 375809632 | bytes 8388608 | tf_op jit(solution)/shard_map/grad/pallas_call | solution.py:537
  241.7 17.7 %shard_map.158 = (bf16[1024,896]{1,0:T(8,128)(2,1)}, bf16[1024,256]{1,0:T(8,128)(2,1)}) custom-call(s32[3]{0:T(128)} %pad_add_fusion.pos_ref, bf16[1024,4096]{1,0:T(8,128)(2,1)} %all-gather.5.cloned.1.call-done.in_ref.refs_2_.acts_ref, bf16[256,1152]{1,0:T(8,128)(2,1)} %collective-permute-done.20.refs_3_.refs_0_, ...), custom_call_target="tpu_custom_call" | custom-call | flops 483183808 | bytes 17825792 | tf_op jit(solution)/shard_map/pallas_call | solution.py:330
  259.4 6.9 %act_bwd.1 = (bf16[1024,1792]{1,0:T(8,128)(2,1)}, bf16[1792,1024]{1,0:T(8,128)(2,1)}) custom-call(bf16[1024,1792]{1,0:T(8,128)(2,1)} %get-tuple-element.80.ab_ref, bf16[1024,896]{1,0:T(8,128)(2,1)} %get-tuple-element.94.du_ref), custom_call_target="tpu_custom_call" | custom-call | flops 400000000 | bytes 14000000 | tf_op jit(solution)/shard_map/act_bwd/pallas_call | solution.py:260
  274.0 8.1 %shard_map.159 = (bf16[2,512,256]{2,1,0:T(8,128)(2,1)}, f32[2,512,128]{2,1,0:T(8,128)}, f32[2,512,128]{2,1,0:T(8,128)}) custom-call(s32[3]{0:T(128)} %pad_add_fusion.pos_ref, bf16[2,512,512]{2,1,0:T(8,128)(2,1)} %get-tuple-element.100.seq_ref, bf16[1024,256]{1,0:T(8,128)(2,1)} %get-tuple-element.101.own_ref, bf16[512,256]{1,0:T(8,128)(2,1)} %copy-done.60, ...), custom_call_target="tpu_custom_call" | custom-call | flops 800000000 | bytes 4000000 | tf_op jit(solution)/shard_map/pallas_call | solution.py:142
  283.1 6.5 collective-permute-done.38
  294.4 13.1 %grad.5 = (f32[896,256]{1,0:T(8,128)}, f32[896,256]{1,0:T(8,128)}, f32[896,256]{1,0:T(8,128)}, f32[896,256]{1,0:T(8,128)}, f32[896,256]{1,0:T(8,128)}, /*index=5...) custom-call(s32[3]{0:T(128)} %pad_add_fusion.pos_ref, bf16[1792,1024]{1,0:T(8,128)(2,1)} %get-tuple-element.98.refs_0_, ...), custom_call_target="tpu_custom_call" | custom-call | flops 375809632 | bytes 8388608 | tf_op jit(solution)/shard_map/grad/pallas_call | solution.py:537
  316.2 15.5 %shard_map.161 = f32[512,4096]{1,0:T(8,128)} custom-call(s32[3]{0:T(128)} %pad_add_fusion.pos_ref, bf16[16,64,1792]{2,1,0:T(8,128)(2,1)} %bitcast.22, bf16[8,64,384]{2,1,0:T(8,128)(2,1)} %bitcast.29, bf16[8,64,384]{2,1,0:T(8,128)(2,1)} %bitcast.31, bf16[256,2176]{1,0:T(8,128)(2,1)} %copy-done.1, bf16[256,2176]{1,0:T(8,128)(2,1)} %copy-done, ...), custom_call_target="tpu_custom_call" | custom-call | flops 456340288 | bytes 26214400 | tf_op jit(solution)/shard_map/pallas_call | solution.py:424
  334.5 20.3 %collective-permute-done.45 = f32[896,256]{1,0:T(8,128)S(1)} collective-permute-done((f32[896,256]{1,0:T(8,128)}, f32[896,256]{1,0:T(8,128)S(1)}, u32[]{:S(2)}, u32[]{:S(2)}) %collective-permute-start.45) | collective-permute-done | bytes 917536 | tf_op jit(solution)/shard_map/ppermute | solution.py:615
  356.9 13.2 %grad.6 = (f32[896,256]{1,0:T(8,128)}, f32[896,256]{1,0:T(8,128)}, f32[896,256]{1,0:T(8,128)}, f32[896,256]{1,0:T(8,128)}, f32[896,256]{1,0:T(8,128)}, /*index=5...) custom-call(s32[3]{0:T(128)} %pad_add_fusion.pos_ref, bf16[1792,1024]{1,0:T(8,128)(2,1)} %get-tuple-element.98.refs_0_, ...), custom_call_target="tpu_custom_call" | custom-call | flops 375809632 | bytes 8388608 | tf_op jit(solution)/shard_map/grad/pallas_call | solution.py:537
  370.1 15.7 %shard_map.162 = f32[512,4096]{1,0:T(8,128)} custom-call(s32[3]{0:T(128)} %pad_add_fusion.pos_ref, bf16[16,64,1792]{2,1,0:T(8,128)(2,1)} %bitcast.23, bf16[8,64,384]{2,1,0:T(8,128)(2,1)} %bitcast.30, bf16[8,64,384]{2,1,0:T(8,128)(2,1)} %bitcast.32, bf16[256,2176]{1,0:T(8,128)(2,1)} %copy-done.1, bf16[256,2176]{1,0:T(8,128)(2,1)} %copy-done, ...), custom_call_target="tpu_custom_call" | custom-call | flops 456340288 | bytes 26214400 | tf_op jit(solution)/shard_map/pallas_call | solution.py:424
  392.9 15.8 %collective-permute-done.74 = f32[896,256]{1,0:T(8,128)} collective-permute-done((f32[896,256]{1,0:T(8,128)}, f32[896,256]{1,0:T(8,128)}, u32[]{:S(2)}, u32[]{:S(2)}) %collective-permute-start.74) | collective-permute-done | bytes 917536 | tf_op jit(solution)/shard_map/ppermute | solution.py:615
  420.6 6.7 collective-permute-done.72
  430.7 16.3 %collective-permute-done.66 = f32[896,256]{1,0:T(8,128)S(1)} collective-permute-done((f32[896,256]{1,0:T(8,128)}, f32[896,256]{1,0:T(8,128)S(1)}, u32[]{:S(2)}, u32[]{:S(2)}) %collective-permute-start.66) | collective-permute-done | bytes 917536 | tf_op jit(solution)/shard_map/ppermute | solution.py:615
  447.0 3.4 collective-permute-start.54
  451.5 13.1 %grad.7 = (f32[640,256]{1,0:T(8,128)}, f32[640,256]{1,0:T(8,128)}, f32[640,256]{1,0:T(8,128)}, f32[640,256]{1,0:T(8,128)}, f32[640,256]{1,0:T(8,128)}, /*index=5...) custom-call(s32[3]{0:T(128)} %pad_add_fusion.pos_ref, bf16[256,1024]{1,0:T(8,128)(2,1)} %copy-done.18, ...), custom_call_target="tpu_custom_call" | custom-call | flops 268435456 | bytes 8388608 | tf_op jit(solution)/shard_map/grad/pallas_call | solution.py:537
  466.6 3.4 collective-permute-start.59
  471.6 14.6 %collective-permute-done.54 = f32[896,256]{1,0:T(8,128)} collective-permute-done((f32[896,256]{1,0:T(8,128)}, f32[896,256]{1,0:T(8,128)}, u32[]{:S(2)}, u32[]{:S(2)}) %collective-permute-start.54) | collective-permute-done | bytes 917536 | tf_op jit(solution)/shard_map/ppermute | solution.py:615
  492.7 7.9 %collective-permute-done.57 = f32[640,256]{1,0:T(8,128)S(1)} collective-permute-done((f32[640,256]{1,0:T(8,128)}, f32[640,256]{1,0:T(8,128)S(1)}, u32[]{:S(2)}, u32[]{:S(2)}) %collective-permute-start.57) | collective-permute-done | bytes 655392 | tf_op jit(solution)/shard_map/ppermute | solution.py:615
  501.4 13.0 %collective-permute-done.62 = f32[640,256]{1,0:T(8,128)S(1)} collective-permute-done((f32[640,256]{1,0:T(8,128)}, f32[640,256]{1,0:T(8,128)S(1)}, u32[]{:S(2)}, u32[]{:S(2)}) %collective-permute-start.62) | collective-permute-done | bytes 655392 | tf_op jit(solution)/shard_map/ppermute | solution.py:615
  520.0 13.9 %collective-permute-done.51 = f32[896,256]{1,0:T(8,128)S(1)} collective-permute-done((f32[896,256]{1,0:T(8,128)S(1)}, f32[896,256]{1,0:T(8,128)S(1)}, u32[]{:S(2)}, u32[]{:S(2)}) %collective-permute-start.51) | collective-permute-done | bytes 917536 | tf_op jit(solution)/shard_map/ppermute | solution.py:615
  533.9 5.1 collective-permute-start.73
  544.3 9.6 %collective-permute-done.61 = f32[640,256]{1,0:T(8,128)S(1)} collective-permute-done((f32[640,256]{1,0:T(8,128)S(1)}, f32[640,256]{1,0:T(8,128)S(1)}, u32[]{:S(2)}, u32[]{:S(2)}) %collective-permute-start.61) | collective-permute-done | bytes 655392 | tf_op jit(solution)/shard_map/ppermute | solution.py:615
  553.9 7.3 %collective-permute-start.70 = (f32[896,256]{1,0:T(8,128)}, f32[896,256]{1,0:T(8,128)}, u32[]{:S(2)}, u32[]{:S(2)}) collective-permute-start(f32[896,256]{1,0:T(8,128)} %add_add_fusion.3), channel_id=1, source_target_pairs={{0,8},{1,24},{8,0},{9,16},{16,9},{17,25},{24,1},{25,17},{2,10},{3,... | collective-permute-start | bytes 2752520 | tf_op jit(solution)/shard_map/ppermute | solution.py:631
  567.3 7.3 %collective-permute-done.73.first_ref = f32[896,256]{1,0:T(8,128)S(1)} collective-permute-done((f32[896,256]{1,0:T(8,128)S(1)}, f32[896,256]{1,0:T(8,128)S(1)}, u32[]{:S(2)}, u32[]{:S(2)}) %collective-permute-start.73) | collective-permute-done | bytes 917536 | tf_op jit(solution)/shard_map/ppermute | solution.py:631
  577.5 4.4 collective-permute-start.56
  581.9 3.4 shard_map.165
  591.9 10.6 %collective-permute-done.70.second_ref = f32[896,256]{1,0:T(8,128)} collective-permute-done((f32[896,256]{1,0:T(8,128)}, f32[896,256]{1,0:T(8,128)}, u32[]{:S(2)}, u32[]{:S(2)}) %collective-permute-start.70) | collective-permute-done | bytes 917536 | tf_op jit(solution)/shard_map/ppermute | solution.py:631
  605.6 8.4 %collective-permute-done.67.first_ref = f32[896,256]{1,0:T(8,128)} collective-permute-done((f32[896,256]{1,0:T(8,128)}, f32[896,256]{1,0:T(8,128)}, u32[]{:S(2)}, u32[]{:S(2)}) %collective-permute-start.67) | collective-permute-done | bytes 917536 | tf_op jit(solution)/shard_map/ppermute | solution.py:631
  614.0 3.7 shard_map.164
  617.8 23.2 %collective-permute-done.52.first_ref = f32[896,256]{1,0:T(8,128)} collective-permute-done((f32[896,256]{1,0:T(8,128)}, f32[896,256]{1,0:T(8,128)}, u32[]{:S(2)}, u32[]{:S(2)}) %collective-permute-start.52) | collective-permute-done | bytes 917536 | tf_op jit(solution)/shard_map/ppermute | solution.py:631
  640.9 3.7 shard_map.163
  647.3 20.4 %reduce-scatter.4.cloned.1.call-done = f32[64,4096]{1,0:T(8,128)} async-done(((f32[1024,4096]{1,0:T(8,128)}), f32[64,4096]{1,0:T(8,128)}) %reduce-scatter.4.cloned.1.call-update) | async-done | bytes 1048592 | tf_op jit(solution)/shard_map/reduce_scatter | solution.py:747
  (320 shorter events, 154.2 us)
Async XLA Ops:
  7.2 118.6 %all-gather.3.cloned.1.call-start = ((), (), s32[]{:S(2)}) async-start(), calls=%async_computation.3 | async-start | bytes 8912896 | tf_op jit(solution)/shard_map/all_gather | solution.py:730
  12.5 28.8 %collective-permute-start.1 = (bf16[256,2176]{1,0:T(8,128)(2,1)}, bf16[256,2176]{1,0:T(8,128)(2,1)S(1)}, u32[]{:S(2)}, u32[]{:S(2)}) collective-permute-start(bf16[256,2176]{1,0:T(8,128)(2,1)} %get-tuple-element.148), channel_id=1, source_target_pairs={{0,8},{1,24},{8,0},{9,16},{16,9},{17,25},{24,1},{25,17},{2,10},{3,... | collective-permute-start | bytes 3342344 | tf_op jit(solution)/shard_map/ppermute | solution.py:631
  42.3 172.0 %all-gather.5.cloned.1.call-start = ((), (), s32[]{:S(2)}) async-start(), calls=%async_computation.5 | async-start | bytes 8912896 | tf_op jit(solution)/shard_map/all_gather | solution.py:731
  43.0 601.7 %reduce-scatter.6.cloned.1.call-start = ((), (), s32[]{:S(2)}) async-start(), calls=%async_computation.6 | async-start | bytes 8912896 | tf_op jit(solution)/shard_map/reduce_scatter | solution.py:765
  47.7 29.9 %collective-permute-start.9 = (bf16[256,2176]{1,0:T(8,128)(2,1)S(1)}, bf16[256,2176]{1,0:T(8,128)(2,1)S(1)}, u32[]{:S(2)}, u32[]{:S(2)}) collective-permute-start(bf16[256,2176]{1,0:T(8,128)(2,1)S(1)} %collective-permute-done.1.refs_1_.refs_4_), channel_id=1, source_target_pairs={{0,32},{32,64},{64,96},{96,0},{1,33},{33,65},{65,97},{97,1},{2,34}... | collective-permute-start | bytes 3342344 | tf_op jit(solution)/shard_map/ppermute | solution.py:615
  49.4 28.3 %collective-permute-start.5 = (bf16[256,2176]{1,0:T(8,128)(2,1)S(1)}, bf16[256,2176]{1,0:T(8,128)(2,1)S(1)}, u32[]{:S(2)}, u32[]{:S(2)}) collective-permute-start(bf16[256,2176]{1,0:T(8,128)(2,1)S(1)} %collective-permute-done.1.refs_1_.refs_4_), channel_id=1, source_target_pairs={{0,96},{32,0},{64,32},{96,64},{1,97},{33,1},{65,33},{97,65},{2,98}... | collective-permute-start | bytes 3342344 | tf_op jit(solution)/shard_map/ppermute | solution.py:615
  51.5 26.7 %collective-permute-start.3 = (bf16[256,2176]{1,0:T(8,128)(2,1)S(1)}, bf16[256,2176]{1,0:T(8,128)(2,1)S(1)}, u32[]{:S(2)}, u32[]{:S(2)}) collective-permute-start(bf16[256,2176]{1,0:T(8,128)(2,1)S(1)} %collective-permute-done.1.refs_1_.refs_4_), channel_id=1, source_target_pairs={{0,1},{1,0},{2,3},{3,2},{4,5},{5,4},{6,7},{7,6},{8,9},{9,8},{10,11... | collective-permute-start | bytes 3342344 | tf_op jit(solution)/shard_map/ppermute | solution.py:619
  51.5 44.5 %collective-permute-start.8 = (bf16[256,2176]{1,0:T(8,128)(2,1)S(1)}, bf16[256,2176]{1,0:T(8,128)(2,1)S(1)}, u32[]{:S(2)}, u32[]{:S(2)}) collective-permute-start(bf16[256,2176]{1,0:T(8,128)(2,1)S(1)} %collective-permute-done.refs_0_.refs_3_), channel_id=1, source_target_pairs={{0,32},{32,64},{64,96},{96,0},{1,33},{33,65},{65,97},{97,1},{2,34}... | collective-permute-start | bytes 3342344 | tf_op jit(solution)/shard_map/ppermute | solution.py:615
  74.3 27.7 %collective-permute-start.4 = (bf16[256,2176]{1,0:T(8,128)(2,1)S(1)}, bf16[256,2176]{1,0:T(8,128)(2,1)S(1)}, u32[]{:S(2)}, u32[]{:S(2)}) collective-permute-start(bf16[256,2176]{1,0:T(8,128)(2,1)S(1)} %collective-permute-done.refs_0_.refs_3_), channel_id=1, source_target_pairs={{0,96},{32,0},{64,32},{96,64},{1,97},{33,1},{65,33},{97,65},{2,98}... | collective-permute-start | bytes 3342344 | tf_op jit(solution)/shard_map/ppermute | solution.py:615
  78.2 41.3 %collective-permute-start.13 = (bf16[256,2176]{1,0:T(8,128)(2,1)S(1)}, bf16[256,2176]{1,0:T(8,128)(2,1)S(1)}, u32[]{:S(2)}, u32[]{:S(2)}) collective-permute-start(bf16[256,2176]{1,0:T(8,128)(2,1)S(1)} %collective-permute-done.5.refs_5_.refs_8_), channel_id=1, source_target_pairs={{0,96},{32,0},{64,32},{96,64},{1,97},{33,1},{65,33},{97,65},{2,98}... | collective-permute-start | bytes 3342344 | tf_op jit(solution)/shard_map/ppermute | solution.py:615
  120.0 34.3 %collective-permute-start.33 = (bf16[256,1152]{1,0:T(8,128)(2,1)}, bf16[256,1152]{1,0:T(8,128)(2,1)}, u32[]{:S(2)}, u32[]{:S(2)}) collective-permute-start(bf16[256,1152]{1,0:T(8,128)(2,1)} %collective-permute-done.21.refs_4_.refs_1_), channel_id=1, source_target_pairs={{0,32},{32,64},{64,96},{96,0},{1,33},{33,65},{65,97},{97,1},{2,34}... | collective-permute-start | bytes 1769480 | tf_op jit(solution)/shard_map/ppermute | solution.py:615
  121.7 36.0 %collective-permute-start.25 = (bf16[256,1152]{1,0:T(8,128)(2,1)}, bf16[256,1152]{1,0:T(8,128)(2,1)}, u32[]{:S(2)}, u32[]{:S(2)}) collective-permute-start(bf16[256,1152]{1,0:T(8,128)(2,1)} %collective-permute-done.21.refs_4_.refs_1_), channel_id=1, source_target_pairs={{0,96},{32,0},{64,32},{96,64},{1,97},{33,1},{65,33},{97,65},{2,98}... | collective-permute-start | bytes 1769480 | tf_op jit(solution)/shard_map/ppermute | solution.py:615
  124.2 34.9 %collective-permute-start.23 = (bf16[256,1152]{1,0:T(8,128)(2,1)}, bf16[256,1152]{1,0:T(8,128)(2,1)}, u32[]{:S(2)}, u32[]{:S(2)}) collective-permute-start(bf16[256,1152]{1,0:T(8,128)(2,1)} %collective-permute-done.21.refs_4_.refs_1_), channel_id=1, source_target_pairs={{0,1},{1,0},{2,3},{3,2},{4,5},{5,4},{6,7},{7,6},{8,9},{9,8},{10,11... | collective-permute-start | bytes 1769480 | tf_op jit(solution)/shard_map/ppermute | solution.py:619
  125.3 34.3 %collective-permute-start.28 = (bf16[256,1152]{1,0:T(8,128)(2,1)}, bf16[256,1152]{1,0:T(8,128)(2,1)}, u32[]{:S(2)}, u32[]{:S(2)}) collective-permute-start(bf16[256,1152]{1,0:T(8,128)(2,1)} %collective-permute-done.20.refs_3_.refs_0_), channel_id=1, source_target_pairs={{0,32},{32,64},{64,96},{96,0},{1,33},{33,65},{65,97},{97,1},{2,34}... | collective-permute-start | bytes 1769480 | tf_op jit(solution)/shard_map/ppermute | solution.py:615
  154.3 36.2 %collective-permute-start.24 = (bf16[256,1152]{1,0:T(8,128)(2,1)}, bf16[256,1152]{1,0:T(8,128)(2,1)}, u32[]{:S(2)}, u32[]{:S(2)}) collective-permute-start(bf16[256,1152]{1,0:T(8,128)(2,1)} %collective-permute-done.20.refs_3_.refs_0_), channel_id=1, source_target_pairs={{0,96},{32,0},{64,32},{96,64},{1,97},{33,1},{65,33},{97,65},{2,98}... | collective-permute-start | bytes 1769480 | tf_op jit(solution)/shard_map/ppermute | solution.py:615
  159.6 32.0 %collective-permute-start.22 = (bf16[256,1152]{1,0:T(8,128)(2,1)}, bf16[256,1152]{1,0:T(8,128)(2,1)}, u32[]{:S(2)}, u32[]{:S(2)}) collective-permute-start(bf16[256,1152]{1,0:T(8,128)(2,1)} %collective-permute-done.20.refs_3_.refs_0_), channel_id=1, source_target_pairs={{0,1},{1,0},{2,3},{3,2},{4,5},{5,4},{6,7},{7,6},{8,9},{9,8},{10,11... | collective-permute-start | bytes 1769480 | tf_op jit(solution)/shard_map/ppermute | solution.py:619
  218.9 75.4 %collective-permute-start.42 = (bf16[1024,2048]{1,0:T(8,128)(2,1)}, bf16[1024,2048]{1,0:T(8,128)(2,1)}, u32[]{:S(2)}, u32[]{:S(2)}) collective-permute-start(bf16[1024,2048]{1,0:T(8,128)(2,1)} %shard_map.154), channel_id=1, source_target_pairs={{0,1},{1,0},{2,3},{3,2},{4,5},{5,4},{6,7},{7,6},{8,9},{9,8},{10,11... | collective-permute-start | bytes 12582920 | tf_op jit(solution)/shard_map/ppermute | solution.py:619
  266.3 28.1 %collective-permute-start.41 = (bf16[1792,1024]{1,0:T(8,128)(2,1)}, bf16[1792,1024]{1,0:T(8,128)(2,1)}, u32[]{:S(2)}, u32[]{:S(2)}) collective-permute-start(bf16[1792,1024]{1,0:T(8,128)(2,1)} %get-tuple-element.98.refs_0_), channel_id=1, source_target_pairs={{0,1},{1,0},{2,3},{3,2},{4,5},{5,4},{6,7},{7,6},{8,9},{9,8},{10,11... | collective-permute-start | bytes 11010056 | tf_op jit(solution)/shard_map/ppermute | solution.py:619
  266.5 25.7 %collective-permute-start.40 = (f32[896,256]{1,0:T(8,128)}, f32[896,256]{1,0:T(8,128)}, u32[]{:S(2)}, u32[]{:S(2)}) collective-permute-start(f32[896,256]{1,0:T(8,128)} %get-tuple-element.105), channel_id=1, source_target_pairs={{0,96},{32,0},{64,32},{96,64},{1,97},{33,1},{65,33},{97,65},{2,98}... | collective-permute-start | bytes 2752520 | tf_op jit(solution)/shard_map/ppermute | solution.py:615
  331.7 314.1 %reduce-scatter.8.cloned.1.call-start = ((), (), s32[]{:S(2)}) async-start(), calls=%async_computation.7 | async-start | bytes 8912896 | tf_op jit(solution)/shard_map/reduce_scatter | solution.py:769
  385.8 281.8 %reduce-scatter.4.cloned.1.call-start = ((), (), s32[]{:S(2)}) async-start(), calls=%async_computation.4 | async-start | bytes 17825792 | tf_op jit(solution)/shard_map/reduce_scatter | solution.py:747
  389.5 26.8 %collective-permute-start.48 = (bf16[256,1024]{1,0:T(8,128)(2,1)S(1)}, bf16[256,1024]{1,0:T(8,128)(2,1)}, u32[]{:S(2)}, u32[]{:S(2)}) collective-permute-start(bf16[256,1024]{1,0:T(8,128)(2,1)S(1)} %maximum_bitcast_fusion.1.refs_0_), channel_id=1, source_target_pairs={{0,1},{1,0},{2,3},{3,2},{4,5},{5,4},{6,7},{7,6},{8,9},{9,8},{10,11... | collective-permute-start | bytes 1572872 | tf_op jit(solution)/shard_map/ppermute | solution.py:619
  391.4 35.9 %collective-permute-start.72 = (f32[896,256]{1,0:T(8,128)}, f32[896,256]{1,0:T(8,128)S(1)}, u32[]{:S(2)}, u32[]{:S(2)}) collective-permute-start(f32[896,256]{1,0:T(8,128)} %get-tuple-element.145), channel_id=1, source_target_pairs={{0,96},{32,0},{64,32},{96,64},{1,97},{33,1},{65,33},{97,65},{2,98}... | collective-permute-start | bytes 2752520 | tf_op jit(solution)/shard_map/ppermute | solution.py:615
  391.6 36.7 %collective-permute-start.71 = (f32[896,256]{1,0:T(8,128)}, f32[896,256]{1,0:T(8,128)}, u32[]{:S(2)}, u32[]{:S(2)}) collective-permute-start(f32[896,256]{1,0:T(8,128)} %add.116), channel_id=1, source_target_pairs={{0,32},{32,64},{64,96},{96,0},{1,33},{33,65},{65,97},{97,1},{2,34}... | collective-permute-start | bytes 2752520 | tf_op jit(solution)/shard_map/ppermute | solution.py:615
  413.1 33.8 %collective-permute-start.66 = (f32[896,256]{1,0:T(8,128)}, f32[896,256]{1,0:T(8,128)S(1)}, u32[]{:S(2)}, u32[]{:S(2)}) collective-permute-start(f32[896,256]{1,0:T(8,128)} %get-tuple-element.141), channel_id=1, source_target_pairs={{0,96},{32,0},{64,32},{96,64},{1,97},{33,1},{65,33},{97,65},{2,98}... | collective-permute-start | bytes 2752520 | tf_op jit(solution)/shard_map/ppermute | solution.py:615
  417.2 33.2 %collective-permute-start.49 = (bf16[384,1024]{1,0:T(8,128)(2,1)S(1)}, bf16[384,1024]{1,0:T(8,128)(2,1)S(1)}, u32[]{:S(2)}, u32[]{:S(2)}) collective-permute-start(bf16[384,1024]{1,0:T(8,128)(2,1)S(1)} %maximum_bitcast_fusion.refs_4_), channel_id=1, source_target_pairs={{0,1},{1,0},{2,3},{3,2},{4,5},{5,4},{6,7},{7,6},{8,9},{9,8},{10,11... | collective-permute-start | bytes 2359304 | tf_op jit(solution)/shard_map/ppermute | solution.py:619
  427.3 37.4 %collective-permute-start.68 = (f32[896,256]{1,0:T(8,128)}, f32[896,256]{1,0:T(8,128)}, u32[]{:S(2)}, u32[]{:S(2)}) collective-permute-start(f32[896,256]{1,0:T(8,128)} %get-tuple-element.143), channel_id=1, source_target_pairs={{0,32},{32,64},{64,96},{96,0},{1,33},{33,65},{65,97},{97,1},{2,34}... | collective-permute-start | bytes 2752520 | tf_op jit(solution)/shard_map/ppermute | solution.py:615
  428.3 38.3 %collective-permute-start.69 = (f32[896,256]{1,0:T(8,128)}, f32[896,256]{1,0:T(8,128)}, u32[]{:S(2)}, u32[]{:S(2)}) collective-permute-start(f32[896,256]{1,0:T(8,128)} %add.119), channel_id=1, source_target_pairs={{0,96},{32,0},{64,32},{96,64},{1,97},{33,1},{65,33},{97,65},{2,98}... | collective-permute-start | bytes 2752520 | tf_op jit(solution)/shard_map/ppermute | solution.py:615
  430.7 39.3 %collective-permute-start.47 = (f32[896,256]{1,0:T(8,128)}, f32[896,256]{1,0:T(8,128)}, u32[]{:S(2)}, u32[]{:S(2)}) collective-permute-start(f32[896,256]{1,0:T(8,128)} %get-tuple-element.122), channel_id=1, source_target_pairs={{0,32},{32,64},{64,96},{96,0},{1,33},{33,65},{65,97},{97,1},{2,34}... | collective-permute-start | bytes 2752520 | tf_op jit(solution)/shard_map/ppermute | solution.py:615
  447.0 39.3 %collective-permute-start.54 = (f32[896,256]{1,0:T(8,128)}, f32[896,256]{1,0:T(8,128)}, u32[]{:S(2)}, u32[]{:S(2)}) collective-permute-start(f32[896,256]{1,0:T(8,128)} %get-tuple-element.130), channel_id=1, source_target_pairs={{0,96},{32,0},{64,32},{96,64},{1,97},{33,1},{65,33},{97,65},{2,98}... | collective-permute-start | bytes 2752520 | tf_op jit(solution)/shard_map/ppermute | solution.py:615
  451.3 38.4 %collective-permute-start.65 = (f32[896,256]{1,0:T(8,128)}, f32[896,256]{1,0:T(8,128)}, u32[]{:S(2)}, u32[]{:S(2)}) collective-permute-start(f32[896,256]{1,0:T(8,128)} %add.118), channel_id=1, source_target_pairs={{0,32},{32,64},{64,96},{96,0},{1,33},{33,65},{65,97},{97,1},{2,34}... | collective-permute-start | bytes 2752520 | tf_op jit(solution)/shard_map/ppermute | solution.py:615
  464.7 35.8 %collective-permute-start.57 = (f32[640,256]{1,0:T(8,128)}, f32[640,256]{1,0:T(8,128)S(1)}, u32[]{:S(2)}, u32[]{:S(2)}) collective-permute-start(f32[640,256]{1,0:T(8,128)} %get-tuple-element.133), channel_id=1, source_target_pairs={{0,32},{32,64},{64,96},{96,0},{1,33},{33,65},{65,97},{97,1},{2,34}... | collective-permute-start | bytes 1966088 | tf_op jit(solution)/shard_map/ppermute | solution.py:615
  466.6 33.9 %collective-permute-start.59 = (f32[640,256]{1,0:T(8,128)}, f32[640,256]{1,0:T(8,128)S(1)}, u32[]{:S(2)}, u32[]{:S(2)}) collective-permute-start(f32[640,256]{1,0:T(8,128)} %get-tuple-element.134), channel_id=1, source_target_pairs={{0,96},{32,0},{64,32},{96,64},{1,97},{33,1},{65,33},{97,65},{2,98}... | collective-permute-start | bytes 1966088 | tf_op jit(solution)/shard_map/ppermute | solution.py:615
  470.0 44.3 %collective-permute-start.62 = (f32[640,256]{1,0:T(8,128)}, f32[640,256]{1,0:T(8,128)S(1)}, u32[]{:S(2)}, u32[]{:S(2)}) collective-permute-start(f32[640,256]{1,0:T(8,128)} %get-tuple-element.138), channel_id=1, source_target_pairs={{0,96},{32,0},{64,32},{96,64},{1,97},{33,1},{65,33},{97,65},{2,98}... | collective-permute-start | bytes 1966088 | tf_op jit(solution)/shard_map/ppermute | solution.py:615
  486.3 47.6 %collective-permute-start.51 = (f32[896,256]{1,0:T(8,128)S(1)}, f32[896,256]{1,0:T(8,128)S(1)}, u32[]{:S(2)}, u32[]{:S(2)}) collective-permute-start(f32[896,256]{1,0:T(8,128)S(1)} %copy-done.56), channel_id=1, source_target_pairs={{0,96},{32,0},{64,32},{96,64},{1,97},{33,1},{65,33},{97,65},{2,98}... | collective-permute-start | bytes 2752520 | tf_op jit(solution)/shard_map/ppermute | solution.py:615
  489.7 49.3 %collective-permute-start.50 = (f32[896,256]{1,0:T(8,128)S(1)}, f32[896,256]{1,0:T(8,128)S(1)}, u32[]{:S(2)}, u32[]{:S(2)}) collective-permute-start(f32[896,256]{1,0:T(8,128)S(1)} %add.121), channel_id=1, source_target_pairs={{0,32},{32,64},{64,96},{96,0},{1,33},{33,65},{65,97},{97,1},{2,34}... | collective-permute-start | bytes 2752520 | tf_op jit(solution)/shard_map/ppermute | solution.py:615
  500.5 60.6 %collective-permute-start.53 = (f32[896,256]{1,0:T(8,128)S(1)}, f32[896,256]{1,0:T(8,128)S(1)}, u32[]{:S(2)}, u32[]{:S(2)}) collective-permute-start(f32[896,256]{1,0:T(8,128)S(1)} %copy-done.55), channel_id=1, source_target_pairs={{0,32},{32,64},{64,96},{96,0},{1,33},{33,65},{65,97},{97,1},{2,34}... | collective-permute-start | bytes 2752520 | tf_op jit(solution)/shard_map/ppermute | solution.py:615
  500.6 53.3 %collective-permute-start.61 = (f32[640,256]{1,0:T(8,128)S(1)}, f32[640,256]{1,0:T(8,128)S(1)}, u32[]{:S(2)}, u32[]{:S(2)}) collective-permute-start(f32[640,256]{1,0:T(8,128)S(1)} %copy-done.58), channel_id=1, source_target_pairs={{0,32},{32,64},{64,96},{96,0},{1,33},{33,65},{65,97},{97,1},{2,34}... | collective-permute-start | bytes 1966088 | tf_op jit(solution)/shard_map/ppermute | solution.py:615
  514.4 48.5 %collective-permute-start.55 = (f32[896,256]{1,0:T(8,128)S(1)}, f32[896,256]{1,0:T(8,128)S(1)}, u32[]{:S(2)}, u32[]{:S(2)}) collective-permute-start(f32[896,256]{1,0:T(8,128)S(1)} %add.125), channel_id=1, source_target_pairs={{0,96},{32,0},{64,32},{96,64},{1,97},{33,1},{65,33},{97,65},{2,98}... | collective-permute-start | bytes 2752520 | tf_op jit(solution)/shard_map/ppermute | solution.py:615
  533.9 40.7 %collective-permute-start.73 = (f32[896,256]{1,0:T(8,128)S(1)}, f32[896,256]{1,0:T(8,128)S(1)}, u32[]{:S(2)}, u32[]{:S(2)}) collective-permute-start(f32[896,256]{1,0:T(8,128)S(1)} %add_add_fusion.2), channel_id=1, source_target_pairs={{0,0},{1,16},{8,8},{9,24},{16,1},{17,17},{24,9},{25,25},{2,2},{3,1... | collective-permute-start | bytes 2752520 | tf_op jit(solution)/shard_map/ppermute | solution.py:631
  539.0 38.5 %collective-permute-start.58 = (f32[640,256]{1,0:T(8,128)S(1)}, f32[640,256]{1,0:T(8,128)}, u32[]{:S(2)}, u32[]{:S(2)}) collective-permute-start(f32[640,256]{1,0:T(8,128)S(1)} %add.127), channel_id=1, source_target_pairs={{0,32},{32,64},{64,96},{96,0},{1,33},{33,65},{65,97},{97,1},{2,34}... | collective-permute-start | bytes 1966088 | tf_op jit(solution)/shard_map/ppermute | solution.py:615
  553.9 48.6 %collective-permute-start.70 = (f32[896,256]{1,0:T(8,128)}, f32[896,256]{1,0:T(8,128)}, u32[]{:S(2)}, u32[]{:S(2)}) collective-permute-start(f32[896,256]{1,0:T(8,128)} %add_add_fusion.3), channel_id=1, source_target_pairs={{0,8},{1,24},{8,0},{9,16},{16,9},{17,25},{24,1},{25,17},{2,10},{3,... | collective-permute-start | bytes 2752520 | tf_op jit(solution)/shard_map/ppermute | solution.py:631
  561.2 26.7 %collective-permute-start.63 = (f32[640,256]{1,0:T(8,128)}, f32[640,256]{1,0:T(8,128)}, u32[]{:S(2)}, u32[]{:S(2)}) collective-permute-start(f32[640,256]{1,0:T(8,128)} %add.131), channel_id=1, source_target_pairs={{0,96},{32,0},{64,32},{96,64},{1,97},{33,1},{65,33},{97,65},{2,98}... | collective-permute-start | bytes 1966088 | tf_op jit(solution)/shard_map/ppermute | solution.py:615
  562.9 51.1 %collective-permute-start.67 = (f32[896,256]{1,0:T(8,128)}, f32[896,256]{1,0:T(8,128)}, u32[]{:S(2)}, u32[]{:S(2)}) collective-permute-start(f32[896,256]{1,0:T(8,128)} %add_add_fusion.4), channel_id=1, source_target_pairs={{0,0},{1,16},{8,8},{9,24},{16,1},{17,17},{24,9},{25,25},{2,2},{3,1... | collective-permute-start | bytes 2752520 | tf_op jit(solution)/shard_map/ppermute | solution.py:631
  575.6 65.3 %collective-permute-start.52 = (f32[896,256]{1,0:T(8,128)}, f32[896,256]{1,0:T(8,128)}, u32[]{:S(2)}, u32[]{:S(2)}) collective-permute-start(f32[896,256]{1,0:T(8,128)} %add_add_fusion.6), channel_id=1, source_target_pairs={{0,0},{1,16},{8,8},{9,24},{16,1},{17,17},{24,9},{25,25},{2,2},{3,1... | collective-permute-start | bytes 2752520 | tf_op jit(solution)/shard_map/ppermute | solution.py:631
  577.5 63.4 %collective-permute-start.56 = (f32[896,256]{1,0:T(8,128)}, f32[896,256]{1,0:T(8,128)}, u32[]{:S(2)}, u32[]{:S(2)}) collective-permute-start(f32[896,256]{1,0:T(8,128)} %add_add_fusion.5), channel_id=1, source_target_pairs={{0,8},{1,24},{8,0},{9,16},{16,9},{17,25},{24,1},{25,17},{2,10},{3,... | collective-permute-start | bytes 2752520 | tf_op jit(solution)/shard_map/ppermute | solution.py:631
  587.9 82.4 %collective-permute-start.60 = (f32[640,256]{1,0:T(8,128)}, f32[640,256]{1,0:T(8,128)}, u32[]{:S(2)}, u32[]{:S(2)}) collective-permute-start(f32[640,256]{1,0:T(8,128)} %add_add_fusion.8), channel_id=1, source_target_pairs={{0,0},{1,16},{8,8},{9,24},{16,1},{17,17},{24,9},{25,25},{2,2},{3,1... | collective-permute-start | bytes 1966088 | tf_op jit(solution)/shard_map/ppermute | solution.py:631
  602.5 67.8 %collective-permute-start.64 = (f32[640,256]{1,0:T(8,128)}, f32[640,256]{1,0:T(8,128)}, u32[]{:S(2)}, u32[]{:S(2)}) collective-permute-start(f32[640,256]{1,0:T(8,128)} %add_add_fusion.7), channel_id=1, source_target_pairs={{0,8},{1,24},{8,0},{9,16},{16,9},{17,25},{24,1},{25,17},{2,10},{3,... | collective-permute-start | bytes 1966088 | tf_op jit(solution)/shard_map/ppermute | solution.py:631
  (97 other events, 1289.6 us)
Sparse Core Ops, SparseCore 0:
  42.4 76.8 all-gather.2
  121.5 74.7 all-gather.4
  331.8 80.4 reduce-scatter.5
  415.6 85.8 reduce-scatter.7
  504.7 162.9 reduce-scatter.3

commit v6 on v5

--- a/solution.py
+++ b/solution.py
@@ -550,14 +550,18 @@
     )(pos, *args)
 
 
-def place(pos, first, second, height, block, transpose):
+def sources(pos_ref, own_ref, first_ref, second_ref):
+    return ((pos_ref[3] == 1, 0, own_ref), (pos_ref[3] == 0, 0, first_ref), (True, 1, second_ref))
+
+
+def place(pos, own, first, second, height, block, transpose):
     cols = first.shape[1]
     spec = pl.BlockSpec((height, cols), lambda n, pos: (block, 0))
 
-    def kernel(pos_ref, first_ref, second_ref, out_ref):
-        for idx, ref in enumerate((first_ref, second_ref)):
-
-            @pl.when(pl.program_id(0) == idx)
+    def kernel(pos_ref, own_ref, first_ref, second_ref, out_ref):
+        for chosen, idx, ref in sources(pos_ref, own_ref, first_ref, second_ref):
+
+            @pl.when(jnp.logical_and(pl.program_id(0) == idx, chosen))
             def _(ref=ref):
                 out_ref[...] = ref[...].T if transpose else ref[...]
 
@@ -569,25 +573,28 @@
         grid_spec=pltpu.PrefetchScalarGridSpec(
             num_scalar_prefetch=1,
             grid=(2,),
-            in_specs=[spec, spec],
+            in_specs=[spec] * 3,
             out_specs=pl.BlockSpec((cols, height), lambda n, pos: (0, order(n, pos))) if transpose else pl.BlockSpec((height, cols), lambda n, pos: (order(n, pos), 0)),
         ),
         out_shape=jax.ShapeDtypeStruct((cols, 2 * height) if transpose else (2 * height, cols), F32),
         compiler_params=params(),
         cost_estimate=cost(2e9, 16 * height * cols),
-    )(pos, first, second)
-
-
-def place_attn(pos, first, second, o_blk, head):
+    )(pos, own, first, second)
+
+
+def place_attn(pos, own, first, second, o_blk, head):
     rows, cols = first.shape
     qk = 2 * head
 
-    def kernel(pos_ref, first_ref, second_ref, out_ref, qkv_ref):
-        for idx, ref in enumerate((first_ref, second_ref)):
-            bit = 1 - pos_ref[2] if idx else pos_ref[2]
-            out_ref[pl.ds(pl.multiple_of(bit * o_blk, o_blk), o_blk), :] = ref[:o_blk, :]
-            qkv_ref[:, pl.ds(pl.multiple_of(bit * qk, qk), qk)] = ref[o_blk : o_blk + qk, :].T
-            qkv_ref[:, pl.ds(pl.multiple_of(2 * qk + bit * head, head), head)] = ref[o_blk + qk :, :].T
+    def kernel(pos_ref, own_ref, first_ref, second_ref, out_ref, qkv_ref):
+        for chosen, idx, ref in sources(pos_ref, own_ref, first_ref, second_ref):
+
+            @pl.when(chosen)
+            def _(idx=idx, ref=ref):
+                bit = 1 - pos_ref[2] if idx else pos_ref[2]
+                out_ref[pl.ds(pl.multiple_of(bit * o_blk, o_blk), o_blk), :] = ref[:o_blk, :]
+                qkv_ref[:, pl.ds(pl.multiple_of(bit * qk, qk), qk)] = ref[o_blk : o_blk + qk, :].T
+                qkv_ref[:, pl.ds(pl.multiple_of(2 * qk + bit * head, head), head)] = ref[o_blk + qk :, :].T
 
     def whole(*shape):
         return pl.BlockSpec(shape, lambda n, pos: (0, 0))
@@ -595,12 +602,12 @@
     shapes = ((2 * o_blk, cols), (cols, 2 * (qk + head)))
     return pl.pallas_call(
         kernel,
-        grid_spec=pltpu.PrefetchScalarGridSpec(num_scalar_prefetch=1, grid=(1,), in_specs=[whole(rows, cols)] * 2, out_specs=[whole(*shape) for shape in shapes]),
+        grid_spec=pltpu.PrefetchScalarGridSpec(num_scalar_prefetch=1, grid=(1,), in_specs=[whole(rows, cols)] * 3, out_specs=[whole(*shape) for shape in shapes]),
         out_shape=[jax.ShapeDtypeStruct(shape, F32) for shape in shapes],
         compiler_params=params(),
         cost_estimate=cost(2e9, 16 * rows * cols),
         name="p_attn",
-    )(pos, first, second)
+    )(pos, own, first, second)
 
 
 def after(val, *earlier):
@@ -623,11 +630,11 @@
     return lax.ppermute(val, "y", [(src, src ^ 1) for src in range(NY)])
 
 
-def turn(val, flip):
+def turn(val, flip, home):
     def place_of(y_pos, c_pos):
         return y_pos * NC + c_pos
 
-    pairs = [(place_of(2 * a + b, c), place_of(2 * c + (b ^ flip), a)) for a in range(2) for b in range(2) for c in range(NC)]
+    pairs = [(place_of(2 * a + b, c), place_of(2 * c + (b ^ flip), a)) for a in range(2) for b in range(2) for c in range(NC) if home or flip or a != c]
     return lax.ppermute(val, ("y", "c"), pairs)
 
 
@@ -662,7 +669,7 @@
         c_pos = lax.axis_index("c")
         even_y = y_pos % 2 == 0
         first_c = c_pos == 0
-        pos = jnp.stack([z_pos, c_pos, y_pos % 2]).astype(jnp.int32)
+        pos = jnp.stack([z_pos, c_pos, y_pos % 2, y_pos // 2 == c_pos]).astype(jnp.int32)
         chunk = x_in.shape[1]
         head = 2 * rope_cos.shape[1]
         seq = rope_cos.shape[0]
@@ -671,7 +678,7 @@
         qkv_blk = o_blk + head
 
         def gather_rows(blocks):
-            return [turn(jnp.where(even_y, blocks[flip], blocks[1 - flip]), flip) for flip in range(2)]
+            return [turn(jnp.where(even_y, blocks[flip], blocks[1 - flip]), flip, True) for flip in range(2)]
 
         def gather_weight(piece):
             left, right = [], []
@@ -700,7 +707,7 @@
             direct, passed, own = state[:3]
             first = own[0] + after(passed[0], *earlier) + direct[1]
             second = own[1] + direct[0] + passed[1]
-            return turn(first, 0), turn(second, 1)
+            return first, turn(first, 0, False), turn(second, 1, False)
 
         def my_rows(val, mine):
             return lax.dynamic_slice_in_dim(val, (c_pos if mine else 1 - c_pos) * seq, seq, axis=0)
@@ -760,22 +767,19 @@
         g_gate = grad_start([(d_gate_up_t, d_gate_up_recv, h_all, h_recv, ff_blk, 0)], *g_act[3])
         d_own, d_other = attn_post(after(pos, g_gate[3][0]), d_queries, keep, got, cos_tab, sin_tab)
         d_got = swap_c(d_other)
-        half = chunk // 2
-        dh_low = nt_pieces(pos, [d_gate_up, d_own, d_got], wf_parts, chunk, 0, half)
-        d_h_low = lax.psum_scatter(dh_low, ("y", "x"), scatter_dimension=0, tiled=True)
-        g_gate = grad_pass(g_gate, dh_low)
+        dh_part = nt_pieces(pos, [d_gate_up, d_own, d_got], wf_parts, chunk, 0, chunk)
+        d_h = lax.psum_scatter(dh_part, ("y", "x"), scatter_dimension=0, tiled=True)
+        g_gate = grad_pass(g_gate, dh_part)
         g_up = grad_start([(d_gate_up_t, d_gate_up_recv, h_all, h_recv, ff_blk, 1)], *g_gate[3])
-        dh_high = nt_pieces(after(pos, g_up[3][0]), [d_gate_up, d_own, d_got], wf_parts, chunk, half, half)
-        d_h_high = lax.psum_scatter(dh_high, ("y", "x"), scatter_dimension=0, tiled=True)
-        b_act = grad_back(g_act, dh_high)
-        d_h = jnp.concatenate([d_h_low, d_h_high], axis=0).astype(BF16)
+        b_act = grad_back(g_act, g_up[3][0])
+        d_h = d_h.astype(BF16)
         dx_out = (dy_in[0].astype(F32) + norm_pull(d_h.astype(F32))[0]).astype(BF16)[None]
 
         attn_t = both_rows(attn_own, attn_got).T
         d_qkv_t = both_rows(d_own, d_got).T
         attn_recv = swap_c(attn_t)
         d_qkv_recv = swap_c(d_qkv_t)
-        g_attn = grad_start([(attn_t, attn_recv, dy_all, dy_recv, o_blk, 0), (d_qkv_t, d_qkv_recv, h_all, h_recv, qkv_blk, 0)], dh_high)
+        g_attn = grad_start([(attn_t, attn_recv, dy_all, dy_recv, o_blk, 0), (d_qkv_t, d_qkv_recv, h_all, h_recv, qkv_blk, 0)], g_up[3][0])
         g_up = grad_pass(g_up, g_attn[3][0])
         g_attn = grad_pass(g_attn)
         b_gate = grad_back(g_gate)

time: 690 us -> 643 us (0.932)
  waiting for transfers between devices: 298 us -> 265 us
  starting transfers between devices: 112 us -> 101 us
    reduce_scatter x1, waiting for transfers between devices: 20.4 us -> 0.02 us  [layer(): lax.psum_scatter(y_part, ('y', 'x'), scatter_dimension=0, tiled=True)]
    ppermute x36, waiting for transfers between devices: 166 us -> 154 us  [hop_z(): return lax.ppermute(val, 'z', ring(step, NZ))]
    pallas_call x3 -> x2, Pallas kernels: 48 us -> 43.7 us  [nt_pieces(): pl.pallas_call(functools.partial(nt_kernel, keys, sides, first_row), grid...]
  transfers between devices with their start and end apart: 82 -> 81, of which waited for: 35 -> 32; matrix products, arithmetic and copies ran while one was open for 6% -> 7% of each run, Pallas kernels for 25% -> 25%
where the time goes in v6:
time: 643 us; the launch traced here: 635 us
  waiting for transfers between devices  265 us (41%)
  Pallas kernels  194 us (30%)
  starting transfers between devices  101 us (16%)
  other arithmetic  40 us (6%)
  local copies, waits for them, and re-layouts  20.2 us (3%)
  between operations  15.1 us (2%)
    ppermute x36, waiting for transfers between devices, hop_z(): return lax.ppermute(val, 'z', ring(step, NZ))  154 us
    ppermute x12, waiting for transfers between devices, turn(): return lax.ppermute(val, ('y', 'c'), pairs)  89.3 us
    pallas_call x4, Pallas kernels, grad_pieces(): pl.pallas_call(functools.partial(grad_kernel, heights), grid_spec=pltpu.P...  53 us
    pallas_call x2, Pallas kernels, nn_pieces(): pl.pallas_call(functools.partial(nn_kernel, keys, 2, len(widths), tile),...  45.1 us
    pallas_call x2, Pallas kernels, nt_pieces(): pl.pallas_call(functools.partial(nt_kernel, keys, sides, first_row), grid...  43.7 us
    ppermute x36, starting transfers between devices, hop_z(): return lax.ppermute(val, 'z', ring(step, NZ))  42.9 us
    ppermute x12, starting transfers between devices, turn(): return lax.ppermute(val, ('y', 'c'), pairs)  34.1 us
    ppermute x26, starting transfers between devices, swap_c(): return lax.ppermute(val, 'c', [(0, 1), (1, 0)])  20.4 us
  transfers between devices with their start and end apart: 81, of which 32 were waited for; matrix products, arithmetic and copies ran while one was open for 7% of the time, Pallas kernels for 25%

profile of v6, /device:TPU:1, one launch (start us, length us, event | category | flops | bytes accessed | tf_op | source)
XLA Modules:
  0.0 634.8 jit_solution(5559614850156539468)
XLA Ops:
  12.5 4.1 collective-permute-start.1
  22.4 18.9 %collective-permute-done.1.refs_1_.refs_4_ = bf16[256,2176]{1,0:T(8,128)(2,1)S(1)} collective-permute-done((bf16[256,2176]{1,0:T(8,128)(2,1)}, bf16[256,2176]{1,0:T(8,128)(2,1)S(1)}, u32[]{:S(2)}, u32[]{:S(2)}) %collective-permute-start.1) | collective-permute-done | bytes 1114144 | tf_op jit(solution)/shard_map/ppermute | solution.py:638
  51.5 4.4 collective-permute-done.21.refs_4_.refs_1_
  58.5 15.9 %collective-permute-done.20.refs_3_.refs_0_ = bf16[256,1152]{1,0:T(8,128)(2,1)} collective-permute-done((bf16[256,1152]{1,0:T(8,128)(2,1)S(1)}, bf16[256,1152]{1,0:T(8,128)(2,1)}, u32[]{:S(2)}, u32[]{:S(2)}) %collective-permute-start.20) | collective-permute-done | bytes 589856 | tf_op jit(solution)/shard_map/ppermute | solution.py:638
  74.3 3.3 collective-permute-start.4
  79.4 16.7 %collective-permute-done.8.refs_8_.refs_15_ = bf16[256,2176]{1,0:T(8,128)(2,1)S(1)} collective-permute-done((bf16[256,2176]{1,0:T(8,128)(2,1)S(1)}, bf16[256,2176]{1,0:T(8,128)(2,1)S(1)}, u32[]{:S(2)}, u32[]{:S(2)}) %collective-permute-start.8) | collective-permute-done | bytes 1114144 | tf_op jit(solution)/shard_map/ppermute | solution.py:622
  96.4 5.6 collective-permute-done.4.refs_4_.refs_7_
  102.7 16.8 %collective-permute-done.13.refs_13_.refs_12_ = bf16[256,2176]{1,0:T(8,128)(2,1)S(1)} collective-permute-done((bf16[256,2176]{1,0:T(8,128)(2,1)S(1)}, bf16[256,2176]{1,0:T(8,128)(2,1)S(1)}, u32[]{:S(2)}, u32[]{:S(2)}) %collective-permute-start.13) | collective-permute-done | bytes 1114144 | tf_op jit(solution)/shard_map/ppermute | solution.py:622
  127.2 27.4 %shard_map.153 = (bf16[1024,1792]{1,0:T(8,128)(2,1)}, bf16[1024,384]{1,0:T(8,128)(2,1)}) custom-call(s32[4]{0:T(128)} %pad_add_fusion.pos_ref, bf16[1024,4096]{1,0:T(8,128)(2,1)} %all-gather.3.cloned.1.call-done.acts_ref.in_ref.refs_2_.refs_6_, bf16[256,2176]{1,0:T(8,128)(2,1)} %copy-done.3, bf16[256,2176]{1,0:T(8,128)(2,1)} %copy-done.2, ...), custom_call_target="tpu_custom_call" | custom-call | flops 912680576 | bytes 26214400 | tf_op jit(solution)/shard_map/pallas_call | solution.py:330
  161.2 6.8 %collective-permute-done.18.other_third_ref = bf16[512,128]{1,0:T(8,128)(2,1)S(1)} collective-permute-done((bf16[512,128]{1,0:T(8,128)(2,1)S(1)}, bf16[512,128]{1,0:T(8,128)(2,1)S(1)}, u32[]{:S(2)}, u32[]{:S(2)}) %collective-permute-start.18) | collective-permute-done | bytes 131104 | tf_op jit(solution)/shard_map/ppermute | solution.py:643
  168.3 5.3 collective-permute-done.17.own_third_ref
  175.8 4.8 act_fwd.1
  180.6 4.3 shard_map.154
  185.0 5.7 shard_map.155
  198.3 16.9 %shard_map.156 = f32[1024,4096]{1,0:T(8,128)} custom-call(s32[4]{0:T(128)} %pad_add_fusion.pos_ref, bf16[16,64,896]{2,1,0:T(8,128)(2,1)} %bitcast.30, bf16[8,64,256]{2,1,0:T(8,128)(2,1)} %bitcast.33, bf16[8,64,256]{2,1,0:T(8,128)(2,1)} %bitcast.34, bf16[256,1152]{1,0:T(8,128)(2,1)} %collective-permute-done.20.refs_3_.refs_0_, ...), custom_call_target="tpu_custom_call" | custom-call | flops 483183808 | bytes 26214400 | tf_op jit(solution)/shard_map/pallas_call | solution.py:424
  215.2 4.1 shard_map.157
  219.9 8.5 %collective-permute-start.42 = (bf16[1024,2048]{1,0:T(8,128)(2,1)}, bf16[1024,2048]{1,0:T(8,128)(2,1)}, u32[]{:S(2)}, u32[]{:S(2)}) collective-permute-start(bf16[1024,2048]{1,0:T(8,128)(2,1)} %shard_map.154), channel_id=1, source_target_pairs={{0,1},{1,0},{2,3},{3,2},{4,5},{5,4},{6,7},{7,6},{8,9},{9,8},{10,11... | collective-permute-start | bytes 12582920 | tf_op jit(solution)/shard_map/ppermute | solution.py:626
  229.5 13.2 %grad.4 = (f32[896,256]{1,0:T(8,128)}, f32[896,256]{1,0:T(8,128)}, f32[896,256]{1,0:T(8,128)}, f32[896,256]{1,0:T(8,128)}, f32[896,256]{1,0:T(8,128)}, /*index=5...) custom-call(s32[4]{0:T(128)} %pad_add_fusion.pos_ref, bf16[896,1024]{1,0:T(8,128)(2,1)} %get-tuple-element.80.refs_0_, ...), custom_call_target="tpu_custom_call" | custom-call | flops 375809632 | bytes 8388608 | tf_op jit(solution)/shard_map/grad/pallas_call | solution.py:537
  242.7 17.7 %shard_map.158 = (bf16[1024,896]{1,0:T(8,128)(2,1)}, bf16[1024,256]{1,0:T(8,128)(2,1)}) custom-call(s32[4]{0:T(128)} %pad_add_fusion.pos_ref, bf16[1024,4096]{1,0:T(8,128)(2,1)} %all-gather.5.cloned.1.call-done.in_ref.refs_2_.acts_ref, bf16[256,1152]{1,0:T(8,128)(2,1)} %collective-permute-done.20.refs_3_.refs_0_, ...), custom_call_target="tpu_custom_call" | custom-call | flops 483183808 | bytes 17825792 | tf_op jit(solution)/shard_map/pallas_call | solution.py:330
  260.4 6.9 %act_bwd.1 = (bf16[1024,1792]{1,0:T(8,128)(2,1)}, bf16[1792,1024]{1,0:T(8,128)(2,1)}) custom-call(bf16[1024,1792]{1,0:T(8,128)(2,1)} %get-tuple-element.79.ab_ref, bf16[1024,896]{1,0:T(8,128)(2,1)} %get-tuple-element.93.du_ref), custom_call_target="tpu_custom_call" | custom-call | flops 400000000 | bytes 14000000 | tf_op jit(solution)/shard_map/act_bwd/pallas_call | solution.py:260
  275.0 8.1 %shard_map.159 = (bf16[2,512,256]{2,1,0:T(8,128)(2,1)}, f32[2,512,128]{2,1,0:T(8,128)}, f32[2,512,128]{2,1,0:T(8,128)}) custom-call(s32[4]{0:T(128)} %pad_add_fusion.pos_ref, bf16[2,512,512]{2,1,0:T(8,128)(2,1)} %get-tuple-element.99.seq_ref, bf16[1024,256]{1,0:T(8,128)(2,1)} %get-tuple-element.100.own_ref, bf16[512,256]{1,0:T(8,128)(2,1)} %copy-done.55, ...), custom_call_target="tpu_custom_call" | custom-call | flops 800000000 | bytes 4000000 | tf_op jit(solution)/shard_map/pallas_call | solution.py:142
  284.4 6.2 collective-permute-done.38
  295.3 13.1 %grad.5 = (f32[896,256]{1,0:T(8,128)}, f32[896,256]{1,0:T(8,128)}, f32[896,256]{1,0:T(8,128)}, f32[896,256]{1,0:T(8,128)}, f32[896,256]{1,0:T(8,128)}, /*index=5...) custom-call(s32[4]{0:T(128)} %pad_add_fusion.pos_ref, bf16[1792,1024]{1,0:T(8,128)(2,1)} %get-tuple-element.97.refs_0_, ...), custom_call_target="tpu_custom_call" | custom-call | flops 375809632 | bytes 8388608 | tf_op jit(solution)/shard_map/grad/pallas_call | solution.py:537
  308.5 3.2 shard_map.160
  317.1 26.8 %shard_map.161 = f32[1024,4096]{1,0:T(8,128)} custom-call(s32[4]{0:T(128)} %pad_add_fusion.pos_ref, bf16[16,64,1792]{2,1,0:T(8,128)(2,1)} %bitcast.28, bf16[8,64,384]{2,1,0:T(8,128)(2,1)} %bitcast.31, bf16[8,64,384]{2,1,0:T(8,128)(2,1)} %bitcast.32, bf16[256,2176]{1,0:T(8,128)(2,1)} %copy-done.3, bf16[256,2176]{1,0:T(8,128)(2,1)} %copy-done.2, ...), custom_call_target="tpu_custom_call" | custom-call | flops 912680576 | bytes 34603008 | tf_op jit(solution)/shard_map/pallas_call | solution.py:424
  350.1 17.6 %collective-permute-done.74 = f32[896,256]{1,0:T(8,128)S(1)} collective-permute-done((f32[896,256]{1,0:T(8,128)}, f32[896,256]{1,0:T(8,128)S(1)}, u32[]{:S(2)}, u32[]{:S(2)}) %collective-permute-start.74) | collective-permute-done | bytes 917536 | tf_op jit(solution)/shard_map/ppermute | solution.py:622
  374.6 11.7 %collective-permute-done.72 = f32[896,256]{1,0:T(8,128)} collective-permute-done((f32[896,256]{1,0:T(8,128)}, f32[896,256]{1,0:T(8,128)}, u32[]{:S(2)}, u32[]{:S(2)}) %collective-permute-start.72) | collective-permute-done | bytes 917536 | tf_op jit(solution)/shard_map/ppermute | solution.py:622
  388.9 3.4 collective-permute-start.66
  392.4 13.6 %collective-permute-done.46 = f32[896,256]{1,0:T(8,128)} collective-permute-done((f32[896,256]{1,0:T(8,128)}, f32[896,256]{1,0:T(8,128)}, u32[]{:S(2)}, u32[]{:S(2)}) %collective-permute-start.46) | collective-permute-done | bytes 917536 | tf_op jit(solution)/shard_map/ppermute | solution.py:622
  410.4 13.7 %grad.6 = (f32[896,256]{1,0:T(8,128)}, f32[896,256]{1,0:T(8,128)}, f32[896,256]{1,0:T(8,128)}, f32[896,256]{1,0:T(8,128)}, f32[896,256]{1,0:T(8,128)}, /*index=5...) custom-call(s32[4]{0:T(128)} %pad_add_fusion.pos_ref, bf16[1792,1024]{1,0:T(8,128)(2,1)} %get-tuple-element.97.refs_0_, ...), custom_call_target="tpu_custom_call" | custom-call | flops 375809632 | bytes 8388608 | tf_op jit(solution)/shard_map/grad/pallas_call | solution.py:537
  428.7 13.0 %grad.7 = (f32[640,256]{1,0:T(8,128)}, f32[640,256]{1,0:T(8,128)}, f32[640,256]{1,0:T(8,128)}, f32[640,256]{1,0:T(8,128)}, f32[640,256]{1,0:T(8,128)}, /*index=5...) custom-call(s32[4]{0:T(128)} %pad_add_fusion.pos_ref, bf16[256,1024]{1,0:T(8,128)(2,1)} %copy-done.18, ...), custom_call_target="tpu_custom_call" | custom-call | flops 268435456 | bytes 8388608 | tf_op jit(solution)/shard_map/grad/pallas_call | solution.py:537
  444.8 3.9 collective-permute-done.65
  449.9 18.5 %collective-permute-done.47 = f32[896,256]{1,0:T(8,128)} collective-permute-done((f32[896,256]{1,0:T(8,128)}, f32[896,256]{1,0:T(8,128)}, u32[]{:S(2)}, u32[]{:S(2)}) %collective-permute-start.47) | collective-permute-done | bytes 917536 | tf_op jit(solution)/shard_map/ppermute | solution.py:622
  471.2 11.3 %collective-permute-done.57 = f32[640,256]{1,0:T(8,128)S(1)} collective-permute-done((f32[640,256]{1,0:T(8,128)}, f32[640,256]{1,0:T(8,128)S(1)}, u32[]{:S(2)}, u32[]{:S(2)}) %collective-permute-start.57) | collective-permute-done | bytes 655392 | tf_op jit(solution)/shard_map/ppermute | solution.py:622
  487.5 8.1 %collective-permute-done.62 = f32[640,256]{1,0:T(8,128)S(1)} collective-permute-done((f32[640,256]{1,0:T(8,128)}, f32[640,256]{1,0:T(8,128)S(1)}, u32[]{:S(2)}, u32[]{:S(2)}) %collective-permute-start.62) | collective-permute-done | bytes 655392 | tf_op jit(solution)/shard_map/ppermute | solution.py:622
  501.0 14.3 %collective-permute-done.69 = f32[896,256]{1,0:T(8,128)S(1)} collective-permute-done((f32[896,256]{1,0:T(8,128)S(1)}, f32[896,256]{1,0:T(8,128)S(1)}, u32[]{:S(2)}, u32[]{:S(2)}) %collective-permute-start.69) | collective-permute-done | bytes 917536 | tf_op jit(solution)/shard_map/ppermute | solution.py:622
  515.2 8.1 %collective-permute-start.73 = (f32[896,256]{1,0:T(8,128)S(1)}, f32[896,256]{1,0:T(8,128)S(1)}, u32[]{:S(2)}, u32[]{:S(2)}) collective-permute-start(f32[896,256]{1,0:T(8,128)S(1)} %add_add_fusion.2.own_ref), channel_id=1, source_target_pairs={{1,16},{9,24},{16,1},{24,9},{3,18},{11,26},{18,3},{26,11},{5,20},{... | collective-permute-start | bytes 2752520 | tf_op jit(solution)/shard_map/ppermute | solution.py:638
  528.5 9.6 %collective-permute-done.61 = f32[640,256]{1,0:T(8,128)S(1)} collective-permute-done((f32[640,256]{1,0:T(8,128)S(1)}, f32[640,256]{1,0:T(8,128)S(1)}, u32[]{:S(2)}, u32[]{:S(2)}) %collective-permute-start.61) | collective-permute-done | bytes 655392 | tf_op jit(solution)/shard_map/ppermute | solution.py:622
  538.1 6.7 %collective-permute-start.67 = (f32[896,256]{1,0:T(8,128)}, f32[896,256]{1,0:T(8,128)}, u32[]{:S(2)}, u32[]{:S(2)}) collective-permute-start(f32[896,256]{1,0:T(8,128)} %add_add_fusion.4.own_ref), channel_id=1, source_target_pairs={{1,16},{9,24},{16,1},{24,9},{3,18},{11,26},{18,3},{26,11},{5,20},{... | collective-permute-start | bytes 2752520 | tf_op jit(solution)/shard_map/ppermute | solution.py:638
  546.1 12.2 %collective-permute-done.73.first_ref = f32[896,256]{1,0:T(8,128)S(1)} collective-permute-done((f32[896,256]{1,0:T(8,128)S(1)}, f32[896,256]{1,0:T(8,128)S(1)}, u32[]{:S(2)}, u32[]{:S(2)}) %collective-permute-start.73) | collective-permute-done | bytes 917536 | tf_op jit(solution)/shard_map/ppermute | solution.py:638
  563.6 3.7 shard_map.164
  569.9 2.7 collective-permute-start.60
  574.7 9.0 %collective-permute-done.67.first_ref = f32[896,256]{1,0:T(8,128)} collective-permute-done((f32[896,256]{1,0:T(8,128)}, f32[896,256]{1,0:T(8,128)}, u32[]{:S(2)}, u32[]{:S(2)}) %collective-permute-start.67) | collective-permute-done | bytes 917536 | tf_op jit(solution)/shard_map/ppermute | solution.py:638
  583.7 4.0 shard_map.163
  587.7 27.1 %collective-permute-done.52.first_ref = f32[896,256]{1,0:T(8,128)} collective-permute-done((f32[896,256]{1,0:T(8,128)}, f32[896,256]{1,0:T(8,128)}, u32[]{:S(2)}, u32[]{:S(2)}) %collective-permute-start.52) | collective-permute-done | bytes 917536 | tf_op jit(solution)/shard_map/ppermute | solution.py:638
  614.9 4.0 shard_map.162
  620.8 2.7 fusion.8
  624.4 3.5 p_attn.1
  (304 shorter events, 132.6 us)
Async XLA Ops:
  7.2 120.0 %all-gather.3.cloned.1.call-start = ((), (), s32[]{:S(2)}) async-start(), calls=%async_computation.2 | async-start | bytes 8912896 | tf_op jit(solution)/shard_map/all_gather | solution.py:737
  12.5 28.8 %collective-permute-start.1 = (bf16[256,2176]{1,0:T(8,128)(2,1)}, bf16[256,2176]{1,0:T(8,128)(2,1)S(1)}, u32[]{:S(2)}, u32[]{:S(2)}) collective-permute-start(bf16[256,2176]{1,0:T(8,128)(2,1)} %get-tuple-element.146), channel_id=1, source_target_pairs={{0,8},{1,24},{8,0},{9,16},{16,9},{17,25},{24,1},{25,17},{2,10},{3,... | collective-permute-start | bytes 3342344 | tf_op jit(solution)/shard_map/ppermute | solution.py:638
  16.6 25.7 %collective-permute-start = (bf16[256,2176]{1,0:T(8,128)(2,1)}, bf16[256,2176]{1,0:T(8,128)(2,1)S(1)}, u32[]{:S(2)}, u32[]{:S(2)}) collective-permute-start(bf16[256,2176]{1,0:T(8,128)(2,1)} %get-tuple-element.147), channel_id=1, source_target_pairs={{0,0},{1,16},{8,8},{9,24},{16,1},{17,17},{24,9},{25,25},{2,2},{3,1... | collective-permute-start | bytes 3342344 | tf_op jit(solution)/shard_map/ppermute | solution.py:638
  42.3 172.9 %all-gather.5.cloned.1.call-start = ((), (), s32[]{:S(2)}) async-start(), calls=%async_computation.4 | async-start | bytes 8912896 | tf_op jit(solution)/shard_map/all_gather | solution.py:738
  43.0 575.9 %reduce-scatter.5.cloned.1.call-start = ((), (), s32[]{:S(2)}) async-start(), calls=%async_computation.5 | async-start | bytes 17825792 | tf_op jit(solution)/shard_map/reduce_scatter | solution.py:771
  47.7 29.9 %collective-permute-start.9 = (bf16[256,2176]{1,0:T(8,128)(2,1)S(1)}, bf16[256,2176]{1,0:T(8,128)(2,1)S(1)}, u32[]{:S(2)}, u32[]{:S(2)}) collective-permute-start(bf16[256,2176]{1,0:T(8,128)(2,1)S(1)} %collective-permute-done.1.refs_1_.refs_4_), channel_id=1, source_target_pairs={{0,32},{32,64},{64,96},{96,0},{1,33},{33,65},{65,97},{97,1},{2,34}... | collective-permute-start | bytes 3342344 | tf_op jit(solution)/shard_map/ppermute | solution.py:622
  49.4 28.3 %collective-permute-start.5 = (bf16[256,2176]{1,0:T(8,128)(2,1)S(1)}, bf16[256,2176]{1,0:T(8,128)(2,1)S(1)}, u32[]{:S(2)}, u32[]{:S(2)}) collective-permute-start(bf16[256,2176]{1,0:T(8,128)(2,1)S(1)} %collective-permute-done.1.refs_1_.refs_4_), channel_id=1, source_target_pairs={{0,96},{32,0},{64,32},{96,64},{1,97},{33,1},{65,33},{97,65},{2,98}... | collective-permute-start | bytes 3342344 | tf_op jit(solution)/shard_map/ppermute | solution.py:622
  51.5 26.7 %collective-permute-start.3 = (bf16[256,2176]{1,0:T(8,128)(2,1)S(1)}, bf16[256,2176]{1,0:T(8,128)(2,1)S(1)}, u32[]{:S(2)}, u32[]{:S(2)}) collective-permute-start(bf16[256,2176]{1,0:T(8,128)(2,1)S(1)} %collective-permute-done.1.refs_1_.refs_4_), channel_id=1, source_target_pairs={{0,1},{1,0},{2,3},{3,2},{4,5},{5,4},{6,7},{7,6},{8,9},{9,8},{10,11... | collective-permute-start | bytes 3342344 | tf_op jit(solution)/shard_map/ppermute | solution.py:626
  51.5 44.5 %collective-permute-start.8 = (bf16[256,2176]{1,0:T(8,128)(2,1)S(1)}, bf16[256,2176]{1,0:T(8,128)(2,1)S(1)}, u32[]{:S(2)}, u32[]{:S(2)}) collective-permute-start(bf16[256,2176]{1,0:T(8,128)(2,1)S(1)} %collective-permute-done.refs_0_.refs_3_), channel_id=1, source_target_pairs={{0,32},{32,64},{64,96},{96,0},{1,33},{33,65},{65,97},{97,1},{2,34}... | collective-permute-start | bytes 3342344 | tf_op jit(solution)/shard_map/ppermute | solution.py:622
  74.3 27.7 %collective-permute-start.4 = (bf16[256,2176]{1,0:T(8,128)(2,1)S(1)}, bf16[256,2176]{1,0:T(8,128)(2,1)S(1)}, u32[]{:S(2)}, u32[]{:S(2)}) collective-permute-start(bf16[256,2176]{1,0:T(8,128)(2,1)S(1)} %collective-permute-done.refs_0_.refs_3_), channel_id=1, source_target_pairs={{0,96},{32,0},{64,32},{96,64},{1,97},{33,1},{65,33},{97,65},{2,98}... | collective-permute-start | bytes 3342344 | tf_op jit(solution)/shard_map/ppermute | solution.py:622
  78.2 41.3 %collective-permute-start.13 = (bf16[256,2176]{1,0:T(8,128)(2,1)S(1)}, bf16[256,2176]{1,0:T(8,128)(2,1)S(1)}, u32[]{:S(2)}, u32[]{:S(2)}) collective-permute-start(bf16[256,2176]{1,0:T(8,128)(2,1)S(1)} %collective-permute-done.5.refs_5_.refs_8_), channel_id=1, source_target_pairs={{0,96},{32,0},{64,32},{96,64},{1,97},{33,1},{65,33},{97,65},{2,98}... | collective-permute-start | bytes 3342344 | tf_op jit(solution)/shard_map/ppermute | solution.py:622
  120.0 36.3 %collective-permute-start.33 = (bf16[256,1152]{1,0:T(8,128)(2,1)}, bf16[256,1152]{1,0:T(8,128)(2,1)}, u32[]{:S(2)}, u32[]{:S(2)}) collective-permute-start(bf16[256,1152]{1,0:T(8,128)(2,1)} %collective-permute-done.21.refs_4_.refs_1_), channel_id=1, source_target_pairs={{0,32},{32,64},{64,96},{96,0},{1,33},{33,65},{65,97},{97,1},{2,34}... | collective-permute-start | bytes 1769480 | tf_op jit(solution)/shard_map/ppermute | solution.py:622
  121.7 37.3 %collective-permute-start.25 = (bf16[256,1152]{1,0:T(8,128)(2,1)}, bf16[256,1152]{1,0:T(8,128)(2,1)}, u32[]{:S(2)}, u32[]{:S(2)}) collective-permute-start(bf16[256,1152]{1,0:T(8,128)(2,1)} %collective-permute-done.21.refs_4_.refs_1_), channel_id=1, source_target_pairs={{0,96},{32,0},{64,32},{96,64},{1,97},{33,1},{65,33},{97,65},{2,98}... | collective-permute-start | bytes 1769480 | tf_op jit(solution)/shard_map/ppermute | solution.py:622
  124.2 36.0 %collective-permute-start.23 = (bf16[256,1152]{1,0:T(8,128)(2,1)}, bf16[256,1152]{1,0:T(8,128)(2,1)}, u32[]{:S(2)}, u32[]{:S(2)}) collective-permute-start(bf16[256,1152]{1,0:T(8,128)(2,1)} %collective-permute-done.21.refs_4_.refs_1_), channel_id=1, source_target_pairs={{0,1},{1,0},{2,3},{3,2},{4,5},{5,4},{6,7},{7,6},{8,9},{9,8},{10,11... | collective-permute-start | bytes 1769480 | tf_op jit(solution)/shard_map/ppermute | solution.py:626
  126.4 34.5 %collective-permute-start.28 = (bf16[256,1152]{1,0:T(8,128)(2,1)}, bf16[256,1152]{1,0:T(8,128)(2,1)}, u32[]{:S(2)}, u32[]{:S(2)}) collective-permute-start(bf16[256,1152]{1,0:T(8,128)(2,1)} %collective-permute-done.20.refs_3_.refs_0_), channel_id=1, source_target_pairs={{0,32},{32,64},{64,96},{96,0},{1,33},{33,65},{65,97},{97,1},{2,34}... | collective-permute-start | bytes 1769480 | tf_op jit(solution)/shard_map/ppermute | solution.py:622
  156.3 35.4 %collective-permute-start.24 = (bf16[256,1152]{1,0:T(8,128)(2,1)}, bf16[256,1152]{1,0:T(8,128)(2,1)}, u32[]{:S(2)}, u32[]{:S(2)}) collective-permute-start(bf16[256,1152]{1,0:T(8,128)(2,1)} %collective-permute-done.20.refs_3_.refs_0_), channel_id=1, source_target_pairs={{0,96},{32,0},{64,32},{96,64},{1,97},{33,1},{65,33},{97,65},{2,98}... | collective-permute-start | bytes 1769480 | tf_op jit(solution)/shard_map/ppermute | solution.py:622
  160.9 31.7 %collective-permute-start.22 = (bf16[256,1152]{1,0:T(8,128)(2,1)}, bf16[256,1152]{1,0:T(8,128)(2,1)}, u32[]{:S(2)}, u32[]{:S(2)}) collective-permute-start(bf16[256,1152]{1,0:T(8,128)(2,1)} %collective-permute-done.20.refs_3_.refs_0_), channel_id=1, source_target_pairs={{0,1},{1,0},{2,3},{3,2},{4,5},{5,4},{6,7},{7,6},{8,9},{9,8},{10,11... | collective-permute-start | bytes 1769480 | tf_op jit(solution)/shard_map/ppermute | solution.py:626
  219.9 75.4 %collective-permute-start.42 = (bf16[1024,2048]{1,0:T(8,128)(2,1)}, bf16[1024,2048]{1,0:T(8,128)(2,1)}, u32[]{:S(2)}, u32[]{:S(2)}) collective-permute-start(bf16[1024,2048]{1,0:T(8,128)(2,1)} %shard_map.154), channel_id=1, source_target_pairs={{0,1},{1,0},{2,3},{3,2},{4,5},{5,4},{6,7},{7,6},{8,9},{9,8},{10,11... | collective-permute-start | bytes 12582920 | tf_op jit(solution)/shard_map/ppermute | solution.py:626
  267.3 28.0 %collective-permute-start.41 = (bf16[1792,1024]{1,0:T(8,128)(2,1)}, bf16[1792,1024]{1,0:T(8,128)(2,1)}, u32[]{:S(2)}, u32[]{:S(2)}) collective-permute-start(bf16[1792,1024]{1,0:T(8,128)(2,1)} %get-tuple-element.97.refs_0_), channel_id=1, source_target_pairs={{0,1},{1,0},{2,3},{3,2},{4,5},{5,4},{6,7},{7,6},{8,9},{9,8},{10,11... | collective-permute-start | bytes 11010056 | tf_op jit(solution)/shard_map/ppermute | solution.py:626
  344.0 276.7 %reduce-scatter.3.cloned.1.call-start = ((), (), s32[]{:S(2)}) async-start(), calls=%async_computation.3 | async-start | bytes 17825792 | tf_op jit(solution)/shard_map/reduce_scatter | solution.py:754
  348.6 37.7 %collective-permute-start.72 = (f32[896,256]{1,0:T(8,128)}, f32[896,256]{1,0:T(8,128)}, u32[]{:S(2)}, u32[]{:S(2)}) collective-permute-start(f32[896,256]{1,0:T(8,128)} %get-tuple-element.143), channel_id=1, source_target_pairs={{0,96},{32,0},{64,32},{96,64},{1,97},{33,1},{65,33},{97,65},{2,98}... | collective-permute-start | bytes 2752520 | tf_op jit(solution)/shard_map/ppermute | solution.py:622
  348.6 40.4 %collective-permute-start.45 = (f32[896,256]{1,0:T(8,128)}, f32[896,256]{1,0:T(8,128)}, u32[]{:S(2)}, u32[]{:S(2)}) collective-permute-start(f32[896,256]{1,0:T(8,128)} %get-tuple-element.113), channel_id=1, source_target_pairs={{0,32},{32,64},{64,96},{96,0},{1,33},{33,65},{65,97},{97,1},{2,34}... | collective-permute-start | bytes 2752520 | tf_op jit(solution)/shard_map/ppermute | solution.py:622
  367.7 56.5 %collective-permute-start.71 = (f32[896,256]{1,0:T(8,128)}, f32[896,256]{1,0:T(8,128)}, u32[]{:S(2)}, u32[]{:S(2)}) collective-permute-start(f32[896,256]{1,0:T(8,128)} %add.115), channel_id=1, source_target_pairs={{0,32},{32,64},{64,96},{96,0},{1,33},{33,65},{65,97},{97,1},{2,34}... | collective-permute-start | bytes 2752520 | tf_op jit(solution)/shard_map/ppermute | solution.py:622
  367.7 38.3 %collective-permute-start.46 = (f32[896,256]{1,0:T(8,128)}, f32[896,256]{1,0:T(8,128)}, u32[]{:S(2)}, u32[]{:S(2)}) collective-permute-start(f32[896,256]{1,0:T(8,128)} %get-tuple-element.116), channel_id=1, source_target_pairs={{0,96},{32,0},{64,32},{96,64},{1,97},{33,1},{65,33},{97,65},{2,98}... | collective-permute-start | bytes 2752520 | tf_op jit(solution)/shard_map/ppermute | solution.py:622
  373.2 52.9 %collective-permute-start.76 = (f32[896,256]{1,0:T(8,128)}, f32[896,256]{1,0:T(8,128)}, u32[]{:S(2)}, u32[]{:S(2)}) collective-permute-start(f32[896,256]{1,0:T(8,128)} %add_add_fusion.1), channel_id=1, source_target_pairs={{0,8},{1,24},{8,0},{9,16},{16,9},{17,25},{24,1},{25,17},{2,10},{3,... | collective-permute-start | bytes 2752520 | tf_op jit(solution)/shard_map/ppermute | solution.py:638
  386.3 42.3 %collective-permute-start.49 = (bf16[384,1024]{1,0:T(8,128)(2,1)}, bf16[384,1024]{1,0:T(8,128)(2,1)}, u32[]{:S(2)}, u32[]{:S(2)}) collective-permute-start(bf16[384,1024]{1,0:T(8,128)(2,1)} %maximum_bitcast_fusion.refs_4_), channel_id=1, source_target_pairs={{0,1},{1,0},{2,3},{3,2},{4,5},{5,4},{6,7},{7,6},{8,9},{9,8},{10,11... | collective-permute-start | bytes 2359304 | tf_op jit(solution)/shard_map/ppermute | solution.py:626
  388.9 52.9 %collective-permute-start.66 = (f32[896,256]{1,0:T(8,128)}, f32[896,256]{1,0:T(8,128)}, u32[]{:S(2)}, u32[]{:S(2)}) collective-permute-start(f32[896,256]{1,0:T(8,128)} %get-tuple-element.139), channel_id=1, source_target_pairs={{0,96},{32,0},{64,32},{96,64},{1,97},{33,1},{65,33},{97,65},{2,98}... | collective-permute-start | bytes 2752520 | tf_op jit(solution)/shard_map/ppermute | solution.py:622
  406.0 37.6 %collective-permute-start.68 = (f32[896,256]{1,0:T(8,128)}, f32[896,256]{1,0:T(8,128)}, u32[]{:S(2)}, u32[]{:S(2)}) collective-permute-start(f32[896,256]{1,0:T(8,128)} %get-tuple-element.141), channel_id=1, source_target_pairs={{0,32},{32,64},{64,96},{96,0},{1,33},{33,65},{65,97},{97,1},{2,34}... | collective-permute-start | bytes 2752520 | tf_op jit(solution)/shard_map/ppermute | solution.py:622
  426.0 42.3 %collective-permute-start.47 = (f32[896,256]{1,0:T(8,128)}, f32[896,256]{1,0:T(8,128)}, u32[]{:S(2)}, u32[]{:S(2)}) collective-permute-start(f32[896,256]{1,0:T(8,128)} %get-tuple-element.120), channel_id=1, source_target_pairs={{0,32},{32,64},{64,96},{96,0},{1,33},{33,65},{65,97},{97,1},{2,34}... | collective-permute-start | bytes 2752520 | tf_op jit(solution)/shard_map/ppermute | solution.py:622
  428.7 54.9 %collective-permute-start.54 = (f32[896,256]{1,0:T(8,128)}, f32[896,256]{1,0:T(8,128)}, u32[]{:S(2)}, u32[]{:S(2)}) collective-permute-start(f32[896,256]{1,0:T(8,128)} %get-tuple-element.128), channel_id=1, source_target_pairs={{0,96},{32,0},{64,32},{96,64},{1,97},{33,1},{65,33},{97,65},{2,98}... | collective-permute-start | bytes 2752520 | tf_op jit(solution)/shard_map/ppermute | solution.py:622
  441.8 40.6 %collective-permute-start.57 = (f32[640,256]{1,0:T(8,128)}, f32[640,256]{1,0:T(8,128)S(1)}, u32[]{:S(2)}, u32[]{:S(2)}) collective-permute-start(f32[640,256]{1,0:T(8,128)} %get-tuple-element.131), channel_id=1, source_target_pairs={{0,32},{32,64},{64,96},{96,0},{1,33},{33,65},{65,97},{97,1},{2,34}... | collective-permute-start | bytes 1966088 | tf_op jit(solution)/shard_map/ppermute | solution.py:622
  443.6 52.1 %collective-permute-start.51 = (f32[896,256]{1,0:T(8,128)}, f32[896,256]{1,0:T(8,128)S(1)}, u32[]{:S(2)}, u32[]{:S(2)}) collective-permute-start(f32[896,256]{1,0:T(8,128)} %get-tuple-element.124), channel_id=1, source_target_pairs={{0,96},{32,0},{64,32},{96,64},{1,97},{33,1},{65,33},{97,65},{2,98}... | collective-permute-start | bytes 2752520 | tf_op jit(solution)/shard_map/ppermute | solution.py:622
  448.7 38.5 %collective-permute-start.59 = (f32[640,256]{1,0:T(8,128)}, f32[640,256]{1,0:T(8,128)S(1)}, u32[]{:S(2)}, u32[]{:S(2)}) collective-permute-start(f32[640,256]{1,0:T(8,128)} %get-tuple-element.132), channel_id=1, source_target_pairs={{0,96},{32,0},{64,32},{96,64},{1,97},{33,1},{65,33},{97,65},{2,98}... | collective-permute-start | bytes 1966088 | tf_op jit(solution)/shard_map/ppermute | solution.py:622
  468.4 27.2 %collective-permute-start.62 = (f32[640,256]{1,0:T(8,128)}, f32[640,256]{1,0:T(8,128)S(1)}, u32[]{:S(2)}, u32[]{:S(2)}) collective-permute-start(f32[640,256]{1,0:T(8,128)} %get-tuple-element.136), channel_id=1, source_target_pairs={{0,96},{32,0},{64,32},{96,64},{1,97},{33,1},{65,33},{97,65},{2,98}... | collective-permute-start | bytes 1966088 | tf_op jit(solution)/shard_map/ppermute | solution.py:622
  482.4 32.8 %collective-permute-start.69 = (f32[896,256]{1,0:T(8,128)S(1)}, f32[896,256]{1,0:T(8,128)S(1)}, u32[]{:S(2)}, u32[]{:S(2)}) collective-permute-start(f32[896,256]{1,0:T(8,128)S(1)} %copy-done.35), channel_id=1, source_target_pairs={{0,96},{32,0},{64,32},{96,64},{1,97},{33,1},{65,33},{97,65},{2,98}... | collective-permute-start | bytes 2752520 | tf_op jit(solution)/shard_map/ppermute | solution.py:622
  483.6 39.7 %collective-permute-start.50 = (f32[896,256]{1,0:T(8,128)S(1)}, f32[896,256]{1,0:T(8,128)S(1)}, u32[]{:S(2)}, u32[]{:S(2)}) collective-permute-start(f32[896,256]{1,0:T(8,128)S(1)} %add.120), channel_id=1, source_target_pairs={{0,32},{32,64},{64,96},{96,0},{1,33},{33,65},{65,97},{97,1},{2,34}... | collective-permute-start | bytes 2752520 | tf_op jit(solution)/shard_map/ppermute | solution.py:622
  487.3 50.8 %collective-permute-start.53 = (f32[896,256]{1,0:T(8,128)S(1)}, f32[896,256]{1,0:T(8,128)S(1)}, u32[]{:S(2)}, u32[]{:S(2)}) collective-permute-start(f32[896,256]{1,0:T(8,128)S(1)} %copy-done.52), channel_id=1, source_target_pairs={{0,32},{32,64},{64,96},{96,0},{1,33},{33,65},{65,97},{97,1},{2,34}... | collective-permute-start | bytes 2752520 | tf_op jit(solution)/shard_map/ppermute | solution.py:622
  495.6 42.6 %collective-permute-start.61 = (f32[640,256]{1,0:T(8,128)S(1)}, f32[640,256]{1,0:T(8,128)S(1)}, u32[]{:S(2)}, u32[]{:S(2)}) collective-permute-start(f32[640,256]{1,0:T(8,128)S(1)} %copy-done.53), channel_id=1, source_target_pairs={{0,32},{32,64},{64,96},{96,0},{1,33},{33,65},{65,97},{97,1},{2,34}... | collective-permute-start | bytes 1966088 | tf_op jit(solution)/shard_map/ppermute | solution.py:622
  495.6 49.2 %collective-permute-start.55 = (f32[896,256]{1,0:T(8,128)S(1)}, f32[896,256]{1,0:T(8,128)S(1)}, u32[]{:S(2)}, u32[]{:S(2)}) collective-permute-start(f32[896,256]{1,0:T(8,128)S(1)} %add.124), channel_id=1, source_target_pairs={{0,96},{32,0},{64,32},{96,64},{1,97},{33,1},{65,33},{97,65},{2,98}... | collective-permute-start | bytes 2752520 | tf_op jit(solution)/shard_map/ppermute | solution.py:622
  515.2 43.1 %collective-permute-start.73 = (f32[896,256]{1,0:T(8,128)S(1)}, f32[896,256]{1,0:T(8,128)S(1)}, u32[]{:S(2)}, u32[]{:S(2)}) collective-permute-start(f32[896,256]{1,0:T(8,128)S(1)} %add_add_fusion.2.own_ref), channel_id=1, source_target_pairs={{1,16},{9,24},{16,1},{24,9},{3,18},{11,26},{18,3},{26,11},{5,20},{... | collective-permute-start | bytes 2752520 | tf_op jit(solution)/shard_map/ppermute | solution.py:638
  523.4 37.8 %collective-permute-start.58 = (f32[640,256]{1,0:T(8,128)S(1)}, f32[640,256]{1,0:T(8,128)}, u32[]{:S(2)}, u32[]{:S(2)}) collective-permute-start(f32[640,256]{1,0:T(8,128)S(1)} %add.126), channel_id=1, source_target_pairs={{0,32},{32,64},{64,96},{96,0},{1,33},{33,65},{65,97},{97,1},{2,34}... | collective-permute-start | bytes 1966088 | tf_op jit(solution)/shard_map/ppermute | solution.py:622
  538.1 31.8 %collective-permute-start.63 = (f32[640,256]{1,0:T(8,128)}, f32[640,256]{1,0:T(8,128)}, u32[]{:S(2)}, u32[]{:S(2)}) collective-permute-start(f32[640,256]{1,0:T(8,128)} %add.130), channel_id=1, source_target_pairs={{0,96},{32,0},{64,32},{96,64},{1,97},{33,1},{65,33},{97,65},{2,98}... | collective-permute-start | bytes 1966088 | tf_op jit(solution)/shard_map/ppermute | solution.py:622
  538.1 45.5 %collective-permute-start.67 = (f32[896,256]{1,0:T(8,128)}, f32[896,256]{1,0:T(8,128)}, u32[]{:S(2)}, u32[]{:S(2)}) collective-permute-start(f32[896,256]{1,0:T(8,128)} %add_add_fusion.4.own_ref), channel_id=1, source_target_pairs={{1,16},{9,24},{16,1},{24,9},{3,18},{11,26},{18,3},{26,11},{5,20},{... | collective-permute-start | bytes 2752520 | tf_op jit(solution)/shard_map/ppermute | solution.py:638
  544.9 38.8 %collective-permute-start.70 = (f32[896,256]{1,0:T(8,128)}, f32[896,256]{1,0:T(8,128)}, u32[]{:S(2)}, u32[]{:S(2)}) collective-permute-start(f32[896,256]{1,0:T(8,128)} %add_add_fusion.3), channel_id=1, source_target_pairs={{0,8},{1,24},{8,0},{9,16},{16,9},{17,25},{24,1},{25,17},{2,10},{3,... | collective-permute-start | bytes 2752520 | tf_op jit(solution)/shard_map/ppermute | solution.py:638
  559.2 55.7 %collective-permute-start.52 = (f32[896,256]{1,0:T(8,128)}, f32[896,256]{1,0:T(8,128)}, u32[]{:S(2)}, u32[]{:S(2)}) collective-permute-start(f32[896,256]{1,0:T(8,128)} %add_add_fusion.6.own_ref), channel_id=1, source_target_pairs={{1,16},{9,24},{16,1},{24,9},{3,18},{11,26},{18,3},{26,11},{5,20},{... | collective-permute-start | bytes 2752520 | tf_op jit(solution)/shard_map/ppermute | solution.py:638
  561.1 53.7 %collective-permute-start.56 = (f32[896,256]{1,0:T(8,128)}, f32[896,256]{1,0:T(8,128)}, u32[]{:S(2)}, u32[]{:S(2)}) collective-permute-start(f32[896,256]{1,0:T(8,128)} %add_add_fusion.5), channel_id=1, source_target_pairs={{0,8},{1,24},{8,0},{9,16},{16,9},{17,25},{24,1},{25,17},{2,10},{3,... | collective-permute-start | bytes 2752520 | tf_op jit(solution)/shard_map/ppermute | solution.py:638
  569.9 54.5 %collective-permute-start.60 = (f32[640,256]{1,0:T(8,128)}, f32[640,256]{1,0:T(8,128)}, u32[]{:S(2)}, u32[]{:S(2)}) collective-permute-start(f32[640,256]{1,0:T(8,128)} %add_add_fusion.8.own_ref), channel_id=1, source_target_pairs={{1,16},{9,24},{16,1},{24,9},{3,18},{11,26},{18,3},{26,11},{5,20},{... | collective-permute-start | bytes 1966088 | tf_op jit(solution)/shard_map/ppermute | solution.py:638
  583.7 40.7 %collective-permute-start.64 = (f32[640,256]{1,0:T(8,128)}, f32[640,256]{1,0:T(8,128)}, u32[]{:S(2)}, u32[]{:S(2)}) collective-permute-start(f32[640,256]{1,0:T(8,128)} %add_add_fusion.7), channel_id=1, source_target_pairs={{0,8},{1,24},{8,0},{9,16},{16,9},{17,25},{24,1},{25,17},{2,10},{3,... | collective-permute-start | bytes 1966088 | tf_op jit(solution)/shard_map/ppermute | solution.py:638
  (91 other events, 1207.7 us)
Sparse Core Ops, SparseCore 0:
  42.4 76.8 all-gather.2
  121.5 74.7 all-gather.4
  344.1 116.5 reduce-scatter.4
  463.9 144.0 reduce-scatter.2

commit v7 on v6

--- a/solution.py
+++ b/solution.py
@@ -678,7 +678,10 @@
         qkv_blk = o_blk + head
 
         def gather_rows(blocks):
-            return [turn(jnp.where(even_y, blocks[flip], blocks[1 - flip]), flip, True) for flip in range(2)]
+            got = []
+            for flip in (1, 0):
+                got.insert(0, turn(jnp.where(even_y, blocks[flip], blocks[1 - flip]), flip, True))
+            return got
 
         def gather_weight(piece):
             left, right = [], []
@@ -734,8 +737,8 @@
 
         x_rows = after(x_in[0], cos_tab, sin_tab).astype(F32)
         normed, norm_pull = jax.vjp(lambda row_vals: norm_fwd(row_vals, norm_gain), x_rows)
-        h_all = lax.all_gather(after(normed.astype(BF16), wf_piece[0], wf_piece[1]), ("y", "x"), axis=0, tiled=True)
-        dy_all = lax.all_gather(after(dy_in[0], *wf_piece), ("y", "x"), axis=0, tiled=True)
+        h_all = lax.all_gather(after(normed.astype(BF16), wf_piece[1]), ("y", "x"), axis=0, tiled=True)
+        dy_all = lax.all_gather(after(dy_in[0], wf_piece[1]), ("y", "x"), axis=0, tiled=True)
         wf_parts = gather_weight(wf_piece)
         ws_parts = gather_weight(ws_piece)
 
@@ -746,15 +749,15 @@
         third_other = swap_yc(my_rows(third, False))
         act_val, act_t = act_fwd(after(gate_up, qkv_tok))
         act_recv = swap_c(act_t)
-        h_picked = pick_cols(after(pos, act_t), h_all)
-        h_recv = swap_c(h_picked)
-        qkv_seq, attn_own, attn_other = attn_fwd(after(pos, h_picked), qkv_tok, qkv_other, third_own, third_other, cos_tab, sin_tab)
+        qkv_seq, attn_own, attn_other = attn_fwd(after(pos, act_t), qkv_tok, qkv_other, third_own, third_other, cos_tab, sin_tab)
         attn_got = swap_c(attn_other)
         y_part = nt_pieces(after(pos, attn_own), [act_val, attn_own, attn_got], ws_parts, chunk, 0, chunk)
         mix_sum = lax.psum_scatter(y_part, ("y", "x"), scatter_dimension=0, tiled=True)
         y_out = (x_rows + mix_sum).astype(BF16)[None]
 
-        dy_picked = pick_cols(after(pos, y_part), dy_all)
+        h_picked = pick_cols(after(pos, y_part), h_all)
+        h_recv = swap_c(h_picked)
+        dy_picked = pick_cols(after(pos, h_picked), dy_all)
         dy_recv = swap_c(dy_picked)
         g_act = grad_start([(act_t, act_recv, dy_all, dy_recv, ff_blk, 0)], dy_picked)
         d_act, d_attn = nn_pieces(after(pos, g_act[3][0]), dy_all, ws_parts, (ff_blk, o_blk), 256)
@@ -765,13 +768,13 @@
         got = swap_y(send)
         g_act = grad_pass(g_act, d_queries)
         g_gate = grad_start([(d_gate_up_t, d_gate_up_recv, h_all, h_recv, ff_blk, 0)], *g_act[3])
+        b_act = grad_back(g_act, g_gate[3][0])
         d_own, d_other = attn_post(after(pos, g_gate[3][0]), d_queries, keep, got, cos_tab, sin_tab)
         d_got = swap_c(d_other)
         dh_part = nt_pieces(pos, [d_gate_up, d_own, d_got], wf_parts, chunk, 0, chunk)
         d_h = lax.psum_scatter(dh_part, ("y", "x"), scatter_dimension=0, tiled=True)
         g_gate = grad_pass(g_gate, dh_part)
         g_up = grad_start([(d_gate_up_t, d_gate_up_recv, h_all, h_recv, ff_blk, 1)], *g_gate[3])
-        b_act = grad_back(g_act, g_up[3][0])
         d_h = d_h.astype(BF16)
         dx_out = (dy_in[0].astype(F32) + norm_pull(d_h.astype(F32))[0]).astype(BF16)[None]
 

time: 643 us -> 660 us (1.026)
  starting transfers between devices: 101 us -> 127 us
  waiting for transfers between devices: 265 us -> 256 us
    ppermute x12, starting transfers between devices: 34.1 us -> 60.2 us  [turn(): return lax.ppermute(val, ('y', 'c'), pairs)]
    ppermute x12, waiting for transfers between devices: 89.3 us -> 77.8 us  [turn(): return lax.ppermute(val, ('y', 'c'), pairs)]
  transfers between devices with their start and end apart: 81 -> 81, of which waited for: 32 -> 32; matrix products, arithmetic and copies ran while one was open for 7% -> 7% of each run, Pallas kernels for 25% -> 24%
where the time goes in v7:
time: 660 us; the launch traced here: 652 us
  waiting for transfers between devices  256 us (39%)
  Pallas kernels  193 us (29%)
  starting transfers between devices  127 us (19%)
  other arithmetic  41 us (6%)
  local copies, waits for them, and re-layouts  19.2 us (3%)
  between operations  15.1 us (2%)
    ppermute x36, waiting for transfers between devices, hop_z(): return lax.ppermute(val, 'z', ring(step, NZ))  159 us
    ppermute x12, waiting for transfers between devices, turn(): return lax.ppermute(val, ('y', 'c'), pairs)  77.8 us
    ppermute x12, starting transfers between devices, turn(): return lax.ppermute(val, ('y', 'c'), pairs)  60.2 us
    pallas_call x4, Pallas kernels, grad_pieces(): pl.pallas_call(functools.partial(grad_kernel, heights), grid_spec=pltpu.P...  52.9 us
    pallas_call x2, Pallas kernels, nn_pieces(): pl.pallas_call(functools.partial(nn_kernel, keys, 2, len(widths), tile),...  44.7 us
    pallas_call x2, Pallas kernels, nt_pieces(): pl.pallas_call(functools.partial(nt_kernel, keys, sides, first_row), grid...  43.8 us
    ppermute x36, starting transfers between devices, hop_z(): return lax.ppermute(val, 'z', ring(step, NZ))  38.2 us
    ppermute x26, starting transfers between devices, swap_c(): return lax.ppermute(val, 'c', [(0, 1), (1, 0)])  23.5 us
  transfers between devices with their start and end apart: 81, of which 32 were waited for; matrix products, arithmetic and copies ran while one was open for 7% of the time, Pallas kernels for 24%

profile of v7, /device:TPU:1, one launch (start us, length us, event | category | flops | bytes accessed | tf_op | source)
XLA Modules:
  0.0 651.6 jit_solution(9924527557384191692)
XLA Ops:
  12.1 4.1 collective-permute-start
  19.8 9.6 %collective-permute-done.refs_1_.refs_4_ = bf16[256,2176]{1,0:T(8,128)(2,1)S(1)} collective-permute-done((bf16[256,2176]{1,0:T(8,128)(2,1)S(1)}, bf16[256,2176]{1,0:T(8,128)(2,1)S(1)}, u32[]{:S(2)}, u32[]{:S(2)}) %collective-permute-start) | collective-permute-done | bytes 1114144 | tf_op jit(solution)/shard_map/ppermute | solution.py:638
  30.2 3.8 collective-permute-start.1
  37.1 26.5 %collective-permute-done.1.refs_0_.refs_3_ = bf16[256,2176]{1,0:T(8,128)(2,1)S(1)} collective-permute-done((bf16[256,2176]{1,0:T(8,128)(2,1)}, bf16[256,2176]{1,0:T(8,128)(2,1)S(1)}, u32[]{:S(2)}, u32[]{:S(2)}) %collective-permute-start.1) | collective-permute-done | bytes 1114144 | tf_op jit(solution)/shard_map/ppermute | solution.py:638
  68.8 4.6 collective-permute-start.20
  73.4 18.0 %collective-permute-done.20.refs_3_.refs_0_ = bf16[256,1152]{1,0:T(8,128)(2,1)} collective-permute-done((bf16[256,1152]{1,0:T(8,128)(2,1)S(1)}, bf16[256,1152]{1,0:T(8,128)(2,1)}, u32[]{:S(2)}, u32[]{:S(2)}) %collective-permute-start.20) | collective-permute-done | bytes 589856 | tf_op jit(solution)/shard_map/ppermute | solution.py:638
  92.6 16.9 %collective-permute-done.5.refs_5_.refs_8_ = bf16[256,2176]{1,0:T(8,128)(2,1)S(1)} collective-permute-done((bf16[256,2176]{1,0:T(8,128)(2,1)S(1)}, bf16[256,2176]{1,0:T(8,128)(2,1)S(1)}, u32[]{:S(2)}, u32[]{:S(2)}) %collective-permute-start.5) | collective-permute-done | bytes 1114144 | tf_op jit(solution)/shard_map/ppermute | solution.py:622
  111.9 6.3 collective-permute-done.9.refs_9_.refs_16_
  118.8 12.1 %collective-permute-done.12.refs_12_.refs_11_ = bf16[256,2176]{1,0:T(8,128)(2,1)} collective-permute-done((bf16[256,2176]{1,0:T(8,128)(2,1)S(1)}, bf16[256,2176]{1,0:T(8,128)(2,1)}, u32[]{:S(2)}, u32[]{:S(2)}) %collective-permute-start.12) | collective-permute-done | bytes 1114144 | tf_op jit(solution)/shard_map/ppermute | solution.py:622
  137.5 27.1 %shard_map.153 = (bf16[1024,1792]{1,0:T(8,128)(2,1)}, bf16[1024,384]{1,0:T(8,128)(2,1)}) custom-call(s32[4]{0:T(128)} %pad_add_fusion.pos_ref, bf16[1024,4096]{1,0:T(8,128)(2,1)} %all-gather.3.cloned.1.call-done.acts_ref.in_ref.refs_2_.refs_6_, bf16[256,2176]{1,0:T(8,128)(2,1)} %copy-done.3, bf16[256,2176]{1,0:T(8,128)(2,1)} %copy-done.2, ...), custom_call_target="tpu_custom_call" | custom-call | flops 912680576 | bytes 26214400 | tf_op jit(solution)/shard_map/pallas_call | solution.py:330
  173.0 6.8 %collective-permute-done.18.other_third_ref = bf16[512,128]{1,0:T(8,128)(2,1)S(1)} collective-permute-done((bf16[512,128]{1,0:T(8,128)(2,1)S(1)}, bf16[512,128]{1,0:T(8,128)(2,1)S(1)}, u32[]{:S(2)}, u32[]{:S(2)}) %collective-permute-start.18) | collective-permute-done | bytes 131104 | tf_op jit(solution)/shard_map/ppermute | solution.py:643
  179.7 4.9 collective-permute-done.17.own_third_ref
  186.8 4.8 act_fwd.1
  191.6 5.6 shard_map.154
  205.6 16.9 %shard_map.155 = f32[1024,4096]{1,0:T(8,128)} custom-call(s32[4]{0:T(128)} %pad_add_fusion.pos_ref, bf16[16,64,896]{2,1,0:T(8,128)(2,1)} %bitcast.30, bf16[8,64,256]{2,1,0:T(8,128)(2,1)} %bitcast.33, bf16[8,64,256]{2,1,0:T(8,128)(2,1)} %bitcast.34, bf16[256,1152]{1,0:T(8,128)(2,1)} %collective-permute-done.20.refs_3_.refs_0_, ...), custom_call_target="tpu_custom_call" | custom-call | flops 483183808 | bytes 26214400 | tf_op jit(solution)/shard_map/pallas_call | solution.py:424
  222.5 4.1 shard_map.156
  226.7 4.1 shard_map.157
  231.4 8.7 %collective-permute-start.42 = (bf16[1024,2048]{1,0:T(8,128)(2,1)}, bf16[1024,2048]{1,0:T(8,128)(2,1)}, u32[]{:S(2)}, u32[]{:S(2)}) collective-permute-start(bf16[1024,2048]{1,0:T(8,128)(2,1)} %shard_map.156), channel_id=1, source_target_pairs={{0,1},{1,0},{2,3},{3,2},{4,5},{5,4},{6,7},{7,6},{8,9},{9,8},{10,11... | collective-permute-start | bytes 12582920 | tf_op jit(solution)/shard_map/ppermute | solution.py:626
  241.0 13.2 %grad.4 = (f32[896,256]{1,0:T(8,128)}, f32[896,256]{1,0:T(8,128)}, f32[896,256]{1,0:T(8,128)}, f32[896,256]{1,0:T(8,128)}, f32[896,256]{1,0:T(8,128)}, /*index=5...) custom-call(s32[4]{0:T(128)} %pad_add_fusion.pos_ref, bf16[896,1024]{1,0:T(8,128)(2,1)} %get-tuple-element.80.refs_0_, ...), custom_call_target="tpu_custom_call" | custom-call | flops 375809632 | bytes 8388608 | tf_op jit(solution)/shard_map/grad/pallas_call | solution.py:537
  254.1 17.7 %shard_map.158 = (bf16[1024,896]{1,0:T(8,128)(2,1)}, bf16[1024,256]{1,0:T(8,128)(2,1)}) custom-call(s32[4]{0:T(128)} %pad_add_fusion.pos_ref, bf16[1024,4096]{1,0:T(8,128)(2,1)} %all-gather.5.cloned.1.call-done.in_ref.refs_2_.acts_ref, bf16[256,1152]{1,0:T(8,128)(2,1)} %collective-permute-done.20.refs_3_.refs_0_, ...), custom_call_target="tpu_custom_call" | custom-call | flops 483183808 | bytes 17825792 | tf_op jit(solution)/shard_map/pallas_call | solution.py:330
  271.8 6.9 %act_bwd.1 = (bf16[1024,1792]{1,0:T(8,128)(2,1)}, bf16[1792,1024]{1,0:T(8,128)(2,1)}) custom-call(bf16[1024,1792]{1,0:T(8,128)(2,1)} %get-tuple-element.79.ab_ref, bf16[1024,896]{1,0:T(8,128)(2,1)} %get-tuple-element.93.du_ref), custom_call_target="tpu_custom_call" | custom-call | flops 400000000 | bytes 14000000 | tf_op jit(solution)/shard_map/act_bwd/pallas_call | solution.py:260
  286.4 8.1 %shard_map.159 = (bf16[2,512,256]{2,1,0:T(8,128)(2,1)}, f32[2,512,128]{2,1,0:T(8,128)}, f32[2,512,128]{2,1,0:T(8,128)}) custom-call(s32[4]{0:T(128)} %pad_add_fusion.pos_ref, bf16[2,512,512]{2,1,0:T(8,128)(2,1)} %get-tuple-element.99.seq_ref, bf16[1024,256]{1,0:T(8,128)(2,1)} %get-tuple-element.100.own_ref, bf16[512,256]{1,0:T(8,128)(2,1)} %copy-done.49, ...), custom_call_target="tpu_custom_call" | custom-call | flops 800000000 | bytes 4000000 | tf_op jit(solution)/shard_map/pallas_call | solution.py:142
  296.7 5.6 collective-permute-done.38
  307.0 13.2 %grad.5 = (f32[896,256]{1,0:T(8,128)}, f32[896,256]{1,0:T(8,128)}, f32[896,256]{1,0:T(8,128)}, f32[896,256]{1,0:T(8,128)}, f32[896,256]{1,0:T(8,128)}, /*index=5...) custom-call(s32[4]{0:T(128)} %pad_add_fusion.pos_ref, bf16[1792,1024]{1,0:T(8,128)(2,1)} %get-tuple-element.97.refs_0_, ...), custom_call_target="tpu_custom_call" | custom-call | flops 375809632 | bytes 8388608 | tf_op jit(solution)/shard_map/grad/pallas_call | solution.py:537
  328.7 26.9 %shard_map.161 = f32[1024,4096]{1,0:T(8,128)} custom-call(s32[4]{0:T(128)} %pad_add_fusion.pos_ref, bf16[16,64,1792]{2,1,0:T(8,128)(2,1)} %bitcast.28, bf16[8,64,384]{2,1,0:T(8,128)(2,1)} %bitcast.31, bf16[8,64,384]{2,1,0:T(8,128)(2,1)} %bitcast.32, bf16[256,2176]{1,0:T(8,128)(2,1)} %copy-done.3, bf16[256,2176]{1,0:T(8,128)(2,1)} %copy-done.2, ...), custom_call_target="tpu_custom_call" | custom-call | flops 912680576 | bytes 34603008 | tf_op jit(solution)/shard_map/pallas_call | solution.py:424
  361.9 17.4 %collective-permute-done.74 = f32[896,256]{1,0:T(8,128)} collective-permute-done((f32[896,256]{1,0:T(8,128)}, f32[896,256]{1,0:T(8,128)}, u32[]{:S(2)}, u32[]{:S(2)}) %collective-permute-start.74) | collective-permute-done | bytes 917536 | tf_op jit(solution)/shard_map/ppermute | solution.py:622
  382.0 7.8 %collective-permute-start.76 = (f32[896,256]{1,0:T(8,128)}, f32[896,256]{1,0:T(8,128)}, u32[]{:S(2)}, u32[]{:S(2)}) collective-permute-start(f32[896,256]{1,0:T(8,128)} %add_add_fusion.1), channel_id=1, source_target_pairs={{0,8},{1,24},{8,0},{9,16},{16,9},{17,25},{24,1},{25,17},{2,10},{3,... | collective-permute-start | bytes 2752520 | tf_op jit(solution)/shard_map/ppermute | solution.py:638
  389.8 9.2 %collective-permute-done.71 = f32[896,256]{1,0:T(8,128)S(1)} collective-permute-done((f32[896,256]{1,0:T(8,128)}, f32[896,256]{1,0:T(8,128)S(1)}, u32[]{:S(2)}, u32[]{:S(2)}) %collective-permute-start.71) | collective-permute-done | bytes 917536 | tf_op jit(solution)/shard_map/ppermute | solution.py:622
  400.1 9.1 %collective-permute-start.73 = (f32[896,256]{1,0:T(8,128)}, f32[896,256]{1,0:T(8,128)}, u32[]{:S(2)}, u32[]{:S(2)}) collective-permute-start(f32[896,256]{1,0:T(8,128)} %add_add_fusion.2.own_ref), channel_id=1, source_target_pairs={{1,16},{9,24},{16,1},{24,9},{3,18},{11,26},{18,3},{26,11},{5,20},{... | collective-permute-start | bytes 2752520 | tf_op jit(solution)/shard_map/ppermute | solution.py:638
  412.2 6.4 collective-permute-done.45
  421.0 3.6 collective-permute-start.49
  429.1 13.4 %grad.6 = (f32[896,256]{1,0:T(8,128)}, f32[896,256]{1,0:T(8,128)}, f32[896,256]{1,0:T(8,128)}, f32[896,256]{1,0:T(8,128)}, f32[896,256]{1,0:T(8,128)}, /*index=5...) custom-call(s32[4]{0:T(128)} %pad_add_fusion.pos_ref, bf16[1792,1024]{1,0:T(8,128)(2,1)} %get-tuple-element.97.refs_0_, ...), custom_call_target="tpu_custom_call" | custom-call | flops 375809632 | bytes 8388608 | tf_op jit(solution)/shard_map/grad/pallas_call | solution.py:537
  447.0 13.2 %grad.7 = (f32[640,256]{1,0:T(8,128)}, f32[640,256]{1,0:T(8,128)}, f32[640,256]{1,0:T(8,128)}, f32[640,256]{1,0:T(8,128)}, f32[640,256]{1,0:T(8,128)}, /*index=5...) custom-call(s32[4]{0:T(128)} %pad_add_fusion.pos_ref, bf16[256,1024]{1,0:T(8,128)(2,1)} %maximum_bitcast_fusion.1.refs_0_, ...), custom_call_target="tpu_custom_call" | custom-call | flops 268435456 | bytes 8388608 | tf_op jit(solution)/shard_map/grad/pallas_call | solution.py:537
  460.2 5.7 collective-permute-done.68
  465.9 19.7 %collective-permute-done.47 = f32[896,256]{1,0:T(8,128)} collective-permute-done((f32[896,256]{1,0:T(8,128)}, f32[896,256]{1,0:T(8,128)}, u32[]{:S(2)}, u32[]{:S(2)}) %collective-permute-start.47) | collective-permute-done | bytes 917536 | tf_op jit(solution)/shard_map/ppermute | solution.py:622
  485.6 19.7 %collective-permute-done.65 = f32[896,256]{1,0:T(8,128)} collective-permute-done((f32[896,256]{1,0:T(8,128)}, f32[896,256]{1,0:T(8,128)}, u32[]{:S(2)}, u32[]{:S(2)}) %collective-permute-start.65) | collective-permute-done | bytes 917536 | tf_op jit(solution)/shard_map/ppermute | solution.py:622
  509.7 9.6 %collective-permute-done.57 = f32[640,256]{1,0:T(8,128)S(1)} collective-permute-done((f32[640,256]{1,0:T(8,128)}, f32[640,256]{1,0:T(8,128)S(1)}, u32[]{:S(2)}, u32[]{:S(2)}) %collective-permute-start.57) | collective-permute-done | bytes 655392 | tf_op jit(solution)/shard_map/ppermute | solution.py:622
  527.3 11.7 %collective-permute-done.50 = f32[896,256]{1,0:T(8,128)S(1)} collective-permute-done((f32[896,256]{1,0:T(8,128)S(1)}, f32[896,256]{1,0:T(8,128)S(1)}, u32[]{:S(2)}, u32[]{:S(2)}) %collective-permute-start.50) | collective-permute-done | bytes 917536 | tf_op jit(solution)/shard_map/ppermute | solution.py:622
  547.8 10.8 %collective-permute-done.53 = f32[896,256]{1,0:T(8,128)S(1)} collective-permute-done((f32[896,256]{1,0:T(8,128)S(1)}, f32[896,256]{1,0:T(8,128)S(1)}, u32[]{:S(2)}, u32[]{:S(2)}) %collective-permute-start.53) | collective-permute-done | bytes 917536 | tf_op jit(solution)/shard_map/ppermute | solution.py:622
  558.6 8.4 %collective-permute-start.67 = (f32[896,256]{1,0:T(8,128)}, f32[896,256]{1,0:T(8,128)}, u32[]{:S(2)}, u32[]{:S(2)}) collective-permute-start(f32[896,256]{1,0:T(8,128)} %add_add_fusion.4.own_ref), channel_id=1, source_target_pairs={{1,16},{9,24},{16,1},{24,9},{3,18},{11,26},{18,3},{26,11},{5,20},{... | collective-permute-start | bytes 2752520 | tf_op jit(solution)/shard_map/ppermute | solution.py:638
  573.4 8.5 %collective-permute-start.52 = (f32[896,256]{1,0:T(8,128)}, f32[896,256]{1,0:T(8,128)}, u32[]{:S(2)}, u32[]{:S(2)}) collective-permute-start(f32[896,256]{1,0:T(8,128)} %add_add_fusion.6.own_ref), channel_id=1, source_target_pairs={{1,16},{9,24},{16,1},{24,9},{3,18},{11,26},{18,3},{26,11},{5,20},{... | collective-permute-start | bytes 2752520 | tf_op jit(solution)/shard_map/ppermute | solution.py:638
  582.0 4.7 collective-permute-done.58
  586.7 6.5 %collective-permute-start.56 = (f32[896,256]{1,0:T(8,128)}, f32[896,256]{1,0:T(8,128)}, u32[]{:S(2)}, u32[]{:S(2)}) collective-permute-start(f32[896,256]{1,0:T(8,128)} %add_add_fusion.5), channel_id=1, source_target_pairs={{0,8},{1,24},{8,0},{9,16},{16,9},{17,25},{24,1},{25,17},{2,10},{3,... | collective-permute-start | bytes 2752520 | tf_op jit(solution)/shard_map/ppermute | solution.py:638
  593.2 3.8 shard_map.164
  605.4 4.0 shard_map.163
  609.4 17.2 %collective-permute-done.52.first_ref = f32[896,256]{1,0:T(8,128)} collective-permute-done((f32[896,256]{1,0:T(8,128)}, f32[896,256]{1,0:T(8,128)}, u32[]{:S(2)}, u32[]{:S(2)}) %collective-permute-start.52) | collective-permute-done | bytes 917536 | tf_op jit(solution)/shard_map/ppermute | solution.py:638
  627.6 4.0 shard_map.162
  636.2 4.4 collective-permute-done.60.first_ref
  (292 shorter events, 141.4 us)
Async XLA Ops:
  7.2 130.3 %all-gather.3.cloned.1.call-start = ((), (), s32[]{:S(2)}) async-start(), calls=%async_computation.2 | async-start | bytes 8912896 | tf_op jit(solution)/shard_map/all_gather | solution.py:740
  29.4 197.2 %all-gather.5.cloned.1.call-start = ((), (), s32[]{:S(2)}) async-start(), calls=%async_computation.4 | async-start | bytes 8912896 | tf_op jit(solution)/shard_map/all_gather | solution.py:741
  30.2 601.4 %reduce-scatter.5.cloned.1.call-start = ((), (), s32[]{:S(2)}) async-start(), calls=%async_computation.5 | async-start | bytes 17825792 | tf_op jit(solution)/shard_map/reduce_scatter | solution.py:775
  30.2 33.4 %collective-permute-start.1 = (bf16[256,2176]{1,0:T(8,128)(2,1)}, bf16[256,2176]{1,0:T(8,128)(2,1)S(1)}, u32[]{:S(2)}, u32[]{:S(2)}) collective-permute-start(bf16[256,2176]{1,0:T(8,128)(2,1)} %get-tuple-element.146), channel_id=1, source_target_pairs={{0,0},{1,16},{8,8},{9,24},{16,1},{17,17},{24,9},{25,25},{2,2},{3,1... | collective-permute-start | bytes 3342344 | tf_op jit(solution)/shard_map/ppermute | solution.py:638
  36.0 32.8 %collective-permute-start.21 = (bf16[256,1152]{1,0:T(8,128)(2,1)S(1)}, bf16[256,1152]{1,0:T(8,128)(2,1)}, u32[]{:S(2)}, u32[]{:S(2)}) collective-permute-start(bf16[256,1152]{1,0:T(8,128)(2,1)S(1)} %get-tuple-element.148), channel_id=1, source_target_pairs={{0,8},{1,24},{8,0},{9,16},{16,9},{17,25},{24,1},{25,17},{2,10},{3,... | collective-permute-start | bytes 1769480 | tf_op jit(solution)/shard_map/ppermute | solution.py:638
  63.6 27.8 %collective-permute-start.8 = (bf16[256,2176]{1,0:T(8,128)(2,1)S(1)}, bf16[256,2176]{1,0:T(8,128)(2,1)S(1)}, u32[]{:S(2)}, u32[]{:S(2)}) collective-permute-start(bf16[256,2176]{1,0:T(8,128)(2,1)S(1)} %collective-permute-done.1.refs_0_.refs_3_), channel_id=1, source_target_pairs={{0,32},{32,64},{64,96},{96,0},{1,33},{33,65},{65,97},{97,1},{2,34}... | collective-permute-start | bytes 3342344 | tf_op jit(solution)/shard_map/ppermute | solution.py:622
  65.2 26.3 %collective-permute-start.4 = (bf16[256,2176]{1,0:T(8,128)(2,1)S(1)}, bf16[256,2176]{1,0:T(8,128)(2,1)S(1)}, u32[]{:S(2)}, u32[]{:S(2)}) collective-permute-start(bf16[256,2176]{1,0:T(8,128)(2,1)S(1)} %collective-permute-done.1.refs_0_.refs_3_), channel_id=1, source_target_pairs={{0,96},{32,0},{64,32},{96,64},{1,97},{33,1},{65,33},{97,65},{2,98}... | collective-permute-start | bytes 3342344 | tf_op jit(solution)/shard_map/ppermute | solution.py:622
  67.4 42.1 %collective-permute-start.5 = (bf16[256,2176]{1,0:T(8,128)(2,1)S(1)}, bf16[256,2176]{1,0:T(8,128)(2,1)S(1)}, u32[]{:S(2)}, u32[]{:S(2)}) collective-permute-start(bf16[256,2176]{1,0:T(8,128)(2,1)S(1)} %collective-permute-done.refs_1_.refs_4_), channel_id=1, source_target_pairs={{0,96},{32,0},{64,32},{96,64},{1,97},{33,1},{65,33},{97,65},{2,98}... | collective-permute-start | bytes 3342344 | tf_op jit(solution)/shard_map/ppermute | solution.py:622
  91.4 26.8 %collective-permute-start.9 = (bf16[256,2176]{1,0:T(8,128)(2,1)S(1)}, bf16[256,2176]{1,0:T(8,128)(2,1)S(1)}, u32[]{:S(2)}, u32[]{:S(2)}) collective-permute-start(bf16[256,2176]{1,0:T(8,128)(2,1)S(1)} %collective-permute-done.refs_1_.refs_4_), channel_id=1, source_target_pairs={{0,32},{32,64},{64,96},{96,0},{1,33},{33,65},{65,97},{97,1},{2,34}... | collective-permute-start | bytes 3342344 | tf_op jit(solution)/shard_map/ppermute | solution.py:622
  91.4 26.8 %collective-permute-start.3 = (bf16[256,2176]{1,0:T(8,128)(2,1)S(1)}, bf16[256,2176]{1,0:T(8,128)(2,1)S(1)}, u32[]{:S(2)}, u32[]{:S(2)}) collective-permute-start(bf16[256,2176]{1,0:T(8,128)(2,1)S(1)} %collective-permute-done.refs_1_.refs_4_), channel_id=1, source_target_pairs={{0,1},{1,0},{2,3},{3,2},{4,5},{5,4},{6,7},{7,6},{8,9},{9,8},{10,11... | collective-permute-start | bytes 3342344 | tf_op jit(solution)/shard_map/ppermute | solution.py:626
  91.5 39.4 %collective-permute-start.12 = (bf16[256,2176]{1,0:T(8,128)(2,1)S(1)}, bf16[256,2176]{1,0:T(8,128)(2,1)}, u32[]{:S(2)}, u32[]{:S(2)}) collective-permute-start(bf16[256,2176]{1,0:T(8,128)(2,1)S(1)} %collective-permute-done.8.refs_8_.refs_15_), channel_id=1, source_target_pairs={{0,32},{32,64},{64,96},{96,0},{1,33},{33,65},{65,97},{97,1},{2,34}... | collective-permute-start | bytes 3342344 | tf_op jit(solution)/shard_map/ppermute | solution.py:622
  92.6 38.3 %collective-permute-start.10 = (bf16[256,2176]{1,0:T(8,128)(2,1)S(1)}, bf16[256,2176]{1,0:T(8,128)(2,1)S(1)}, u32[]{:S(2)}, u32[]{:S(2)}) collective-permute-start(bf16[256,2176]{1,0:T(8,128)(2,1)S(1)} %collective-permute-done.8.refs_8_.refs_15_), channel_id=1, source_target_pairs={{0,1},{1,0},{2,3},{3,2},{4,5},{5,4},{6,7},{7,6},{8,9},{9,8},{10,11... | collective-permute-start | bytes 3342344 | tf_op jit(solution)/shard_map/ppermute | solution.py:626
  131.7 34.1 %collective-permute-start.33 = (bf16[256,1152]{1,0:T(8,128)(2,1)}, bf16[256,1152]{1,0:T(8,128)(2,1)}, u32[]{:S(2)}, u32[]{:S(2)}) collective-permute-start(bf16[256,1152]{1,0:T(8,128)(2,1)} %collective-permute-done.21.refs_4_.refs_1_), channel_id=1, source_target_pairs={{0,32},{32,64},{64,96},{96,0},{1,33},{33,65},{65,97},{97,1},{2,34}... | collective-permute-start | bytes 1769480 | tf_op jit(solution)/shard_map/ppermute | solution.py:622
  131.8 37.9 %collective-permute-start.25 = (bf16[256,1152]{1,0:T(8,128)(2,1)}, bf16[256,1152]{1,0:T(8,128)(2,1)}, u32[]{:S(2)}, u32[]{:S(2)}) collective-permute-start(bf16[256,1152]{1,0:T(8,128)(2,1)} %collective-permute-done.21.refs_4_.refs_1_), channel_id=1, source_target_pairs={{0,96},{32,0},{64,32},{96,64},{1,97},{33,1},{65,33},{97,65},{2,98}... | collective-permute-start | bytes 1769480 | tf_op jit(solution)/shard_map/ppermute | solution.py:622
  135.5 36.9 %collective-permute-start.23 = (bf16[256,1152]{1,0:T(8,128)(2,1)}, bf16[256,1152]{1,0:T(8,128)(2,1)}, u32[]{:S(2)}, u32[]{:S(2)}) collective-permute-start(bf16[256,1152]{1,0:T(8,128)(2,1)} %collective-permute-done.21.refs_4_.refs_1_), channel_id=1, source_target_pairs={{0,1},{1,0},{2,3},{3,2},{4,5},{5,4},{6,7},{7,6},{8,9},{9,8},{10,11... | collective-permute-start | bytes 1769480 | tf_op jit(solution)/shard_map/ppermute | solution.py:626
  137.2 35.3 %collective-permute-start.28 = (bf16[256,1152]{1,0:T(8,128)(2,1)}, bf16[256,1152]{1,0:T(8,128)(2,1)}, u32[]{:S(2)}, u32[]{:S(2)}) collective-permute-start(bf16[256,1152]{1,0:T(8,128)(2,1)} %collective-permute-done.20.refs_3_.refs_0_), channel_id=1, source_target_pairs={{0,32},{32,64},{64,96},{96,0},{1,33},{33,65},{65,97},{97,1},{2,34}... | collective-permute-start | bytes 1769480 | tf_op jit(solution)/shard_map/ppermute | solution.py:622
  165.8 32.5 %collective-permute-start.24 = (bf16[256,1152]{1,0:T(8,128)(2,1)}, bf16[256,1152]{1,0:T(8,128)(2,1)}, u32[]{:S(2)}, u32[]{:S(2)}) collective-permute-start(bf16[256,1152]{1,0:T(8,128)(2,1)} %collective-permute-done.20.refs_3_.refs_0_), channel_id=1, source_target_pairs={{0,96},{32,0},{64,32},{96,64},{1,97},{33,1},{65,33},{97,65},{2,98}... | collective-permute-start | bytes 1769480 | tf_op jit(solution)/shard_map/ppermute | solution.py:622
  172.5 27.4 %collective-permute-start.22 = (bf16[256,1152]{1,0:T(8,128)(2,1)}, bf16[256,1152]{1,0:T(8,128)(2,1)}, u32[]{:S(2)}, u32[]{:S(2)}) collective-permute-start(bf16[256,1152]{1,0:T(8,128)(2,1)} %collective-permute-done.20.refs_3_.refs_0_), channel_id=1, source_target_pairs={{0,1},{1,0},{2,3},{3,2},{4,5},{5,4},{6,7},{7,6},{8,9},{9,8},{10,11... | collective-permute-start | bytes 1769480 | tf_op jit(solution)/shard_map/ppermute | solution.py:626
  231.4 75.7 %collective-permute-start.42 = (bf16[1024,2048]{1,0:T(8,128)(2,1)}, bf16[1024,2048]{1,0:T(8,128)(2,1)}, u32[]{:S(2)}, u32[]{:S(2)}) collective-permute-start(bf16[1024,2048]{1,0:T(8,128)(2,1)} %shard_map.156), channel_id=1, source_target_pairs={{0,1},{1,0},{2,3},{3,2},{4,5},{5,4},{6,7},{7,6},{8,9},{9,8},{10,11... | collective-permute-start | bytes 12582920 | tf_op jit(solution)/shard_map/ppermute | solution.py:626
  278.7 28.3 %collective-permute-start.41 = (bf16[1792,1024]{1,0:T(8,128)(2,1)}, bf16[1792,1024]{1,0:T(8,128)(2,1)}, u32[]{:S(2)}, u32[]{:S(2)}) collective-permute-start(bf16[1792,1024]{1,0:T(8,128)(2,1)} %get-tuple-element.97.refs_0_), channel_id=1, source_target_pairs={{0,1},{1,0},{2,3},{3,2},{4,5},{5,4},{6,7},{7,6},{8,9},{9,8},{10,11... | collective-permute-start | bytes 11010056 | tf_op jit(solution)/shard_map/ppermute | solution.py:626
  279.2 25.6 %collective-permute-start.40 = (f32[896,256]{1,0:T(8,128)}, f32[896,256]{1,0:T(8,128)}, u32[]{:S(2)}, u32[]{:S(2)}) collective-permute-start(f32[896,256]{1,0:T(8,128)} %get-tuple-element.104), channel_id=1, source_target_pairs={{0,96},{32,0},{64,32},{96,64},{1,97},{33,1},{65,33},{97,65},{2,98}... | collective-permute-start | bytes 2752520 | tf_op jit(solution)/shard_map/ppermute | solution.py:622
  294.5 25.7 %collective-permute-start.43 = (f32[2,512,128]{2,1,0:T(8,128)}, f32[2,512,128]{2,1,0:T(8,128)}, u32[]{:S(2)}, u32[]{:S(2)}) collective-permute-start(f32[2,512,128]{2,1,0:T(8,128)} %get-tuple-element.109), channel_id=1, source_target_pairs={{0,8},{8,0},{16,24},{24,16},{1,9},{9,1},{17,25},{25,17},{2,10},{10... | collective-permute-start | bytes 1572872 | tf_op jit(solution)/shard_map/ppermute | solution.py:630
  355.6 277.8 %reduce-scatter.3.cloned.1.call-start = ((), (), s32[]{:S(2)}) async-start(), calls=%async_computation.3 | async-start | bytes 17825792 | tf_op jit(solution)/shard_map/reduce_scatter | solution.py:755
  359.0 40.0 %collective-permute-start.71 = (f32[896,256]{1,0:T(8,128)}, f32[896,256]{1,0:T(8,128)S(1)}, u32[]{:S(2)}, u32[]{:S(2)}) collective-permute-start(f32[896,256]{1,0:T(8,128)} %add.115), channel_id=1, source_target_pairs={{0,32},{32,64},{64,96},{96,0},{1,33},{33,65},{65,97},{97,1},{2,34}... | collective-permute-start | bytes 2752520 | tf_op jit(solution)/shard_map/ppermute | solution.py:622
  359.0 40.0 %collective-permute-start.72 = (f32[896,256]{1,0:T(8,128)}, f32[896,256]{1,0:T(8,128)S(1)}, u32[]{:S(2)}, u32[]{:S(2)}) collective-permute-start(f32[896,256]{1,0:T(8,128)} %get-tuple-element.143), channel_id=1, source_target_pairs={{0,96},{32,0},{64,32},{96,64},{1,97},{33,1},{65,33},{97,65},{2,98}... | collective-permute-start | bytes 2752520 | tf_op jit(solution)/shard_map/ppermute | solution.py:622
  361.8 56.8 %collective-permute-start.45 = (f32[896,256]{1,0:T(8,128)}, f32[896,256]{1,0:T(8,128)}, u32[]{:S(2)}, u32[]{:S(2)}) collective-permute-start(f32[896,256]{1,0:T(8,128)} %get-tuple-element.113), channel_id=1, source_target_pairs={{0,32},{32,64},{64,96},{96,0},{1,33},{33,65},{65,97},{97,1},{2,34}... | collective-permute-start | bytes 2752520 | tf_op jit(solution)/shard_map/ppermute | solution.py:622
  382.0 60.6 %collective-permute-start.76 = (f32[896,256]{1,0:T(8,128)}, f32[896,256]{1,0:T(8,128)}, u32[]{:S(2)}, u32[]{:S(2)}) collective-permute-start(f32[896,256]{1,0:T(8,128)} %add_add_fusion.1), channel_id=1, source_target_pairs={{0,8},{1,24},{8,0},{9,16},{16,9},{17,25},{24,1},{25,17},{2,10},{3,... | collective-permute-start | bytes 2752520 | tf_op jit(solution)/shard_map/ppermute | solution.py:638
  400.1 43.2 %collective-permute-start.73 = (f32[896,256]{1,0:T(8,128)}, f32[896,256]{1,0:T(8,128)}, u32[]{:S(2)}, u32[]{:S(2)}) collective-permute-start(f32[896,256]{1,0:T(8,128)} %add_add_fusion.2.own_ref), channel_id=1, source_target_pairs={{1,16},{9,24},{16,1},{24,9},{3,18},{11,26},{18,3},{26,11},{5,20},{... | collective-permute-start | bytes 2752520 | tf_op jit(solution)/shard_map/ppermute | solution.py:638
  409.2 35.2 %collective-permute-start.66 = (f32[896,256]{1,0:T(8,128)}, f32[896,256]{1,0:T(8,128)}, u32[]{:S(2)}, u32[]{:S(2)}) collective-permute-start(f32[896,256]{1,0:T(8,128)} %get-tuple-element.139), channel_id=1, source_target_pairs={{0,96},{32,0},{64,32},{96,64},{1,97},{33,1},{65,33},{97,65},{2,98}... | collective-permute-start | bytes 2752520 | tf_op jit(solution)/shard_map/ppermute | solution.py:622
  442.6 43.0 %collective-permute-start.47 = (f32[896,256]{1,0:T(8,128)}, f32[896,256]{1,0:T(8,128)}, u32[]{:S(2)}, u32[]{:S(2)}) collective-permute-start(f32[896,256]{1,0:T(8,128)} %get-tuple-element.120), channel_id=1, source_target_pairs={{0,32},{32,64},{64,96},{96,0},{1,33},{33,65},{65,97},{97,1},{2,34}... | collective-permute-start | bytes 2752520 | tf_op jit(solution)/shard_map/ppermute | solution.py:622
  443.2 62.0 %collective-permute-start.65 = (f32[896,256]{1,0:T(8,128)}, f32[896,256]{1,0:T(8,128)}, u32[]{:S(2)}, u32[]{:S(2)}) collective-permute-start(f32[896,256]{1,0:T(8,128)} %add.118), channel_id=1, source_target_pairs={{0,32},{32,64},{64,96},{96,0},{1,33},{33,65},{65,97},{97,1},{2,34}... | collective-permute-start | bytes 2752520 | tf_op jit(solution)/shard_map/ppermute | solution.py:622
  444.4 62.5 %collective-permute-start.54 = (f32[896,256]{1,0:T(8,128)}, f32[896,256]{1,0:T(8,128)}, u32[]{:S(2)}, u32[]{:S(2)}) collective-permute-start(f32[896,256]{1,0:T(8,128)} %get-tuple-element.128), channel_id=1, source_target_pairs={{0,96},{32,0},{64,32},{96,64},{1,97},{33,1},{65,33},{97,65},{2,98}... | collective-permute-start | bytes 2752520 | tf_op jit(solution)/shard_map/ppermute | solution.py:622
  445.9 76.1 %collective-permute-start.51 = (f32[896,256]{1,0:T(8,128)}, f32[896,256]{1,0:T(8,128)}, u32[]{:S(2)}, u32[]{:S(2)}) collective-permute-start(f32[896,256]{1,0:T(8,128)} %get-tuple-element.124), channel_id=1, source_target_pairs={{0,96},{32,0},{64,32},{96,64},{1,97},{33,1},{65,33},{97,65},{2,98}... | collective-permute-start | bytes 2752520 | tf_op jit(solution)/shard_map/ppermute | solution.py:622
  465.9 53.4 %collective-permute-start.57 = (f32[640,256]{1,0:T(8,128)}, f32[640,256]{1,0:T(8,128)S(1)}, u32[]{:S(2)}, u32[]{:S(2)}) collective-permute-start(f32[640,256]{1,0:T(8,128)} %get-tuple-element.131), channel_id=1, source_target_pairs={{0,32},{32,64},{64,96},{96,0},{1,33},{33,65},{65,97},{97,1},{2,34}... | collective-permute-start | bytes 1966088 | tf_op jit(solution)/shard_map/ppermute | solution.py:622
  485.6 33.7 %collective-permute-start.62 = (f32[640,256]{1,0:T(8,128)}, f32[640,256]{1,0:T(8,128)S(1)}, u32[]{:S(2)}, u32[]{:S(2)}) collective-permute-start(f32[640,256]{1,0:T(8,128)} %get-tuple-element.136), channel_id=1, source_target_pairs={{0,96},{32,0},{64,32},{96,64},{1,97},{33,1},{65,33},{97,65},{2,98}... | collective-permute-start | bytes 1966088 | tf_op jit(solution)/shard_map/ppermute | solution.py:622
  506.9 32.1 %collective-permute-start.50 = (f32[896,256]{1,0:T(8,128)S(1)}, f32[896,256]{1,0:T(8,128)S(1)}, u32[]{:S(2)}, u32[]{:S(2)}) collective-permute-start(f32[896,256]{1,0:T(8,128)S(1)} %add.120), channel_id=1, source_target_pairs={{0,32},{32,64},{64,96},{96,0},{1,33},{33,65},{65,97},{97,1},{2,34}... | collective-permute-start | bytes 2752520 | tf_op jit(solution)/shard_map/ppermute | solution.py:622
  519.3 39.3 %collective-permute-start.53 = (f32[896,256]{1,0:T(8,128)S(1)}, f32[896,256]{1,0:T(8,128)S(1)}, u32[]{:S(2)}, u32[]{:S(2)}) collective-permute-start(f32[896,256]{1,0:T(8,128)S(1)} %copy-done.45), channel_id=1, source_target_pairs={{0,32},{32,64},{64,96},{96,0},{1,33},{33,65},{65,97},{97,1},{2,34}... | collective-permute-start | bytes 2752520 | tf_op jit(solution)/shard_map/ppermute | solution.py:622
  519.3 25.8 %collective-permute-start.59 = (f32[640,256]{1,0:T(8,128)S(1)}, f32[640,256]{1,0:T(8,128)S(1)}, u32[]{:S(2)}, u32[]{:S(2)}) collective-permute-start(f32[640,256]{1,0:T(8,128)S(1)} %copy-done.47), channel_id=1, source_target_pairs={{0,96},{32,0},{64,32},{96,64},{1,97},{33,1},{65,33},{97,65},{2,98}... | collective-permute-start | bytes 1966088 | tf_op jit(solution)/shard_map/ppermute | solution.py:622
  522.0 45.0 %collective-permute-start.55 = (f32[896,256]{1,0:T(8,128)S(1)}, f32[896,256]{1,0:T(8,128)S(1)}, u32[]{:S(2)}, u32[]{:S(2)}) collective-permute-start(f32[896,256]{1,0:T(8,128)S(1)} %add.124), channel_id=1, source_target_pairs={{0,96},{32,0},{64,32},{96,64},{1,97},{33,1},{65,33},{97,65},{2,98}... | collective-permute-start | bytes 2752520 | tf_op jit(solution)/shard_map/ppermute | solution.py:622
  526.1 46.5 %collective-permute-start.61 = (f32[640,256]{1,0:T(8,128)S(1)}, f32[640,256]{1,0:T(8,128)S(1)}, u32[]{:S(2)}, u32[]{:S(2)}) collective-permute-start(f32[640,256]{1,0:T(8,128)S(1)} %copy-done.46), channel_id=1, source_target_pairs={{0,32},{32,64},{64,96},{96,0},{1,33},{33,65},{65,97},{97,1},{2,34}... | collective-permute-start | bytes 1966088 | tf_op jit(solution)/shard_map/ppermute | solution.py:622
  539.0 47.8 %collective-permute-start.58 = (f32[640,256]{1,0:T(8,128)S(1)}, f32[640,256]{1,0:T(8,128)}, u32[]{:S(2)}, u32[]{:S(2)}) collective-permute-start(f32[640,256]{1,0:T(8,128)S(1)} %add.126), channel_id=1, source_target_pairs={{0,32},{32,64},{64,96},{96,0},{1,33},{33,65},{65,97},{97,1},{2,34}... | collective-permute-start | bytes 1966088 | tf_op jit(solution)/shard_map/ppermute | solution.py:622
  545.1 54.5 %collective-permute-start.63 = (f32[640,256]{1,0:T(8,128)}, f32[640,256]{1,0:T(8,128)}, u32[]{:S(2)}, u32[]{:S(2)}) collective-permute-start(f32[640,256]{1,0:T(8,128)} %add.130), channel_id=1, source_target_pairs={{0,96},{32,0},{64,32},{96,64},{1,97},{33,1},{65,33},{97,65},{2,98}... | collective-permute-start | bytes 1966088 | tf_op jit(solution)/shard_map/ppermute | solution.py:622
  558.6 45.0 %collective-permute-start.67 = (f32[896,256]{1,0:T(8,128)}, f32[896,256]{1,0:T(8,128)}, u32[]{:S(2)}, u32[]{:S(2)}) collective-permute-start(f32[896,256]{1,0:T(8,128)} %add_add_fusion.4.own_ref), channel_id=1, source_target_pairs={{1,16},{9,24},{16,1},{24,9},{3,18},{11,26},{18,3},{26,11},{5,20},{... | collective-permute-start | bytes 2752520 | tf_op jit(solution)/shard_map/ppermute | solution.py:638
  567.1 38.4 %collective-permute-start.70 = (f32[896,256]{1,0:T(8,128)}, f32[896,256]{1,0:T(8,128)}, u32[]{:S(2)}, u32[]{:S(2)}) collective-permute-start(f32[896,256]{1,0:T(8,128)} %add_add_fusion.3), channel_id=1, source_target_pairs={{0,8},{1,24},{8,0},{9,16},{16,9},{17,25},{24,1},{25,17},{2,10},{3,... | collective-permute-start | bytes 2752520 | tf_op jit(solution)/shard_map/ppermute | solution.py:638
  573.4 53.2 %collective-permute-start.52 = (f32[896,256]{1,0:T(8,128)}, f32[896,256]{1,0:T(8,128)}, u32[]{:S(2)}, u32[]{:S(2)}) collective-permute-start(f32[896,256]{1,0:T(8,128)} %add_add_fusion.6.own_ref), channel_id=1, source_target_pairs={{1,16},{9,24},{16,1},{24,9},{3,18},{11,26},{18,3},{26,11},{5,20},{... | collective-permute-start | bytes 2752520 | tf_op jit(solution)/shard_map/ppermute | solution.py:638
  586.7 40.9 %collective-permute-start.56 = (f32[896,256]{1,0:T(8,128)}, f32[896,256]{1,0:T(8,128)}, u32[]{:S(2)}, u32[]{:S(2)}) collective-permute-start(f32[896,256]{1,0:T(8,128)} %add_add_fusion.5), channel_id=1, source_target_pairs={{0,8},{1,24},{8,0},{9,16},{16,9},{17,25},{24,1},{25,17},{2,10},{3,... | collective-permute-start | bytes 2752520 | tf_op jit(solution)/shard_map/ppermute | solution.py:638
  599.6 41.0 %collective-permute-start.60 = (f32[640,256]{1,0:T(8,128)}, f32[640,256]{1,0:T(8,128)}, u32[]{:S(2)}, u32[]{:S(2)}) collective-permute-start(f32[640,256]{1,0:T(8,128)} %add_add_fusion.8.own_ref), channel_id=1, source_target_pairs={{1,16},{9,24},{16,1},{24,9},{3,18},{11,26},{18,3},{26,11},{5,20},{... | collective-permute-start | bytes 1966088 | tf_op jit(solution)/shard_map/ppermute | solution.py:638
  603.6 37.5 %collective-permute-start.64 = (f32[640,256]{1,0:T(8,128)}, f32[640,256]{1,0:T(8,128)}, u32[]{:S(2)}, u32[]{:S(2)}) collective-permute-start(f32[640,256]{1,0:T(8,128)} %add_add_fusion.7), channel_id=1, source_target_pairs={{0,8},{1,24},{8,0},{9,16},{16,9},{17,25},{24,1},{25,17},{2,10},{3,... | collective-permute-start | bytes 1966088 | tf_op jit(solution)/shard_map/ppermute | solution.py:638
  (85 other events, 1122.5 us)
Sparse Core Ops, SparseCore 0:
  29.5 86.9 all-gather.2
  118.7 72.9 all-gather.4
  355.7 131.5 reduce-scatter.4
  490.6 132.0 reduce-scatter.2

commit v8 on v6

--- a/solution.py
+++ b/solution.py
@@ -678,7 +678,10 @@
         qkv_blk = o_blk + head
 
         def gather_rows(blocks):
-            return [turn(jnp.where(even_y, blocks[flip], blocks[1 - flip]), flip, True) for flip in range(2)]
+            got = []
+            for flip in (1, 0):
+                got.insert(0, turn(jnp.where(even_y, blocks[flip], blocks[1 - flip]), flip, True))
+            return got
 
         def gather_weight(piece):
             left, right = [], []
@@ -734,8 +737,8 @@
 
         x_rows = after(x_in[0], cos_tab, sin_tab).astype(F32)
         normed, norm_pull = jax.vjp(lambda row_vals: norm_fwd(row_vals, norm_gain), x_rows)
-        h_all = lax.all_gather(after(normed.astype(BF16), wf_piece[0], wf_piece[1]), ("y", "x"), axis=0, tiled=True)
-        dy_all = lax.all_gather(after(dy_in[0], *wf_piece), ("y", "x"), axis=0, tiled=True)
+        h_all = lax.all_gather(after(normed.astype(BF16), wf_piece[1]), ("y", "x"), axis=0, tiled=True)
+        dy_all = lax.all_gather(after(dy_in[0], wf_piece[1]), ("y", "x"), axis=0, tiled=True)
         wf_parts = gather_weight(wf_piece)
         ws_parts = gather_weight(ws_piece)
 
@@ -756,10 +759,10 @@
 
         dy_picked = pick_cols(after(pos, y_part), dy_all)
         dy_recv = swap_c(dy_picked)
-        g_act = grad_start([(act_t, act_recv, dy_all, dy_recv, ff_blk, 0)], dy_picked)
-        d_act, d_attn = nn_pieces(after(pos, g_act[3][0]), dy_all, ws_parts, (ff_blk, o_blk), 256)
+        d_act, d_attn = nn_pieces(after(pos, dy_picked), dy_all, ws_parts, (ff_blk, o_blk), 256)
         d_attn_other = swap_c(my_rows(d_attn, False))
-        d_gate_up, d_gate_up_t = act_bwd(gate_up, d_act)
+        g_act = grad_start([(act_t, act_recv, dy_all, dy_recv, ff_blk, 0)], d_attn)
+        d_gate_up, d_gate_up_t = act_bwd(gate_up, after(d_act, g_act[3][0]))
         d_gate_up_recv = swap_c(d_gate_up_t)
         d_queries, keep, send = attn_bwd(after(pos, d_gate_up_t), qkv_seq, d_attn, d_attn_other, cos_tab, sin_tab)
         got = swap_y(send)

time: 643 us -> 658 us (1.023)
  starting transfers between devices: 101 us -> 128 us
  waiting for transfers between devices: 265 us -> 255 us
    ppermute x12, starting transfers between devices: 34.1 us -> 58.3 us  [turn(): return lax.ppermute(val, ('y', 'c'), pairs)]
    ppermute x36, waiting for transfers between devices: 154 us -> 135 us  [hop_z(): return lax.ppermute(val, 'z', ring(step, NZ))]
    ppermute x12, waiting for transfers between devices: 89.3 us -> 100 us  [turn(): return lax.ppermute(val, ('y', 'c'), pairs)]
  transfers between devices with their start and end apart: 81 -> 81, of which waited for: 32 -> 29; matrix products, arithmetic and copies ran while one was open for 7% -> 7% of each run, Pallas kernels for 25% -> 24%
where the time goes in v8:
time: 658 us; the launch traced here: 650 us
  waiting for transfers between devices  255 us (39%)
  Pallas kernels  193 us (29%)
  starting transfers between devices  128 us (19%)
  other arithmetic  39.6 us (6%)
  local copies, waits for them, and re-layouts  19.1 us (3%)
  between operations  15.2 us (2%)
    ppermute x36, waiting for transfers between devices, hop_z(): return lax.ppermute(val, 'z', ring(step, NZ))  135 us
    ppermute x12, waiting for transfers between devices, turn(): return lax.ppermute(val, ('y', 'c'), pairs)  100 us
    ppermute x12, starting transfers between devices, turn(): return lax.ppermute(val, ('y', 'c'), pairs)  58.3 us
    pallas_call x4, Pallas kernels, grad_pieces(): pl.pallas_call(functools.partial(grad_kernel, heights), grid_spec=pltpu.P...  53 us
    pallas_call x2, Pallas kernels, nn_pieces(): pl.pallas_call(functools.partial(nn_kernel, keys, 2, len(widths), tile),...  44.7 us
    ppermute x36, starting transfers between devices, hop_z(): return lax.ppermute(val, 'z', ring(step, NZ))  43.9 us
    pallas_call x2, Pallas kernels, nt_pieces(): pl.pallas_call(functools.partial(nt_kernel, keys, sides, first_row), grid...  43.7 us
    ppermute x26, starting transfers between devices, swap_c(): return lax.ppermute(val, 'c', [(0, 1), (1, 0)])  21 us
  transfers between devices with their start and end apart: 81, of which 29 were waited for; matrix products, arithmetic and copies ran while one was open for 7% of the time, Pallas kernels for 24%

profile of v8, /device:TPU:1, one launch (start us, length us, event | category | flops | bytes accessed | tf_op | source)
XLA Modules:
  0.0 650.0 jit_solution(16909200072040107307)
XLA Ops:
  12.1 4.1 collective-permute-start
  19.8 9.6 %collective-permute-done.refs_1_.refs_4_ = bf16[256,2176]{1,0:T(8,128)(2,1)S(1)} collective-permute-done((bf16[256,2176]{1,0:T(8,128)(2,1)S(1)}, bf16[256,2176]{1,0:T(8,128)(2,1)S(1)}, u32[]{:S(2)}, u32[]{:S(2)}) %collective-permute-start) | collective-permute-done | bytes 1114144 | tf_op jit(solution)/shard_map/ppermute | solution.py:638
  30.2 3.8 collective-permute-start.1
  37.1 26.5 %collective-permute-done.1.refs_0_.refs_3_ = bf16[256,2176]{1,0:T(8,128)(2,1)S(1)} collective-permute-done((bf16[256,2176]{1,0:T(8,128)(2,1)}, bf16[256,2176]{1,0:T(8,128)(2,1)S(1)}, u32[]{:S(2)}, u32[]{:S(2)}) %collective-permute-start.1) | collective-permute-done | bytes 1114144 | tf_op jit(solution)/shard_map/ppermute | solution.py:638
  68.8 4.6 collective-permute-start.20
  73.4 18.0 %collective-permute-done.20.refs_3_.refs_0_ = bf16[256,1152]{1,0:T(8,128)(2,1)} collective-permute-done((bf16[256,1152]{1,0:T(8,128)(2,1)S(1)}, bf16[256,1152]{1,0:T(8,128)(2,1)}, u32[]{:S(2)}, u32[]{:S(2)}) %collective-permute-start.20) | collective-permute-done | bytes 589856 | tf_op jit(solution)/shard_map/ppermute | solution.py:638
  92.6 16.9 %collective-permute-done.5.refs_5_.refs_8_ = bf16[256,2176]{1,0:T(8,128)(2,1)S(1)} collective-permute-done((bf16[256,2176]{1,0:T(8,128)(2,1)S(1)}, bf16[256,2176]{1,0:T(8,128)(2,1)S(1)}, u32[]{:S(2)}, u32[]{:S(2)}) %collective-permute-start.5) | collective-permute-done | bytes 1114144 | tf_op jit(solution)/shard_map/ppermute | solution.py:622
  111.9 6.3 collective-permute-done.9.refs_9_.refs_16_
  118.8 12.1 %collective-permute-done.12.refs_12_.refs_11_ = bf16[256,2176]{1,0:T(8,128)(2,1)} collective-permute-done((bf16[256,2176]{1,0:T(8,128)(2,1)S(1)}, bf16[256,2176]{1,0:T(8,128)(2,1)}, u32[]{:S(2)}, u32[]{:S(2)}) %collective-permute-start.12) | collective-permute-done | bytes 1114144 | tf_op jit(solution)/shard_map/ppermute | solution.py:622
  137.4 27.1 %shard_map.153 = (bf16[1024,1792]{1,0:T(8,128)(2,1)}, bf16[1024,384]{1,0:T(8,128)(2,1)}) custom-call(s32[4]{0:T(128)} %pad_add_fusion.pos_ref, bf16[1024,4096]{1,0:T(8,128)(2,1)} %all-gather.3.cloned.1.call-done.acts_ref.in_ref.refs_2_.refs_6_, bf16[256,2176]{1,0:T(8,128)(2,1)} %copy-done.3, bf16[256,2176]{1,0:T(8,128)(2,1)} %copy-done.2, ...), custom_call_target="tpu_custom_call" | custom-call | flops 912680576 | bytes 26214400 | tf_op jit(solution)/shard_map/pallas_call | solution.py:330
  173.0 6.8 %collective-permute-done.18.other_third_ref = bf16[512,128]{1,0:T(8,128)(2,1)S(1)} collective-permute-done((bf16[512,128]{1,0:T(8,128)(2,1)S(1)}, bf16[512,128]{1,0:T(8,128)(2,1)S(1)}, u32[]{:S(2)}, u32[]{:S(2)}) %collective-permute-start.18) | collective-permute-done | bytes 131104 | tf_op jit(solution)/shard_map/ppermute | solution.py:643
  179.7 4.9 collective-permute-done.17.own_third_ref
  186.8 4.8 act_fwd.1
  191.6 4.1 shard_map.154
  195.8 5.6 shard_map.155
  209.7 16.9 %shard_map.156 = f32[1024,4096]{1,0:T(8,128)} custom-call(s32[4]{0:T(128)} %pad_add_fusion.pos_ref, bf16[16,64,896]{2,1,0:T(8,128)(2,1)} %bitcast.30, bf16[8,64,256]{2,1,0:T(8,128)(2,1)} %bitcast.33, bf16[8,64,256]{2,1,0:T(8,128)(2,1)} %bitcast.34, bf16[256,1152]{1,0:T(8,128)(2,1)} %collective-permute-done.20.refs_3_.refs_0_, ...), custom_call_target="tpu_custom_call" | custom-call | flops 483183808 | bytes 26214400 | tf_op jit(solution)/shard_map/pallas_call | solution.py:424
  226.6 4.1 shard_map.157
  231.3 8.5 %collective-permute-start.42 = (bf16[1024,2048]{1,0:T(8,128)(2,1)}, bf16[1024,2048]{1,0:T(8,128)(2,1)}, u32[]{:S(2)}, u32[]{:S(2)}) collective-permute-start(bf16[1024,2048]{1,0:T(8,128)(2,1)} %shard_map.154), channel_id=1, source_target_pairs={{0,1},{1,0},{2,3},{3,2},{4,5},{5,4},{6,7},{7,6},{8,9},{9,8},{10,11... | collective-permute-start | bytes 12582920 | tf_op jit(solution)/shard_map/ppermute | solution.py:626
  239.9 17.6 %shard_map.158 = (bf16[1024,896]{1,0:T(8,128)(2,1)}, bf16[1024,256]{1,0:T(8,128)(2,1)}) custom-call(s32[4]{0:T(128)} %pad_add_fusion.pos_ref, bf16[1024,4096]{1,0:T(8,128)(2,1)} %all-gather.5.cloned.1.call-done.in_ref.acts_ref.refs_2_, bf16[256,1152]{1,0:T(8,128)(2,1)} %collective-permute-done.20.refs_3_.refs_0_, ...), custom_call_target="tpu_custom_call" | custom-call | flops 483183808 | bytes 17825792 | tf_op jit(solution)/shard_map/pallas_call | solution.py:330
  257.6 13.2 %grad.4 = (f32[896,256]{1,0:T(8,128)}, f32[896,256]{1,0:T(8,128)}, f32[896,256]{1,0:T(8,128)}, f32[896,256]{1,0:T(8,128)}, f32[896,256]{1,0:T(8,128)}, /*index=5...) custom-call(s32[4]{0:T(128)} %pad_add_fusion.pos_ref, bf16[896,1024]{1,0:T(8,128)(2,1)} %get-tuple-element.81.refs_0_, ...), custom_call_target="tpu_custom_call" | custom-call | flops 375809632 | bytes 8388608 | tf_op jit(solution)/shard_map/grad/pallas_call | solution.py:537
  270.7 6.9 %act_bwd.1 = (bf16[1024,1792]{1,0:T(8,128)(2,1)}, bf16[1792,1024]{1,0:T(8,128)(2,1)}) custom-call(bf16[1024,1792]{1,0:T(8,128)(2,1)} %get-tuple-element.80.ab_ref, bf16[1024,896]{1,0:T(8,128)(2,1)} %get-tuple-element.96.du_ref), custom_call_target="tpu_custom_call" | custom-call | flops 400000000 | bytes 14000000 | tf_op jit(solution)/shard_map/act_bwd/pallas_call | solution.py:260
  285.4 8.1 %shard_map.159 = (bf16[2,512,256]{2,1,0:T(8,128)(2,1)}, f32[2,512,128]{2,1,0:T(8,128)}, f32[2,512,128]{2,1,0:T(8,128)}) custom-call(s32[4]{0:T(128)} %pad_add_fusion.pos_ref, bf16[2,512,512]{2,1,0:T(8,128)(2,1)} %get-tuple-element.102.seq_ref, bf16[1024,256]{1,0:T(8,128)(2,1)} %get-tuple-element.93.own_ref, bf16[512,256]{1,0:T(8,128)(2,1)} %copy-done.53, ...), custom_call_target="tpu_custom_call" | custom-call | flops 800000000 | bytes 4000000 | tf_op jit(solution)/shard_map/pallas_call | solution.py:142
  295.2 6.0 collective-permute-done.38
  306.0 13.1 %grad.5 = (f32[896,256]{1,0:T(8,128)}, f32[896,256]{1,0:T(8,128)}, f32[896,256]{1,0:T(8,128)}, f32[896,256]{1,0:T(8,128)}, f32[896,256]{1,0:T(8,128)}, /*index=5...) custom-call(s32[4]{0:T(128)} %pad_add_fusion.pos_ref, bf16[1792,1024]{1,0:T(8,128)(2,1)} %get-tuple-element.100.refs_0_, ...), custom_call_target="tpu_custom_call" | custom-call | flops 375809632 | bytes 8388608 | tf_op jit(solution)/shard_map/grad/pallas_call | solution.py:537
  319.1 3.2 shard_map.160
  327.6 26.8 %shard_map.161 = f32[1024,4096]{1,0:T(8,128)} custom-call(s32[4]{0:T(128)} %pad_add_fusion.pos_ref, bf16[16,64,1792]{2,1,0:T(8,128)(2,1)} %bitcast.28, bf16[8,64,384]{2,1,0:T(8,128)(2,1)} %bitcast.31, bf16[8,64,384]{2,1,0:T(8,128)(2,1)} %bitcast.32, bf16[256,2176]{1,0:T(8,128)(2,1)} %copy-done.3, bf16[256,2176]{1,0:T(8,128)(2,1)} %copy-done.2, ...), custom_call_target="tpu_custom_call" | custom-call | flops 912680576 | bytes 34603008 | tf_op jit(solution)/shard_map/pallas_call | solution.py:424
  360.5 17.6 %collective-permute-done.74 = f32[896,256]{1,0:T(8,128)S(1)} collective-permute-done((f32[896,256]{1,0:T(8,128)}, f32[896,256]{1,0:T(8,128)S(1)}, u32[]{:S(2)}, u32[]{:S(2)}) %collective-permute-start.74) | collective-permute-done | bytes 917536 | tf_op jit(solution)/shard_map/ppermute | solution.py:622
  383.5 7.9 %collective-permute-start.76 = (f32[896,256]{1,0:T(8,128)}, f32[896,256]{1,0:T(8,128)}, u32[]{:S(2)}, u32[]{:S(2)}) collective-permute-start(f32[896,256]{1,0:T(8,128)} %add_add_fusion.1), channel_id=1, source_target_pairs={{0,8},{1,24},{8,0},{9,16},{16,9},{17,25},{24,1},{25,17},{2,10},{3,... | collective-permute-start | bytes 2752520 | tf_op jit(solution)/shard_map/ppermute | solution.py:638
  392.5 4.3 collective-permute-done.72
  399.4 3.4 collective-permute-start.66
  402.8 13.6 %collective-permute-done.46 = f32[896,256]{1,0:T(8,128)} collective-permute-done((f32[896,256]{1,0:T(8,128)}, f32[896,256]{1,0:T(8,128)}, u32[]{:S(2)}, u32[]{:S(2)}) %collective-permute-start.46) | collective-permute-done | bytes 917536 | tf_op jit(solution)/shard_map/ppermute | solution.py:622
  420.9 13.6 %grad.6 = (f32[896,256]{1,0:T(8,128)}, f32[896,256]{1,0:T(8,128)}, f32[896,256]{1,0:T(8,128)}, f32[896,256]{1,0:T(8,128)}, f32[896,256]{1,0:T(8,128)}, /*index=5...) custom-call(s32[4]{0:T(128)} %pad_add_fusion.pos_ref, bf16[1792,1024]{1,0:T(8,128)(2,1)} %get-tuple-element.100.refs_0_, ...), custom_call_target="tpu_custom_call" | custom-call | flops 375809632 | bytes 8388608 | tf_op jit(solution)/shard_map/grad/pallas_call | solution.py:537
  439.1 13.1 %grad.7 = (f32[640,256]{1,0:T(8,128)}, f32[640,256]{1,0:T(8,128)}, f32[640,256]{1,0:T(8,128)}, f32[640,256]{1,0:T(8,128)}, f32[640,256]{1,0:T(8,128)}, /*index=5...) custom-call(s32[4]{0:T(128)} %pad_add_fusion.pos_ref, bf16[256,1024]{1,0:T(8,128)(2,1)} %copy-done.16, ...), custom_call_target="tpu_custom_call" | custom-call | flops 268435456 | bytes 8388608 | tf_op jit(solution)/shard_map/grad/pallas_call | solution.py:537
  455.2 3.9 collective-permute-done.65
  460.6 18.2 %collective-permute-done.47 = f32[896,256]{1,0:T(8,128)} collective-permute-done((f32[896,256]{1,0:T(8,128)}, f32[896,256]{1,0:T(8,128)}, u32[]{:S(2)}, u32[]{:S(2)}) %collective-permute-start.47) | collective-permute-done | bytes 917536 | tf_op jit(solution)/shard_map/ppermute | solution.py:622
  481.8 11.0 %collective-permute-done.57 = f32[640,256]{1,0:T(8,128)S(1)} collective-permute-done((f32[640,256]{1,0:T(8,128)}, f32[640,256]{1,0:T(8,128)S(1)}, u32[]{:S(2)}, u32[]{:S(2)}) %collective-permute-start.57) | collective-permute-done | bytes 655392 | tf_op jit(solution)/shard_map/ppermute | solution.py:622
  497.9 7.0 %collective-permute-done.62 = f32[640,256]{1,0:T(8,128)S(1)} collective-permute-done((f32[640,256]{1,0:T(8,128)}, f32[640,256]{1,0:T(8,128)S(1)}, u32[]{:S(2)}, u32[]{:S(2)}) %collective-permute-start.62) | collective-permute-done | bytes 655392 | tf_op jit(solution)/shard_map/ppermute | solution.py:622
  510.3 14.2 %collective-permute-done.69 = f32[896,256]{1,0:T(8,128)S(1)} collective-permute-done((f32[896,256]{1,0:T(8,128)S(1)}, f32[896,256]{1,0:T(8,128)S(1)}, u32[]{:S(2)}, u32[]{:S(2)}) %collective-permute-start.69) | collective-permute-done | bytes 917536 | tf_op jit(solution)/shard_map/ppermute | solution.py:622
  524.5 15.8 %collective-permute-start.73 = (f32[896,256]{1,0:T(8,128)S(1)}, f32[896,256]{1,0:T(8,128)S(1)}, u32[]{:S(2)}, u32[]{:S(2)}) collective-permute-start(f32[896,256]{1,0:T(8,128)S(1)} %add_add_fusion.2.own_ref), channel_id=1, source_target_pairs={{1,16},{9,24},{16,1},{24,9},{3,18},{11,26},{18,3},{26,11},{5,20},{... | collective-permute-start | bytes 2752520 | tf_op jit(solution)/shard_map/ppermute | solution.py:638
  545.4 3.6 collective-permute-done.61
  549.0 12.6 %collective-permute-start.67 = (f32[896,256]{1,0:T(8,128)}, f32[896,256]{1,0:T(8,128)}, u32[]{:S(2)}, u32[]{:S(2)}) collective-permute-start(f32[896,256]{1,0:T(8,128)} %add_add_fusion.4.own_ref), channel_id=1, source_target_pairs={{1,16},{9,24},{16,1},{24,9},{3,18},{11,26},{18,3},{26,11},{5,20},{... | collective-permute-start | bytes 2752520 | tf_op jit(solution)/shard_map/ppermute | solution.py:638
  563.1 10.5 %collective-permute-done.73.first_ref = f32[896,256]{1,0:T(8,128)S(1)} collective-permute-done((f32[896,256]{1,0:T(8,128)S(1)}, f32[896,256]{1,0:T(8,128)S(1)}, u32[]{:S(2)}, u32[]{:S(2)}) %collective-permute-start.73) | collective-permute-done | bytes 917536 | tf_op jit(solution)/shard_map/ppermute | solution.py:638
  579.7 3.7 shard_map.164
  590.5 10.7 %collective-permute-done.67.first_ref = f32[896,256]{1,0:T(8,128)} collective-permute-done((f32[896,256]{1,0:T(8,128)}, f32[896,256]{1,0:T(8,128)}, u32[]{:S(2)}, u32[]{:S(2)}) %collective-permute-start.67) | collective-permute-done | bytes 917536 | tf_op jit(solution)/shard_map/ppermute | solution.py:638
  601.8 4.0 shard_map.163
  605.8 24.1 %collective-permute-done.52.first_ref = f32[896,256]{1,0:T(8,128)} collective-permute-done((f32[896,256]{1,0:T(8,128)}, f32[896,256]{1,0:T(8,128)}, u32[]{:S(2)}, u32[]{:S(2)}) %collective-permute-start.52) | collective-permute-done | bytes 917536 | tf_op jit(solution)/shard_map/ppermute | solution.py:638
  629.9 4.0 shard_map.162
  639.5 3.5 p_attn.1
  (300 shorter events, 134.9 us)
Async XLA Ops:
  7.2 130.3 %all-gather.3.cloned.1.call-start = ((), (), s32[]{:S(2)}) async-start(), calls=%async_computation.2 | async-start | bytes 8912896 | tf_op jit(solution)/shard_map/all_gather | solution.py:740
  29.4 197.2 %all-gather.5.cloned.1.call-start = ((), (), s32[]{:S(2)}) async-start(), calls=%async_computation.4 | async-start | bytes 8912896 | tf_op jit(solution)/shard_map/all_gather | solution.py:741
  30.2 603.7 %reduce-scatter.5.cloned.1.call-start = ((), (), s32[]{:S(2)}) async-start(), calls=%async_computation.5 | async-start | bytes 17825792 | tf_op jit(solution)/shard_map/reduce_scatter | solution.py:774
  30.2 33.4 %collective-permute-start.1 = (bf16[256,2176]{1,0:T(8,128)(2,1)}, bf16[256,2176]{1,0:T(8,128)(2,1)S(1)}, u32[]{:S(2)}, u32[]{:S(2)}) collective-permute-start(bf16[256,2176]{1,0:T(8,128)(2,1)} %get-tuple-element.148), channel_id=1, source_target_pairs={{0,0},{1,16},{8,8},{9,24},{16,1},{17,17},{24,9},{25,25},{2,2},{3,1... | collective-permute-start | bytes 3342344 | tf_op jit(solution)/shard_map/ppermute | solution.py:638
  36.0 32.8 %collective-permute-start.21 = (bf16[256,1152]{1,0:T(8,128)(2,1)S(1)}, bf16[256,1152]{1,0:T(8,128)(2,1)}, u32[]{:S(2)}, u32[]{:S(2)}) collective-permute-start(bf16[256,1152]{1,0:T(8,128)(2,1)S(1)} %get-tuple-element.150), channel_id=1, source_target_pairs={{0,8},{1,24},{8,0},{9,16},{16,9},{17,25},{24,1},{25,17},{2,10},{3,... | collective-permute-start | bytes 1769480 | tf_op jit(solution)/shard_map/ppermute | solution.py:638
  63.6 27.8 %collective-permute-start.8 = (bf16[256,2176]{1,0:T(8,128)(2,1)S(1)}, bf16[256,2176]{1,0:T(8,128)(2,1)S(1)}, u32[]{:S(2)}, u32[]{:S(2)}) collective-permute-start(bf16[256,2176]{1,0:T(8,128)(2,1)S(1)} %collective-permute-done.1.refs_0_.refs_3_), channel_id=1, source_target_pairs={{0,32},{32,64},{64,96},{96,0},{1,33},{33,65},{65,97},{97,1},{2,34}... | collective-permute-start | bytes 3342344 | tf_op jit(solution)/shard_map/ppermute | solution.py:622
  67.4 42.1 %collective-permute-start.5 = (bf16[256,2176]{1,0:T(8,128)(2,1)S(1)}, bf16[256,2176]{1,0:T(8,128)(2,1)S(1)}, u32[]{:S(2)}, u32[]{:S(2)}) collective-permute-start(bf16[256,2176]{1,0:T(8,128)(2,1)S(1)} %collective-permute-done.refs_1_.refs_4_), channel_id=1, source_target_pairs={{0,96},{32,0},{64,32},{96,64},{1,97},{33,1},{65,33},{97,65},{2,98}... | collective-permute-start | bytes 3342344 | tf_op jit(solution)/shard_map/ppermute | solution.py:622
  91.4 26.8 %collective-permute-start.9 = (bf16[256,2176]{1,0:T(8,128)(2,1)S(1)}, bf16[256,2176]{1,0:T(8,128)(2,1)S(1)}, u32[]{:S(2)}, u32[]{:S(2)}) collective-permute-start(bf16[256,2176]{1,0:T(8,128)(2,1)S(1)} %collective-permute-done.refs_1_.refs_4_), channel_id=1, source_target_pairs={{0,32},{32,64},{64,96},{96,0},{1,33},{33,65},{65,97},{97,1},{2,34}... | collective-permute-start | bytes 3342344 | tf_op jit(solution)/shard_map/ppermute | solution.py:622
  91.4 26.8 %collective-permute-start.3 = (bf16[256,2176]{1,0:T(8,128)(2,1)S(1)}, bf16[256,2176]{1,0:T(8,128)(2,1)S(1)}, u32[]{:S(2)}, u32[]{:S(2)}) collective-permute-start(bf16[256,2176]{1,0:T(8,128)(2,1)S(1)} %collective-permute-done.refs_1_.refs_4_), channel_id=1, source_target_pairs={{0,1},{1,0},{2,3},{3,2},{4,5},{5,4},{6,7},{7,6},{8,9},{9,8},{10,11... | collective-permute-start | bytes 3342344 | tf_op jit(solution)/shard_map/ppermute | solution.py:626
  91.5 39.4 %collective-permute-start.12 = (bf16[256,2176]{1,0:T(8,128)(2,1)S(1)}, bf16[256,2176]{1,0:T(8,128)(2,1)}, u32[]{:S(2)}, u32[]{:S(2)}) collective-permute-start(bf16[256,2176]{1,0:T(8,128)(2,1)S(1)} %collective-permute-done.8.refs_8_.refs_15_), channel_id=1, source_target_pairs={{0,32},{32,64},{64,96},{96,0},{1,33},{33,65},{65,97},{97,1},{2,34}... | collective-permute-start | bytes 3342344 | tf_op jit(solution)/shard_map/ppermute | solution.py:622
  92.6 38.3 %collective-permute-start.10 = (bf16[256,2176]{1,0:T(8,128)(2,1)S(1)}, bf16[256,2176]{1,0:T(8,128)(2,1)S(1)}, u32[]{:S(2)}, u32[]{:S(2)}) collective-permute-start(bf16[256,2176]{1,0:T(8,128)(2,1)S(1)} %collective-permute-done.8.refs_8_.refs_15_), channel_id=1, source_target_pairs={{0,1},{1,0},{2,3},{3,2},{4,5},{5,4},{6,7},{7,6},{8,9},{9,8},{10,11... | collective-permute-start | bytes 3342344 | tf_op jit(solution)/shard_map/ppermute | solution.py:626
  131.7 34.1 %collective-permute-start.33 = (bf16[256,1152]{1,0:T(8,128)(2,1)}, bf16[256,1152]{1,0:T(8,128)(2,1)}, u32[]{:S(2)}, u32[]{:S(2)}) collective-permute-start(bf16[256,1152]{1,0:T(8,128)(2,1)} %collective-permute-done.21.refs_4_.refs_1_), channel_id=1, source_target_pairs={{0,32},{32,64},{64,96},{96,0},{1,33},{33,65},{65,97},{97,1},{2,34}... | collective-permute-start | bytes 1769480 | tf_op jit(solution)/shard_map/ppermute | solution.py:622
  131.8 37.9 %collective-permute-start.25 = (bf16[256,1152]{1,0:T(8,128)(2,1)}, bf16[256,1152]{1,0:T(8,128)(2,1)}, u32[]{:S(2)}, u32[]{:S(2)}) collective-permute-start(bf16[256,1152]{1,0:T(8,128)(2,1)} %collective-permute-done.21.refs_4_.refs_1_), channel_id=1, source_target_pairs={{0,96},{32,0},{64,32},{96,64},{1,97},{33,1},{65,33},{97,65},{2,98}... | collective-permute-start | bytes 1769480 | tf_op jit(solution)/shard_map/ppermute | solution.py:622
  135.5 36.9 %collective-permute-start.23 = (bf16[256,1152]{1,0:T(8,128)(2,1)}, bf16[256,1152]{1,0:T(8,128)(2,1)}, u32[]{:S(2)}, u32[]{:S(2)}) collective-permute-start(bf16[256,1152]{1,0:T(8,128)(2,1)} %collective-permute-done.21.refs_4_.refs_1_), channel_id=1, source_target_pairs={{0,1},{1,0},{2,3},{3,2},{4,5},{5,4},{6,7},{7,6},{8,9},{9,8},{10,11... | collective-permute-start | bytes 1769480 | tf_op jit(solution)/shard_map/ppermute | solution.py:626
  137.2 35.3 %collective-permute-start.28 = (bf16[256,1152]{1,0:T(8,128)(2,1)}, bf16[256,1152]{1,0:T(8,128)(2,1)}, u32[]{:S(2)}, u32[]{:S(2)}) collective-permute-start(bf16[256,1152]{1,0:T(8,128)(2,1)} %collective-permute-done.20.refs_3_.refs_0_), channel_id=1, source_target_pairs={{0,32},{32,64},{64,96},{96,0},{1,33},{33,65},{65,97},{97,1},{2,34}... | collective-permute-start | bytes 1769480 | tf_op jit(solution)/shard_map/ppermute | solution.py:622
  165.8 36.7 %collective-permute-start.24 = (bf16[256,1152]{1,0:T(8,128)(2,1)}, bf16[256,1152]{1,0:T(8,128)(2,1)}, u32[]{:S(2)}, u32[]{:S(2)}) collective-permute-start(bf16[256,1152]{1,0:T(8,128)(2,1)} %collective-permute-done.20.refs_3_.refs_0_), channel_id=1, source_target_pairs={{0,96},{32,0},{64,32},{96,64},{1,97},{33,1},{65,33},{97,65},{2,98}... | collective-permute-start | bytes 1769480 | tf_op jit(solution)/shard_map/ppermute | solution.py:622
  172.5 31.5 %collective-permute-start.22 = (bf16[256,1152]{1,0:T(8,128)(2,1)}, bf16[256,1152]{1,0:T(8,128)(2,1)}, u32[]{:S(2)}, u32[]{:S(2)}) collective-permute-start(bf16[256,1152]{1,0:T(8,128)(2,1)} %collective-permute-done.20.refs_3_.refs_0_), channel_id=1, source_target_pairs={{0,1},{1,0},{2,3},{3,2},{4,5},{5,4},{6,7},{7,6},{8,9},{9,8},{10,11... | collective-permute-start | bytes 1769480 | tf_op jit(solution)/shard_map/ppermute | solution.py:626
  230.7 26.8 %collective-permute-start.37 = (bf16[1024,2048]{1,0:T(8,128)(2,1)}, bf16[1024,2048]{1,0:T(8,128)(2,1)}, u32[]{:S(2)}, u32[]{:S(2)}) collective-permute-start(bf16[1024,2048]{1,0:T(8,128)(2,1)} %shard_map.157), channel_id=1, source_target_pairs={{0,1},{1,0},{2,3},{3,2},{4,5},{5,4},{6,7},{7,6},{8,9},{9,8},{10,11... | collective-permute-start | bytes 12582920 | tf_op jit(solution)/shard_map/ppermute | solution.py:626
  231.3 74.6 %collective-permute-start.42 = (bf16[1024,2048]{1,0:T(8,128)(2,1)}, bf16[1024,2048]{1,0:T(8,128)(2,1)}, u32[]{:S(2)}, u32[]{:S(2)}) collective-permute-start(bf16[1024,2048]{1,0:T(8,128)(2,1)} %shard_map.154), channel_id=1, source_target_pairs={{0,1},{1,0},{2,3},{3,2},{4,5},{5,4},{6,7},{7,6},{8,9},{9,8},{10,11... | collective-permute-start | bytes 12582920 | tf_op jit(solution)/shard_map/ppermute | solution.py:626
  277.7 28.3 %collective-permute-start.41 = (bf16[1792,1024]{1,0:T(8,128)(2,1)}, bf16[1792,1024]{1,0:T(8,128)(2,1)}, u32[]{:S(2)}, u32[]{:S(2)}) collective-permute-start(bf16[1792,1024]{1,0:T(8,128)(2,1)} %get-tuple-element.100.refs_0_), channel_id=1, source_target_pairs={{0,1},{1,0},{2,3},{3,2},{4,5},{5,4},{6,7},{7,6},{8,9},{9,8},{10,11... | collective-permute-start | bytes 11010056 | tf_op jit(solution)/shard_map/ppermute | solution.py:626
  354.4 281.3 %reduce-scatter.3.cloned.1.call-start = ((), (), s32[]{:S(2)}) async-start(), calls=%async_computation.3 | async-start | bytes 17825792 | tf_op jit(solution)/shard_map/reduce_scatter | solution.py:757
  359.1 37.7 %collective-permute-start.72 = (f32[896,256]{1,0:T(8,128)}, f32[896,256]{1,0:T(8,128)}, u32[]{:S(2)}, u32[]{:S(2)}) collective-permute-start(f32[896,256]{1,0:T(8,128)} %get-tuple-element.145), channel_id=1, source_target_pairs={{0,96},{32,0},{64,32},{96,64},{1,97},{33,1},{65,33},{97,65},{2,98}... | collective-permute-start | bytes 2752520 | tf_op jit(solution)/shard_map/ppermute | solution.py:622
  359.1 40.4 %collective-permute-start.45 = (f32[896,256]{1,0:T(8,128)}, f32[896,256]{1,0:T(8,128)}, u32[]{:S(2)}, u32[]{:S(2)}) collective-permute-start(f32[896,256]{1,0:T(8,128)} %get-tuple-element.115), channel_id=1, source_target_pairs={{0,32},{32,64},{64,96},{96,0},{1,33},{33,65},{65,97},{97,1},{2,34}... | collective-permute-start | bytes 2752520 | tf_op jit(solution)/shard_map/ppermute | solution.py:622
  378.1 56.3 %collective-permute-start.71 = (f32[896,256]{1,0:T(8,128)}, f32[896,256]{1,0:T(8,128)}, u32[]{:S(2)}, u32[]{:S(2)}) collective-permute-start(f32[896,256]{1,0:T(8,128)} %add.115), channel_id=1, source_target_pairs={{0,32},{32,64},{64,96},{96,0},{1,33},{33,65},{65,97},{97,1},{2,34}... | collective-permute-start | bytes 2752520 | tf_op jit(solution)/shard_map/ppermute | solution.py:622
  378.2 38.3 %collective-permute-start.46 = (f32[896,256]{1,0:T(8,128)}, f32[896,256]{1,0:T(8,128)}, u32[]{:S(2)}, u32[]{:S(2)}) collective-permute-start(f32[896,256]{1,0:T(8,128)} %get-tuple-element.118), channel_id=1, source_target_pairs={{0,96},{32,0},{64,32},{96,64},{1,97},{33,1},{65,33},{97,65},{2,98}... | collective-permute-start | bytes 2752520 | tf_op jit(solution)/shard_map/ppermute | solution.py:622
  383.5 53.0 %collective-permute-start.76 = (f32[896,256]{1,0:T(8,128)}, f32[896,256]{1,0:T(8,128)}, u32[]{:S(2)}, u32[]{:S(2)}) collective-permute-start(f32[896,256]{1,0:T(8,128)} %add_add_fusion.1), channel_id=1, source_target_pairs={{0,8},{1,24},{8,0},{9,16},{16,9},{17,25},{24,1},{25,17},{2,10},{3,... | collective-permute-start | bytes 2752520 | tf_op jit(solution)/shard_map/ppermute | solution.py:638
  396.8 41.8 %collective-permute-start.49 = (bf16[384,1024]{1,0:T(8,128)(2,1)}, bf16[384,1024]{1,0:T(8,128)(2,1)}, u32[]{:S(2)}, u32[]{:S(2)}) collective-permute-start(bf16[384,1024]{1,0:T(8,128)(2,1)} %maximum_bitcast_fusion.refs_4_), channel_id=1, source_target_pairs={{0,1},{1,0},{2,3},{3,2},{4,5},{5,4},{6,7},{7,6},{8,9},{9,8},{10,11... | collective-permute-start | bytes 2359304 | tf_op jit(solution)/shard_map/ppermute | solution.py:626
  399.4 52.8 %collective-permute-start.66 = (f32[896,256]{1,0:T(8,128)}, f32[896,256]{1,0:T(8,128)}, u32[]{:S(2)}, u32[]{:S(2)}) collective-permute-start(f32[896,256]{1,0:T(8,128)} %get-tuple-element.141), channel_id=1, source_target_pairs={{0,96},{32,0},{64,32},{96,64},{1,97},{33,1},{65,33},{97,65},{2,98}... | collective-permute-start | bytes 2752520 | tf_op jit(solution)/shard_map/ppermute | solution.py:622
  416.5 37.1 %collective-permute-start.68 = (f32[896,256]{1,0:T(8,128)}, f32[896,256]{1,0:T(8,128)}, u32[]{:S(2)}, u32[]{:S(2)}) collective-permute-start(f32[896,256]{1,0:T(8,128)} %get-tuple-element.143), channel_id=1, source_target_pairs={{0,32},{32,64},{64,96},{96,0},{1,33},{33,65},{65,97},{97,1},{2,34}... | collective-permute-start | bytes 2752520 | tf_op jit(solution)/shard_map/ppermute | solution.py:622
  436.4 42.4 %collective-permute-start.47 = (f32[896,256]{1,0:T(8,128)}, f32[896,256]{1,0:T(8,128)}, u32[]{:S(2)}, u32[]{:S(2)}) collective-permute-start(f32[896,256]{1,0:T(8,128)} %get-tuple-element.122), channel_id=1, source_target_pairs={{0,32},{32,64},{64,96},{96,0},{1,33},{33,65},{65,97},{97,1},{2,34}... | collective-permute-start | bytes 2752520 | tf_op jit(solution)/shard_map/ppermute | solution.py:622
  438.6 55.7 %collective-permute-start.54 = (f32[896,256]{1,0:T(8,128)}, f32[896,256]{1,0:T(8,128)}, u32[]{:S(2)}, u32[]{:S(2)}) collective-permute-start(f32[896,256]{1,0:T(8,128)} %get-tuple-element.130), channel_id=1, source_target_pairs={{0,96},{32,0},{64,32},{96,64},{1,97},{33,1},{65,33},{97,65},{2,98}... | collective-permute-start | bytes 2752520 | tf_op jit(solution)/shard_map/ppermute | solution.py:622
  452.2 40.6 %collective-permute-start.57 = (f32[640,256]{1,0:T(8,128)}, f32[640,256]{1,0:T(8,128)S(1)}, u32[]{:S(2)}, u32[]{:S(2)}) collective-permute-start(f32[640,256]{1,0:T(8,128)} %get-tuple-element.133), channel_id=1, source_target_pairs={{0,32},{32,64},{64,96},{96,0},{1,33},{33,65},{65,97},{97,1},{2,34}... | collective-permute-start | bytes 1966088 | tf_op jit(solution)/shard_map/ppermute | solution.py:622
  453.5 51.8 %collective-permute-start.51 = (f32[896,256]{1,0:T(8,128)}, f32[896,256]{1,0:T(8,128)S(1)}, u32[]{:S(2)}, u32[]{:S(2)}) collective-permute-start(f32[896,256]{1,0:T(8,128)} %get-tuple-element.126), channel_id=1, source_target_pairs={{0,96},{32,0},{64,32},{96,64},{1,97},{33,1},{65,33},{97,65},{2,98}... | collective-permute-start | bytes 2752520 | tf_op jit(solution)/shard_map/ppermute | solution.py:622
  459.1 38.6 %collective-permute-start.59 = (f32[640,256]{1,0:T(8,128)}, f32[640,256]{1,0:T(8,128)S(1)}, u32[]{:S(2)}, u32[]{:S(2)}) collective-permute-start(f32[640,256]{1,0:T(8,128)} %get-tuple-element.134), channel_id=1, source_target_pairs={{0,96},{32,0},{64,32},{96,64},{1,97},{33,1},{65,33},{97,65},{2,98}... | collective-permute-start | bytes 1966088 | tf_op jit(solution)/shard_map/ppermute | solution.py:622
  492.8 31.7 %collective-permute-start.69 = (f32[896,256]{1,0:T(8,128)S(1)}, f32[896,256]{1,0:T(8,128)S(1)}, u32[]{:S(2)}, u32[]{:S(2)}) collective-permute-start(f32[896,256]{1,0:T(8,128)S(1)} %copy-done.33), channel_id=1, source_target_pairs={{0,96},{32,0},{64,32},{96,64},{1,97},{33,1},{65,33},{97,65},{2,98}... | collective-permute-start | bytes 2752520 | tf_op jit(solution)/shard_map/ppermute | solution.py:622
  494.3 46.0 %collective-permute-start.50 = (f32[896,256]{1,0:T(8,128)S(1)}, f32[896,256]{1,0:T(8,128)S(1)}, u32[]{:S(2)}, u32[]{:S(2)}) collective-permute-start(f32[896,256]{1,0:T(8,128)S(1)} %add.120), channel_id=1, source_target_pairs={{0,32},{32,64},{64,96},{96,0},{1,33},{33,65},{65,97},{97,1},{2,34}... | collective-permute-start | bytes 2752520 | tf_op jit(solution)/shard_map/ppermute | solution.py:622
  497.8 51.2 %collective-permute-start.53 = (f32[896,256]{1,0:T(8,128)S(1)}, f32[896,256]{1,0:T(8,128)S(1)}, u32[]{:S(2)}, u32[]{:S(2)}) collective-permute-start(f32[896,256]{1,0:T(8,128)S(1)} %copy-done.50), channel_id=1, source_target_pairs={{0,32},{32,64},{64,96},{96,0},{1,33},{33,65},{65,97},{97,1},{2,34}... | collective-permute-start | bytes 2752520 | tf_op jit(solution)/shard_map/ppermute | solution.py:622
  504.8 44.2 %collective-permute-start.61 = (f32[640,256]{1,0:T(8,128)S(1)}, f32[640,256]{1,0:T(8,128)S(1)}, u32[]{:S(2)}, u32[]{:S(2)}) collective-permute-start(f32[640,256]{1,0:T(8,128)S(1)} %copy-done.51), channel_id=1, source_target_pairs={{0,32},{32,64},{64,96},{96,0},{1,33},{33,65},{65,97},{97,1},{2,34}... | collective-permute-start | bytes 1966088 | tf_op jit(solution)/shard_map/ppermute | solution.py:622
  505.4 56.3 %collective-permute-start.55 = (f32[896,256]{1,0:T(8,128)S(1)}, f32[896,256]{1,0:T(8,128)S(1)}, u32[]{:S(2)}, u32[]{:S(2)}) collective-permute-start(f32[896,256]{1,0:T(8,128)S(1)} %add.124), channel_id=1, source_target_pairs={{0,96},{32,0},{64,32},{96,64},{1,97},{33,1},{65,33},{97,65},{2,98}... | collective-permute-start | bytes 2752520 | tf_op jit(solution)/shard_map/ppermute | solution.py:622
  524.5 49.1 %collective-permute-start.73 = (f32[896,256]{1,0:T(8,128)S(1)}, f32[896,256]{1,0:T(8,128)S(1)}, u32[]{:S(2)}, u32[]{:S(2)}) collective-permute-start(f32[896,256]{1,0:T(8,128)S(1)} %add_add_fusion.2.own_ref), channel_id=1, source_target_pairs={{1,16},{9,24},{16,1},{24,9},{3,18},{11,26},{18,3},{26,11},{5,20},{... | collective-permute-start | bytes 2752520 | tf_op jit(solution)/shard_map/ppermute | solution.py:638
  540.3 36.9 %collective-permute-start.58 = (f32[640,256]{1,0:T(8,128)S(1)}, f32[640,256]{1,0:T(8,128)}, u32[]{:S(2)}, u32[]{:S(2)}) collective-permute-start(f32[640,256]{1,0:T(8,128)S(1)} %add.126), channel_id=1, source_target_pairs={{0,32},{32,64},{64,96},{96,0},{1,33},{33,65},{65,97},{97,1},{2,34}... | collective-permute-start | bytes 1966088 | tf_op jit(solution)/shard_map/ppermute | solution.py:622
  549.0 36.9 %collective-permute-start.63 = (f32[640,256]{1,0:T(8,128)}, f32[640,256]{1,0:T(8,128)}, u32[]{:S(2)}, u32[]{:S(2)}) collective-permute-start(f32[640,256]{1,0:T(8,128)} %add.130), channel_id=1, source_target_pairs={{0,96},{32,0},{64,32},{96,64},{1,97},{33,1},{65,33},{97,65},{2,98}... | collective-permute-start | bytes 1966088 | tf_op jit(solution)/shard_map/ppermute | solution.py:622
  549.0 52.1 %collective-permute-start.67 = (f32[896,256]{1,0:T(8,128)}, f32[896,256]{1,0:T(8,128)}, u32[]{:S(2)}, u32[]{:S(2)}) collective-permute-start(f32[896,256]{1,0:T(8,128)} %add_add_fusion.4.own_ref), channel_id=1, source_target_pairs={{1,16},{9,24},{16,1},{24,9},{3,18},{11,26},{18,3},{26,11},{5,20},{... | collective-permute-start | bytes 2752520 | tf_op jit(solution)/shard_map/ppermute | solution.py:638
  561.6 40.1 %collective-permute-start.70 = (f32[896,256]{1,0:T(8,128)}, f32[896,256]{1,0:T(8,128)}, u32[]{:S(2)}, u32[]{:S(2)}) collective-permute-start(f32[896,256]{1,0:T(8,128)} %add_add_fusion.3), channel_id=1, source_target_pairs={{0,8},{1,24},{8,0},{9,16},{16,9},{17,25},{24,1},{25,17},{2,10},{3,... | collective-permute-start | bytes 2752520 | tf_op jit(solution)/shard_map/ppermute | solution.py:638
  574.5 55.4 %collective-permute-start.52 = (f32[896,256]{1,0:T(8,128)}, f32[896,256]{1,0:T(8,128)}, u32[]{:S(2)}, u32[]{:S(2)}) collective-permute-start(f32[896,256]{1,0:T(8,128)} %add_add_fusion.6.own_ref), channel_id=1, source_target_pairs={{1,16},{9,24},{16,1},{24,9},{3,18},{11,26},{18,3},{26,11},{5,20},{... | collective-permute-start | bytes 2752520 | tf_op jit(solution)/shard_map/ppermute | solution.py:638
  577.2 52.7 %collective-permute-start.56 = (f32[896,256]{1,0:T(8,128)}, f32[896,256]{1,0:T(8,128)}, u32[]{:S(2)}, u32[]{:S(2)}) collective-permute-start(f32[896,256]{1,0:T(8,128)} %add_add_fusion.5), channel_id=1, source_target_pairs={{0,8},{1,24},{8,0},{9,16},{16,9},{17,25},{24,1},{25,17},{2,10},{3,... | collective-permute-start | bytes 2752520 | tf_op jit(solution)/shard_map/ppermute | solution.py:638
  585.9 53.6 %collective-permute-start.60 = (f32[640,256]{1,0:T(8,128)}, f32[640,256]{1,0:T(8,128)}, u32[]{:S(2)}, u32[]{:S(2)}) collective-permute-start(f32[640,256]{1,0:T(8,128)} %add_add_fusion.8.own_ref), channel_id=1, source_target_pairs={{1,16},{9,24},{16,1},{24,9},{3,18},{11,26},{18,3},{26,11},{5,20},{... | collective-permute-start | bytes 1966088 | tf_op jit(solution)/shard_map/ppermute | solution.py:638
  601.2 38.3 %collective-permute-start.64 = (f32[640,256]{1,0:T(8,128)}, f32[640,256]{1,0:T(8,128)}, u32[]{:S(2)}, u32[]{:S(2)}) collective-permute-start(f32[640,256]{1,0:T(8,128)} %add_add_fusion.7), channel_id=1, source_target_pairs={{0,8},{1,24},{8,0},{9,16},{16,9},{17,25},{24,1},{25,17},{2,10},{3,... | collective-permute-start | bytes 1966088 | tf_op jit(solution)/shard_map/ppermute | solution.py:638
  (89 other events, 1260.4 us)
Sparse Core Ops, SparseCore 0:
  29.5 86.9 all-gather.2
  118.7 72.9 all-gather.4
  354.5 121.2 reduce-scatter.4
  479.1 141.5 reduce-scatter.2

commit v9 on v7

--- a/solution.py
+++ b/solution.py
@@ -278,7 +278,7 @@
     return pl.multiple_of((1 - pos_ref[2] if part else pos_ref[2]) * half, half)
 
 
-def nn_kernel(keys, first, count_out, tile, pos_ref, acts_ref, *refs):
+def nn_kernel(keys, first, count_out, tile, first_col, pos_ref, acts_ref, *refs):
     count = len(keys)
     halves = refs[: 2 * count]
     outs = refs[2 * count : 2 * count + count_out]
@@ -291,7 +291,8 @@
         copies.append([pltpu.make_async_copy(acts_ref.at[:, cols], acts_buf.at[:, pl.ds(idx * block, block)], acts_sem.at[idx])])
         for part in range(2):
             rows = pl.ds(idx * block + half_start(pos_ref, part, half), half)
-            copies[-1].append(pltpu.make_async_copy(halves[2 * idx + part], w_buf.at[rows], w_sem.at[2 * idx + part]))
+            source = halves[2 * idx + part].at[:, pl.ds(first_col, w_buf.shape[1])]
+            copies[-1].append(pltpu.make_async_copy(source, w_buf.at[rows], w_sem.at[2 * idx + part]))
     for group in copies:
         for copy in group:
             copy.start()
@@ -320,7 +321,7 @@
             start += width
 
 
-def nn_pieces(pos, acts, parts, widths, tile):
+def nn_pieces(pos, acts, parts, first_col, widths, tile):
     keys = [(step, other) for step in (0, 1, 3, 2) for other in range(2)]
     halves = [parts[step][other][part] for step, other in keys for part in range(2)]
     tokens, depth = acts.shape
@@ -328,7 +329,7 @@
     count = len(keys)
     anywhere = pl.BlockSpec(memory_space=pl.ANY)
     return pl.pallas_call(
-        functools.partial(nn_kernel, keys, 2, len(widths), tile),
+        functools.partial(nn_kernel, keys, 2, len(widths), tile, first_col),
         grid_spec=pltpu.PrefetchScalarGridSpec(
             num_scalar_prefetch=1,
             grid=(1,),
@@ -742,12 +743,13 @@
         wf_parts = gather_weight(wf_piece)
         ws_parts = gather_weight(ws_piece)
 
-        gate_up, qkv_tok = nn_pieces(pos, h_all, wf_parts, (2 * ff_blk, qkv_blk), 512)
+        (qkv_tok,) = nn_pieces(pos, h_all, wf_parts, 2 * ff_blk, (qkv_blk,), 512)
         third = qkv_tok[:, o_blk:]
         qkv_other = swap_c(my_rows(qkv_tok, False))
         third_own = swap_y(my_rows(third, True))
         third_other = swap_yc(my_rows(third, False))
-        act_val, act_t = act_fwd(after(gate_up, qkv_tok))
+        (gate_up,) = nn_pieces(after(pos, qkv_tok), h_all, wf_parts, 0, (2 * ff_blk,), 512)
+        act_val, act_t = act_fwd(gate_up)
         act_recv = swap_c(act_t)
         qkv_seq, attn_own, attn_other = attn_fwd(after(pos, act_t), qkv_tok, qkv_other, third_own, third_other, cos_tab, sin_tab)
         attn_got = swap_c(attn_other)
@@ -759,22 +761,22 @@
         h_recv = swap_c(h_picked)
         dy_picked = pick_cols(after(pos, h_picked), dy_all)
         dy_recv = swap_c(dy_picked)
-        g_act = grad_start([(act_t, act_recv, dy_all, dy_recv, ff_blk, 0)], dy_picked)
-        d_act, d_attn = nn_pieces(after(pos, g_act[3][0]), dy_all, ws_parts, (ff_blk, o_blk), 256)
+        d_act, d_attn = nn_pieces(after(pos, dy_picked), dy_all, ws_parts, 0, (ff_blk, o_blk), 256)
         d_attn_other = swap_c(my_rows(d_attn, False))
-        d_gate_up, d_gate_up_t = act_bwd(gate_up, d_act)
+        g_act = grad_start([(act_t, act_recv, dy_all, dy_recv, ff_blk, 0)], d_attn)
+        d_gate_up, d_gate_up_t = act_bwd(gate_up, after(d_act, g_act[3][0]))
         d_gate_up_recv = swap_c(d_gate_up_t)
         d_queries, keep, send = attn_bwd(after(pos, d_gate_up_t), qkv_seq, d_attn, d_attn_other, cos_tab, sin_tab)
         got = swap_y(send)
         g_act = grad_pass(g_act, d_queries)
         g_gate = grad_start([(d_gate_up_t, d_gate_up_recv, h_all, h_recv, ff_blk, 0)], *g_act[3])
-        b_act = grad_back(g_act, g_gate[3][0])
         d_own, d_other = attn_post(after(pos, g_gate[3][0]), d_queries, keep, got, cos_tab, sin_tab)
         d_got = swap_c(d_other)
         dh_part = nt_pieces(pos, [d_gate_up, d_own, d_got], wf_parts, chunk, 0, chunk)
         d_h = lax.psum_scatter(dh_part, ("y", "x"), scatter_dimension=0, tiled=True)
         g_gate = grad_pass(g_gate, dh_part)
         g_up = grad_start([(d_gate_up_t, d_gate_up_recv, h_all, h_recv, ff_blk, 1)], *g_gate[3])
+        b_act = grad_back(g_act, g_up[3][0])
         d_h = d_h.astype(BF16)
         dx_out = (dy_in[0].astype(F32) + norm_pull(d_h.astype(F32))[0]).astype(BF16)[None]
 

time: 660 us -> 669 us (1.014)
    ppermute x12, waiting for transfers between devices: 77.8 us -> 101 us  [turn(): return lax.ppermute(val, ('y', 'c'), pairs)]
    ppermute x36, waiting for transfers between devices: 159 us -> 142 us  [hop_z(): return lax.ppermute(val, 'z', ring(step, NZ))]
    pallas_call x2 -> x3, Pallas kernels: 44.7 us -> 50.7 us  [nn_pieces(): pl.pallas_call(functools.partial(nn_kernel, keys, 2, len(widths), tile, f...]
  transfers between devices with their start and end apart: 81 -> 81, of which waited for: 32 -> 30; matrix products, arithmetic and copies ran while one was open for 7% -> 8% of each run, Pallas kernels for 24% -> 25%
where the time goes in v9:
time: 669 us; the launch traced here: 658 us
  waiting for transfers between devices  257 us (38%)
  Pallas kernels  199 us (30%)
  starting transfers between devices  124 us (19%)
  other arithmetic  39.8 us (6%)
  local copies, waits for them, and re-layouts  23.5 us (4%)
  between operations  15.2 us (2%)
    ppermute x36, waiting for transfers between devices, hop_z(): return lax.ppermute(val, 'z', ring(step, NZ))  142 us
    ppermute x12, waiting for transfers between devices, turn(): return lax.ppermute(val, ('y', 'c'), pairs)  101 us
    ppermute x12, starting transfers between devices, turn(): return lax.ppermute(val, ('y', 'c'), pairs)  54.3 us
    pallas_call x4, Pallas kernels, grad_pieces(): pl.pallas_call(functools.partial(grad_kernel, heights), grid_spec=pltpu.P...  52.7 us
    pallas_call x3, Pallas kernels, nn_pieces(): pl.pallas_call(functools.partial(nn_kernel, keys, 2, len(widths), tile, f...  50.7 us
    pallas_call x2, Pallas kernels, nt_pieces(): pl.pallas_call(functools.partial(nt_kernel, keys, sides, first_row), grid...  43.7 us
    ppermute x36, starting transfers between devices, hop_z(): return lax.ppermute(val, 'z', ring(step, NZ))  42.8 us
    ppermute x26, starting transfers between devices, swap_c(): return lax.ppermute(val, 'c', [(0, 1), (1, 0)])  22.7 us
  transfers between devices with their start and end apart: 81, of which 30 were waited for; matrix products, arithmetic and copies ran while one was open for 8% of the time, Pallas kernels for 25%

profile of v9, /device:TPU:1, one launch (start us, length us, event | category | flops | bytes accessed | tf_op | source)
XLA Modules:
  0.0 658.4 jit_solution(10596781213733488915)
XLA Ops:
  12.1 4.1 collective-permute-start
  19.8 9.6 %collective-permute-done.refs_1_.refs_4_ = bf16[256,2176]{1,0:T(8,128)(2,1)S(1)} collective-permute-done((bf16[256,2176]{1,0:T(8,128)(2,1)S(1)}, bf16[256,2176]{1,0:T(8,128)(2,1)S(1)}, u32[]{:S(2)}, u32[]{:S(2)}) %collective-permute-start) | collective-permute-done | bytes 1114144 | tf_op jit(solution)/shard_map/ppermute | solution.py:639
  30.2 3.8 collective-permute-start.1
  39.8 23.9 %collective-permute-done.1.refs_0_.refs_3_ = bf16[256,2176]{1,0:T(8,128)(2,1)S(1)} collective-permute-done((bf16[256,2176]{1,0:T(8,128)(2,1)}, bf16[256,2176]{1,0:T(8,128)(2,1)S(1)}, u32[]{:S(2)}, u32[]{:S(2)}) %collective-permute-start.1) | collective-permute-done | bytes 1114144 | tf_op jit(solution)/shard_map/ppermute | solution.py:639
  68.9 4.7 collective-permute-start.20
  73.5 20.2 %collective-permute-done.20.refs_3_.refs_0_ = bf16[256,1152]{1,0:T(8,128)(2,1)} collective-permute-done((bf16[256,1152]{1,0:T(8,128)(2,1)S(1)}, bf16[256,1152]{1,0:T(8,128)(2,1)}, u32[]{:S(2)}, u32[]{:S(2)}) %collective-permute-start.20) | collective-permute-done | bytes 589856 | tf_op jit(solution)/shard_map/ppermute | solution.py:639
  94.4 15.1 %collective-permute-done.5.refs_5_.refs_8_ = bf16[256,2176]{1,0:T(8,128)(2,1)S(1)} collective-permute-done((bf16[256,2176]{1,0:T(8,128)(2,1)S(1)}, bf16[256,2176]{1,0:T(8,128)(2,1)S(1)}, u32[]{:S(2)}, u32[]{:S(2)}) %collective-permute-start.5) | collective-permute-done | bytes 1114144 | tf_op jit(solution)/shard_map/ppermute | solution.py:623
  112.0 8.4 %collective-permute-done.9.refs_9_.refs_16_ = bf16[256,2176]{1,0:T(8,128)(2,1)S(1)} collective-permute-done((bf16[256,2176]{1,0:T(8,128)(2,1)S(1)}, bf16[256,2176]{1,0:T(8,128)(2,1)S(1)}, u32[]{:S(2)}, u32[]{:S(2)}) %collective-permute-start.9) | collective-permute-done | bytes 1114144 | tf_op jit(solution)/shard_map/ppermute | solution.py:623
  121.0 12.5 %collective-permute-done.12.refs_12_.refs_11_ = bf16[256,2176]{1,0:T(8,128)(2,1)S(1)} collective-permute-done((bf16[256,2176]{1,0:T(8,128)(2,1)S(1)}, bf16[256,2176]{1,0:T(8,128)(2,1)S(1)}, u32[]{:S(2)}, u32[]{:S(2)}) %collective-permute-start.12) | collective-permute-done | bytes 1114144 | tf_op jit(solution)/shard_map/ppermute | solution.py:623
  140.7 9.6 %shard_map.153.own_ref = bf16[1024,384]{1,0:T(8,128)(2,1)} custom-call(s32[4]{0:T(128)} %pad_add_fusion.pos_ref, bf16[1024,4096]{1,0:T(8,128)(2,1)} %all-gather.3.cloned.1.call-done.acts_ref.in_ref.refs_2_.refs_6_, bf16[256,2176]{1,0:T(8,128)(2,1)} %copy-done.1, bf16[256,2176]{1,0:T(8,128)(2,1)} %copy-done, bf16[256,2176]{1,0:T(8,128)(2,1)} %copy-done.4, ...), custom_call_target="tpu_custom_call" | custom-call | flops 161061280 | bytes 11534336 | tf_op jit(solution)/shard_map/pallas_call | solution.py:331
  158.0 4.9 collective-permute-done.28.refs_15_.refs_8_
  165.3 5.0 collective-permute-done.17.own_third_ref
  172.6 23.4 %shard_map.154.ab_ref = bf16[1024,1792]{1,0:T(8,128)(2,1)} custom-call(s32[4]{0:T(128)} %pad_add_fusion.pos_ref, bf16[1024,4096]{1,0:T(8,128)(2,1)} %all-gather.3.cloned.1.call-done.acts_ref.in_ref.refs_2_.refs_6_, bf16[256,2176]{1,0:T(8,128)(2,1)} %copy-done.1, bf16[256,2176]{1,0:T(8,128)(2,1)} %copy-done, bf16[256,2176]{1,0:T(8,128)(2,1)} %copy-done.4, ...), custom_call_target="tpu_custom_call" | custom-call | flops 751619264 | bytes 23068672 | tf_op jit(solution)/shard_map/pallas_call | solution.py:331
  196.0 4.8 act_fwd.1
  200.8 5.6 shard_map.155
  214.6 16.9 %shard_map.156 = f32[1024,4096]{1,0:T(8,128)} custom-call(s32[4]{0:T(128)} %pad_add_fusion.pos_ref, bf16[16,64,896]{2,1,0:T(8,128)(2,1)} %bitcast.30, bf16[8,64,256]{2,1,0:T(8,128)(2,1)} %bitcast.33, bf16[8,64,256]{2,1,0:T(8,128)(2,1)} %bitcast.34, bf16[256,1152]{1,0:T(8,128)(2,1)} %collective-permute-done.20.refs_3_.refs_0_, ...), custom_call_target="tpu_custom_call" | custom-call | flops 483183808 | bytes 26214400 | tf_op jit(solution)/shard_map/pallas_call | solution.py:425
  231.5 4.1 shard_map.157
  235.7 4.1 shard_map.158
  240.1 8.9 %collective-permute-start.36 = (bf16[896,1024]{1,0:T(8,128)(2,1)}, bf16[896,1024]{1,0:T(8,128)(2,1)}, u32[]{:S(2)}, u32[]{:S(2)}) collective-permute-start(bf16[896,1024]{1,0:T(8,128)(2,1)} %get-tuple-element.79.refs_0_), channel_id=1, source_target_pairs={{0,1},{1,0},{2,3},{3,2},{4,5},{5,4},{6,7},{7,6},{8,9},{9,8},{10,11... | collective-permute-start | bytes 5505032 | tf_op jit(solution)/shard_map/ppermute | solution.py:627
  249.3 17.6 %shard_map.159 = (bf16[1024,896]{1,0:T(8,128)(2,1)}, bf16[1024,256]{1,0:T(8,128)(2,1)}) custom-call(s32[4]{0:T(128)} %pad_add_fusion.pos_ref, bf16[1024,4096]{1,0:T(8,128)(2,1)} %all-gather.5.cloned.1.call-done.in_ref.acts_ref.refs_2_, bf16[256,1152]{1,0:T(8,128)(2,1)} %collective-permute-done.20.refs_3_.refs_0_, ...), custom_call_target="tpu_custom_call" | custom-call | flops 483183808 | bytes 17825792 | tf_op jit(solution)/shard_map/pallas_call | solution.py:331
  267.0 13.2 %grad.4 = (f32[896,256]{1,0:T(8,128)}, f32[896,256]{1,0:T(8,128)}, f32[896,256]{1,0:T(8,128)}, f32[896,256]{1,0:T(8,128)}, f32[896,256]{1,0:T(8,128)}, /*index=5...) custom-call(s32[4]{0:T(128)} %pad_add_fusion.pos_ref, bf16[896,1024]{1,0:T(8,128)(2,1)} %get-tuple-element.79.refs_0_, ...), custom_call_target="tpu_custom_call" | custom-call | flops 375809632 | bytes 8388608 | tf_op jit(solution)/shard_map/grad/pallas_call | solution.py:538
  280.1 6.9 %act_bwd.1 = (bf16[1024,1792]{1,0:T(8,128)(2,1)}, bf16[1792,1024]{1,0:T(8,128)(2,1)}) custom-call(bf16[1024,1792]{1,0:T(8,128)(2,1)} %shard_map.154.ab_ref, bf16[1024,896]{1,0:T(8,128)(2,1)} %get-tuple-element.93.du_ref), custom_call_target="tpu_custom_call" | custom-call | flops 400000000 | bytes 14000000 | tf_op jit(solution)/shard_map/act_bwd/pallas_call | solution.py:260
  294.8 8.1 %shard_map.160 = (bf16[2,512,256]{2,1,0:T(8,128)(2,1)}, f32[2,512,128]{2,1,0:T(8,128)}, f32[2,512,128]{2,1,0:T(8,128)}) custom-call(s32[4]{0:T(128)} %pad_add_fusion.pos_ref, bf16[2,512,512]{2,1,0:T(8,128)(2,1)} %get-tuple-element.99.seq_ref, bf16[1024,256]{1,0:T(8,128)(2,1)} %get-tuple-element.90.own_ref, bf16[512,256]{1,0:T(8,128)(2,1)} %copy-done.54, ...), custom_call_target="tpu_custom_call" | custom-call | flops 800000000 | bytes 4000000 | tf_op jit(solution)/shard_map/pallas_call | solution.py:142
  304.7 5.7 collective-permute-done.38
  315.2 13.1 %grad.5 = (f32[896,256]{1,0:T(8,128)}, f32[896,256]{1,0:T(8,128)}, f32[896,256]{1,0:T(8,128)}, f32[896,256]{1,0:T(8,128)}, f32[896,256]{1,0:T(8,128)}, /*index=5...) custom-call(s32[4]{0:T(128)} %pad_add_fusion.pos_ref, bf16[1792,1024]{1,0:T(8,128)(2,1)} %get-tuple-element.97.refs_0_, ...), custom_call_target="tpu_custom_call" | custom-call | flops 375809632 | bytes 8388608 | tf_op jit(solution)/shard_map/grad/pallas_call | solution.py:538
  336.9 26.8 %shard_map.162 = f32[1024,4096]{1,0:T(8,128)} custom-call(s32[4]{0:T(128)} %pad_add_fusion.pos_ref, bf16[16,64,1792]{2,1,0:T(8,128)(2,1)} %bitcast.28, bf16[8,64,384]{2,1,0:T(8,128)(2,1)} %bitcast.31, bf16[8,64,384]{2,1,0:T(8,128)(2,1)} %bitcast.32, bf16[256,2176]{1,0:T(8,128)(2,1)} %copy-done.1, bf16[256,2176]{1,0:T(8,128)(2,1)} %copy-done, ...), custom_call_target="tpu_custom_call" | custom-call | flops 912680576 | bytes 34603008 | tf_op jit(solution)/shard_map/pallas_call | solution.py:425
  369.8 17.6 %collective-permute-done.74 = f32[896,256]{1,0:T(8,128)S(1)} collective-permute-done((f32[896,256]{1,0:T(8,128)}, f32[896,256]{1,0:T(8,128)S(1)}, u32[]{:S(2)}, u32[]{:S(2)}) %collective-permute-start.74) | collective-permute-done | bytes 917536 | tf_op jit(solution)/shard_map/ppermute | solution.py:623
  392.8 6.9 %collective-permute-start.76 = (f32[896,256]{1,0:T(8,128)}, f32[896,256]{1,0:T(8,128)}, u32[]{:S(2)}, u32[]{:S(2)}) collective-permute-start(f32[896,256]{1,0:T(8,128)} %add_add_fusion.1), channel_id=1, source_target_pairs={{0,8},{1,24},{8,0},{9,16},{16,9},{17,25},{24,1},{25,17},{2,10},{3,... | collective-permute-start | bytes 2752520 | tf_op jit(solution)/shard_map/ppermute | solution.py:639
  400.7 5.3 collective-permute-done.72
  408.7 3.4 collective-permute-start.66
  412.1 13.6 %collective-permute-done.46 = f32[896,256]{1,0:T(8,128)} collective-permute-done((f32[896,256]{1,0:T(8,128)}, f32[896,256]{1,0:T(8,128)}, u32[]{:S(2)}, u32[]{:S(2)}) %collective-permute-start.46) | collective-permute-done | bytes 917536 | tf_op jit(solution)/shard_map/ppermute | solution.py:623
  430.2 13.3 %grad.6 = (f32[896,256]{1,0:T(8,128)}, f32[896,256]{1,0:T(8,128)}, f32[896,256]{1,0:T(8,128)}, f32[896,256]{1,0:T(8,128)}, f32[896,256]{1,0:T(8,128)}, /*index=5...) custom-call(s32[4]{0:T(128)} %pad_add_fusion.pos_ref, bf16[1792,1024]{1,0:T(8,128)(2,1)} %get-tuple-element.97.refs_0_, ...), custom_call_target="tpu_custom_call" | custom-call | flops 375809632 | bytes 8388608 | tf_op jit(solution)/shard_map/grad/pallas_call | solution.py:538
  448.2 13.1 %grad.7 = (f32[640,256]{1,0:T(8,128)}, f32[640,256]{1,0:T(8,128)}, f32[640,256]{1,0:T(8,128)}, f32[640,256]{1,0:T(8,128)}, f32[640,256]{1,0:T(8,128)}, /*index=5...) custom-call(s32[4]{0:T(128)} %pad_add_fusion.pos_ref, bf16[256,1024]{1,0:T(8,128)(2,1)} %copy-done.18, ...), custom_call_target="tpu_custom_call" | custom-call | flops 268435456 | bytes 8388608 | tf_op jit(solution)/shard_map/grad/pallas_call | solution.py:538
  464.3 3.9 collective-permute-done.65
  469.9 17.9 %collective-permute-done.47 = f32[896,256]{1,0:T(8,128)} collective-permute-done((f32[896,256]{1,0:T(8,128)}, f32[896,256]{1,0:T(8,128)}, u32[]{:S(2)}, u32[]{:S(2)}) %collective-permute-start.47) | collective-permute-done | bytes 917536 | tf_op jit(solution)/shard_map/ppermute | solution.py:623
  491.2 10.7 %collective-permute-done.57 = f32[640,256]{1,0:T(8,128)S(1)} collective-permute-done((f32[640,256]{1,0:T(8,128)}, f32[640,256]{1,0:T(8,128)S(1)}, u32[]{:S(2)}, u32[]{:S(2)}) %collective-permute-start.57) | collective-permute-done | bytes 655392 | tf_op jit(solution)/shard_map/ppermute | solution.py:623
  507.1 7.5 %collective-permute-done.62 = f32[640,256]{1,0:T(8,128)S(1)} collective-permute-done((f32[640,256]{1,0:T(8,128)}, f32[640,256]{1,0:T(8,128)S(1)}, u32[]{:S(2)}, u32[]{:S(2)}) %collective-permute-start.62) | collective-permute-done | bytes 655392 | tf_op jit(solution)/shard_map/ppermute | solution.py:623
  520.2 14.1 %collective-permute-done.69 = f32[896,256]{1,0:T(8,128)S(1)} collective-permute-done((f32[896,256]{1,0:T(8,128)S(1)}, f32[896,256]{1,0:T(8,128)S(1)}, u32[]{:S(2)}, u32[]{:S(2)}) %collective-permute-start.69) | collective-permute-done | bytes 917536 | tf_op jit(solution)/shard_map/ppermute | solution.py:623
  534.3 14.3 %collective-permute-start.73 = (f32[896,256]{1,0:T(8,128)S(1)}, f32[896,256]{1,0:T(8,128)S(1)}, u32[]{:S(2)}, u32[]{:S(2)}) collective-permute-start(f32[896,256]{1,0:T(8,128)S(1)} %add_add_fusion.2.own_ref), channel_id=1, source_target_pairs={{1,16},{9,24},{16,1},{24,9},{3,18},{11,26},{18,3},{26,11},{5,20},{... | collective-permute-start | bytes 2752520 | tf_op jit(solution)/shard_map/ppermute | solution.py:639
  553.8 4.6 collective-permute-done.61
  558.4 11.6 %collective-permute-start.67 = (f32[896,256]{1,0:T(8,128)}, f32[896,256]{1,0:T(8,128)}, u32[]{:S(2)}, u32[]{:S(2)}) collective-permute-start(f32[896,256]{1,0:T(8,128)} %add_add_fusion.4.own_ref), channel_id=1, source_target_pairs={{1,16},{9,24},{16,1},{24,9},{3,18},{11,26},{18,3},{26,11},{5,20},{... | collective-permute-start | bytes 2752520 | tf_op jit(solution)/shard_map/ppermute | solution.py:639
  571.4 10.5 %collective-permute-done.73.first_ref = f32[896,256]{1,0:T(8,128)S(1)} collective-permute-done((f32[896,256]{1,0:T(8,128)S(1)}, f32[896,256]{1,0:T(8,128)S(1)}, u32[]{:S(2)}, u32[]{:S(2)}) %collective-permute-start.73) | collective-permute-done | bytes 917536 | tf_op jit(solution)/shard_map/ppermute | solution.py:639
  588.0 3.7 shard_map.165
  598.6 10.6 %collective-permute-done.67.first_ref = f32[896,256]{1,0:T(8,128)} collective-permute-done((f32[896,256]{1,0:T(8,128)}, f32[896,256]{1,0:T(8,128)}, u32[]{:S(2)}, u32[]{:S(2)}) %collective-permute-start.67) | collective-permute-done | bytes 917536 | tf_op jit(solution)/shard_map/ppermute | solution.py:639
  609.3 4.0 shard_map.164
  613.3 24.9 %collective-permute-done.52.first_ref = f32[896,256]{1,0:T(8,128)} collective-permute-done((f32[896,256]{1,0:T(8,128)}, f32[896,256]{1,0:T(8,128)}, u32[]{:S(2)}, u32[]{:S(2)}) %collective-permute-start.52) | collective-permute-done | bytes 917536 | tf_op jit(solution)/shard_map/ppermute | solution.py:639
  638.2 4.0 shard_map.163
  647.9 3.5 p_attn.1
  (303 shorter events, 143.0 us)
Async XLA Ops:
  7.2 133.6 %all-gather.3.cloned.1.call-start = ((), (), s32[]{:S(2)}) async-start(), calls=%async_computation.2 | async-start | bytes 8912896 | tf_op jit(solution)/shard_map/all_gather | solution.py:741
  29.4 206.3 %all-gather.5.cloned.1.call-start = ((), (), s32[]{:S(2)}) async-start(), calls=%async_computation.4 | async-start | bytes 8912896 | tf_op jit(solution)/shard_map/all_gather | solution.py:742
  30.2 612.0 %reduce-scatter.5.cloned.1.call-start = ((), (), s32[]{:S(2)}) async-start(), calls=%async_computation.5 | async-start | bytes 17825792 | tf_op jit(solution)/shard_map/reduce_scatter | solution.py:776
  30.2 33.4 %collective-permute-start.1 = (bf16[256,2176]{1,0:T(8,128)(2,1)}, bf16[256,2176]{1,0:T(8,128)(2,1)S(1)}, u32[]{:S(2)}, u32[]{:S(2)}) collective-permute-start(bf16[256,2176]{1,0:T(8,128)(2,1)} %get-tuple-element.145), channel_id=1, source_target_pairs={{0,0},{1,16},{8,8},{9,24},{16,1},{17,17},{24,9},{25,25},{2,2},{3,1... | collective-permute-start | bytes 3342344 | tf_op jit(solution)/shard_map/ppermute | solution.py:639
  38.6 30.2 %collective-permute-start.21 = (bf16[256,1152]{1,0:T(8,128)(2,1)S(1)}, bf16[256,1152]{1,0:T(8,128)(2,1)}, u32[]{:S(2)}, u32[]{:S(2)}) collective-permute-start(bf16[256,1152]{1,0:T(8,128)(2,1)S(1)} %get-tuple-element.147), channel_id=1, source_target_pairs={{0,8},{1,24},{8,0},{9,16},{16,9},{17,25},{24,1},{25,17},{2,10},{3,... | collective-permute-start | bytes 1769480 | tf_op jit(solution)/shard_map/ppermute | solution.py:639
  63.6 30.1 %collective-permute-start.8 = (bf16[256,2176]{1,0:T(8,128)(2,1)S(1)}, bf16[256,2176]{1,0:T(8,128)(2,1)S(1)}, u32[]{:S(2)}, u32[]{:S(2)}) collective-permute-start(bf16[256,2176]{1,0:T(8,128)(2,1)S(1)} %collective-permute-done.1.refs_0_.refs_3_), channel_id=1, source_target_pairs={{0,32},{32,64},{64,96},{96,0},{1,33},{33,65},{65,97},{97,1},{2,34}... | collective-permute-start | bytes 3342344 | tf_op jit(solution)/shard_map/ppermute | solution.py:623
  65.3 28.5 %collective-permute-start.4 = (bf16[256,2176]{1,0:T(8,128)(2,1)S(1)}, bf16[256,2176]{1,0:T(8,128)(2,1)S(1)}, u32[]{:S(2)}, u32[]{:S(2)}) collective-permute-start(bf16[256,2176]{1,0:T(8,128)(2,1)S(1)} %collective-permute-done.1.refs_0_.refs_3_), channel_id=1, source_target_pairs={{0,96},{32,0},{64,32},{96,64},{1,97},{33,1},{65,33},{97,65},{2,98}... | collective-permute-start | bytes 3342344 | tf_op jit(solution)/shard_map/ppermute | solution.py:623
  67.4 42.1 %collective-permute-start.5 = (bf16[256,2176]{1,0:T(8,128)(2,1)S(1)}, bf16[256,2176]{1,0:T(8,128)(2,1)S(1)}, u32[]{:S(2)}, u32[]{:S(2)}) collective-permute-start(bf16[256,2176]{1,0:T(8,128)(2,1)S(1)} %collective-permute-done.refs_1_.refs_4_), channel_id=1, source_target_pairs={{0,96},{32,0},{64,32},{96,64},{1,97},{33,1},{65,33},{97,65},{2,98}... | collective-permute-start | bytes 3342344 | tf_op jit(solution)/shard_map/ppermute | solution.py:623
  93.8 39.7 %collective-permute-start.12 = (bf16[256,2176]{1,0:T(8,128)(2,1)S(1)}, bf16[256,2176]{1,0:T(8,128)(2,1)S(1)}, u32[]{:S(2)}, u32[]{:S(2)}) collective-permute-start(bf16[256,2176]{1,0:T(8,128)(2,1)S(1)} %collective-permute-done.8.refs_8_.refs_15_), channel_id=1, source_target_pairs={{0,32},{32,64},{64,96},{96,0},{1,33},{33,65},{65,97},{97,1},{2,34}... | collective-permute-start | bytes 3342344 | tf_op jit(solution)/shard_map/ppermute | solution.py:623
  93.9 39.6 %collective-permute-start.10 = (bf16[256,2176]{1,0:T(8,128)(2,1)S(1)}, bf16[256,2176]{1,0:T(8,128)(2,1)S(1)}, u32[]{:S(2)}, u32[]{:S(2)}) collective-permute-start(bf16[256,2176]{1,0:T(8,128)(2,1)S(1)} %collective-permute-done.8.refs_8_.refs_15_), channel_id=1, source_target_pairs={{0,1},{1,0},{2,3},{3,2},{4,5},{5,4},{6,7},{7,6},{8,9},{9,8},{10,11... | collective-permute-start | bytes 3342344 | tf_op jit(solution)/shard_map/ppermute | solution.py:627
  151.9 55.7 %collective-permute-start.24 = (bf16[256,1152]{1,0:T(8,128)(2,1)}, bf16[256,1152]{1,0:T(8,128)(2,1)}, u32[]{:S(2)}, u32[]{:S(2)}) collective-permute-start(bf16[256,1152]{1,0:T(8,128)(2,1)} %collective-permute-done.20.refs_3_.refs_0_), channel_id=1, source_target_pairs={{0,96},{32,0},{64,32},{96,64},{1,97},{33,1},{65,33},{97,65},{2,98}... | collective-permute-start | bytes 1769480 | tf_op jit(solution)/shard_map/ppermute | solution.py:623
  162.9 46.0 %collective-permute-start.22 = (bf16[256,1152]{1,0:T(8,128)(2,1)}, bf16[256,1152]{1,0:T(8,128)(2,1)}, u32[]{:S(2)}, u32[]{:S(2)}) collective-permute-start(bf16[256,1152]{1,0:T(8,128)(2,1)} %collective-permute-done.20.refs_3_.refs_0_), channel_id=1, source_target_pairs={{0,1},{1,0},{2,3},{3,2},{4,5},{5,4},{6,7},{7,6},{8,9},{9,8},{10,11... | collective-permute-start | bytes 1769480 | tf_op jit(solution)/shard_map/ppermute | solution.py:627
  165.3 43.7 %collective-permute-start.35 = (bf16[256,1152]{1,0:T(8,128)(2,1)}, bf16[256,1152]{1,0:T(8,128)(2,1)}, u32[]{:S(2)}, u32[]{:S(2)}) collective-permute-start(bf16[256,1152]{1,0:T(8,128)(2,1)} %collective-permute-done.33.refs_16_.refs_9_), channel_id=1, source_target_pairs={{0,1},{1,0},{2,3},{3,2},{4,5},{5,4},{6,7},{7,6},{8,9},{9,8},{10,11... | collective-permute-start | bytes 1769480 | tf_op jit(solution)/shard_map/ppermute | solution.py:627
  170.4 39.1 %collective-permute-start.30 = (bf16[256,1152]{1,0:T(8,128)(2,1)}, bf16[256,1152]{1,0:T(8,128)(2,1)}, u32[]{:S(2)}, u32[]{:S(2)}) collective-permute-start(bf16[256,1152]{1,0:T(8,128)(2,1)} %collective-permute-done.25.refs_8_.refs_5_), channel_id=1, source_target_pairs={{0,96},{32,0},{64,32},{96,64},{1,97},{33,1},{65,33},{97,65},{2,98}... | collective-permute-start | bytes 1769480 | tf_op jit(solution)/shard_map/ppermute | solution.py:623
  171.8 37.8 %collective-permute-start.29 = (bf16[256,1152]{1,0:T(8,128)(2,1)}, bf16[256,1152]{1,0:T(8,128)(2,1)}, u32[]{:S(2)}, u32[]{:S(2)}) collective-permute-start(bf16[256,1152]{1,0:T(8,128)(2,1)} %collective-permute-done.28.refs_15_.refs_8_), channel_id=1, source_target_pairs={{0,32},{32,64},{64,96},{96,0},{1,33},{33,65},{65,97},{97,1},{2,34}... | collective-permute-start | bytes 1769480 | tf_op jit(solution)/shard_map/ppermute | solution.py:623
  239.8 27.1 %collective-permute-start.37 = (bf16[1024,2048]{1,0:T(8,128)(2,1)}, bf16[1024,2048]{1,0:T(8,128)(2,1)}, u32[]{:S(2)}, u32[]{:S(2)}) collective-permute-start(bf16[1024,2048]{1,0:T(8,128)(2,1)} %shard_map.158), channel_id=1, source_target_pairs={{0,1},{1,0},{2,3},{3,2},{4,5},{5,4},{6,7},{7,6},{8,9},{9,8},{10,11... | collective-permute-start | bytes 12582920 | tf_op jit(solution)/shard_map/ppermute | solution.py:627
  240.1 26.8 %collective-permute-start.36 = (bf16[896,1024]{1,0:T(8,128)(2,1)}, bf16[896,1024]{1,0:T(8,128)(2,1)}, u32[]{:S(2)}, u32[]{:S(2)}) collective-permute-start(bf16[896,1024]{1,0:T(8,128)(2,1)} %get-tuple-element.79.refs_0_), channel_id=1, source_target_pairs={{0,1},{1,0},{2,3},{3,2},{4,5},{5,4},{6,7},{7,6},{8,9},{9,8},{10,11... | collective-permute-start | bytes 5505032 | tf_op jit(solution)/shard_map/ppermute | solution.py:627
  249.0 66.2 %collective-permute-start.42 = (bf16[1024,2048]{1,0:T(8,128)(2,1)}, bf16[1024,2048]{1,0:T(8,128)(2,1)}, u32[]{:S(2)}, u32[]{:S(2)}) collective-permute-start(bf16[1024,2048]{1,0:T(8,128)(2,1)} %shard_map.157), channel_id=1, source_target_pairs={{0,1},{1,0},{2,3},{3,2},{4,5},{5,4},{6,7},{7,6},{8,9},{9,8},{10,11... | collective-permute-start | bytes 12582920 | tf_op jit(solution)/shard_map/ppermute | solution.py:627
  287.1 28.1 %collective-permute-start.41 = (bf16[1792,1024]{1,0:T(8,128)(2,1)}, bf16[1792,1024]{1,0:T(8,128)(2,1)}, u32[]{:S(2)}, u32[]{:S(2)}) collective-permute-start(bf16[1792,1024]{1,0:T(8,128)(2,1)} %get-tuple-element.97.refs_0_), channel_id=1, source_target_pairs={{0,1},{1,0},{2,3},{3,2},{4,5},{5,4},{6,7},{7,6},{8,9},{9,8},{10,11... | collective-permute-start | bytes 11010056 | tf_op jit(solution)/shard_map/ppermute | solution.py:627
  363.7 280.3 %reduce-scatter.3.cloned.1.call-start = ((), (), s32[]{:S(2)}) async-start(), calls=%async_computation.3 | async-start | bytes 17825792 | tf_op jit(solution)/shard_map/reduce_scatter | solution.py:757
  368.4 37.7 %collective-permute-start.72 = (f32[896,256]{1,0:T(8,128)}, f32[896,256]{1,0:T(8,128)}, u32[]{:S(2)}, u32[]{:S(2)}) collective-permute-start(f32[896,256]{1,0:T(8,128)} %get-tuple-element.142), channel_id=1, source_target_pairs={{0,96},{32,0},{64,32},{96,64},{1,97},{33,1},{65,33},{97,65},{2,98}... | collective-permute-start | bytes 2752520 | tf_op jit(solution)/shard_map/ppermute | solution.py:623
  368.4 40.4 %collective-permute-start.45 = (f32[896,256]{1,0:T(8,128)}, f32[896,256]{1,0:T(8,128)}, u32[]{:S(2)}, u32[]{:S(2)}) collective-permute-start(f32[896,256]{1,0:T(8,128)} %get-tuple-element.112), channel_id=1, source_target_pairs={{0,32},{32,64},{64,96},{96,0},{1,33},{33,65},{65,97},{97,1},{2,34}... | collective-permute-start | bytes 2752520 | tf_op jit(solution)/shard_map/ppermute | solution.py:623
  387.4 56.1 %collective-permute-start.71 = (f32[896,256]{1,0:T(8,128)}, f32[896,256]{1,0:T(8,128)}, u32[]{:S(2)}, u32[]{:S(2)}) collective-permute-start(f32[896,256]{1,0:T(8,128)} %add.115), channel_id=1, source_target_pairs={{0,32},{32,64},{64,96},{96,0},{1,33},{33,65},{65,97},{97,1},{2,34}... | collective-permute-start | bytes 2752520 | tf_op jit(solution)/shard_map/ppermute | solution.py:623
  387.4 38.3 %collective-permute-start.46 = (f32[896,256]{1,0:T(8,128)}, f32[896,256]{1,0:T(8,128)}, u32[]{:S(2)}, u32[]{:S(2)}) collective-permute-start(f32[896,256]{1,0:T(8,128)} %get-tuple-element.115), channel_id=1, source_target_pairs={{0,96},{32,0},{64,32},{96,64},{1,97},{33,1},{65,33},{97,65},{2,98}... | collective-permute-start | bytes 2752520 | tf_op jit(solution)/shard_map/ppermute | solution.py:623
  392.8 52.7 %collective-permute-start.76 = (f32[896,256]{1,0:T(8,128)}, f32[896,256]{1,0:T(8,128)}, u32[]{:S(2)}, u32[]{:S(2)}) collective-permute-start(f32[896,256]{1,0:T(8,128)} %add_add_fusion.1), channel_id=1, source_target_pairs={{0,8},{1,24},{8,0},{9,16},{16,9},{17,25},{24,1},{25,17},{2,10},{3,... | collective-permute-start | bytes 2752520 | tf_op jit(solution)/shard_map/ppermute | solution.py:639
  406.1 42.1 %collective-permute-start.49 = (bf16[384,1024]{1,0:T(8,128)(2,1)}, bf16[384,1024]{1,0:T(8,128)(2,1)}, u32[]{:S(2)}, u32[]{:S(2)}) collective-permute-start(bf16[384,1024]{1,0:T(8,128)(2,1)} %maximum_bitcast_fusion.refs_4_), channel_id=1, source_target_pairs={{0,1},{1,0},{2,3},{3,2},{4,5},{5,4},{6,7},{7,6},{8,9},{9,8},{10,11... | collective-permute-start | bytes 2359304 | tf_op jit(solution)/shard_map/ppermute | solution.py:627
  408.7 52.6 %collective-permute-start.66 = (f32[896,256]{1,0:T(8,128)}, f32[896,256]{1,0:T(8,128)}, u32[]{:S(2)}, u32[]{:S(2)}) collective-permute-start(f32[896,256]{1,0:T(8,128)} %get-tuple-element.138), channel_id=1, source_target_pairs={{0,96},{32,0},{64,32},{96,64},{1,97},{33,1},{65,33},{97,65},{2,98}... | collective-permute-start | bytes 2752520 | tf_op jit(solution)/shard_map/ppermute | solution.py:623
  425.7 37.3 %collective-permute-start.68 = (f32[896,256]{1,0:T(8,128)}, f32[896,256]{1,0:T(8,128)}, u32[]{:S(2)}, u32[]{:S(2)}) collective-permute-start(f32[896,256]{1,0:T(8,128)} %get-tuple-element.140), channel_id=1, source_target_pairs={{0,32},{32,64},{64,96},{96,0},{1,33},{33,65},{65,97},{97,1},{2,34}... | collective-permute-start | bytes 2752520 | tf_op jit(solution)/shard_map/ppermute | solution.py:623
  445.5 42.3 %collective-permute-start.47 = (f32[896,256]{1,0:T(8,128)}, f32[896,256]{1,0:T(8,128)}, u32[]{:S(2)}, u32[]{:S(2)}) collective-permute-start(f32[896,256]{1,0:T(8,128)} %get-tuple-element.119), channel_id=1, source_target_pairs={{0,32},{32,64},{64,96},{96,0},{1,33},{33,65},{65,97},{97,1},{2,34}... | collective-permute-start | bytes 2752520 | tf_op jit(solution)/shard_map/ppermute | solution.py:623
  448.1 55.5 %collective-permute-start.54 = (f32[896,256]{1,0:T(8,128)}, f32[896,256]{1,0:T(8,128)}, u32[]{:S(2)}, u32[]{:S(2)}) collective-permute-start(f32[896,256]{1,0:T(8,128)} %get-tuple-element.127), channel_id=1, source_target_pairs={{0,96},{32,0},{64,32},{96,64},{1,97},{33,1},{65,33},{97,65},{2,98}... | collective-permute-start | bytes 2752520 | tf_op jit(solution)/shard_map/ppermute | solution.py:623
  461.3 40.6 %collective-permute-start.57 = (f32[640,256]{1,0:T(8,128)}, f32[640,256]{1,0:T(8,128)S(1)}, u32[]{:S(2)}, u32[]{:S(2)}) collective-permute-start(f32[640,256]{1,0:T(8,128)} %get-tuple-element.130), channel_id=1, source_target_pairs={{0,32},{32,64},{64,96},{96,0},{1,33},{33,65},{65,97},{97,1},{2,34}... | collective-permute-start | bytes 1966088 | tf_op jit(solution)/shard_map/ppermute | solution.py:623
  463.1 51.9 %collective-permute-start.51 = (f32[896,256]{1,0:T(8,128)}, f32[896,256]{1,0:T(8,128)S(1)}, u32[]{:S(2)}, u32[]{:S(2)}) collective-permute-start(f32[896,256]{1,0:T(8,128)} %get-tuple-element.123), channel_id=1, source_target_pairs={{0,96},{32,0},{64,32},{96,64},{1,97},{33,1},{65,33},{97,65},{2,98}... | collective-permute-start | bytes 2752520 | tf_op jit(solution)/shard_map/ppermute | solution.py:623
  468.2 38.9 %collective-permute-start.59 = (f32[640,256]{1,0:T(8,128)}, f32[640,256]{1,0:T(8,128)S(1)}, u32[]{:S(2)}, u32[]{:S(2)}) collective-permute-start(f32[640,256]{1,0:T(8,128)} %get-tuple-element.131), channel_id=1, source_target_pairs={{0,96},{32,0},{64,32},{96,64},{1,97},{33,1},{65,33},{97,65},{2,98}... | collective-permute-start | bytes 1966088 | tf_op jit(solution)/shard_map/ppermute | solution.py:623
  487.8 26.8 %collective-permute-start.62 = (f32[640,256]{1,0:T(8,128)}, f32[640,256]{1,0:T(8,128)S(1)}, u32[]{:S(2)}, u32[]{:S(2)}) collective-permute-start(f32[640,256]{1,0:T(8,128)} %get-tuple-element.135), channel_id=1, source_target_pairs={{0,96},{32,0},{64,32},{96,64},{1,97},{33,1},{65,33},{97,65},{2,98}... | collective-permute-start | bytes 1966088 | tf_op jit(solution)/shard_map/ppermute | solution.py:623
  501.9 32.4 %collective-permute-start.69 = (f32[896,256]{1,0:T(8,128)S(1)}, f32[896,256]{1,0:T(8,128)S(1)}, u32[]{:S(2)}, u32[]{:S(2)}) collective-permute-start(f32[896,256]{1,0:T(8,128)S(1)} %copy-done.35), channel_id=1, source_target_pairs={{0,96},{32,0},{64,32},{96,64},{1,97},{33,1},{65,33},{97,65},{2,98}... | collective-permute-start | bytes 2752520 | tf_op jit(solution)/shard_map/ppermute | solution.py:623
  503.6 45.0 %collective-permute-start.50 = (f32[896,256]{1,0:T(8,128)S(1)}, f32[896,256]{1,0:T(8,128)S(1)}, u32[]{:S(2)}, u32[]{:S(2)}) collective-permute-start(f32[896,256]{1,0:T(8,128)S(1)} %add.120), channel_id=1, source_target_pairs={{0,32},{32,64},{64,96},{96,0},{1,33},{33,65},{65,97},{97,1},{2,34}... | collective-permute-start | bytes 2752520 | tf_op jit(solution)/shard_map/ppermute | solution.py:623
  507.1 51.2 %collective-permute-start.53 = (f32[896,256]{1,0:T(8,128)S(1)}, f32[896,256]{1,0:T(8,128)S(1)}, u32[]{:S(2)}, u32[]{:S(2)}) collective-permute-start(f32[896,256]{1,0:T(8,128)S(1)} %copy-done.51), channel_id=1, source_target_pairs={{0,32},{32,64},{64,96},{96,0},{1,33},{33,65},{65,97},{97,1},{2,34}... | collective-permute-start | bytes 2752520 | tf_op jit(solution)/shard_map/ppermute | solution.py:623
  514.6 43.8 %collective-permute-start.61 = (f32[640,256]{1,0:T(8,128)S(1)}, f32[640,256]{1,0:T(8,128)S(1)}, u32[]{:S(2)}, u32[]{:S(2)}) collective-permute-start(f32[640,256]{1,0:T(8,128)S(1)} %copy-done.52), channel_id=1, source_target_pairs={{0,32},{32,64},{64,96},{96,0},{1,33},{33,65},{65,97},{97,1},{2,34}... | collective-permute-start | bytes 1966088 | tf_op jit(solution)/shard_map/ppermute | solution.py:623
  515.0 55.0 %collective-permute-start.55 = (f32[896,256]{1,0:T(8,128)S(1)}, f32[896,256]{1,0:T(8,128)S(1)}, u32[]{:S(2)}, u32[]{:S(2)}) collective-permute-start(f32[896,256]{1,0:T(8,128)S(1)} %add.124), channel_id=1, source_target_pairs={{0,96},{32,0},{64,32},{96,64},{1,97},{33,1},{65,33},{97,65},{2,98}... | collective-permute-start | bytes 2752520 | tf_op jit(solution)/shard_map/ppermute | solution.py:623
  534.3 47.6 %collective-permute-start.73 = (f32[896,256]{1,0:T(8,128)S(1)}, f32[896,256]{1,0:T(8,128)S(1)}, u32[]{:S(2)}, u32[]{:S(2)}) collective-permute-start(f32[896,256]{1,0:T(8,128)S(1)} %add_add_fusion.2.own_ref), channel_id=1, source_target_pairs={{1,16},{9,24},{16,1},{24,9},{3,18},{11,26},{18,3},{26,11},{5,20},{... | collective-permute-start | bytes 2752520 | tf_op jit(solution)/shard_map/ppermute | solution.py:639
  548.6 36.7 %collective-permute-start.58 = (f32[640,256]{1,0:T(8,128)S(1)}, f32[640,256]{1,0:T(8,128)}, u32[]{:S(2)}, u32[]{:S(2)}) collective-permute-start(f32[640,256]{1,0:T(8,128)S(1)} %add.126), channel_id=1, source_target_pairs={{0,32},{32,64},{64,96},{96,0},{1,33},{33,65},{65,97},{97,1},{2,34}... | collective-permute-start | bytes 1966088 | tf_op jit(solution)/shard_map/ppermute | solution.py:623
  558.4 35.9 %collective-permute-start.63 = (f32[640,256]{1,0:T(8,128)}, f32[640,256]{1,0:T(8,128)}, u32[]{:S(2)}, u32[]{:S(2)}) collective-permute-start(f32[640,256]{1,0:T(8,128)} %add.130), channel_id=1, source_target_pairs={{0,96},{32,0},{64,32},{96,64},{1,97},{33,1},{65,33},{97,65},{2,98}... | collective-permute-start | bytes 1966088 | tf_op jit(solution)/shard_map/ppermute | solution.py:623
  558.4 50.7 %collective-permute-start.67 = (f32[896,256]{1,0:T(8,128)}, f32[896,256]{1,0:T(8,128)}, u32[]{:S(2)}, u32[]{:S(2)}) collective-permute-start(f32[896,256]{1,0:T(8,128)} %add_add_fusion.4.own_ref), channel_id=1, source_target_pairs={{1,16},{9,24},{16,1},{24,9},{3,18},{11,26},{18,3},{26,11},{5,20},{... | collective-permute-start | bytes 2752520 | tf_op jit(solution)/shard_map/ppermute | solution.py:639
  570.0 39.3 %collective-permute-start.70 = (f32[896,256]{1,0:T(8,128)}, f32[896,256]{1,0:T(8,128)}, u32[]{:S(2)}, u32[]{:S(2)}) collective-permute-start(f32[896,256]{1,0:T(8,128)} %add_add_fusion.3), channel_id=1, source_target_pairs={{0,8},{1,24},{8,0},{9,16},{16,9},{17,25},{24,1},{25,17},{2,10},{3,... | collective-permute-start | bytes 2752520 | tf_op jit(solution)/shard_map/ppermute | solution.py:639
  582.8 55.4 %collective-permute-start.52 = (f32[896,256]{1,0:T(8,128)}, f32[896,256]{1,0:T(8,128)}, u32[]{:S(2)}, u32[]{:S(2)}) collective-permute-start(f32[896,256]{1,0:T(8,128)} %add_add_fusion.6.own_ref), channel_id=1, source_target_pairs={{1,16},{9,24},{16,1},{24,9},{3,18},{11,26},{18,3},{26,11},{5,20},{... | collective-permute-start | bytes 2752520 | tf_op jit(solution)/shard_map/ppermute | solution.py:639
  585.3 52.9 %collective-permute-start.56 = (f32[896,256]{1,0:T(8,128)}, f32[896,256]{1,0:T(8,128)}, u32[]{:S(2)}, u32[]{:S(2)}) collective-permute-start(f32[896,256]{1,0:T(8,128)} %add_add_fusion.5), channel_id=1, source_target_pairs={{0,8},{1,24},{8,0},{9,16},{16,9},{17,25},{24,1},{25,17},{2,10},{3,... | collective-permute-start | bytes 2752520 | tf_op jit(solution)/shard_map/ppermute | solution.py:639
  594.3 53.6 %collective-permute-start.60 = (f32[640,256]{1,0:T(8,128)}, f32[640,256]{1,0:T(8,128)}, u32[]{:S(2)}, u32[]{:S(2)}) collective-permute-start(f32[640,256]{1,0:T(8,128)} %add_add_fusion.8.own_ref), channel_id=1, source_target_pairs={{1,16},{9,24},{16,1},{24,9},{3,18},{11,26},{18,3},{26,11},{5,20},{... | collective-permute-start | bytes 1966088 | tf_op jit(solution)/shard_map/ppermute | solution.py:639
  609.1 38.8 %collective-permute-start.64 = (f32[640,256]{1,0:T(8,128)}, f32[640,256]{1,0:T(8,128)}, u32[]{:S(2)}, u32[]{:S(2)}) collective-permute-start(f32[640,256]{1,0:T(8,128)} %add_add_fusion.7), channel_id=1, source_target_pairs={{0,8},{1,24},{8,0},{9,16},{16,9},{17,25},{24,1},{25,17},{2,10},{3,... | collective-permute-start | bytes 1966088 | tf_op jit(solution)/shard_map/ppermute | solution.py:639
  (90 other events, 1247.0 us)
Sparse Core Ops, SparseCore 0:
  29.5 86.2 all-gather.2
  118.0 73.3 all-gather.4
  363.8 120.3 reduce-scatter.4
  487.5 141.7 reduce-scatter.2

commit v10 on v9

--- a/solution.py
+++ b/solution.py
@@ -768,13 +768,13 @@
         d_gate_up_recv = swap_c(d_gate_up_t)
         d_queries, keep, send = attn_bwd(after(pos, d_gate_up_t), qkv_seq, d_attn, d_attn_other, cos_tab, sin_tab)
         got = swap_y(send)
-        g_act = grad_pass(g_act, d_queries)
-        g_gate = grad_start([(d_gate_up_t, d_gate_up_recv, h_all, h_recv, ff_blk, 0)], *g_act[3])
+        g_gate = grad_start([(d_gate_up_t, d_gate_up_recv, h_all, h_recv, ff_blk, 0)], d_queries)
         d_own, d_other = attn_post(after(pos, g_gate[3][0]), d_queries, keep, got, cos_tab, sin_tab)
         d_got = swap_c(d_other)
         dh_part = nt_pieces(pos, [d_gate_up, d_own, d_got], wf_parts, chunk, 0, chunk)
         d_h = lax.psum_scatter(dh_part, ("y", "x"), scatter_dimension=0, tiled=True)
-        g_gate = grad_pass(g_gate, dh_part)
+        g_act = grad_pass(g_act, dh_part)
+        g_gate = grad_pass(g_gate, *g_act[3])
         g_up = grad_start([(d_gate_up_t, d_gate_up_recv, h_all, h_recv, ff_blk, 1)], *g_gate[3])
         b_act = grad_back(g_act, g_up[3][0])
         d_h = d_h.astype(BF16)

time: 669 us -> 655 us (0.979)
  waiting for transfers between devices: 257 us -> 246 us
    ppermute x12, waiting for transfers between devices: 101 us -> 74.8 us  [turn(): return lax.ppermute(val, ('y', 'c'), pairs)]
    ppermute x36, waiting for transfers between devices: 142 us -> 154 us  [hop_z(): return lax.ppermute(val, 'z', ring(step, NZ))]
    ppermute x26, starting transfers between devices: 22.7 us -> 14.4 us  [swap_c(): return lax.ppermute(val, 'c', [(0, 1), (1, 0)])]
  transfers between devices with their start and end apart: 81 -> 81, of which waited for: 30 -> 29; matrix products, arithmetic and copies ran while one was open for 8% -> 7% of each run, Pallas kernels for 25% -> 25%
where the time goes in v10:
time: 655 us; the launch traced here: 644 us
  waiting for transfers between devices  246 us (38%)
  Pallas kernels  199 us (30%)
  starting transfers between devices  122 us (19%)
  other arithmetic  38.5 us (6%)
  local copies, waits for them, and re-layouts  24 us (4%)
  between operations  15 us (2%)
    ppermute x36, waiting for transfers between devices, hop_z(): return lax.ppermute(val, 'z', ring(step, NZ))  154 us
    ppermute x12, waiting for transfers between devices, turn(): return lax.ppermute(val, ('y', 'c'), pairs)  74.8 us
    ppermute x12, starting transfers between devices, turn(): return lax.ppermute(val, ('y', 'c'), pairs)  59.3 us
    pallas_call x4, Pallas kernels, grad_pieces(): pl.pallas_call(functools.partial(grad_kernel, heights), grid_spec=pltpu.P...  52.6 us
    pallas_call x3, Pallas kernels, nn_pieces(): pl.pallas_call(functools.partial(nn_kernel, keys, 2, len(widths), tile, f...  50.7 us
    ppermute x36, starting transfers between devices, hop_z(): return lax.ppermute(val, 'z', ring(step, NZ))  44.1 us
    pallas_call x2, Pallas kernels, nt_pieces(): pl.pallas_call(functools.partial(nt_kernel, keys, sides, first_row), grid...  43.8 us
    pallas_call x3, Pallas kernels, per_sequence(): pl.pallas_call(kernel, grid_spec=pltpu.PrefetchScalarGridSpec(num_scalar_...  16.9 us
  transfers between devices with their start and end apart: 81, of which 29 were waited for; matrix products, arithmetic and copies ran while one was open for 7% of the time, Pallas kernels for 25%

profile of v10, /device:TPU:1, one launch (start us, length us, event | category | flops | bytes accessed | tf_op | source)
XLA Modules:
  0.0 644.2 jit_solution(16433323194953430890)
XLA Ops:
  12.1 4.1 collective-permute-start
  19.8 9.6 %collective-permute-done.refs_1_.refs_4_ = bf16[256,2176]{1,0:T(8,128)(2,1)S(1)} collective-permute-done((bf16[256,2176]{1,0:T(8,128)(2,1)S(1)}, bf16[256,2176]{1,0:T(8,128)(2,1)S(1)}, u32[]{:S(2)}, u32[]{:S(2)}) %collective-permute-start) | collective-permute-done | bytes 1114144 | tf_op jit(solution)/shard_map/ppermute | solution.py:639
  30.2 3.8 collective-permute-start.1
  39.8 23.9 %collective-permute-done.1.refs_0_.refs_3_ = bf16[256,2176]{1,0:T(8,128)(2,1)S(1)} collective-permute-done((bf16[256,2176]{1,0:T(8,128)(2,1)}, bf16[256,2176]{1,0:T(8,128)(2,1)S(1)}, u32[]{:S(2)}, u32[]{:S(2)}) %collective-permute-start.1) | collective-permute-done | bytes 1114144 | tf_op jit(solution)/shard_map/ppermute | solution.py:639
  68.9 4.7 collective-permute-start.20
  73.5 20.2 %collective-permute-done.20.refs_3_.refs_0_ = bf16[256,1152]{1,0:T(8,128)(2,1)} collective-permute-done((bf16[256,1152]{1,0:T(8,128)(2,1)S(1)}, bf16[256,1152]{1,0:T(8,128)(2,1)}, u32[]{:S(2)}, u32[]{:S(2)}) %collective-permute-start.20) | collective-permute-done | bytes 589856 | tf_op jit(solution)/shard_map/ppermute | solution.py:639
  94.4 15.1 %collective-permute-done.5.refs_5_.refs_8_ = bf16[256,2176]{1,0:T(8,128)(2,1)S(1)} collective-permute-done((bf16[256,2176]{1,0:T(8,128)(2,1)S(1)}, bf16[256,2176]{1,0:T(8,128)(2,1)S(1)}, u32[]{:S(2)}, u32[]{:S(2)}) %collective-permute-start.5) | collective-permute-done | bytes 1114144 | tf_op jit(solution)/shard_map/ppermute | solution.py:623
  112.0 8.4 %collective-permute-done.9.refs_9_.refs_16_ = bf16[256,2176]{1,0:T(8,128)(2,1)S(1)} collective-permute-done((bf16[256,2176]{1,0:T(8,128)(2,1)S(1)}, bf16[256,2176]{1,0:T(8,128)(2,1)S(1)}, u32[]{:S(2)}, u32[]{:S(2)}) %collective-permute-start.9) | collective-permute-done | bytes 1114144 | tf_op jit(solution)/shard_map/ppermute | solution.py:623
  121.0 12.5 %collective-permute-done.12.refs_12_.refs_11_ = bf16[256,2176]{1,0:T(8,128)(2,1)S(1)} collective-permute-done((bf16[256,2176]{1,0:T(8,128)(2,1)S(1)}, bf16[256,2176]{1,0:T(8,128)(2,1)S(1)}, u32[]{:S(2)}, u32[]{:S(2)}) %collective-permute-start.12) | collective-permute-done | bytes 1114144 | tf_op jit(solution)/shard_map/ppermute | solution.py:623
  140.7 9.6 %shard_map.153.own_ref = bf16[1024,384]{1,0:T(8,128)(2,1)} custom-call(s32[4]{0:T(128)} %pad_add_fusion.pos_ref, bf16[1024,4096]{1,0:T(8,128)(2,1)} %all-gather.3.cloned.1.call-done.acts_ref.in_ref.refs_2_.refs_6_, bf16[256,2176]{1,0:T(8,128)(2,1)} %copy-done.1, bf16[256,2176]{1,0:T(8,128)(2,1)} %copy-done, bf16[256,2176]{1,0:T(8,128)(2,1)} %copy-done.4, ...), custom_call_target="tpu_custom_call" | custom-call | flops 161061280 | bytes 11534336 | tf_op jit(solution)/shard_map/pallas_call | solution.py:331
  157.9 5.0 collective-permute-done.28.refs_15_.refs_8_
  165.2 5.0 collective-permute-done.17.own_third_ref
  172.4 23.4 %shard_map.154.ab_ref = bf16[1024,1792]{1,0:T(8,128)(2,1)} custom-call(s32[4]{0:T(128)} %pad_add_fusion.pos_ref, bf16[1024,4096]{1,0:T(8,128)(2,1)} %all-gather.3.cloned.1.call-done.acts_ref.in_ref.refs_2_.refs_6_, bf16[256,2176]{1,0:T(8,128)(2,1)} %copy-done.1, bf16[256,2176]{1,0:T(8,128)(2,1)} %copy-done, bf16[256,2176]{1,0:T(8,128)(2,1)} %copy-done.4, ...), custom_call_target="tpu_custom_call" | custom-call | flops 751619264 | bytes 23068672 | tf_op jit(solution)/shard_map/pallas_call | solution.py:331
  195.9 4.8 act_fwd.1
  200.7 5.6 shard_map.155
  214.5 16.9 %shard_map.156 = f32[1024,4096]{1,0:T(8,128)} custom-call(s32[4]{0:T(128)} %pad_add_fusion.pos_ref, bf16[16,64,896]{2,1,0:T(8,128)(2,1)} %bitcast.30, bf16[8,64,256]{2,1,0:T(8,128)(2,1)} %bitcast.33, bf16[8,64,256]{2,1,0:T(8,128)(2,1)} %bitcast.34, bf16[256,1152]{1,0:T(8,128)(2,1)} %collective-permute-done.20.refs_3_.refs_0_, ...), custom_call_target="tpu_custom_call" | custom-call | flops 483183808 | bytes 26214400 | tf_op jit(solution)/shard_map/pallas_call | solution.py:425
  231.4 4.1 shard_map.157
  235.6 4.1 shard_map.158
  240.6 17.6 %shard_map.159 = (bf16[1024,896]{1,0:T(8,128)(2,1)}, bf16[1024,256]{1,0:T(8,128)(2,1)}) custom-call(s32[4]{0:T(128)} %pad_add_fusion.pos_ref, bf16[1024,4096]{1,0:T(8,128)(2,1)} %all-gather.5.cloned.1.call-done.in_ref.acts_ref.refs_2_, bf16[256,1152]{1,0:T(8,128)(2,1)} %collective-permute-done.20.refs_3_.refs_0_, ...), custom_call_target="tpu_custom_call" | custom-call | flops 483183808 | bytes 17825792 | tf_op jit(solution)/shard_map/pallas_call | solution.py:331
  258.3 13.2 %grad.4 = (f32[896,256]{1,0:T(8,128)}, f32[896,256]{1,0:T(8,128)}, f32[896,256]{1,0:T(8,128)}, f32[896,256]{1,0:T(8,128)}, f32[896,256]{1,0:T(8,128)}, /*index=5...) custom-call(s32[4]{0:T(128)} %pad_add_fusion.pos_ref, bf16[896,1024]{1,0:T(8,128)(2,1)} %get-tuple-element.79.refs_0_, ...), custom_call_target="tpu_custom_call" | custom-call | flops 375809632 | bytes 8388608 | tf_op jit(solution)/shard_map/grad/pallas_call | solution.py:538
  271.5 6.9 %act_bwd.1 = (bf16[1024,1792]{1,0:T(8,128)(2,1)}, bf16[1792,1024]{1,0:T(8,128)(2,1)}) custom-call(bf16[1024,1792]{1,0:T(8,128)(2,1)} %shard_map.154.ab_ref, bf16[1024,896]{1,0:T(8,128)(2,1)} %get-tuple-element.93.du_ref), custom_call_target="tpu_custom_call" | custom-call | flops 400000000 | bytes 14000000 | tf_op jit(solution)/shard_map/act_bwd/pallas_call | solution.py:260
  280.0 5.4 collective-permute-done.38.other_ref
  286.1 8.1 %shard_map.160 = (bf16[2,512,256]{2,1,0:T(8,128)(2,1)}, f32[2,512,128]{2,1,0:T(8,128)}, f32[2,512,128]{2,1,0:T(8,128)}) custom-call(s32[4]{0:T(128)} %pad_add_fusion.pos_ref, bf16[2,512,512]{2,1,0:T(8,128)(2,1)} %get-tuple-element.97.seq_ref, bf16[1024,256]{1,0:T(8,128)(2,1)} %get-tuple-element.90.own_ref, bf16[512,256]{1,0:T(8,128)(2,1)} %copy-done.58, ...), custom_call_target="tpu_custom_call" | custom-call | flops 800000000 | bytes 4000000 | tf_op jit(solution)/shard_map/pallas_call | solution.py:142
  296.2 13.2 %grad.5 = (f32[896,256]{1,0:T(8,128)}, f32[896,256]{1,0:T(8,128)}, f32[896,256]{1,0:T(8,128)}, f32[896,256]{1,0:T(8,128)}, f32[896,256]{1,0:T(8,128)}, /*index=5...) custom-call(s32[4]{0:T(128)} %pad_add_fusion.pos_ref, bf16[1792,1024]{1,0:T(8,128)(2,1)} %get-tuple-element.95.refs_0_, ...), custom_call_target="tpu_custom_call" | custom-call | flops 375809632 | bytes 8388608 | tf_op jit(solution)/shard_map/grad/pallas_call | solution.py:538
  317.4 26.8 %shard_map.162 = f32[1024,4096]{1,0:T(8,128)} custom-call(s32[4]{0:T(128)} %pad_add_fusion.pos_ref, bf16[16,64,1792]{2,1,0:T(8,128)(2,1)} %bitcast.28, bf16[8,64,384]{2,1,0:T(8,128)(2,1)} %bitcast.31, bf16[8,64,384]{2,1,0:T(8,128)(2,1)} %bitcast.32, bf16[256,2176]{1,0:T(8,128)(2,1)} %copy-done.1, bf16[256,2176]{1,0:T(8,128)(2,1)} %copy-done, ...), custom_call_target="tpu_custom_call" | custom-call | flops 912680576 | bytes 34603008 | tf_op jit(solution)/shard_map/pallas_call | solution.py:425
  347.0 20.1 %collective-permute-done.45 = f32[896,256]{1,0:T(8,128)S(1)} collective-permute-done((f32[896,256]{1,0:T(8,128)S(1)}, f32[896,256]{1,0:T(8,128)S(1)}, u32[]{:S(2)}, u32[]{:S(2)}) %collective-permute-start.45) | collective-permute-done | bytes 917536 | tf_op jit(solution)/shard_map/ppermute | solution.py:623
  375.6 14.2 %collective-permute-done.75 = f32[896,256]{1,0:T(8,128)} collective-permute-done((f32[896,256]{1,0:T(8,128)}, f32[896,256]{1,0:T(8,128)}, u32[]{:S(2)}, u32[]{:S(2)}) %collective-permute-start.75) | collective-permute-done | bytes 917536 | tf_op jit(solution)/shard_map/ppermute | solution.py:623
  396.2 7.6 %collective-permute-start.76 = (f32[896,256]{1,0:T(8,128)}, f32[896,256]{1,0:T(8,128)}, u32[]{:S(2)}, u32[]{:S(2)}) collective-permute-start(f32[896,256]{1,0:T(8,128)} %add_add_fusion.1), channel_id=1, source_target_pairs={{0,8},{1,24},{8,0},{9,16},{16,9},{17,25},{24,1},{25,17},{2,10},{3,... | collective-permute-start | bytes 2752520 | tf_op jit(solution)/shard_map/ppermute | solution.py:639
  404.8 4.6 collective-permute-done.72
  409.4 3.6 collective-permute-start.49
  415.3 13.8 %collective-permute-done.46 = f32[896,256]{1,0:T(8,128)} collective-permute-done((f32[896,256]{1,0:T(8,128)}, f32[896,256]{1,0:T(8,128)}, u32[]{:S(2)}, u32[]{:S(2)}) %collective-permute-start.46) | collective-permute-done | bytes 917536 | tf_op jit(solution)/shard_map/ppermute | solution.py:623
  433.5 13.2 %grad.6 = (f32[896,256]{1,0:T(8,128)}, f32[896,256]{1,0:T(8,128)}, f32[896,256]{1,0:T(8,128)}, f32[896,256]{1,0:T(8,128)}, f32[896,256]{1,0:T(8,128)}, /*index=5...) custom-call(s32[4]{0:T(128)} %pad_add_fusion.pos_ref, bf16[1792,1024]{1,0:T(8,128)(2,1)} %get-tuple-element.95.refs_0_, ...), custom_call_target="tpu_custom_call" | custom-call | flops 375809632 | bytes 8388608 | tf_op jit(solution)/shard_map/grad/pallas_call | solution.py:538
  452.3 13.1 %grad.7 = (f32[640,256]{1,0:T(8,128)}, f32[640,256]{1,0:T(8,128)}, f32[640,256]{1,0:T(8,128)}, f32[640,256]{1,0:T(8,128)}, f32[640,256]{1,0:T(8,128)}, /*index=5...) custom-call(s32[4]{0:T(128)} %pad_add_fusion.pos_ref, bf16[256,1024]{1,0:T(8,128)(2,1)} %copy-done.18, ...), custom_call_target="tpu_custom_call" | custom-call | flops 268435456 | bytes 8388608 | tf_op jit(solution)/shard_map/grad/pallas_call | solution.py:538
  468.3 6.9 %collective-permute-done.65 = f32[896,256]{1,0:T(8,128)} collective-permute-done((f32[896,256]{1,0:T(8,128)}, f32[896,256]{1,0:T(8,128)}, u32[]{:S(2)}, u32[]{:S(2)}) %collective-permute-start.65) | collective-permute-done | bytes 917536 | tf_op jit(solution)/shard_map/ppermute | solution.py:623
  477.8 17.1 %collective-permute-done.47 = f32[896,256]{1,0:T(8,128)} collective-permute-done((f32[896,256]{1,0:T(8,128)}, f32[896,256]{1,0:T(8,128)}, u32[]{:S(2)}, u32[]{:S(2)}) %collective-permute-start.47) | collective-permute-done | bytes 917536 | tf_op jit(solution)/shard_map/ppermute | solution.py:623
  499.2 9.7 %collective-permute-done.57 = f32[640,256]{1,0:T(8,128)S(1)} collective-permute-done((f32[640,256]{1,0:T(8,128)}, f32[640,256]{1,0:T(8,128)S(1)}, u32[]{:S(2)}, u32[]{:S(2)}) %collective-permute-start.57) | collective-permute-done | bytes 655392 | tf_op jit(solution)/shard_map/ppermute | solution.py:623
  523.2 13.9 %collective-permute-done.69 = f32[896,256]{1,0:T(8,128)S(1)} collective-permute-done((f32[896,256]{1,0:T(8,128)S(1)}, f32[896,256]{1,0:T(8,128)S(1)}, u32[]{:S(2)}, u32[]{:S(2)}) %collective-permute-start.69) | collective-permute-done | bytes 917536 | tf_op jit(solution)/shard_map/ppermute | solution.py:623
  537.0 15.5 %collective-permute-start.73 = (f32[896,256]{1,0:T(8,128)S(1)}, f32[896,256]{1,0:T(8,128)S(1)}, u32[]{:S(2)}, u32[]{:S(2)}) collective-permute-start(f32[896,256]{1,0:T(8,128)S(1)} %add_add_fusion.2.own_ref), channel_id=1, source_target_pairs={{1,16},{9,24},{16,1},{24,9},{3,18},{11,26},{18,3},{26,11},{5,20},{... | collective-permute-start | bytes 2752520 | tf_op jit(solution)/shard_map/ppermute | solution.py:639
  557.5 9.8 %collective-permute-done.61 = f32[640,256]{1,0:T(8,128)S(1)} collective-permute-done((f32[640,256]{1,0:T(8,128)S(1)}, f32[640,256]{1,0:T(8,128)S(1)}, u32[]{:S(2)}, u32[]{:S(2)}) %collective-permute-start.61) | collective-permute-done | bytes 655392 | tf_op jit(solution)/shard_map/ppermute | solution.py:623
  567.3 9.5 %collective-permute-start.67 = (f32[896,256]{1,0:T(8,128)}, f32[896,256]{1,0:T(8,128)}, u32[]{:S(2)}, u32[]{:S(2)}) collective-permute-start(f32[896,256]{1,0:T(8,128)} %add_add_fusion.4.own_ref), channel_id=1, source_target_pairs={{1,16},{9,24},{16,1},{24,9},{3,18},{11,26},{18,3},{26,11},{5,20},{... | collective-permute-start | bytes 2752520 | tf_op jit(solution)/shard_map/ppermute | solution.py:639
  579.0 4.0 collective-permute-start.52
  583.1 3.9 collective-permute-start.56
  587.0 3.7 shard_map.165
  597.7 3.5 collective-permute-done.67.first_ref
  603.8 4.0 shard_map.164
  607.8 13.1 %collective-permute-done.52.first_ref = f32[896,256]{1,0:T(8,128)} collective-permute-done((f32[896,256]{1,0:T(8,128)}, f32[896,256]{1,0:T(8,128)}, u32[]{:S(2)}, u32[]{:S(2)}) %collective-permute-start.52) | collective-permute-done | bytes 917536 | tf_op jit(solution)/shard_map/ppermute | solution.py:639
  620.9 4.0 shard_map.163
  629.5 4.5 collective-permute-done.60.first_ref
  (311 shorter events, 143.8 us)
Async XLA Ops:
  7.2 133.5 %all-gather.3.cloned.1.call-start = ((), (), s32[]{:S(2)}) async-start(), calls=%async_computation.2 | async-start | bytes 8912896 | tf_op jit(solution)/shard_map/all_gather | solution.py:741
  29.4 206.2 %all-gather.5.cloned.1.call-start = ((), (), s32[]{:S(2)}) async-start(), calls=%async_computation.4 | async-start | bytes 8912896 | tf_op jit(solution)/shard_map/all_gather | solution.py:742
  30.2 594.7 %reduce-scatter.5.cloned.1.call-start = ((), (), s32[]{:S(2)}) async-start(), calls=%async_computation.5 | async-start | bytes 17825792 | tf_op jit(solution)/shard_map/reduce_scatter | solution.py:775
  30.2 33.4 %collective-permute-start.1 = (bf16[256,2176]{1,0:T(8,128)(2,1)}, bf16[256,2176]{1,0:T(8,128)(2,1)S(1)}, u32[]{:S(2)}, u32[]{:S(2)}) collective-permute-start(bf16[256,2176]{1,0:T(8,128)(2,1)} %get-tuple-element.145), channel_id=1, source_target_pairs={{0,0},{1,16},{8,8},{9,24},{16,1},{17,17},{24,9},{25,25},{2,2},{3,1... | collective-permute-start | bytes 3342344 | tf_op jit(solution)/shard_map/ppermute | solution.py:639
  38.6 30.2 %collective-permute-start.21 = (bf16[256,1152]{1,0:T(8,128)(2,1)S(1)}, bf16[256,1152]{1,0:T(8,128)(2,1)}, u32[]{:S(2)}, u32[]{:S(2)}) collective-permute-start(bf16[256,1152]{1,0:T(8,128)(2,1)S(1)} %get-tuple-element.147), channel_id=1, source_target_pairs={{0,8},{1,24},{8,0},{9,16},{16,9},{17,25},{24,1},{25,17},{2,10},{3,... | collective-permute-start | bytes 1769480 | tf_op jit(solution)/shard_map/ppermute | solution.py:639
  63.6 30.1 %collective-permute-start.8 = (bf16[256,2176]{1,0:T(8,128)(2,1)S(1)}, bf16[256,2176]{1,0:T(8,128)(2,1)S(1)}, u32[]{:S(2)}, u32[]{:S(2)}) collective-permute-start(bf16[256,2176]{1,0:T(8,128)(2,1)S(1)} %collective-permute-done.1.refs_0_.refs_3_), channel_id=1, source_target_pairs={{0,32},{32,64},{64,96},{96,0},{1,33},{33,65},{65,97},{97,1},{2,34}... | collective-permute-start | bytes 3342344 | tf_op jit(solution)/shard_map/ppermute | solution.py:623
  65.3 28.5 %collective-permute-start.4 = (bf16[256,2176]{1,0:T(8,128)(2,1)S(1)}, bf16[256,2176]{1,0:T(8,128)(2,1)S(1)}, u32[]{:S(2)}, u32[]{:S(2)}) collective-permute-start(bf16[256,2176]{1,0:T(8,128)(2,1)S(1)} %collective-permute-done.1.refs_0_.refs_3_), channel_id=1, source_target_pairs={{0,96},{32,0},{64,32},{96,64},{1,97},{33,1},{65,33},{97,65},{2,98}... | collective-permute-start | bytes 3342344 | tf_op jit(solution)/shard_map/ppermute | solution.py:623
  67.4 42.1 %collective-permute-start.5 = (bf16[256,2176]{1,0:T(8,128)(2,1)S(1)}, bf16[256,2176]{1,0:T(8,128)(2,1)S(1)}, u32[]{:S(2)}, u32[]{:S(2)}) collective-permute-start(bf16[256,2176]{1,0:T(8,128)(2,1)S(1)} %collective-permute-done.refs_1_.refs_4_), channel_id=1, source_target_pairs={{0,96},{32,0},{64,32},{96,64},{1,97},{33,1},{65,33},{97,65},{2,98}... | collective-permute-start | bytes 3342344 | tf_op jit(solution)/shard_map/ppermute | solution.py:623
  93.7 26.7 %collective-permute-start.9 = (bf16[256,2176]{1,0:T(8,128)(2,1)S(1)}, bf16[256,2176]{1,0:T(8,128)(2,1)S(1)}, u32[]{:S(2)}, u32[]{:S(2)}) collective-permute-start(bf16[256,2176]{1,0:T(8,128)(2,1)S(1)} %collective-permute-done.refs_1_.refs_4_), channel_id=1, source_target_pairs={{0,32},{32,64},{64,96},{96,0},{1,33},{33,65},{65,97},{97,1},{2,34}... | collective-permute-start | bytes 3342344 | tf_op jit(solution)/shard_map/ppermute | solution.py:623
  93.7 26.7 %collective-permute-start.3 = (bf16[256,2176]{1,0:T(8,128)(2,1)S(1)}, bf16[256,2176]{1,0:T(8,128)(2,1)S(1)}, u32[]{:S(2)}, u32[]{:S(2)}) collective-permute-start(bf16[256,2176]{1,0:T(8,128)(2,1)S(1)} %collective-permute-done.refs_1_.refs_4_), channel_id=1, source_target_pairs={{0,1},{1,0},{2,3},{3,2},{4,5},{5,4},{6,7},{7,6},{8,9},{9,8},{10,11... | collective-permute-start | bytes 3342344 | tf_op jit(solution)/shard_map/ppermute | solution.py:627
  93.8 39.7 %collective-permute-start.12 = (bf16[256,2176]{1,0:T(8,128)(2,1)S(1)}, bf16[256,2176]{1,0:T(8,128)(2,1)S(1)}, u32[]{:S(2)}, u32[]{:S(2)}) collective-permute-start(bf16[256,2176]{1,0:T(8,128)(2,1)S(1)} %collective-permute-done.8.refs_8_.refs_15_), channel_id=1, source_target_pairs={{0,32},{32,64},{64,96},{96,0},{1,33},{33,65},{65,97},{97,1},{2,34}... | collective-permute-start | bytes 3342344 | tf_op jit(solution)/shard_map/ppermute | solution.py:623
  93.9 39.6 %collective-permute-start.10 = (bf16[256,2176]{1,0:T(8,128)(2,1)S(1)}, bf16[256,2176]{1,0:T(8,128)(2,1)S(1)}, u32[]{:S(2)}, u32[]{:S(2)}) collective-permute-start(bf16[256,2176]{1,0:T(8,128)(2,1)S(1)} %collective-permute-done.8.refs_8_.refs_15_), channel_id=1, source_target_pairs={{0,1},{1,0},{2,3},{3,2},{4,5},{5,4},{6,7},{7,6},{8,9},{9,8},{10,11... | collective-permute-start | bytes 3342344 | tf_op jit(solution)/shard_map/ppermute | solution.py:627
  151.8 55.6 %collective-permute-start.24 = (bf16[256,1152]{1,0:T(8,128)(2,1)}, bf16[256,1152]{1,0:T(8,128)(2,1)}, u32[]{:S(2)}, u32[]{:S(2)}) collective-permute-start(bf16[256,1152]{1,0:T(8,128)(2,1)} %collective-permute-done.20.refs_3_.refs_0_), channel_id=1, source_target_pairs={{0,96},{32,0},{64,32},{96,64},{1,97},{33,1},{65,33},{97,65},{2,98}... | collective-permute-start | bytes 1769480 | tf_op jit(solution)/shard_map/ppermute | solution.py:623
  162.9 45.8 %collective-permute-start.22 = (bf16[256,1152]{1,0:T(8,128)(2,1)}, bf16[256,1152]{1,0:T(8,128)(2,1)}, u32[]{:S(2)}, u32[]{:S(2)}) collective-permute-start(bf16[256,1152]{1,0:T(8,128)(2,1)} %collective-permute-done.20.refs_3_.refs_0_), channel_id=1, source_target_pairs={{0,1},{1,0},{2,3},{3,2},{4,5},{5,4},{6,7},{7,6},{8,9},{9,8},{10,11... | collective-permute-start | bytes 1769480 | tf_op jit(solution)/shard_map/ppermute | solution.py:627
  165.2 43.7 %collective-permute-start.35 = (bf16[256,1152]{1,0:T(8,128)(2,1)}, bf16[256,1152]{1,0:T(8,128)(2,1)}, u32[]{:S(2)}, u32[]{:S(2)}) collective-permute-start(bf16[256,1152]{1,0:T(8,128)(2,1)} %collective-permute-done.33.refs_16_.refs_9_), channel_id=1, source_target_pairs={{0,1},{1,0},{2,3},{3,2},{4,5},{5,4},{6,7},{7,6},{8,9},{9,8},{10,11... | collective-permute-start | bytes 1769480 | tf_op jit(solution)/shard_map/ppermute | solution.py:627
  170.2 39.1 %collective-permute-start.30 = (bf16[256,1152]{1,0:T(8,128)(2,1)}, bf16[256,1152]{1,0:T(8,128)(2,1)}, u32[]{:S(2)}, u32[]{:S(2)}) collective-permute-start(bf16[256,1152]{1,0:T(8,128)(2,1)} %collective-permute-done.25.refs_8_.refs_5_), channel_id=1, source_target_pairs={{0,96},{32,0},{64,32},{96,64},{1,97},{33,1},{65,33},{97,65},{2,98}... | collective-permute-start | bytes 1769480 | tf_op jit(solution)/shard_map/ppermute | solution.py:623
  171.6 37.8 %collective-permute-start.29 = (bf16[256,1152]{1,0:T(8,128)(2,1)}, bf16[256,1152]{1,0:T(8,128)(2,1)}, u32[]{:S(2)}, u32[]{:S(2)}) collective-permute-start(bf16[256,1152]{1,0:T(8,128)(2,1)} %collective-permute-done.28.refs_15_.refs_8_), channel_id=1, source_target_pairs={{0,32},{32,64},{64,96},{96,0},{1,33},{33,65},{65,97},{97,1},{2,34}... | collective-permute-start | bytes 1769480 | tf_op jit(solution)/shard_map/ppermute | solution.py:623
  240.5 55.7 %collective-permute-start.40 = (bf16[1024,2048]{1,0:T(8,128)(2,1)}, bf16[1024,2048]{1,0:T(8,128)(2,1)}, u32[]{:S(2)}, u32[]{:S(2)}) collective-permute-start(bf16[1024,2048]{1,0:T(8,128)(2,1)} %shard_map.157), channel_id=1, source_target_pairs={{0,1},{1,0},{2,3},{3,2},{4,5},{5,4},{6,7},{7,6},{8,9},{9,8},{10,11... | collective-permute-start | bytes 12582920 | tf_op jit(solution)/shard_map/ppermute | solution.py:627
  344.3 282.4 %reduce-scatter.3.cloned.1.call-start = ((), (), s32[]{:S(2)}) async-start(), calls=%async_computation.3 | async-start | bytes 17825792 | tf_op jit(solution)/shard_map/reduce_scatter | solution.py:757
  347.0 28.6 %collective-permute-start.74 = (f32[896,256]{1,0:T(8,128)}, f32[896,256]{1,0:T(8,128)S(1)}, u32[]{:S(2)}, u32[]{:S(2)}) collective-permute-start(f32[896,256]{1,0:T(8,128)} %get-tuple-element.144), channel_id=1, source_target_pairs={{0,32},{32,64},{64,96},{96,0},{1,33},{33,65},{65,97},{97,1},{2,34}... | collective-permute-start | bytes 2752520 | tf_op jit(solution)/shard_map/ppermute | solution.py:623
  370.9 32.9 %collective-permute-start.44 = (f32[896,256]{1,0:T(8,128)}, f32[896,256]{1,0:T(8,128)}, u32[]{:S(2)}, u32[]{:S(2)}) collective-permute-start(f32[896,256]{1,0:T(8,128)} %get-tuple-element.109), channel_id=1, source_target_pairs={{0,32},{32,64},{64,96},{96,0},{1,33},{33,65},{65,97},{97,1},{2,34}... | collective-permute-start | bytes 2752520 | tf_op jit(solution)/shard_map/ppermute | solution.py:623
  372.6 36.8 %collective-permute-start.72 = (f32[896,256]{1,0:T(8,128)}, f32[896,256]{1,0:T(8,128)S(1)}, u32[]{:S(2)}, u32[]{:S(2)}) collective-permute-start(f32[896,256]{1,0:T(8,128)} %get-tuple-element.142), channel_id=1, source_target_pairs={{0,96},{32,0},{64,32},{96,64},{1,97},{33,1},{65,33},{97,65},{2,98}... | collective-permute-start | bytes 2752520 | tf_op jit(solution)/shard_map/ppermute | solution.py:623
  375.6 37.4 %collective-permute-start.43 = (f32[896,256]{1,0:T(8,128)}, f32[896,256]{1,0:T(8,128)}, u32[]{:S(2)}, u32[]{:S(2)}) collective-permute-start(f32[896,256]{1,0:T(8,128)} %get-tuple-element.107), channel_id=1, source_target_pairs={{0,32},{32,64},{64,96},{96,0},{1,33},{33,65},{65,97},{97,1},{2,34}... | collective-permute-start | bytes 2752520 | tf_op jit(solution)/shard_map/ppermute | solution.py:623
  389.8 39.3 %collective-permute-start.46 = (f32[896,256]{1,0:T(8,128)}, f32[896,256]{1,0:T(8,128)}, u32[]{:S(2)}, u32[]{:S(2)}) collective-permute-start(f32[896,256]{1,0:T(8,128)} %get-tuple-element.115), channel_id=1, source_target_pairs={{0,96},{32,0},{64,32},{96,64},{1,97},{33,1},{65,33},{97,65},{2,98}... | collective-permute-start | bytes 2752520 | tf_op jit(solution)/shard_map/ppermute | solution.py:623
  396.2 50.6 %collective-permute-start.76 = (f32[896,256]{1,0:T(8,128)}, f32[896,256]{1,0:T(8,128)}, u32[]{:S(2)}, u32[]{:S(2)}) collective-permute-start(f32[896,256]{1,0:T(8,128)} %add_add_fusion.1), channel_id=1, source_target_pairs={{0,8},{1,24},{8,0},{9,16},{16,9},{17,25},{24,1},{25,17},{2,10},{3,... | collective-permute-start | bytes 2752520 | tf_op jit(solution)/shard_map/ppermute | solution.py:639
  403.8 45.0 %collective-permute-start.66 = (f32[896,256]{1,0:T(8,128)}, f32[896,256]{1,0:T(8,128)}, u32[]{:S(2)}, u32[]{:S(2)}) collective-permute-start(f32[896,256]{1,0:T(8,128)} %get-tuple-element.138), channel_id=1, source_target_pairs={{0,96},{32,0},{64,32},{96,64},{1,97},{33,1},{65,33},{97,65},{2,98}... | collective-permute-start | bytes 2752520 | tf_op jit(solution)/shard_map/ppermute | solution.py:623
  409.4 42.0 %collective-permute-start.49 = (bf16[384,1024]{1,0:T(8,128)(2,1)}, bf16[384,1024]{1,0:T(8,128)(2,1)}, u32[]{:S(2)}, u32[]{:S(2)}) collective-permute-start(bf16[384,1024]{1,0:T(8,128)(2,1)} %maximum_bitcast_fusion.refs_4_), channel_id=1, source_target_pairs={{0,1},{1,0},{2,3},{3,2},{4,5},{5,4},{6,7},{7,6},{8,9},{9,8},{10,11... | collective-permute-start | bytes 2359304 | tf_op jit(solution)/shard_map/ppermute | solution.py:627
  413.0 52.5 %collective-permute-start.68 = (f32[896,256]{1,0:T(8,128)}, f32[896,256]{1,0:T(8,128)}, u32[]{:S(2)}, u32[]{:S(2)}) collective-permute-start(f32[896,256]{1,0:T(8,128)} %get-tuple-element.140), channel_id=1, source_target_pairs={{0,32},{32,64},{64,96},{96,0},{1,33},{33,65},{65,97},{97,1},{2,34}... | collective-permute-start | bytes 2752520 | tf_op jit(solution)/shard_map/ppermute | solution.py:623
  429.1 37.3 %collective-permute-start.71 = (f32[896,256]{1,0:T(8,128)}, f32[896,256]{1,0:T(8,128)}, u32[]{:S(2)}, u32[]{:S(2)}) collective-permute-start(f32[896,256]{1,0:T(8,128)} %add.116), channel_id=1, source_target_pairs={{0,32},{32,64},{64,96},{96,0},{1,33},{33,65},{65,97},{97,1},{2,34}... | collective-permute-start | bytes 2752520 | tf_op jit(solution)/shard_map/ppermute | solution.py:623
  446.8 28.4 %collective-permute-start.65 = (f32[896,256]{1,0:T(8,128)}, f32[896,256]{1,0:T(8,128)}, u32[]{:S(2)}, u32[]{:S(2)}) collective-permute-start(f32[896,256]{1,0:T(8,128)} %add.118), channel_id=1, source_target_pairs={{0,32},{32,64},{64,96},{96,0},{1,33},{33,65},{65,97},{97,1},{2,34}... | collective-permute-start | bytes 2752520 | tf_op jit(solution)/shard_map/ppermute | solution.py:623
  448.8 46.1 %collective-permute-start.47 = (f32[896,256]{1,0:T(8,128)}, f32[896,256]{1,0:T(8,128)}, u32[]{:S(2)}, u32[]{:S(2)}) collective-permute-start(f32[896,256]{1,0:T(8,128)} %get-tuple-element.119), channel_id=1, source_target_pairs={{0,32},{32,64},{64,96},{96,0},{1,33},{33,65},{65,97},{97,1},{2,34}... | collective-permute-start | bytes 2752520 | tf_op jit(solution)/shard_map/ppermute | solution.py:623
  451.4 60.1 %collective-permute-start.54 = (f32[896,256]{1,0:T(8,128)}, f32[896,256]{1,0:T(8,128)}, u32[]{:S(2)}, u32[]{:S(2)}) collective-permute-start(f32[896,256]{1,0:T(8,128)} %get-tuple-element.127), channel_id=1, source_target_pairs={{0,96},{32,0},{64,32},{96,64},{1,97},{33,1},{65,33},{97,65},{2,98}... | collective-permute-start | bytes 2752520 | tf_op jit(solution)/shard_map/ppermute | solution.py:623
  465.5 43.4 %collective-permute-start.57 = (f32[640,256]{1,0:T(8,128)}, f32[640,256]{1,0:T(8,128)S(1)}, u32[]{:S(2)}, u32[]{:S(2)}) collective-permute-start(f32[640,256]{1,0:T(8,128)} %get-tuple-element.130), channel_id=1, source_target_pairs={{0,32},{32,64},{64,96},{96,0},{1,33},{33,65},{65,97},{97,1},{2,34}... | collective-permute-start | bytes 1966088 | tf_op jit(solution)/shard_map/ppermute | solution.py:623
  466.4 51.4 %collective-permute-start.51 = (f32[896,256]{1,0:T(8,128)}, f32[896,256]{1,0:T(8,128)S(1)}, u32[]{:S(2)}, u32[]{:S(2)}) collective-permute-start(f32[896,256]{1,0:T(8,128)} %get-tuple-element.123), channel_id=1, source_target_pairs={{0,96},{32,0},{64,32},{96,64},{1,97},{33,1},{65,33},{97,65},{2,98}... | collective-permute-start | bytes 2752520 | tf_op jit(solution)/shard_map/ppermute | solution.py:623
  475.2 39.6 %collective-permute-start.59 = (f32[640,256]{1,0:T(8,128)}, f32[640,256]{1,0:T(8,128)S(1)}, u32[]{:S(2)}, u32[]{:S(2)}) collective-permute-start(f32[640,256]{1,0:T(8,128)} %get-tuple-element.131), channel_id=1, source_target_pairs={{0,96},{32,0},{64,32},{96,64},{1,97},{33,1},{65,33},{97,65},{2,98}... | collective-permute-start | bytes 1966088 | tf_op jit(solution)/shard_map/ppermute | solution.py:623
  508.9 28.1 %collective-permute-start.69 = (f32[896,256]{1,0:T(8,128)S(1)}, f32[896,256]{1,0:T(8,128)S(1)}, u32[]{:S(2)}, u32[]{:S(2)}) collective-permute-start(f32[896,256]{1,0:T(8,128)S(1)} %copy-done.38), channel_id=1, source_target_pairs={{0,96},{32,0},{64,32},{96,64},{1,97},{33,1},{65,33},{97,65},{2,98}... | collective-permute-start | bytes 2752520 | tf_op jit(solution)/shard_map/ppermute | solution.py:623
  511.5 41.0 %collective-permute-start.50 = (f32[896,256]{1,0:T(8,128)S(1)}, f32[896,256]{1,0:T(8,128)S(1)}, u32[]{:S(2)}, u32[]{:S(2)}) collective-permute-start(f32[896,256]{1,0:T(8,128)S(1)} %add.120), channel_id=1, source_target_pairs={{0,32},{32,64},{64,96},{96,0},{1,33},{33,65},{65,97},{97,1},{2,34}... | collective-permute-start | bytes 2752520 | tf_op jit(solution)/shard_map/ppermute | solution.py:623
  514.9 52.4 %collective-permute-start.53 = (f32[896,256]{1,0:T(8,128)S(1)}, f32[896,256]{1,0:T(8,128)S(1)}, u32[]{:S(2)}, u32[]{:S(2)}) collective-permute-start(f32[896,256]{1,0:T(8,128)S(1)} %copy-done.54), channel_id=1, source_target_pairs={{0,32},{32,64},{64,96},{96,0},{1,33},{33,65},{65,97},{97,1},{2,34}... | collective-permute-start | bytes 2752520 | tf_op jit(solution)/shard_map/ppermute | solution.py:623
  517.4 49.9 %collective-permute-start.61 = (f32[640,256]{1,0:T(8,128)S(1)}, f32[640,256]{1,0:T(8,128)S(1)}, u32[]{:S(2)}, u32[]{:S(2)}) collective-permute-start(f32[640,256]{1,0:T(8,128)S(1)} %copy-done.56), channel_id=1, source_target_pairs={{0,32},{32,64},{64,96},{96,0},{1,33},{33,65},{65,97},{97,1},{2,34}... | collective-permute-start | bytes 1966088 | tf_op jit(solution)/shard_map/ppermute | solution.py:623
  517.7 59.1 %collective-permute-start.55 = (f32[896,256]{1,0:T(8,128)S(1)}, f32[896,256]{1,0:T(8,128)S(1)}, u32[]{:S(2)}, u32[]{:S(2)}) collective-permute-start(f32[896,256]{1,0:T(8,128)S(1)} %add.124), channel_id=1, source_target_pairs={{0,96},{32,0},{64,32},{96,64},{1,97},{33,1},{65,33},{97,65},{2,98}... | collective-permute-start | bytes 2752520 | tf_op jit(solution)/shard_map/ppermute | solution.py:623
  537.0 41.1 %collective-permute-start.73 = (f32[896,256]{1,0:T(8,128)S(1)}, f32[896,256]{1,0:T(8,128)S(1)}, u32[]{:S(2)}, u32[]{:S(2)}) collective-permute-start(f32[896,256]{1,0:T(8,128)S(1)} %add_add_fusion.2.own_ref), channel_id=1, source_target_pairs={{1,16},{9,24},{16,1},{24,9},{3,18},{11,26},{18,3},{26,11},{5,20},{... | collective-permute-start | bytes 2752520 | tf_op jit(solution)/shard_map/ppermute | solution.py:639
  552.5 30.6 %collective-permute-start.58 = (f32[640,256]{1,0:T(8,128)S(1)}, f32[640,256]{1,0:T(8,128)}, u32[]{:S(2)}, u32[]{:S(2)}) collective-permute-start(f32[640,256]{1,0:T(8,128)S(1)} %add.126), channel_id=1, source_target_pairs={{0,32},{32,64},{64,96},{96,0},{1,33},{33,65},{65,97},{97,1},{2,34}... | collective-permute-start | bytes 1966088 | tf_op jit(solution)/shard_map/ppermute | solution.py:623
  567.3 33.9 %collective-permute-start.67 = (f32[896,256]{1,0:T(8,128)}, f32[896,256]{1,0:T(8,128)}, u32[]{:S(2)}, u32[]{:S(2)}) collective-permute-start(f32[896,256]{1,0:T(8,128)} %add_add_fusion.4.own_ref), channel_id=1, source_target_pairs={{1,16},{9,24},{16,1},{24,9},{3,18},{11,26},{18,3},{26,11},{5,20},{... | collective-permute-start | bytes 2752520 | tf_op jit(solution)/shard_map/ppermute | solution.py:639
  576.8 27.0 %collective-permute-start.70 = (f32[896,256]{1,0:T(8,128)}, f32[896,256]{1,0:T(8,128)}, u32[]{:S(2)}, u32[]{:S(2)}) collective-permute-start(f32[896,256]{1,0:T(8,128)} %add_add_fusion.3), channel_id=1, source_target_pairs={{0,8},{1,24},{8,0},{9,16},{16,9},{17,25},{24,1},{25,17},{2,10},{3,... | collective-permute-start | bytes 2752520 | tf_op jit(solution)/shard_map/ppermute | solution.py:639
  579.0 41.8 %collective-permute-start.52 = (f32[896,256]{1,0:T(8,128)}, f32[896,256]{1,0:T(8,128)}, u32[]{:S(2)}, u32[]{:S(2)}) collective-permute-start(f32[896,256]{1,0:T(8,128)} %add_add_fusion.6.own_ref), channel_id=1, source_target_pairs={{1,16},{9,24},{16,1},{24,9},{3,18},{11,26},{18,3},{26,11},{5,20},{... | collective-permute-start | bytes 2752520 | tf_op jit(solution)/shard_map/ppermute | solution.py:639
  583.1 37.8 %collective-permute-start.56 = (f32[896,256]{1,0:T(8,128)}, f32[896,256]{1,0:T(8,128)}, u32[]{:S(2)}, u32[]{:S(2)}) collective-permute-start(f32[896,256]{1,0:T(8,128)} %add_add_fusion.5), channel_id=1, source_target_pairs={{0,8},{1,24},{8,0},{9,16},{16,9},{17,25},{24,1},{25,17},{2,10},{3,... | collective-permute-start | bytes 2752520 | tf_op jit(solution)/shard_map/ppermute | solution.py:639
  593.2 40.8 %collective-permute-start.60 = (f32[640,256]{1,0:T(8,128)}, f32[640,256]{1,0:T(8,128)}, u32[]{:S(2)}, u32[]{:S(2)}) collective-permute-start(f32[640,256]{1,0:T(8,128)} %add_add_fusion.8.own_ref), channel_id=1, source_target_pairs={{1,16},{9,24},{16,1},{24,9},{3,18},{11,26},{18,3},{26,11},{5,20},{... | collective-permute-start | bytes 1966088 | tf_op jit(solution)/shard_map/ppermute | solution.py:639
  601.2 32.8 %collective-permute-start.64 = (f32[640,256]{1,0:T(8,128)}, f32[640,256]{1,0:T(8,128)}, u32[]{:S(2)}, u32[]{:S(2)}) collective-permute-start(f32[640,256]{1,0:T(8,128)} %add_add_fusion.7), channel_id=1, source_target_pairs={{0,8},{1,24},{8,0},{9,16},{16,9},{17,25},{24,1},{25,17},{2,10},{3,... | collective-permute-start | bytes 1966088 | tf_op jit(solution)/shard_map/ppermute | solution.py:639
  (94 other events, 1309.3 us)
Sparse Core Ops, SparseCore 0:
  29.5 86.2 all-gather.2
  118.0 73.3 all-gather.4
  344.4 121.2 reduce-scatter.4
  469.0 116.5 reduce-scatter.2

commit v11 on v9

--- a/solution.py
+++ b/solution.py
@@ -757,14 +757,14 @@
         mix_sum = lax.psum_scatter(y_part, ("y", "x"), scatter_dimension=0, tiled=True)
         y_out = (x_rows + mix_sum).astype(BF16)[None]
 
-        h_picked = pick_cols(after(pos, y_part), h_all)
+        dy_picked = pick_cols(after(pos, y_part), dy_all)
+        dy_recv = swap_c(dy_picked)
+        h_picked = pick_cols(after(pos, dy_picked), h_all)
         h_recv = swap_c(h_picked)
-        dy_picked = pick_cols(after(pos, h_picked), dy_all)
-        dy_recv = swap_c(dy_picked)
-        d_act, d_attn = nn_pieces(after(pos, dy_picked), dy_all, ws_parts, 0, (ff_blk, o_blk), 256)
+        g_act = grad_start([(act_t, act_recv, dy_all, dy_recv, ff_blk, 0)], h_picked)
+        d_act, d_attn = nn_pieces(after(pos, g_act[3][0]), dy_all, ws_parts, 0, (ff_blk, o_blk), 256)
         d_attn_other = swap_c(my_rows(d_attn, False))
-        g_act = grad_start([(act_t, act_recv, dy_all, dy_recv, ff_blk, 0)], d_attn)
-        d_gate_up, d_gate_up_t = act_bwd(gate_up, after(d_act, g_act[3][0]))
+        d_gate_up, d_gate_up_t = act_bwd(gate_up, d_act)
         d_gate_up_recv = swap_c(d_gate_up_t)
         d_queries, keep, send = attn_bwd(after(pos, d_gate_up_t), qkv_seq, d_attn, d_attn_other, cos_tab, sin_tab)
         got = swap_y(send)
@@ -777,8 +777,6 @@
         g_gate = grad_pass(g_gate, dh_part)
         g_up = grad_start([(d_gate_up_t, d_gate_up_recv, h_all, h_recv, ff_blk, 1)], *g_gate[3])
         b_act = grad_back(g_act, g_up[3][0])
-        d_h = d_h.astype(BF16)
-        dx_out = (dy_in[0].astype(F32) + norm_pull(d_h.astype(F32))[0]).astype(BF16)[None]
 
         attn_t = both_rows(attn_own, attn_got).T
         d_qkv_t = both_rows(d_own, d_got).T
@@ -793,7 +791,9 @@
         dw_down = place(pos, *b_act, ff_blk, 0, False)
         dw_gate = place(pos, *b_gate, ff_blk, 0, True)
         dw_up = place(pos, *b_up, ff_blk, 0, True)
-        dw_out, dw_qkv = place_attn(after(pos, dx_out, dw_up), *b_attn, o_blk, head)
+        dw_out, dw_qkv = place_attn(after(pos, dw_up), *b_attn, o_blk, head)
+        d_h = after(d_h, dw_out).astype(BF16)
+        dx_out = (dy_in[0].astype(F32) + norm_pull(d_h.astype(F32))[0]).astype(BF16)[None]
         return y_out, dx_out, dw_qkv, dw_out, dw_gate, dw_up, dw_down
 
 

time: 669 us -> 674 us (level)
  waiting for transfers between devices: 257 us -> 289 us
  starting transfers between devices: 124 us -> 105 us
  other arithmetic: 39.8 us -> 29 us
    ppermute x36, waiting for transfers between devices: 142 us -> 168 us  [hop_z(): return lax.ppermute(val, 'z', ring(step, NZ))]
    ppermute x12, starting transfers between devices: 54.3 us -> 45.6 us  [turn(): return lax.ppermute(val, ('y', 'c'), pairs)]
    ppermute x36, starting transfers between devices: 42.8 us -> 34.6 us  [hop_z(): return lax.ppermute(val, 'z', ring(step, NZ))]
    unnamed x118 -> x130, local copies, waits for them, and re-layouts: 11.4 us -> 13.7 us
  transfers between devices with their start and end apart: 81 -> 81, of which waited for: 30 -> 34; matrix products, arithmetic and copies ran while one was open for 8% -> 5% of each run, Pallas kernels for 25% -> 25%
where the time goes in v11:
time: 674 us; the launch traced here: 664 us
  waiting for transfers between devices  289 us (43%)
  Pallas kernels  200 us (30%)
  starting transfers between devices  105 us (16%)
  other arithmetic  29 us (4%)
  local copies, waits for them, and re-layouts  25.8 us (4%)
  between operations  15.3 us (2%)
    ppermute x36, waiting for transfers between devices, hop_z(): return lax.ppermute(val, 'z', ring(step, NZ))  168 us
    ppermute x12, waiting for transfers between devices, turn(): return lax.ppermute(val, ('y', 'c'), pairs)  107 us
    pallas_call x4, Pallas kernels, grad_pieces(): pl.pallas_call(functools.partial(grad_kernel, heights), grid_spec=pltpu.P...  53.5 us
    pallas_call x3, Pallas kernels, nn_pieces(): pl.pallas_call(functools.partial(nn_kernel, keys, 2, len(widths), tile, f...  50.6 us
    ppermute x12, starting transfers between devices, turn(): return lax.ppermute(val, ('y', 'c'), pairs)  45.6 us
    pallas_call x2, Pallas kernels, nt_pieces(): pl.pallas_call(functools.partial(nt_kernel, keys, sides, first_row), grid...  43.8 us
    ppermute x36, starting transfers between devices, hop_z(): return lax.ppermute(val, 'z', ring(step, NZ))  34.6 us
    ppermute x26, starting transfers between devices, swap_c(): return lax.ppermute(val, 'c', [(0, 1), (1, 0)])  20.4 us
  transfers between devices with their start and end apart: 81, of which 34 were waited for; matrix products, arithmetic and copies ran while one was open for 5% of the time, Pallas kernels for 25%

profile of v11, /device:TPU:1, one launch (start us, length us, event | category | flops | bytes accessed | tf_op | source)
XLA Modules:
  0.0 663.7 jit_solution(10840310796465861624)
XLA Ops:
  12.1 4.1 collective-permute-start
  19.8 9.6 %collective-permute-done.refs_1_.refs_4_ = bf16[256,2176]{1,0:T(8,128)(2,1)S(1)} collective-permute-done((bf16[256,2176]{1,0:T(8,128)(2,1)S(1)}, bf16[256,2176]{1,0:T(8,128)(2,1)S(1)}, u32[]{:S(2)}, u32[]{:S(2)}) %collective-permute-start) | collective-permute-done | bytes 1114144 | tf_op jit(solution)/shard_map/ppermute | solution.py:639
  30.2 3.8 collective-permute-start.1
  39.8 23.9 %collective-permute-done.1.refs_0_.refs_3_ = bf16[256,2176]{1,0:T(8,128)(2,1)S(1)} collective-permute-done((bf16[256,2176]{1,0:T(8,128)(2,1)}, bf16[256,2176]{1,0:T(8,128)(2,1)S(1)}, u32[]{:S(2)}, u32[]{:S(2)}) %collective-permute-start.1) | collective-permute-done | bytes 1114144 | tf_op jit(solution)/shard_map/ppermute | solution.py:639
  68.9 4.7 collective-permute-start.20
  73.5 20.2 %collective-permute-done.20.refs_3_.refs_0_ = bf16[256,1152]{1,0:T(8,128)(2,1)} collective-permute-done((bf16[256,1152]{1,0:T(8,128)(2,1)S(1)}, bf16[256,1152]{1,0:T(8,128)(2,1)}, u32[]{:S(2)}, u32[]{:S(2)}) %collective-permute-start.20) | collective-permute-done | bytes 589856 | tf_op jit(solution)/shard_map/ppermute | solution.py:639
  94.4 15.1 %collective-permute-done.5.refs_5_.refs_8_ = bf16[256,2176]{1,0:T(8,128)(2,1)S(1)} collective-permute-done((bf16[256,2176]{1,0:T(8,128)(2,1)S(1)}, bf16[256,2176]{1,0:T(8,128)(2,1)S(1)}, u32[]{:S(2)}, u32[]{:S(2)}) %collective-permute-start.5) | collective-permute-done | bytes 1114144 | tf_op jit(solution)/shard_map/ppermute | solution.py:623
  112.0 8.4 %collective-permute-done.9.refs_9_.refs_16_ = bf16[256,2176]{1,0:T(8,128)(2,1)S(1)} collective-permute-done((bf16[256,2176]{1,0:T(8,128)(2,1)S(1)}, bf16[256,2176]{1,0:T(8,128)(2,1)S(1)}, u32[]{:S(2)}, u32[]{:S(2)}) %collective-permute-start.9) | collective-permute-done | bytes 1114144 | tf_op jit(solution)/shard_map/ppermute | solution.py:623
  121.0 12.5 %collective-permute-done.12.refs_12_.refs_11_ = bf16[256,2176]{1,0:T(8,128)(2,1)S(1)} collective-permute-done((bf16[256,2176]{1,0:T(8,128)(2,1)S(1)}, bf16[256,2176]{1,0:T(8,128)(2,1)S(1)}, u32[]{:S(2)}, u32[]{:S(2)}) %collective-permute-start.12) | collective-permute-done | bytes 1114144 | tf_op jit(solution)/shard_map/ppermute | solution.py:623
  140.9 9.6 %shard_map.153.own_ref = bf16[1024,384]{1,0:T(8,128)(2,1)} custom-call(s32[4]{0:T(128)} %pad_add_fusion.pos_ref, bf16[1024,4096]{1,0:T(8,128)(2,1)} %all-gather.3.cloned.1.call-done.acts_ref.in_ref.refs_2_.refs_6_, bf16[256,2176]{1,0:T(8,128)(2,1)} %copy-done.1, bf16[256,2176]{1,0:T(8,128)(2,1)} %copy-done, bf16[256,2176]{1,0:T(8,128)(2,1)} %copy-done.4, ...), custom_call_target="tpu_custom_call" | custom-call | flops 161061280 | bytes 11534336 | tf_op jit(solution)/shard_map/pallas_call | solution.py:331
  158.1 4.8 collective-permute-done.28.refs_15_.refs_8_
  165.4 5.1 collective-permute-done.17.own_third_ref
  172.7 23.3 %shard_map.154.ab_ref = bf16[1024,1792]{1,0:T(8,128)(2,1)} custom-call(s32[4]{0:T(128)} %pad_add_fusion.pos_ref, bf16[1024,4096]{1,0:T(8,128)(2,1)} %all-gather.3.cloned.1.call-done.acts_ref.in_ref.refs_2_.refs_6_, bf16[256,2176]{1,0:T(8,128)(2,1)} %copy-done.1, bf16[256,2176]{1,0:T(8,128)(2,1)} %copy-done, bf16[256,2176]{1,0:T(8,128)(2,1)} %copy-done.4, ...), custom_call_target="tpu_custom_call" | custom-call | flops 751619264 | bytes 23068672 | tf_op jit(solution)/shard_map/pallas_call | solution.py:331
  196.0 4.8 act_fwd.1
  200.9 5.6 shard_map.155
  214.6 16.9 %shard_map.156 = f32[1024,4096]{1,0:T(8,128)} custom-call(s32[4]{0:T(128)} %pad_add_fusion.pos_ref, bf16[16,64,896]{2,1,0:T(8,128)(2,1)} %bitcast.30, bf16[8,64,256]{2,1,0:T(8,128)(2,1)} %bitcast.33, bf16[8,64,256]{2,1,0:T(8,128)(2,1)} %bitcast.34, bf16[256,1152]{1,0:T(8,128)(2,1)} %collective-permute-done.20.refs_3_.refs_0_, ...), custom_call_target="tpu_custom_call" | custom-call | flops 483183808 | bytes 26214400 | tf_op jit(solution)/shard_map/pallas_call | solution.py:425
  231.6 4.1 shard_map.157
  235.9 9.0 %collective-permute-start.36 = (bf16[896,1024]{1,0:T(8,128)(2,1)}, bf16[896,1024]{1,0:T(8,128)(2,1)}, u32[]{:S(2)}, u32[]{:S(2)}) collective-permute-start(bf16[896,1024]{1,0:T(8,128)(2,1)} %get-tuple-element.79.refs_0_), channel_id=1, source_target_pairs={{0,1},{1,0},{2,3},{3,2},{4,5},{5,4},{6,7},{7,6},{8,9},{9,8},{10,11... | collective-permute-start | bytes 5505032 | tf_op jit(solution)/shard_map/ppermute | solution.py:627
  244.9 4.1 shard_map.158
  249.4 13.2 %grad.4 = (f32[896,256]{1,0:T(8,128)}, f32[896,256]{1,0:T(8,128)}, f32[896,256]{1,0:T(8,128)}, f32[896,256]{1,0:T(8,128)}, f32[896,256]{1,0:T(8,128)}, /*index=5...) custom-call(s32[4]{0:T(128)} %pad_add_fusion.pos_ref, bf16[896,1024]{1,0:T(8,128)(2,1)} %get-tuple-element.79.refs_0_, ...), custom_call_target="tpu_custom_call" | custom-call | flops 375809632 | bytes 8388608 | tf_op jit(solution)/shard_map/grad/pallas_call | solution.py:538
  262.6 17.7 %shard_map.159 = (bf16[1024,896]{1,0:T(8,128)(2,1)}, bf16[1024,256]{1,0:T(8,128)(2,1)}) custom-call(s32[4]{0:T(128)} %pad_add_fusion.pos_ref, bf16[1024,4096]{1,0:T(8,128)(2,1)} %all-gather.5.cloned.1.call-done.in_ref.refs_2_.acts_ref, bf16[256,1152]{1,0:T(8,128)(2,1)} %collective-permute-done.20.refs_3_.refs_0_, ...), custom_call_target="tpu_custom_call" | custom-call | flops 483183808 | bytes 17825792 | tf_op jit(solution)/shard_map/pallas_call | solution.py:331
  280.3 7.0 %act_bwd.1 = (bf16[1024,1792]{1,0:T(8,128)(2,1)}, bf16[1792,1024]{1,0:T(8,128)(2,1)}) custom-call(bf16[1024,1792]{1,0:T(8,128)(2,1)} %shard_map.154.ab_ref, bf16[1024,896]{1,0:T(8,128)(2,1)} %get-tuple-element.91.du_ref), custom_call_target="tpu_custom_call" | custom-call | flops 400000000 | bytes 14000000 | tf_op jit(solution)/shard_map/act_bwd/pallas_call | solution.py:260
  295.0 8.1 %shard_map.160 = (bf16[2,512,256]{2,1,0:T(8,128)(2,1)}, f32[2,512,128]{2,1,0:T(8,128)}, f32[2,512,128]{2,1,0:T(8,128)}) custom-call(s32[4]{0:T(128)} %pad_add_fusion.pos_ref, bf16[2,512,512]{2,1,0:T(8,128)(2,1)} %get-tuple-element.97.seq_ref, bf16[1024,256]{1,0:T(8,128)(2,1)} %get-tuple-element.98.own_ref, bf16[512,256]{1,0:T(8,128)(2,1)} %copy-done.60, ...), custom_call_target="tpu_custom_call" | custom-call | flops 800000000 | bytes 4000000 | tf_op jit(solution)/shard_map/pallas_call | solution.py:142
  304.9 5.6 collective-permute-done.38
  315.3 13.2 %grad.5 = (f32[896,256]{1,0:T(8,128)}, f32[896,256]{1,0:T(8,128)}, f32[896,256]{1,0:T(8,128)}, f32[896,256]{1,0:T(8,128)}, f32[896,256]{1,0:T(8,128)}, /*index=5...) custom-call(s32[4]{0:T(128)} %pad_add_fusion.pos_ref, bf16[1792,1024]{1,0:T(8,128)(2,1)} %get-tuple-element.95.refs_0_, ...), custom_call_target="tpu_custom_call" | custom-call | flops 375809632 | bytes 8388608 | tf_op jit(solution)/shard_map/grad/pallas_call | solution.py:538
  337.1 26.9 %shard_map.162 = f32[1024,4096]{1,0:T(8,128)} custom-call(s32[4]{0:T(128)} %pad_add_fusion.pos_ref, bf16[16,64,1792]{2,1,0:T(8,128)(2,1)} %bitcast.28, bf16[8,64,384]{2,1,0:T(8,128)(2,1)} %bitcast.31, bf16[8,64,384]{2,1,0:T(8,128)(2,1)} %bitcast.32, bf16[256,2176]{1,0:T(8,128)(2,1)} %copy-done.1, bf16[256,2176]{1,0:T(8,128)(2,1)} %copy-done, ...), custom_call_target="tpu_custom_call" | custom-call | flops 912680576 | bytes 34603008 | tf_op jit(solution)/shard_map/pallas_call | solution.py:425
  371.0 16.1 %collective-permute-done.72 = f32[896,256]{1,0:T(8,128)S(1)} collective-permute-done((f32[896,256]{1,0:T(8,128)}, f32[896,256]{1,0:T(8,128)S(1)}, u32[]{:S(2)}, u32[]{:S(2)}) %collective-permute-start.72) | collective-permute-done | bytes 917536 | tf_op jit(solution)/shard_map/ppermute | solution.py:623
  390.1 16.6 %collective-permute-done.46 = f32[896,256]{1,0:T(8,128)S(1)} collective-permute-done((f32[896,256]{1,0:T(8,128)}, f32[896,256]{1,0:T(8,128)S(1)}, u32[]{:S(2)}, u32[]{:S(2)}) %collective-permute-start.46) | collective-permute-done | bytes 917536 | tf_op jit(solution)/shard_map/ppermute | solution.py:623
  410.6 13.6 %grad.6 = (f32[896,256]{1,0:T(8,128)}, f32[896,256]{1,0:T(8,128)}, f32[896,256]{1,0:T(8,128)}, f32[896,256]{1,0:T(8,128)}, f32[896,256]{1,0:T(8,128)}, /*index=5...) custom-call(s32[4]{0:T(128)} %pad_add_fusion.pos_ref, bf16[1792,1024]{1,0:T(8,128)(2,1)} %get-tuple-element.95.refs_0_, ...), custom_call_target="tpu_custom_call" | custom-call | flops 375809632 | bytes 8388608 | tf_op jit(solution)/shard_map/grad/pallas_call | solution.py:538
  424.2 13.6 %grad.7 = (f32[640,256]{1,0:T(8,128)}, f32[640,256]{1,0:T(8,128)}, f32[640,256]{1,0:T(8,128)}, f32[640,256]{1,0:T(8,128)}, f32[640,256]{1,0:T(8,128)}, /*index=5...) custom-call(s32[4]{0:T(128)} %pad_add_fusion.pos_ref, bf16[256,1024]{1,0:T(8,128)(2,1)} %copy-done.20, ...), custom_call_target="tpu_custom_call" | custom-call | flops 268435456 | bytes 8388608 | tf_op jit(solution)/shard_map/grad/pallas_call | solution.py:538
  441.3 4.7 collective-permute-done.66
  449.3 13.7 %collective-permute-done.57 = f32[640,256]{1,0:T(8,128)S(1)} collective-permute-done((f32[640,256]{1,0:T(8,128)}, f32[640,256]{1,0:T(8,128)S(1)}, u32[]{:S(2)}, u32[]{:S(2)}) %collective-permute-start.57) | collective-permute-done | bytes 655392 | tf_op jit(solution)/shard_map/ppermute | solution.py:623
  464.2 18.5 %collective-permute-done.47 = f32[896,256]{1,0:T(8,128)S(1)} collective-permute-done((f32[896,256]{1,0:T(8,128)}, f32[896,256]{1,0:T(8,128)S(1)}, u32[]{:S(2)}, u32[]{:S(2)}) %collective-permute-start.47) | collective-permute-done | bytes 917536 | tf_op jit(solution)/shard_map/ppermute | solution.py:623
  484.6 17.8 %collective-permute-done.65 = f32[896,256]{1,0:T(8,128)S(1)} collective-permute-done((f32[896,256]{1,0:T(8,128)}, f32[896,256]{1,0:T(8,128)S(1)}, u32[]{:S(2)}, u32[]{:S(2)}) %collective-permute-start.65) | collective-permute-done | bytes 917536 | tf_op jit(solution)/shard_map/ppermute | solution.py:623
  508.8 7.7 %collective-permute-done.58 = f32[640,256]{1,0:T(8,128)S(1)} collective-permute-done((f32[640,256]{1,0:T(8,128)S(1)}, f32[640,256]{1,0:T(8,128)S(1)}, u32[]{:S(2)}, u32[]{:S(2)}) %collective-permute-start.58) | collective-permute-done | bytes 655392 | tf_op jit(solution)/shard_map/ppermute | solution.py:623
  520.6 16.7 %collective-permute-done.59 = f32[640,256]{1,0:T(8,128)S(1)} collective-permute-done((f32[640,256]{1,0:T(8,128)S(1)}, f32[640,256]{1,0:T(8,128)S(1)}, u32[]{:S(2)}, u32[]{:S(2)}) %collective-permute-start.59) | collective-permute-done | bytes 655392 | tf_op jit(solution)/shard_map/ppermute | solution.py:623
  537.3 8.0 %collective-permute-start.76 = (f32[896,256]{1,0:T(8,128)S(1)}, f32[896,256]{1,0:T(8,128)S(1)}, u32[]{:S(2)}, u32[]{:S(2)}) collective-permute-start(f32[896,256]{1,0:T(8,128)S(1)} %add_add_fusion.1), channel_id=1, source_target_pairs={{0,8},{1,24},{8,0},{9,16},{16,9},{17,25},{24,1},{25,17},{2,10},{3,... | collective-permute-start | bytes 2752520 | tf_op jit(solution)/shard_map/ppermute | solution.py:639
  549.0 6.9 %collective-permute-done.53 = f32[896,256]{1,0:T(8,128)S(1)} collective-permute-done((f32[896,256]{1,0:T(8,128)S(1)}, f32[896,256]{1,0:T(8,128)S(1)}, u32[]{:S(2)}, u32[]{:S(2)}) %collective-permute-start.53) | collective-permute-done | bytes 917536 | tf_op jit(solution)/shard_map/ppermute | solution.py:623
  555.8 7.2 %collective-permute-start.73 = (f32[896,256]{1,0:T(8,128)S(1)}, f32[896,256]{1,0:T(8,128)S(1)}, u32[]{:S(2)}, u32[]{:S(2)}) collective-permute-start(f32[896,256]{1,0:T(8,128)S(1)} %add_add_fusion.2.own_ref), channel_id=1, source_target_pairs={{1,16},{9,24},{16,1},{24,9},{3,18},{11,26},{18,3},{26,11},{5,20},{... | collective-permute-start | bytes 2752520 | tf_op jit(solution)/shard_map/ppermute | solution.py:639
  570.8 5.9 collective-permute-start.52
  578.2 5.8 collective-permute-done.73.first_ref
  584.0 4.5 collective-permute-start.60
  588.5 29.8 %collective-permute-done.67.first_ref = f32[896,256]{1,0:T(8,128)S(1)} collective-permute-done((f32[896,256]{1,0:T(8,128)S(1)}, f32[896,256]{1,0:T(8,128)S(1)}, u32[]{:S(2)}, u32[]{:S(2)}) %collective-permute-start.67) | collective-permute-done | bytes 917536 | tf_op jit(solution)/shard_map/ppermute | solution.py:639
  621.2 3.7 shard_map.165
  624.9 4.0 shard_map.164
  628.9 9.2 %collective-permute-done.52.first_ref = f32[896,256]{1,0:T(8,128)} collective-permute-done((f32[896,256]{1,0:T(8,128)}, f32[896,256]{1,0:T(8,128)}, u32[]{:S(2)}, u32[]{:S(2)}) %collective-permute-start.52) | collective-permute-done | bytes 917536 | tf_op jit(solution)/shard_map/ppermute | solution.py:639
  638.1 4.0 shard_map.163
  642.0 6.2 collective-permute-done.60.first_ref
  (315 shorter events, 133.1 us)
Async XLA Ops:
  7.2 133.7 %all-gather.3.cloned.1.call-start = ((), (), s32[]{:S(2)}) async-start(), calls=%async_computation.2 | async-start | bytes 8912896 | tf_op jit(solution)/shard_map/all_gather | solution.py:741
  29.4 202.2 %all-gather.5.cloned.1.call-start = ((), (), s32[]{:S(2)}) async-start(), calls=%async_computation.4 | async-start | bytes 8912896 | tf_op jit(solution)/shard_map/all_gather | solution.py:742
  30.2 622.0 %reduce-scatter.5.cloned.1.call-start = ((), (), s32[]{:S(2)}) async-start(), calls=%async_computation.5 | async-start | bytes 17825792 | tf_op jit(solution)/shard_map/reduce_scatter | solution.py:776
  30.2 33.4 %collective-permute-start.1 = (bf16[256,2176]{1,0:T(8,128)(2,1)}, bf16[256,2176]{1,0:T(8,128)(2,1)S(1)}, u32[]{:S(2)}, u32[]{:S(2)}) collective-permute-start(bf16[256,2176]{1,0:T(8,128)(2,1)} %get-tuple-element.145), channel_id=1, source_target_pairs={{0,0},{1,16},{8,8},{9,24},{16,1},{17,17},{24,9},{25,25},{2,2},{3,1... | collective-permute-start | bytes 3342344 | tf_op jit(solution)/shard_map/ppermute | solution.py:639
  38.6 30.2 %collective-permute-start.21 = (bf16[256,1152]{1,0:T(8,128)(2,1)S(1)}, bf16[256,1152]{1,0:T(8,128)(2,1)}, u32[]{:S(2)}, u32[]{:S(2)}) collective-permute-start(bf16[256,1152]{1,0:T(8,128)(2,1)S(1)} %get-tuple-element.147), channel_id=1, source_target_pairs={{0,8},{1,24},{8,0},{9,16},{16,9},{17,25},{24,1},{25,17},{2,10},{3,... | collective-permute-start | bytes 1769480 | tf_op jit(solution)/shard_map/ppermute | solution.py:639
  63.6 30.1 %collective-permute-start.8 = (bf16[256,2176]{1,0:T(8,128)(2,1)S(1)}, bf16[256,2176]{1,0:T(8,128)(2,1)S(1)}, u32[]{:S(2)}, u32[]{:S(2)}) collective-permute-start(bf16[256,2176]{1,0:T(8,128)(2,1)S(1)} %collective-permute-done.1.refs_0_.refs_3_), channel_id=1, source_target_pairs={{0,32},{32,64},{64,96},{96,0},{1,33},{33,65},{65,97},{97,1},{2,34}... | collective-permute-start | bytes 3342344 | tf_op jit(solution)/shard_map/ppermute | solution.py:623
  65.3 28.5 %collective-permute-start.4 = (bf16[256,2176]{1,0:T(8,128)(2,1)S(1)}, bf16[256,2176]{1,0:T(8,128)(2,1)S(1)}, u32[]{:S(2)}, u32[]{:S(2)}) collective-permute-start(bf16[256,2176]{1,0:T(8,128)(2,1)S(1)} %collective-permute-done.1.refs_0_.refs_3_), channel_id=1, source_target_pairs={{0,96},{32,0},{64,32},{96,64},{1,97},{33,1},{65,33},{97,65},{2,98}... | collective-permute-start | bytes 3342344 | tf_op jit(solution)/shard_map/ppermute | solution.py:623
  67.4 26.5 %collective-permute-start.2 = (bf16[256,2176]{1,0:T(8,128)(2,1)S(1)}, bf16[256,2176]{1,0:T(8,128)(2,1)S(1)}, u32[]{:S(2)}, u32[]{:S(2)}) collective-permute-start(bf16[256,2176]{1,0:T(8,128)(2,1)S(1)} %collective-permute-done.1.refs_0_.refs_3_), channel_id=1, source_target_pairs={{0,1},{1,0},{2,3},{3,2},{4,5},{5,4},{6,7},{7,6},{8,9},{9,8},{10,11... | collective-permute-start | bytes 3342344 | tf_op jit(solution)/shard_map/ppermute | solution.py:627
  67.4 42.1 %collective-permute-start.5 = (bf16[256,2176]{1,0:T(8,128)(2,1)S(1)}, bf16[256,2176]{1,0:T(8,128)(2,1)S(1)}, u32[]{:S(2)}, u32[]{:S(2)}) collective-permute-start(bf16[256,2176]{1,0:T(8,128)(2,1)S(1)} %collective-permute-done.refs_1_.refs_4_), channel_id=1, source_target_pairs={{0,96},{32,0},{64,32},{96,64},{1,97},{33,1},{65,33},{97,65},{2,98}... | collective-permute-start | bytes 3342344 | tf_op jit(solution)/shard_map/ppermute | solution.py:623
  93.7 26.7 %collective-permute-start.9 = (bf16[256,2176]{1,0:T(8,128)(2,1)S(1)}, bf16[256,2176]{1,0:T(8,128)(2,1)S(1)}, u32[]{:S(2)}, u32[]{:S(2)}) collective-permute-start(bf16[256,2176]{1,0:T(8,128)(2,1)S(1)} %collective-permute-done.refs_1_.refs_4_), channel_id=1, source_target_pairs={{0,32},{32,64},{64,96},{96,0},{1,33},{33,65},{65,97},{97,1},{2,34}... | collective-permute-start | bytes 3342344 | tf_op jit(solution)/shard_map/ppermute | solution.py:623
  93.7 26.7 %collective-permute-start.3 = (bf16[256,2176]{1,0:T(8,128)(2,1)S(1)}, bf16[256,2176]{1,0:T(8,128)(2,1)S(1)}, u32[]{:S(2)}, u32[]{:S(2)}) collective-permute-start(bf16[256,2176]{1,0:T(8,128)(2,1)S(1)} %collective-permute-done.refs_1_.refs_4_), channel_id=1, source_target_pairs={{0,1},{1,0},{2,3},{3,2},{4,5},{5,4},{6,7},{7,6},{8,9},{9,8},{10,11... | collective-permute-start | bytes 3342344 | tf_op jit(solution)/shard_map/ppermute | solution.py:627
  93.8 39.7 %collective-permute-start.12 = (bf16[256,2176]{1,0:T(8,128)(2,1)S(1)}, bf16[256,2176]{1,0:T(8,128)(2,1)S(1)}, u32[]{:S(2)}, u32[]{:S(2)}) collective-permute-start(bf16[256,2176]{1,0:T(8,128)(2,1)S(1)} %collective-permute-done.8.refs_8_.refs_15_), channel_id=1, source_target_pairs={{0,32},{32,64},{64,96},{96,0},{1,33},{33,65},{65,97},{97,1},{2,34}... | collective-permute-start | bytes 3342344 | tf_op jit(solution)/shard_map/ppermute | solution.py:623
  93.9 39.6 %collective-permute-start.10 = (bf16[256,2176]{1,0:T(8,128)(2,1)S(1)}, bf16[256,2176]{1,0:T(8,128)(2,1)S(1)}, u32[]{:S(2)}, u32[]{:S(2)}) collective-permute-start(bf16[256,2176]{1,0:T(8,128)(2,1)S(1)} %collective-permute-done.8.refs_8_.refs_15_), channel_id=1, source_target_pairs={{0,1},{1,0},{2,3},{3,2},{4,5},{5,4},{6,7},{7,6},{8,9},{9,8},{10,11... | collective-permute-start | bytes 3342344 | tf_op jit(solution)/shard_map/ppermute | solution.py:627
  152.0 55.5 %collective-permute-start.24 = (bf16[256,1152]{1,0:T(8,128)(2,1)}, bf16[256,1152]{1,0:T(8,128)(2,1)}, u32[]{:S(2)}, u32[]{:S(2)}) collective-permute-start(bf16[256,1152]{1,0:T(8,128)(2,1)} %collective-permute-done.20.refs_3_.refs_0_), channel_id=1, source_target_pairs={{0,96},{32,0},{64,32},{96,64},{1,97},{33,1},{65,33},{97,65},{2,98}... | collective-permute-start | bytes 1769480 | tf_op jit(solution)/shard_map/ppermute | solution.py:623
  162.9 46.0 %collective-permute-start.22 = (bf16[256,1152]{1,0:T(8,128)(2,1)}, bf16[256,1152]{1,0:T(8,128)(2,1)}, u32[]{:S(2)}, u32[]{:S(2)}) collective-permute-start(bf16[256,1152]{1,0:T(8,128)(2,1)} %collective-permute-done.20.refs_3_.refs_0_), channel_id=1, source_target_pairs={{0,1},{1,0},{2,3},{3,2},{4,5},{5,4},{6,7},{7,6},{8,9},{9,8},{10,11... | collective-permute-start | bytes 1769480 | tf_op jit(solution)/shard_map/ppermute | solution.py:627
  165.4 43.6 %collective-permute-start.35 = (bf16[256,1152]{1,0:T(8,128)(2,1)}, bf16[256,1152]{1,0:T(8,128)(2,1)}, u32[]{:S(2)}, u32[]{:S(2)}) collective-permute-start(bf16[256,1152]{1,0:T(8,128)(2,1)} %collective-permute-done.33.refs_16_.refs_9_), channel_id=1, source_target_pairs={{0,1},{1,0},{2,3},{3,2},{4,5},{5,4},{6,7},{7,6},{8,9},{9,8},{10,11... | collective-permute-start | bytes 1769480 | tf_op jit(solution)/shard_map/ppermute | solution.py:627
  170.5 38.9 %collective-permute-start.30 = (bf16[256,1152]{1,0:T(8,128)(2,1)}, bf16[256,1152]{1,0:T(8,128)(2,1)}, u32[]{:S(2)}, u32[]{:S(2)}) collective-permute-start(bf16[256,1152]{1,0:T(8,128)(2,1)} %collective-permute-done.25.refs_8_.refs_5_), channel_id=1, source_target_pairs={{0,96},{32,0},{64,32},{96,64},{1,97},{33,1},{65,33},{97,65},{2,98}... | collective-permute-start | bytes 1769480 | tf_op jit(solution)/shard_map/ppermute | solution.py:623
  171.9 37.6 %collective-permute-start.29 = (bf16[256,1152]{1,0:T(8,128)(2,1)}, bf16[256,1152]{1,0:T(8,128)(2,1)}, u32[]{:S(2)}, u32[]{:S(2)}) collective-permute-start(bf16[256,1152]{1,0:T(8,128)(2,1)} %collective-permute-done.28.refs_15_.refs_8_), channel_id=1, source_target_pairs={{0,32},{32,64},{64,96},{96,0},{1,33},{33,65},{65,97},{97,1},{2,34}... | collective-permute-start | bytes 1769480 | tf_op jit(solution)/shard_map/ppermute | solution.py:623
  249.0 66.3 %collective-permute-start.42 = (bf16[1024,2048]{1,0:T(8,128)(2,1)}, bf16[1024,2048]{1,0:T(8,128)(2,1)}, u32[]{:S(2)}, u32[]{:S(2)}) collective-permute-start(bf16[1024,2048]{1,0:T(8,128)(2,1)} %shard_map.158), channel_id=1, source_target_pairs={{0,1},{1,0},{2,3},{3,2},{4,5},{5,4},{6,7},{7,6},{8,9},{9,8},{10,11... | collective-permute-start | bytes 12582920 | tf_op jit(solution)/shard_map/ppermute | solution.py:627
  287.3 28.0 %collective-permute-start.41 = (bf16[1792,1024]{1,0:T(8,128)(2,1)}, bf16[1792,1024]{1,0:T(8,128)(2,1)}, u32[]{:S(2)}, u32[]{:S(2)}) collective-permute-start(bf16[1792,1024]{1,0:T(8,128)(2,1)} %get-tuple-element.95.refs_0_), channel_id=1, source_target_pairs={{0,1},{1,0},{2,3},{3,2},{4,5},{5,4},{6,7},{7,6},{8,9},{9,8},{10,11... | collective-permute-start | bytes 11010056 | tf_op jit(solution)/shard_map/ppermute | solution.py:627
  364.1 289.9 %reduce-scatter.3.cloned.1.call-start = ((), (), s32[]{:S(2)}) async-start(), calls=%async_computation.3 | async-start | bytes 17825792 | tf_op jit(solution)/shard_map/reduce_scatter | solution.py:757
  367.8 38.9 %collective-permute-start.46 = (f32[896,256]{1,0:T(8,128)}, f32[896,256]{1,0:T(8,128)S(1)}, u32[]{:S(2)}, u32[]{:S(2)}) collective-permute-start(f32[896,256]{1,0:T(8,128)} %get-tuple-element.114), channel_id=1, source_target_pairs={{0,96},{32,0},{64,32},{96,64},{1,97},{33,1},{65,33},{97,65},{2,98}... | collective-permute-start | bytes 2752520 | tf_op jit(solution)/shard_map/ppermute | solution.py:623
  370.4 37.9 %collective-permute-start.49 = (bf16[384,1024]{1,0:T(8,128)(2,1)S(1)}, bf16[384,1024]{1,0:T(8,128)(2,1)S(1)}, u32[]{:S(2)}, u32[]{:S(2)}) collective-permute-start(bf16[384,1024]{1,0:T(8,128)(2,1)S(1)} %maximum_bitcast_fusion.refs_4_), channel_id=1, source_target_pairs={{0,1},{1,0},{2,3},{3,2},{4,5},{5,4},{6,7},{7,6},{8,9},{9,8},{10,11... | collective-permute-start | bytes 2359304 | tf_op jit(solution)/shard_map/ppermute | solution.py:627
  371.0 66.8 %collective-permute-start.74 = (f32[896,256]{1,0:T(8,128)}, f32[896,256]{1,0:T(8,128)}, u32[]{:S(2)}, u32[]{:S(2)}) collective-permute-start(f32[896,256]{1,0:T(8,128)} %get-tuple-element.144), channel_id=1, source_target_pairs={{0,32},{32,64},{64,96},{96,0},{1,33},{33,65},{65,97},{97,1},{2,34}... | collective-permute-start | bytes 2752520 | tf_op jit(solution)/shard_map/ppermute | solution.py:623
  387.1 50.8 %collective-permute-start.75 = (f32[896,256]{1,0:T(8,128)}, f32[896,256]{1,0:T(8,128)}, u32[]{:S(2)}, u32[]{:S(2)}) collective-permute-start(f32[896,256]{1,0:T(8,128)} %add.116), channel_id=1, source_target_pairs={{0,96},{32,0},{64,32},{96,64},{1,97},{33,1},{65,33},{97,65},{2,98}... | collective-permute-start | bytes 2752520 | tf_op jit(solution)/shard_map/ppermute | solution.py:623
  390.1 48.6 %collective-permute-start.71 = (f32[896,256]{1,0:T(8,128)}, f32[896,256]{1,0:T(8,128)}, u32[]{:S(2)}, u32[]{:S(2)}) collective-permute-start(f32[896,256]{1,0:T(8,128)} %add.115), channel_id=1, source_target_pairs={{0,32},{32,64},{64,96},{96,0},{1,33},{33,65},{65,97},{97,1},{2,34}... | collective-permute-start | bytes 2752520 | tf_op jit(solution)/shard_map/ppermute | solution.py:623
  406.7 39.3 %collective-permute-start.66 = (f32[896,256]{1,0:T(8,128)}, f32[896,256]{1,0:T(8,128)}, u32[]{:S(2)}, u32[]{:S(2)}) collective-permute-start(f32[896,256]{1,0:T(8,128)} %get-tuple-element.138), channel_id=1, source_target_pairs={{0,96},{32,0},{64,32},{96,64},{1,97},{33,1},{65,33},{97,65},{2,98}... | collective-permute-start | bytes 2752520 | tf_op jit(solution)/shard_map/ppermute | solution.py:623
  408.4 40.7 %collective-permute-start.68 = (f32[896,256]{1,0:T(8,128)}, f32[896,256]{1,0:T(8,128)}, u32[]{:S(2)}, u32[]{:S(2)}) collective-permute-start(f32[896,256]{1,0:T(8,128)} %get-tuple-element.140), channel_id=1, source_target_pairs={{0,32},{32,64},{64,96},{96,0},{1,33},{33,65},{65,97},{97,1},{2,34}... | collective-permute-start | bytes 2752520 | tf_op jit(solution)/shard_map/ppermute | solution.py:623
  437.9 44.8 %collective-permute-start.47 = (f32[896,256]{1,0:T(8,128)}, f32[896,256]{1,0:T(8,128)S(1)}, u32[]{:S(2)}, u32[]{:S(2)}) collective-permute-start(f32[896,256]{1,0:T(8,128)} %get-tuple-element.118), channel_id=1, source_target_pairs={{0,32},{32,64},{64,96},{96,0},{1,33},{33,65},{65,97},{97,1},{2,34}... | collective-permute-start | bytes 2752520 | tf_op jit(solution)/shard_map/ppermute | solution.py:623
  438.8 63.7 %collective-permute-start.65 = (f32[896,256]{1,0:T(8,128)}, f32[896,256]{1,0:T(8,128)S(1)}, u32[]{:S(2)}, u32[]{:S(2)}) collective-permute-start(f32[896,256]{1,0:T(8,128)} %add.117), channel_id=1, source_target_pairs={{0,32},{32,64},{64,96},{96,0},{1,33},{33,65},{65,97},{97,1},{2,34}... | collective-permute-start | bytes 2752520 | tf_op jit(solution)/shard_map/ppermute | solution.py:623
  446.1 57.3 %collective-permute-start.54 = (f32[896,256]{1,0:T(8,128)}, f32[896,256]{1,0:T(8,128)S(1)}, u32[]{:S(2)}, u32[]{:S(2)}) collective-permute-start(f32[896,256]{1,0:T(8,128)} %get-tuple-element.126), channel_id=1, source_target_pairs={{0,96},{32,0},{64,32},{96,64},{1,97},{33,1},{65,33},{97,65},{2,98}... | collective-permute-start | bytes 2752520 | tf_op jit(solution)/shard_map/ppermute | solution.py:623
  449.1 53.4 %collective-permute-start.62 = (f32[640,256]{1,0:T(8,128)}, f32[640,256]{1,0:T(8,128)S(1)}, u32[]{:S(2)}, u32[]{:S(2)}) collective-permute-start(f32[640,256]{1,0:T(8,128)} %get-tuple-element.134), channel_id=1, source_target_pairs={{0,96},{32,0},{64,32},{96,64},{1,97},{33,1},{65,33},{97,65},{2,98}... | collective-permute-start | bytes 1966088 | tf_op jit(solution)/shard_map/ppermute | solution.py:623
  463.0 44.1 %collective-permute-start.69 = (f32[896,256]{1,0:T(8,128)}, f32[896,256]{1,0:T(8,128)S(1)}, u32[]{:S(2)}, u32[]{:S(2)}) collective-permute-start(f32[896,256]{1,0:T(8,128)} %add.118), channel_id=1, source_target_pairs={{0,96},{32,0},{64,32},{96,64},{1,97},{33,1},{65,33},{97,65},{2,98}... | collective-permute-start | bytes 2752520 | tf_op jit(solution)/shard_map/ppermute | solution.py:623
  482.7 33.8 %collective-permute-start.58 = (f32[640,256]{1,0:T(8,128)S(1)}, f32[640,256]{1,0:T(8,128)S(1)}, u32[]{:S(2)}, u32[]{:S(2)}) collective-permute-start(f32[640,256]{1,0:T(8,128)S(1)} %add.125), channel_id=1, source_target_pairs={{0,32},{32,64},{64,96},{96,0},{1,33},{33,65},{65,97},{97,1},{2,34}... | collective-permute-start | bytes 1966088 | tf_op jit(solution)/shard_map/ppermute | solution.py:623
  502.5 42.8 %collective-permute-start.51 = (f32[896,256]{1,0:T(8,128)S(1)}, f32[896,256]{1,0:T(8,128)S(1)}, u32[]{:S(2)}, u32[]{:S(2)}) collective-permute-start(f32[896,256]{1,0:T(8,128)S(1)} %copy-done.56), channel_id=1, source_target_pairs={{0,96},{32,0},{64,32},{96,64},{1,97},{33,1},{65,33},{97,65},{2,98}... | collective-permute-start | bytes 2752520 | tf_op jit(solution)/shard_map/ppermute | solution.py:623
  502.5 34.8 %collective-permute-start.59 = (f32[640,256]{1,0:T(8,128)S(1)}, f32[640,256]{1,0:T(8,128)S(1)}, u32[]{:S(2)}, u32[]{:S(2)}) collective-permute-start(f32[640,256]{1,0:T(8,128)S(1)} %copy-done.58), channel_id=1, source_target_pairs={{0,96},{32,0},{64,32},{96,64},{1,97},{33,1},{65,33},{97,65},{2,98}... | collective-permute-start | bytes 1966088 | tf_op jit(solution)/shard_map/ppermute | solution.py:623
  503.3 41.9 %collective-permute-start.50 = (f32[896,256]{1,0:T(8,128)S(1)}, f32[896,256]{1,0:T(8,128)S(1)}, u32[]{:S(2)}, u32[]{:S(2)}) collective-permute-start(f32[896,256]{1,0:T(8,128)S(1)} %add.119), channel_id=1, source_target_pairs={{0,32},{32,64},{64,96},{96,0},{1,33},{33,65},{65,97},{97,1},{2,34}... | collective-permute-start | bytes 2752520 | tf_op jit(solution)/shard_map/ppermute | solution.py:623
  507.3 48.5 %collective-permute-start.53 = (f32[896,256]{1,0:T(8,128)S(1)}, f32[896,256]{1,0:T(8,128)S(1)}, u32[]{:S(2)}, u32[]{:S(2)}) collective-permute-start(f32[896,256]{1,0:T(8,128)S(1)} %copy-done.55), channel_id=1, source_target_pairs={{0,32},{32,64},{64,96},{96,0},{1,33},{33,65},{65,97},{97,1},{2,34}... | collective-permute-start | bytes 2752520 | tf_op jit(solution)/shard_map/ppermute | solution.py:623
  516.5 46.6 %collective-permute-start.55 = (f32[896,256]{1,0:T(8,128)S(1)}, f32[896,256]{1,0:T(8,128)S(1)}, u32[]{:S(2)}, u32[]{:S(2)}) collective-permute-start(f32[896,256]{1,0:T(8,128)S(1)} %add.123), channel_id=1, source_target_pairs={{0,96},{32,0},{64,32},{96,64},{1,97},{33,1},{65,33},{97,65},{2,98}... | collective-permute-start | bytes 2752520 | tf_op jit(solution)/shard_map/ppermute | solution.py:623
  537.3 33.2 %collective-permute-start.76 = (f32[896,256]{1,0:T(8,128)S(1)}, f32[896,256]{1,0:T(8,128)S(1)}, u32[]{:S(2)}, u32[]{:S(2)}) collective-permute-start(f32[896,256]{1,0:T(8,128)S(1)} %add_add_fusion.1), channel_id=1, source_target_pairs={{0,8},{1,24},{8,0},{9,16},{16,9},{17,25},{24,1},{25,17},{2,10},{3,... | collective-permute-start | bytes 2752520 | tf_op jit(solution)/shard_map/ppermute | solution.py:639
  545.3 31.3 %collective-permute-start.63 = (f32[640,256]{1,0:T(8,128)S(1)}, f32[640,256]{1,0:T(8,128)S(1)}, u32[]{:S(2)}, u32[]{:S(2)}) collective-permute-start(f32[640,256]{1,0:T(8,128)S(1)} %add.129), channel_id=1, source_target_pairs={{0,96},{32,0},{64,32},{96,64},{1,97},{33,1},{65,33},{97,65},{2,98}... | collective-permute-start | bytes 1966088 | tf_op jit(solution)/shard_map/ppermute | solution.py:623
  555.8 28.2 %collective-permute-start.73 = (f32[896,256]{1,0:T(8,128)S(1)}, f32[896,256]{1,0:T(8,128)S(1)}, u32[]{:S(2)}, u32[]{:S(2)}) collective-permute-start(f32[896,256]{1,0:T(8,128)S(1)} %add_add_fusion.2.own_ref), channel_id=1, source_target_pairs={{1,16},{9,24},{16,1},{24,9},{3,18},{11,26},{18,3},{26,11},{5,20},{... | collective-permute-start | bytes 2752520 | tf_op jit(solution)/shard_map/ppermute | solution.py:639
  563.1 55.2 %collective-permute-start.67 = (f32[896,256]{1,0:T(8,128)S(1)}, f32[896,256]{1,0:T(8,128)S(1)}, u32[]{:S(2)}, u32[]{:S(2)}) collective-permute-start(f32[896,256]{1,0:T(8,128)S(1)} %add_add_fusion.4.own_ref), channel_id=1, source_target_pairs={{1,16},{9,24},{16,1},{24,9},{3,18},{11,26},{18,3},{26,11},{5,20},{... | collective-permute-start | bytes 2752520 | tf_op jit(solution)/shard_map/ppermute | solution.py:639
  570.4 54.4 %collective-permute-start.70 = (f32[896,256]{1,0:T(8,128)}, f32[896,256]{1,0:T(8,128)}, u32[]{:S(2)}, u32[]{:S(2)}) collective-permute-start(f32[896,256]{1,0:T(8,128)} %add_add_fusion.3), channel_id=1, source_target_pairs={{0,8},{1,24},{8,0},{9,16},{16,9},{17,25},{24,1},{25,17},{2,10},{3,... | collective-permute-start | bytes 2752520 | tf_op jit(solution)/shard_map/ppermute | solution.py:639
  570.8 67.3 %collective-permute-start.52 = (f32[896,256]{1,0:T(8,128)}, f32[896,256]{1,0:T(8,128)}, u32[]{:S(2)}, u32[]{:S(2)}) collective-permute-start(f32[896,256]{1,0:T(8,128)} %add_add_fusion.6.own_ref), channel_id=1, source_target_pairs={{1,16},{9,24},{16,1},{24,9},{3,18},{11,26},{18,3},{26,11},{5,20},{... | collective-permute-start | bytes 2752520 | tf_op jit(solution)/shard_map/ppermute | solution.py:639
  576.6 61.4 %collective-permute-start.56 = (f32[896,256]{1,0:T(8,128)}, f32[896,256]{1,0:T(8,128)}, u32[]{:S(2)}, u32[]{:S(2)}) collective-permute-start(f32[896,256]{1,0:T(8,128)} %add_add_fusion.5), channel_id=1, source_target_pairs={{0,8},{1,24},{8,0},{9,16},{16,9},{17,25},{24,1},{25,17},{2,10},{3,... | collective-permute-start | bytes 2752520 | tf_op jit(solution)/shard_map/ppermute | solution.py:639
  584.0 64.2 %collective-permute-start.60 = (f32[640,256]{1,0:T(8,128)}, f32[640,256]{1,0:T(8,128)}, u32[]{:S(2)}, u32[]{:S(2)}) collective-permute-start(f32[640,256]{1,0:T(8,128)} %add_add_fusion.8.own_ref), channel_id=1, source_target_pairs={{1,16},{9,24},{16,1},{24,9},{3,18},{11,26},{18,3},{26,11},{5,20},{... | collective-permute-start | bytes 1966088 | tf_op jit(solution)/shard_map/ppermute | solution.py:639
  619.3 29.3 %collective-permute-start.64 = (f32[640,256]{1,0:T(8,128)}, f32[640,256]{1,0:T(8,128)}, u32[]{:S(2)}, u32[]{:S(2)}) collective-permute-start(f32[640,256]{1,0:T(8,128)} %add_add_fusion.7), channel_id=1, source_target_pairs={{0,8},{1,24},{8,0},{9,16},{16,9},{17,25},{24,1},{25,17},{2,10},{3,... | collective-permute-start | bytes 1966088 | tf_op jit(solution)/shard_map/ppermute | solution.py:639
  (96 other events, 1446.7 us)
Sparse Core Ops, SparseCore 0:
  29.5 86.2 all-gather.2
  118.0 73.3 all-gather.4
  364.2 110.2 reduce-scatter.4
  477.7 136.9 reduce-scatter.2
